TPU v7x, 32 devices: a whole 2x2x4 slice. The times are simulated.
32 devices in a mesh: cp: 32 (over z, y, x, core).
Axes of the slice: x: 2, y: 2, z: 4, core: 2. Of those that a mesh axis runs over, the one named last changes fastest.
Arguments:
- hidden: bfloat16 [4, 4096, 2048], P(None, 'cp')
- grad_out: bfloat16 [4, 4096, 2048], P(None, 'cp')
- positions: int32 [4, 4096], P(None, 'cp')
- seg_ids: int32 [4, 4096], P(None, 'cp')
- w_q: bfloat16 [2048, 2048], replicated
- w_k: bfloat16 [2048, 256], replicated
- w_v: bfloat16 [2048, 256], replicated
- w_o: bfloat16 [2048, 2048], replicated
- norm_gain: bfloat16 [2048], replicated
Outputs:
- output 1: bfloat16 [4, 4096, 2048], P(None, 'cp')
- output 2: bfloat16 [4, 4096, 2048], P(None, 'cp')
- output 3: float32 [2048, 2048], replicated
- output 4: float32 [2048, 256], replicated
- output 5: float32 [2048, 256], replicated
- output 6: float32 [2048, 2048], replicated
- output 7: float32 [2048], replicated
All inputs are finite; a program needn't handle non-finite values.
Results may differ from a plain program's by a relative error of at most 0.0143505.
Values are sent between devices in bfloat16 or wider.
A program may use at most 1 GiB of HBM per device.

v0:
```python
import jax
import jax.numpy as jnp
from jax import lax
from jax.sharding import PartitionSpec as P

HEAD_DIM = 128
NORM_EPS = 1e-5
ROPE_BASE = 500000.0
NEG_BIG = -1e30


def norm_apply(hidden_f32, gain_f32):
    inv_rms = lax.rsqrt(jnp.mean(hidden_f32 * hidden_f32, axis=-1, keepdims=True) + NORM_EPS)
    return (hidden_f32 * inv_rms * gain_f32).astype(jnp.bfloat16)


def rope_tables(positions):
    inv_freq = ROPE_BASE ** (-jnp.arange(0, HEAD_DIM, 2).astype(jnp.float32) / HEAD_DIM)
    angles = positions.astype(jnp.float32)[..., None] * inv_freq
    angles = jnp.concatenate([angles, angles], axis=-1)
    return jnp.cos(angles), jnp.sin(angles)


def rotate(proj_in, cos_t, sin_t):
    half_dim = proj_in.shape[-1] // 2
    turned = jnp.concatenate([-proj_in[..., half_dim:], proj_in[..., :half_dim]], axis=-1)
    return proj_in * cos_t + turned * sin_t


def global_index(n_dev, chunk_len):
    chunk_slots = jnp.arange(2 * n_dev)
    owner_rank = chunk_slots // 2
    glob_chunk = jnp.where(chunk_slots % 2 == 0, owner_rank, 2 * n_dev - 1 - owner_rank)
    return (glob_chunk[:, None] * chunk_len + jnp.arange(chunk_len)[None, :]).reshape(-1)


def project(hidden, positions, w_q, w_k, w_v, norm_gain):
    n_batch, n_tok, d_model = hidden.shape
    kv_heads = w_k.shape[1] // HEAD_DIM
    group_size = w_q.shape[1] // (kv_heads * HEAD_DIM)
    hidden_f32 = hidden.astype(jnp.float32)
    normed, norm_pull = jax.vjp(norm_apply, hidden_f32, norm_gain.astype(jnp.float32))
    normed_flat = normed.reshape(n_batch * n_tok, d_model)
    cos_t, sin_t = rope_tables(positions)
    q_lin = jnp.dot(normed_flat, w_q, preferred_element_type=jnp.float32).reshape(n_batch, n_tok, kv_heads, group_size, HEAD_DIM)
    k_lin = jnp.dot(normed_flat, w_k, preferred_element_type=jnp.float32).reshape(n_batch, n_tok, kv_heads, HEAD_DIM)
    queries = rotate(q_lin, cos_t[:, :, None, None], sin_t[:, :, None, None]).astype(jnp.bfloat16)
    keys_loc = rotate(k_lin, cos_t[:, :, None], sin_t[:, :, None]).astype(jnp.bfloat16)
    values_loc = jnp.dot(normed_flat, w_v, preferred_element_type=jnp.float32).astype(jnp.bfloat16).reshape(n_batch, n_tok, kv_heads, HEAD_DIM)
    return hidden_f32, normed_flat, norm_pull, cos_t, sin_t, queries, keys_loc, values_loc


def finish_backward(grad_out, normed_flat, norm_pull, dq_flat, dk_flat, dv_flat, w_q, w_k, w_v):
    grad_wq = lax.psum(jnp.einsum('nd,nk->dk', normed_flat, dq_flat, preferred_element_type=jnp.float32), 'cp')
    grad_wk = lax.psum(jnp.einsum('nd,nk->dk', normed_flat, dk_flat, preferred_element_type=jnp.float32), 'cp')
    grad_wv = lax.psum(jnp.einsum('nd,nk->dk', normed_flat, dv_flat, preferred_element_type=jnp.float32), 'cp')
    d_normed = (jnp.einsum('nk,dk->nd', dq_flat, w_q, preferred_element_type=jnp.float32) + jnp.einsum('nk,dk->nd', dk_flat, w_k, preferred_element_type=jnp.float32) + jnp.einsum('nk,dk->nd', dv_flat, w_v, preferred_element_type=jnp.float32)).astype(jnp.bfloat16).reshape(grad_out.shape)
    d_hidden, d_gain = norm_pull(d_normed)
    grad_hidden = (grad_out.astype(jnp.float32) + d_hidden).astype(jnp.bfloat16)
    return grad_hidden, grad_wq, grad_wk, grad_wv, lax.psum(d_gain, 'cp')


def solution(mesh):
    n_dev = mesh.shape['cp']
    attn_scale = HEAD_DIM ** -0.5

    def local_step(hidden, grad_out, positions, seg_ids, w_q, w_k, w_v, w_o, norm_gain):
        n_batch, n_tok, d_model = hidden.shape
        chunk_len = n_tok // 2
        my_rank = lax.axis_index('cp')
        glob_all = global_index(n_dev, chunk_len)
        glob_local = lax.dynamic_slice_in_dim(glob_all, my_rank * n_tok, n_tok)
        hidden_f32, normed_flat, norm_pull, cos_t, sin_t, queries, keys_loc, values_loc = project(hidden, positions, w_q, w_k, w_v, norm_gain)
        keys_all = lax.all_gather(keys_loc, 'cp', axis=1, tiled=True)
        values_all = lax.all_gather(values_loc, 'cp', axis=1, tiled=True)
        seg_all = lax.all_gather(seg_ids, 'cp', axis=1, tiled=True)
        allowed = ((seg_ids[:, :, None] == seg_all[:, None, :]) & (glob_local[:, None] >= glob_all[None, :])[None])[:, None]
        queries_t = jnp.moveaxis(queries, 2, 0)
        keys_t = jnp.moveaxis(keys_all, 2, 0)
        values_t = jnp.moveaxis(values_all, 2, 0)

        def masked_scores(query_h, key_h):
            scores = jnp.einsum('btgd,bsd->bgts', query_h, key_h, preferred_element_type=jnp.float32) * attn_scale
            return jnp.where(allowed, scores, NEG_BIG)

        def head_forward(operands):
            query_h, key_h, value_h = operands
            scores = masked_scores(query_h, key_h)
            row_max = jnp.max(scores, axis=-1, keepdims=True)
            exp_scores = jnp.exp(scores - row_max)
            row_sum = jnp.sum(exp_scores, axis=-1, keepdims=True)
            attn_probs = (exp_scores / row_sum).astype(jnp.bfloat16)
            attn_h = jnp.einsum('bgts,bsd->btgd', attn_probs, value_h, preferred_element_type=jnp.float32)
            return attn_h.astype(jnp.bfloat16), row_max + jnp.log(row_sum)

        attn_t, lse_t = lax.map(head_forward, (queries_t, keys_t, values_t))
        attn_flat = jnp.moveaxis(attn_t, 0, 2).reshape(n_batch * n_tok, -1)
        dy_flat = grad_out.reshape(n_batch * n_tok, d_model)
        proj_out = jnp.dot(attn_flat, w_o, preferred_element_type=jnp.float32).reshape(n_batch, n_tok, d_model)
        block_out = (hidden_f32 + proj_out).astype(jnp.bfloat16)

        grad_wo = lax.psum(jnp.einsum('nk,nd->kd', attn_flat, dy_flat, preferred_element_type=jnp.float32), 'cp')
        d_attn = jnp.einsum('nd,kd->nk', dy_flat, w_o, preferred_element_type=jnp.float32).astype(jnp.bfloat16)
        d_attn_t = jnp.moveaxis(d_attn.reshape(queries.shape), 2, 0)

        def head_backward(operands):
            query_h, key_h, value_h, attn_h, d_attn_h, lse_h = operands
            attn_probs = jnp.exp(masked_scores(query_h, key_h) - lse_h)
            d_probs = jnp.einsum('btgd,bsd->bgts', d_attn_h, value_h, preferred_element_type=jnp.float32)
            delta_row = jnp.einsum('btgd,btgd->bgt', d_attn_h, attn_h, preferred_element_type=jnp.float32)[..., None]
            d_scores = (attn_probs * (d_probs - delta_row) * attn_scale).astype(jnp.bfloat16)
            d_query = jnp.einsum('bgts,bsd->btgd', d_scores, key_h, preferred_element_type=jnp.float32)
            d_key = jnp.einsum('bgts,btgd->bsd', d_scores, query_h, preferred_element_type=jnp.float32)
            d_value = jnp.einsum('bgts,btgd->bsd', attn_probs.astype(jnp.bfloat16), d_attn_h, preferred_element_type=jnp.float32)
            return d_query, d_key, d_value

        dq_t, dk_t, dv_t = lax.map(head_backward, (queries_t, keys_t, values_t, attn_t, d_attn_t, lse_t))
        dk_own = lax.psum_scatter(dk_t, 'cp', scatter_dimension=2, tiled=True)
        dv_own = lax.psum_scatter(dv_t, 'cp', scatter_dimension=2, tiled=True)
        dq_lin = rotate(dq_t, cos_t[None, :, :, None], -sin_t[None, :, :, None]).astype(jnp.bfloat16)
        dk_lin = rotate(dk_own, cos_t[None], -sin_t[None]).astype(jnp.bfloat16)
        dq_flat = jnp.moveaxis(dq_lin, 0, 2).reshape(n_batch * n_tok, -1)
        dk_flat = jnp.moveaxis(dk_lin, 0, 2).reshape(n_batch * n_tok, -1)
        dv_flat = jnp.moveaxis(dv_own.astype(jnp.bfloat16), 0, 2).reshape(n_batch * n_tok, -1)
        grad_hidden, grad_wq, grad_wk, grad_wv, grad_gain = finish_backward(grad_out, normed_flat, norm_pull, dq_flat, dk_flat, dv_flat, w_q, w_k, w_v)
        return block_out, grad_hidden, grad_wq, grad_wk, grad_wv, grad_wo, grad_gain

    seq_spec = P(None, 'cp', None)
    tok_spec = P(None, 'cp')
    full_spec = P()
    return jax.shard_map(local_step, mesh=mesh, in_specs=(seq_spec, seq_spec, tok_spec, tok_spec, full_spec, full_spec, full_spec, full_spec, full_spec), out_specs=(seq_spec, seq_spec, full_spec, full_spec, full_spec, full_spec, full_spec), check_vma=False)
```

profile of v0, /device:TPU:0, one launch (start us, length us, event | category | flops | bytes accessed | tf_op | source)
XLA Modules:
  0.0 1608.9 jit_solution(14873957435434099028)
XLA Ops:
  24.3 12.3 copy.72
  48.3 8.5 fusion.86
  59.5 44.2 %all_gather.10 = s32[4,4096]{1,0:T(4,128)S(1)} all-gather(s32[4,128]{1,0:T(4,128)S(1)} %copy-done.25), channel_id=1, replica_groups=mesh['cp'=32] {'cp'}, dimensions={1}, use_global_device_ids=true | all-gather | bytes 67584 | tf_op jit(solution)/shard_map/all_gather | solution.py:76
  106.2 11.2 all-gather.5.cloned.1.call-done
  117.5 12.0 copy.38
  129.4 67.6 %all-gather.3.cloned.1.call-done = bf16[4,4096,2,128]{3,1,0,2:T(8,128)(2,1)} async-done(((bf16[4,128,2,128]{3,1,0,2:T(8,128)(2,1)}), bf16[4,4096,2,128]{3,1,0,2:T(8,128)(2,1)}) %all-gather.3.cloned.1.call-update) | async-done | bytes 8388624 | tf_op jit(solution)/shard_map/all_gather | solution.py:75
  197.0 163.9 %while.28 = (s32[]{:T(128)}, bf16[2,4,128,8,128]{2,4,3,1,0:T(8,128)(2,1)}, f32[2,4,8,128,1]{3,2,1,4,0:T(8,128)S(1)}, bf16[2,4,4096,128]{3,2,1,0:T(8,128)(2,1)}, ...) while((s32[]{:T(128)}, ...), condition=%wide.region_4.5_spmd.clone, body=%wide.region_1.4_spmd.clone.sunk | while | flops 8795975680 | bytes 220926064 | solution.py:96
  202.2 26.7 %fusion.153 = (f32[4,8,128]{2,1,0:T(8,128)S(1)}, f32[4,4096,128,8]{2,1,3,0:T(8,128)}) fusion(pred[4,128,4096]{1,2,0:T(8,128)(4,1)S(1)} %and_bitcast_fusion.4, bf16[2,4,128,8,128]{4,2,3,1,0:T(8,128)(2,1)} %get-tuple-element.433, s32[]{:T(128)} %get-tuple-element.418, bf16[2,4,4096,128]{3,2,1,0:T(8,128)(2,1)} %get-tuple-element.432), kind=kOutput, calls=%fused_computation.6.clone.1 | convolution fusion | flops 4345294848 | bytes 74466304 | tf_op jit(solution)/shard_map/while/body/eval_jaxpr/btgd,bsd->bgts/dot_general | solution.py:83
  228.8 21.3 %fusion.154 = f32[4,8,128]{2,1,0:T(8,128)S(1)} fusion(f32[4,4096,128,8]{2,1,3,0:T(8,128)} %get-tuple-element.393, f32[4,8,128]{2,1,0:T(8,128)S(1)} %get-tuple-element.394, pred[4,128,4096]{1,2,0:T(8,128)(4,1)S(1)} %and_bitcast_fusion.4), kind=kLoop, calls=%fused_computation.5.clone.1 | loop fusion | flops 67104768 | bytes 69238784 | tf_op jit(solution)/shard_map/while/body/eval_jaxpr/reduce_sum | solution.py:91
  250.2 28.6 %fusion.155 = bf16[2,4,128,8,128]{2,4,3,1,0:T(8,128)(2,1)} fusion(bf16[2,4,128,8,128]{2,4,3,1,0:T(8,128)(2,1)} %get-tuple-element.419, s32[]{:T(128)} %get-tuple-element.418, f32[4,4096,128,8]{2,1,3,0:T(8,128)} %get-tuple-element.393, f32[4,8,128]{2,1,0:T(8,128)S(1)} %fusion.154, f32[4,8,128]{2,1,0:T(8,128)S(1)} %get-tuple-element.394, ...), kind=kOutput, calls=%fused_computation.16.clone.1 | convolution fusion | flops 4379377664 | bytes 74482688 | tf_op jit(solution)/shard_map/while/body/eval_jaxpr/bgts,bsd->btgd/dot_general | solution.py:93
  283.9 26.7 %fusion.153 = (f32[4,8,128]{2,1,0:T(8,128)S(1)}, f32[4,4096,128,8]{2,1,3,0:T(8,128)}) fusion(pred[4,128,4096]{1,2,0:T(8,128)(4,1)S(1)} %and_bitcast_fusion.4, bf16[2,4,128,8,128]{4,2,3,1,0:T(8,128)(2,1)} %get-tuple-element.433, s32[]{:T(128)} %get-tuple-element.418, bf16[2,4,4096,128]{3,2,1,0:T(8,128)(2,1)} %get-tuple-element.432), kind=kOutput, calls=%fused_computation.6.clone.1 | convolution fusion | flops 4345294848 | bytes 74466304 | tf_op jit(solution)/shard_map/while/body/eval_jaxpr/btgd,bsd->bgts/dot_general | solution.py:83
  310.6 21.3 %fusion.154 = f32[4,8,128]{2,1,0:T(8,128)S(1)} fusion(f32[4,4096,128,8]{2,1,3,0:T(8,128)} %get-tuple-element.393, f32[4,8,128]{2,1,0:T(8,128)S(1)} %get-tuple-element.394, pred[4,128,4096]{1,2,0:T(8,128)(4,1)S(1)} %and_bitcast_fusion.4), kind=kLoop, calls=%fused_computation.5.clone.1 | loop fusion | flops 67104768 | bytes 69238784 | tf_op jit(solution)/shard_map/while/body/eval_jaxpr/reduce_sum | solution.py:91
  332.0 29.0 %fusion.155 = bf16[2,4,128,8,128]{2,4,3,1,0:T(8,128)(2,1)} fusion(bf16[2,4,128,8,128]{2,4,3,1,0:T(8,128)(2,1)} %get-tuple-element.419, s32[]{:T(128)} %get-tuple-element.418, f32[4,4096,128,8]{2,1,3,0:T(8,128)} %get-tuple-element.393, f32[4,8,128]{2,1,0:T(8,128)S(1)} %fusion.154, f32[4,8,128]{2,1,0:T(8,128)S(1)} %get-tuple-element.394, ...), kind=kOutput, calls=%fused_computation.16.clone.1 | convolution fusion | flops 4379377664 | bytes 74482688 | tf_op jit(solution)/shard_map/while/body/eval_jaxpr/bgts,bsd->btgd/dot_general | solution.py:93
  360.9 288.6 %while.29 = (s32[]{:T(128)}, f32[2,4,128,8,128]{2,4,3,1,0:T(8,128)}, f32[2,4,4096,128]{3,2,1,0:T(8,128)}, f32[2,4,4096,128]{3,2,1,0:T(8,128)}, bf16[2,4,4096,128...) while((s32[]{:T(128)}, ...), condition=%wide.region_6.7_spmd.clone, body=%wide.region_5.6_spmd.clone.sunk | while | flops 21665673216 | bytes 374021312 | solution.py:117
  369.9 26.2 %fusion.166 = f32[4,4096,128,8]{2,1,3,0:T(8,128)} fusion(bf16[2,4,4096,128]{3,2,1,0:T(8,128)(2,1)} %get-tuple-element.470, s32[]{:T(128)} %get-tuple-element.452, bf16[2,4,128,8,128]{4,2,3,1,0:T(8,128)(2,1)} %get-tuple-element.471), kind=kOutput, calls=%fused_computation.37.clone.1 | convolution fusion | flops 4294967296 | bytes 72352768 | tf_op jit(solution)/shard_map/while/body/eval_jaxpr/btgd,bsd->bgts/dot_general | solution.py:83
  400.7 42.1 %fusion.167 = bf16[4,8,128,4096]{2,3,1,0:T(8,128)(2,1)} fusion(f32[4,4096,128,8]{2,1,3,0:T(8,128)} %fusion.166, f32[4,8,128]{2,1,0:T(8,128)S(1)} %copy.105, f32[4,8,128]{2,1,0:T(8,128)S(1)} %dynamic-slice_bitcast_fusion.2, pred[4,128,4096]{1,2,0:T(8,128)(4,1)} %and_bitcast_fusion.5, bf16[2,4,4096,128]{3,2,1,0:T(8,128)(2,1)} %get-tuple-element.473, ...), kind=kOutput, calls=%fused_computation.27.clone.3 | convolution fusion | flops 4412407808 | bytes 108037120 | tf_op jit(solution)/shard_map/while/body/eval_jaxpr/btgd,bsd->bgts/dot_general | solution.py:109
  442.9 17.1 %bitcast_dynamic-update-slice_fusion.10 = f32[2,4,4096,128]{3,2,1,0:T(8,128)} fusion(f32[2,4,4096,128]{3,2,1,0:T(8,128)} %get-tuple-element.454, s32[]{:T(128)} %get-tuple-element.452, bf16[4,8,128,4096]{2,3,1,0:T(8,128)(2,1)} %fusion.167, bf16[2,4,128,8,128]{4,2,3,1,0:T(8,128)(2,1)S(1)} %copy-done.1), kind=kOutput, calls=%fused_computation.35.clone.1 | convolution fusion | flops 4294967296 | bytes 42992640 | tf_op jit(solution)/shard_map/while/body/eval_jaxpr/bgts,btgd->bsd/dot_general | solution.py:113
  460.0 18.1 %bitcast_dynamic-update-slice_fusion.9 = f32[2,4,128,8,128]{2,4,3,1,0:T(8,128)} fusion(f32[2,4,128,8,128]{2,4,3,1,0:T(8,128)} %get-tuple-element.453, s32[]{:T(128)} %get-tuple-element.452, bf16[4,8,128,4096]{2,3,1,0:T(8,128)(2,1)} %fusion.167, bf16[2,4,4096,128]{3,2,1,0:T(8,128)(2,1)} %get-tuple-element.470), kind=kOutput, calls=%fused_computation.45.clone.1 | convolution fusion | flops 4294967296 | bytes 39846912 | tf_op jit(solution)/shard_map/while/body/eval_jaxpr/bgts,bsd->btgd/dot_general | solution.py:112
  478.0 27.1 %bitcast_dynamic-update-slice_fusion.11 = f32[2,4,4096,128]{3,2,1,0:T(8,128)} fusion(f32[2,4,4096,128]{3,2,1,0:T(8,128)} %get-tuple-element.455, s32[]{:T(128)} %get-tuple-element.452, f32[4,4096,128,8]{2,1,3,0:T(8,128)} %fusion.166, f32[4,8,128]{2,1,0:T(8,128)S(1)} %dynamic-slice_bitcast_fusion.2, pred[4,128,4096]{1,2,0:T(8,128)(4,1)S(1)} %copy-done.3, ...), kind=kOutput, calls=%fused_computation.34.clone.1 | convolution fusion | flops 4362076160 | bytes 78660608 | tf_op jit(solution)/shard_map/while/body/eval_jaxpr/bgts,btgd->bsd/dot_general | solution.py:114
  513.9 26.2 %fusion.166 = f32[4,4096,128,8]{2,1,3,0:T(8,128)} fusion(bf16[2,4,4096,128]{3,2,1,0:T(8,128)(2,1)} %get-tuple-element.470, s32[]{:T(128)} %get-tuple-element.452, bf16[2,4,128,8,128]{4,2,3,1,0:T(8,128)(2,1)} %get-tuple-element.471), kind=kOutput, calls=%fused_computation.37.clone.1 | convolution fusion | flops 4294967296 | bytes 72352768 | tf_op jit(solution)/shard_map/while/body/eval_jaxpr/btgd,bsd->bgts/dot_general | solution.py:83
  544.7 42.2 %fusion.167 = bf16[4,8,128,4096]{2,3,1,0:T(8,128)(2,1)} fusion(f32[4,4096,128,8]{2,1,3,0:T(8,128)} %fusion.166, f32[4,8,128]{2,1,0:T(8,128)S(1)} %copy.105, f32[4,8,128]{2,1,0:T(8,128)S(1)} %dynamic-slice_bitcast_fusion.2, pred[4,128,4096]{1,2,0:T(8,128)(4,1)} %and_bitcast_fusion.5, bf16[2,4,4096,128]{3,2,1,0:T(8,128)(2,1)} %get-tuple-element.473, ...), kind=kOutput, calls=%fused_computation.27.clone.3 | convolution fusion | flops 4412407808 | bytes 108037120 | tf_op jit(solution)/shard_map/while/body/eval_jaxpr/btgd,bsd->bgts/dot_general | solution.py:109
  586.9 17.1 %bitcast_dynamic-update-slice_fusion.10 = f32[2,4,4096,128]{3,2,1,0:T(8,128)} fusion(f32[2,4,4096,128]{3,2,1,0:T(8,128)} %get-tuple-element.454, s32[]{:T(128)} %get-tuple-element.452, bf16[4,8,128,4096]{2,3,1,0:T(8,128)(2,1)} %fusion.167, bf16[2,4,128,8,128]{4,2,3,1,0:T(8,128)(2,1)S(1)} %copy-done.1), kind=kOutput, calls=%fused_computation.35.clone.1 | convolution fusion | flops 4294967296 | bytes 42992640 | tf_op jit(solution)/shard_map/while/body/eval_jaxpr/bgts,btgd->bsd/dot_general | solution.py:113
  604.0 18.1 %bitcast_dynamic-update-slice_fusion.9 = f32[2,4,128,8,128]{2,4,3,1,0:T(8,128)} fusion(f32[2,4,128,8,128]{2,4,3,1,0:T(8,128)} %get-tuple-element.453, s32[]{:T(128)} %get-tuple-element.452, bf16[4,8,128,4096]{2,3,1,0:T(8,128)(2,1)} %fusion.167, bf16[2,4,4096,128]{3,2,1,0:T(8,128)(2,1)} %get-tuple-element.470), kind=kOutput, calls=%fused_computation.45.clone.1 | convolution fusion | flops 4294967296 | bytes 39846912 | tf_op jit(solution)/shard_map/while/body/eval_jaxpr/bgts,bsd->btgd/dot_general | solution.py:112
  622.1 27.1 %bitcast_dynamic-update-slice_fusion.11 = f32[2,4,4096,128]{3,2,1,0:T(8,128)} fusion(f32[2,4,4096,128]{3,2,1,0:T(8,128)} %get-tuple-element.455, s32[]{:T(128)} %get-tuple-element.452, f32[4,4096,128,8]{2,1,3,0:T(8,128)} %fusion.166, f32[4,8,128]{2,1,0:T(8,128)S(1)} %dynamic-slice_bitcast_fusion.2, pred[4,128,4096]{1,2,0:T(8,128)(4,1)S(1)} %copy-done.3, ...), kind=kOutput, calls=%fused_computation.34.clone.1 | convolution fusion | flops 4362076160 | bytes 78660608 | tf_op jit(solution)/shard_map/while/body/eval_jaxpr/bgts,btgd->bsd/dot_general | solution.py:114
  673.2 12.7 fusion.109
  685.9 8.3 fusion.110
  694.2 137.4 %reduce-scatter.3.cloned.1.call-done = f32[2,4,128,128]{3,2,1,0:T(8,128)} async-done(((f32[2,4,4096,128]{3,2,1,0:T(8,128)}), f32[2,4,128,128]{3,2,1,0:T(8,128)}) %reduce-scatter.3.cloned.1.call-update) | async-done | bytes 524304 | tf_op jit(solution)/shard_map/reduce_scatter | solution.py:118
  837.5 181.3 %reduce-scatter.5.cloned.1.call-done = f32[2,4,128,128]{3,2,1,0:T(8,128)} async-done(((f32[2,4,4096,128]{3,2,1,0:T(8,128)}), f32[2,4,128,128]{3,2,1,0:T(8,128)}) %reduce-scatter.5.cloned.1.call-update) | async-done | bytes 524304 | tf_op jit(solution)/shard_map/reduce_scatter | solution.py:119
  1025.5 9.6 fusion.72
  1043.2 43.7 %psum.39 = f32[2048]{0:T(1024)} all-reduce(f32[2048]{0:T(1024)S(1)} %get-tuple-element.207), channel_id=1, replica_groups=mesh['cp'=32] {'cp'}, use_global_device_ids=true, to_apply=%region_15.16 | all-reduce | flops 2048 | bytes 16384 | tf_op jit(solution)/shard_map/psum | solution.py:60
  1091.8 485.0 %all-reduce.3.cloned.1.call-done = (f32[2048,2048]{1,0:T(8,128)}, f32[2048,256]{1,0:T(8,128)}, f32[2048,256]{1,0:T(8,128)}, f32[2048,2048]{1,0:T(8,128)}) async-done(((f32[2048,2048]{1,0:T(8,128)}, f32[2048,256]{1,0:T(8,128)}, f32[2048,256]{1,0:T(8,128)}, f32[2048,2048]{1,0:T(8,128)}), (f32[2048,2048]{1,0:T(8,128)}, f32[2048,256]{1,0:T(8,128)}, f32[2048,256]{1,0:T(8,128)}, ...) | async-done | bytes 37748752 | tf_op jit(solution)/shard_map/psum | solution.py:54
  1576.8 13.2 copy.138
  (168 shorter events, 132.0 us)
Async XLA Ops:
  7.2 11.9 copy-start
  7.2 110.3 %all-gather.5.cloned.1.call-start = ((), (), s32[]{:S(2)}) async-start(), calls=%async_computation.3 | async-start | bytes 8650752 | tf_op jit(solution)/shard_map/all_gather | solution.py:74
  9.4 8.7 copy-start.28
  10.1 8.0 copy-start.26
  12.6 31.8 %copy-start.11 = (f32[4,128,128]{1,2,0:T(8,128)}, f32[4,128,128]{1,2,0:T(8,128)S(1)}, u32[]{:S(2)}) copy-start(f32[4,128,128]{1,2,0:T(8,128)S(1)} %get-tuple-element.269) | copy-start | bytes 786436
  17.2 19.5 %copy-start.5 = (bf16[4,128,2048]{2,1,0:T(8,128)(2,1)}, bf16[4,128,2048]{2,1,0:T(8,128)(2,1)S(1)}, u32[]{:S(2)}) copy-start(bf16[4,128,2048]{2,1,0:T(8,128)(2,1)S(1)} %fusion.67) | copy-start | bytes 6291460
  19.0 178.0 %all-gather.3.cloned.1.call-start = ((), (), s32[]{:S(2)}) async-start(), calls=%async_computation.2 | async-start | bytes 8650752 | tf_op jit(solution)/shard_map/all_gather | solution.py:75
  23.9 807.7 %reduce-scatter.3.cloned.1.call-start = ((), (), s32[]{:S(2)}) async-start(), calls=%async_computation.4 | async-start | bytes 17301504 | tf_op jit(solution)/shard_map/reduce_scatter | solution.py:118
  369.9 26.2 %copy-start.2 = (pred[128,4096]{0,1:T(8,128)(4,1)S(1)}, pred[128,4096]{0,1:T(8,128)(4,1)}, u32[]{:S(2)}) copy-start(pred[128,4096]{0,1:T(8,128)(4,1)} %get-tuple-element.478) | copy-start | bytes 1572868 | tf_op jit(solution)/shard_map/while
  400.7 42.1 %copy-start.1 = (bf16[2,4,128,8,128]{4,2,3,1,0:T(8,128)(2,1)S(1)}, bf16[2,4,128,8,128]{4,2,3,1,0:T(8,128)(2,1)}, u32[]{:S(2)}) copy-start(bf16[2,4,128,8,128]{4,2,3,1,0:T(8,128)(2,1)} %get-tuple-element.471) | copy-start | bytes 6291460 | tf_op jit(solution)/shard_map/while
  460.0 18.1 %copy-start.3 = (pred[4,128,4096]{1,2,0:T(8,128)(4,1)S(1)}, pred[4,128,4096]{1,2,0:T(8,128)(4,1)}, u32[]{:S(2)}) copy-start(pred[4,128,4096]{1,2,0:T(8,128)(4,1)} %and_bitcast_fusion.5) | copy-start | bytes 6291460 | tf_op jit(solution)/shard_map/while
  513.9 26.2 %copy-start.2 = (pred[128,4096]{0,1:T(8,128)(4,1)S(1)}, pred[128,4096]{0,1:T(8,128)(4,1)}, u32[]{:S(2)}) copy-start(pred[128,4096]{0,1:T(8,128)(4,1)} %get-tuple-element.478) | copy-start | bytes 1572868 | tf_op jit(solution)/shard_map/while
  544.7 42.2 %copy-start.1 = (bf16[2,4,128,8,128]{4,2,3,1,0:T(8,128)(2,1)S(1)}, bf16[2,4,128,8,128]{4,2,3,1,0:T(8,128)(2,1)}, u32[]{:S(2)}) copy-start(bf16[2,4,128,8,128]{4,2,3,1,0:T(8,128)(2,1)} %get-tuple-element.471) | copy-start | bytes 6291460 | tf_op jit(solution)/shard_map/while
  604.0 18.1 %copy-start.3 = (pred[4,128,4096]{1,2,0:T(8,128)(4,1)S(1)}, pred[4,128,4096]{1,2,0:T(8,128)(4,1)}, u32[]{:S(2)}) copy-start(pred[4,128,4096]{1,2,0:T(8,128)(4,1)} %and_bitcast_fusion.5) | copy-start | bytes 6291460 | tf_op jit(solution)/shard_map/while
  649.6 369.2 %reduce-scatter.5.cloned.1.call-start = ((), (), s32[]{:S(2)}) async-start(), calls=%async_computation.5 | async-start | bytes 17301504 | tf_op jit(solution)/shard_map/reduce_scatter | solution.py:119
  650.2 926.6 %all-reduce.3.cloned.1.call-start = ((), (), s32[]{:S(2)}) async-start(), calls=%async_computation.6 | async-start | bytes 75497472 | tf_op jit(solution)/shard_map/psum | solution.py:54
  657.4 8.8 copy-start.4
  673.2 12.7 copy-start.19
  673.2 12.7 copy-start.23
  831.6 3.9 copy-start.6
  1023.9 11.2 slice-start.4
  1025.5 9.6 slice-start.5
  1025.5 9.6 copy-start.20
  1035.1 4.6 copy-start.13
  1035.1 4.6 copy-start.18
  1041.4 45.5 %copy-start.31 = (f32[4,128]{1,0:T(4,128)S(1)}, f32[4,128]{1,0:T(4,128)}, u32[]{:S(2)}) copy-start(f32[4,128]{1,0:T(4,128)} %copy-done.30) | copy-start | bytes 6148
  1041.4 45.5 %copy-start.8 = (bf16[4,128,2048]{2,1,0:T(8,128)(2,1)S(1)}, bf16[4,128,2048]{2,1,0:T(8,128)(2,1)}, u32[]{:S(2)}) copy-start(bf16[4,128,2048]{2,1,0:T(8,128)(2,1)} %param.13) | copy-start | bytes 6291460
  1576.8 17.8 %slice-start = ((s8[16777216]{0:T(1024)(128)(4,1)}), s8[4194304]{0:T(1024)(128)(4,1)S(1)}, s32[]{:S(2)}) async-start(s8[16777216]{0:T(1024)(128)(4,1)} %bitcast.285), calls=%async_computation.7 | async-start | bytes 8388608
  1576.8 13.2 copy-start.22
  1576.8 17.8 %slice-start.1 = ((s8[16777216]{0:T(1024)(128)(4,1)}), s8[4194304]{0:T(1024)(128)(4,1)S(1)}, s32[]{:S(2)}) async-start(s8[16777216]{0:T(1024)(128)(4,1)} %bitcast.285), calls=%async_computation.8 | async-start | bytes 8388608
  1576.8 17.8 %slice-start.2 = ((s8[16777216]{0:T(1024)(128)(4,1)}), s8[4194304]{0:T(1024)(128)(4,1)S(1)}, s32[]{:S(2)}) async-start(s8[16777216]{0:T(1024)(128)(4,1)} %bitcast.285), calls=%async_computation.9 | async-start | bytes 8388608
  1576.8 19.3 %slice-start.3 = ((s8[16777216]{0:T(1024)(128)(4,1)}), s8[4194304]{0:T(1024)(128)(4,1)S(1)}, s32[]{:S(2)}) async-start(s8[16777216]{0:T(1024)(128)(4,1)} %bitcast.285), calls=%async_computation.10 | async-start | bytes 8388608
  (14 other events, 27.0 us)
Sparse Core Ops, SparseCore 0:
  19.1 98.2 all-gather.4
  120.4 76.5 all-gather.2
  649.7 181.8 reduce-scatter.2
  834.3 184.4 reduce-scatter.4
  1025.7 551.0 all-reduce.2
where the time goes:
time: 1610 us
  waiting for transfers between devices  883 us (55%)
  matrix products  432 us (27%)
  other arithmetic  98.7 us (6%)
  local copies, waits for them, and re-layouts  91.2 us (6%)
  blocking collectives  88 us (5%)
    psum x1, waiting for transfers between devices, finish_backward(): lax.psum(jnp.einsum('nd,nk->dk', normed_flat, dq_flat, preferred_element_...  485 us
    reduce_scatter x1, waiting for transfers between devices, local_step(): dv_own = lax.psum_scatter(dv_t, 'cp', scatter_dimension=2, tiled=True)  181 us
    reduce_scatter x1, waiting for transfers between devices, local_step(): dk_own = lax.psum_scatter(dk_t, 'cp', scatter_dimension=2, tiled=True)  137 us
    dot_general x4, matrix products, masked_scores(): jnp.einsum('btgd,bsd->bgts', query_h, key_h, preferred_element_type=jnp.f...  106 us
    dot_general x2, matrix products, head_backward(): jnp.einsum('btgd,bsd->bgts', d_attn_h, value_h, preferred_element_type=jn...  84.3 us
    all_gather x1, waiting for transfers between devices, local_step(): values_all = lax.all_gather(values_loc, 'cp', axis=1, tiled=True)  67.6 us
    dot_general x2, matrix products, head_forward(): jnp.einsum('bgts,bsd->btgd', attn_probs, value_h, preferred_element_type=...  57.6 us
    dot_general x2, matrix products, head_backward(): jnp.einsum('bgts,btgd->bsd', attn_probs.astype(jnp.bfloat16), d_attn_h, p...  54.2 us
  transfers between devices with their start and end apart: 5, of which 5 were waited for; matrix products, arithmetic and copies ran while one was open for 8% of the time, Pallas kernels for 0%

commit v1 on v0

v1 whole, which is shorter than its diff:
```python
import functools

import jax
import jax.numpy as jnp
from jax import lax
from jax.experimental import pallas as pl
from jax.experimental.pallas import tpu as pltpu
from jax.sharding import PartitionSpec as P

HEAD_DIM = 128
NORM_EPS = 1e-5
ROPE_BASE = 500000.0
NEG_BIG = -1e30
LOG2E = 1.4426950408889634
ATTN_SCALE = HEAD_DIM**-0.5
EXP2_SCALE = ATTN_SCALE * LOG2E
CHUNK = 64
BLK = 4 * CHUNK
N_HEADS = 8
N_PAIRS = 8
N_SUPER = 2 * N_PAIRS
MESH = pl.DeviceIdType.MESH
LATER = 2, 3
F32 = jnp.float32
BF16 = jnp.bfloat16

T_SQ, T_LO, T_MX = 0, 2, 6


def rope_tables(positions):
    inv_freq = ROPE_BASE ** (-jnp.arange(0, HEAD_DIM, 2).astype(F32) / HEAD_DIM)
    angles = positions.astype(F32)[..., None] * inv_freq
    return jnp.cos(angles), jnp.sin(angles)


def rotate(x, cos_t, sin_t):
    a, b = x[..., : HEAD_DIM // 2], x[..., HEAD_DIM // 2 :]
    return jnp.concatenate([a * cos_t - b * sin_t, b * cos_t + a * sin_t], axis=-1)


def dot(a, b, ca, cb):
    return lax.dot_general(a, b, ((ca, cb), ((), ())), preferred_element_type=F32)


def row_mean(x):
    return jnp.mean(x, axis=-1, keepdims=True)


def head(h):
    return pl.ds(h * HEAD_DIM, HEAD_DIM)


def dot_t(a, b):
    return dot(a, b, (1,), (1,))


def dyn(x, index, size, axis):
    return lax.dynamic_slice_in_dim(x, index, size, axis)


def pick(x, index, axis):
    return lax.dynamic_index_in_dim(x, index, axis, keepdims=False)


def steps(tab, body):
    b, hf = pl.program_id(0), pl.program_id(1)
    own, first, last_start = tab[T_SQ + hf], tab[T_LO + 2 * b + hf], tab[T_MX + 2 * b + hf]

    def step(s, carry):
        late = s >= N_PAIRS
        at = jnp.where(late, N_SUPER - 1 - s, s), late.astype(jnp.int32)
        full = jnp.logical_and(s < own, s * BLK >= last_start)
        pl.when(full)(lambda: body(s, at, False))
        pl.when(jnp.logical_not(full))(lambda: body(s, at, True))
        return carry

    lax.fori_loop(first, own + 1, step, 0)


def may_use(s, off, st_ref, qi_ref):
    return jnp.logical_and(off >= st_ref[0, 0] - s * BLK, off <= qi_ref[0, 0] - s * BLK)


def fwd_kernel(tab, q_ref, kv_ref, st_ref, qi_ref, ko_ref, o_ref, lse_ref, acc, m_s, l_s):
    m_s[...] = jnp.full_like(m_s, NEG_BIG)
    l_s[...] = jnp.zeros_like(l_s)
    acc[...] = jnp.zeros_like(acc)

    def body(s, at, masked):
        pair, hk = at
        k = kv_ref[pair, 0, 0, hk]
        v_t = kv_ref[pair, 1, 0, hk].T
        mask = may_use(s, ko_ref[hk], st_ref, qi_ref) if masked else None
        for h in range(N_HEADS):
            sc = dot_t(k, q_ref[0, 0, :, head(h)]) * EXP2_SCALE
            if masked:
                sc = jnp.where(mask, sc, NEG_BIG)
            m_old = m_s[h]
            m_new = jnp.maximum(m_old, jnp.max(sc, axis=0, keepdims=True))
            alpha = jnp.exp2(m_old - m_new)
            p = jnp.exp2(sc - m_new)
            m_s[h] = m_new
            l_s[h] = l_s[h] * alpha + jnp.sum(p, axis=0, keepdims=True)
            acc[h] = acc[h] * alpha + jnp.dot(v_t, p.astype(BF16), preferred_element_type=F32)

    steps(tab, body)
    for h in range(N_HEADS):
        o_ref[0, 0, :, head(h)] = (acc[h] / l_s[h]).T.astype(BF16)
        lse_ref[0, 0, h] = m_s[h] + jnp.log2(l_s[h])


def bwd_kernel(tab, q_ref, do_ref, o_ref, kv_ref, lse_ref, st_ref, qi_ref, ko_ref, cos_ref, sin_ref, dq_ref, dkv_ref, dq_acc, delta):
    dq_acc[...] = jnp.zeros_like(dq_acc)
    for h in range(N_HEADS):
        terms = do_ref[0, 0, :, head(h)].astype(F32) * o_ref[0, 0, :, head(h)].astype(F32)
        delta[h] = jnp.sum(terms.T, axis=0, keepdims=True)

    @pl.when(pl.program_id(1) == 0)
    def _():
        dkv_ref[...] = jnp.zeros_like(dkv_ref)

    def body(s, at, masked):
        pair, hk = at
        k = kv_ref[pair, 0, 0, hk]
        v = kv_ref[pair, 1, 0, hk]
        k_t = k.T
        mask = may_use(s, ko_ref[hk], st_ref, qi_ref) if masked else None
        dk = dv = jnp.zeros((BLK, HEAD_DIM), F32)
        for h in range(N_HEADS):
            q = q_ref[0, 0, :, head(h)]
            do = do_ref[0, 0, :, head(h)]
            p = jnp.exp2(dot_t(k, q) * EXP2_SCALE - lse_ref[0, 0, h])
            if masked:
                p = jnp.where(mask, p, 0.0)
            ds = (p * (dot_t(v, do) - delta[h])).astype(BF16)
            dv += jnp.dot(p.astype(BF16), do, preferred_element_type=F32)
            dk += jnp.dot(ds, q, preferred_element_type=F32)
            dq_acc[h] += jnp.dot(k_t, ds, preferred_element_type=F32)
        dkv_ref[pair, 0, 0, hk] += dk
        dkv_ref[pair, 1, 0, hk] += dv

    steps(tab, body)
    cos_t, sin_t = cos_ref[0, 0], sin_ref[0, 0]
    half = HEAD_DIM // 2
    for h in range(N_HEADS):
        a, c = dq_acc[h, :half] * ATTN_SCALE, dq_acc[h, half:] * ATTN_SCALE
        lin = jnp.concatenate([a * cos_t + c * sin_t, c * cos_t - a * sin_t], axis=0)
        dq_ref[0, 0, :, head(h)] = lin.T.astype(BF16)


def attn_specs():
    def at_tile(b, h, t):
        return (b, h) + (0,) * 2

    def at_row(b, h, t):
        return (0, 0, b) + (0,) * 3

    tile = pl.BlockSpec((1, 1, BLK, N_HEADS * HEAD_DIM), at_tile)
    row = pl.BlockSpec((1, 1, 1, BLK), at_tile)
    stat = pl.BlockSpec((1, 1, N_HEADS, 1, BLK), lambda b, h, t: (b, h) + (0,) * 3)
    rope = pl.BlockSpec((1, 1, HEAD_DIM // 2, BLK), at_tile)
    kv = pl.BlockSpec((N_PAIRS, 2, 1, 2, BLK, HEAD_DIM), at_row)
    ko = pl.BlockSpec((2, BLK, BLK), lambda b, h, t: (0,) * 3)
    return tile, row, stat, kv, ko, rope


def flash_fwd(tab, q, kv, start, qidx, koff):
    tile, row, stat, kvs, ko, *_ = attn_specs()
    return pl.pallas_call(
        fwd_kernel,
        name="attn_fwd",
        out_shape=(jax.ShapeDtypeStruct(q.shape, BF16), jax.ShapeDtypeStruct((2, 2, N_HEADS, 1, BLK), F32)),
        grid_spec=pltpu.PrefetchScalarGridSpec(
            num_scalar_prefetch=1,
            grid=(2, 2),
            in_specs=[tile, kvs, row, row, ko],
            out_specs=[tile, stat],
            scratch_shapes=[pltpu.VMEM((N_HEADS, HEAD_DIM, BLK), F32)] + [pltpu.VMEM((N_HEADS, 1, BLK), F32)] * 2,
        ),
        compiler_params=pltpu.CompilerParams(vmem_limit_bytes=40 << 20),
        cost_estimate=pl.CostEstimate(flops=20 * 10**9, bytes_accessed=16 << 20, transcendentals=18 * 10**6),
    )(tab, q, kv, start, qidx, koff)


def flash_bwd(tab, q, do, o, kv, lse, start, qidx, koff, cos_t, sin_t):
    tile, row, stat, kvs, ko, rope = attn_specs()
    return pl.pallas_call(
        bwd_kernel,
        name="attn_bwd",
        out_shape=(
            jax.ShapeDtypeStruct(q.shape, BF16),
            jax.ShapeDtypeStruct(kv.shape, F32),
        ),
        grid_spec=pltpu.PrefetchScalarGridSpec(
            num_scalar_prefetch=1,
            grid=(2, 2),
            in_specs=[tile, tile, tile, kvs, stat, row, row, ko, rope, rope],
            out_specs=[tile, kvs],
            scratch_shapes=[pltpu.VMEM((N_HEADS, HEAD_DIM, BLK), F32), pltpu.VMEM((N_HEADS, 1, BLK), F32)],
        ),
        compiler_params=pltpu.CompilerParams(vmem_limit_bytes=48 << 20),
        cost_estimate=pl.CostEstimate(flops=50 * 10**9, bytes_accessed=32 << 20, transcendentals=18 * 10**6),
    )(tab, q, do, o, kv, lse, start, qidx, koff, cos_t, sin_t)


def turn(x, cos_ref, sin_ref):
    return x * cos_ref[...] + pltpu.roll(x, HEAD_DIM // 2, 1) * sin_ref[...]


def first_kernel(x_ref, g_ref, wk_ref, wv_ref, cos_ref, sin_ref, h_ref, kv_ref):
    x = x_ref[...].astype(F32)
    h = (x * lax.rsqrt(row_mean(x * x) + NORM_EPS) * g_ref[...]).astype(BF16)
    h_ref[...] = h
    k = jnp.dot(h, wk_ref[...], preferred_element_type=F32)
    v = jnp.dot(h, wv_ref[...], preferred_element_type=F32)
    n = kv_ref.shape[3]
    for i in range(2):
        for j, val in enumerate((turn(k[:, i * HEAD_DIM :][:, :HEAD_DIM], cos_ref, sin_ref), v[:, i * HEAD_DIM :][:, :HEAD_DIM])):
            for c in range(2):
                kv_ref[i, c, j] = val[c * n : (c + 1) * n].astype(BF16)


def query_kernel(h_ref, w_ref, cos_ref, sin_ref, q_ref):
    q = jnp.dot(h_ref[...], w_ref[...], preferred_element_type=F32)
    n = q_ref.shape[2]
    for j in range(q.shape[1] // HEAD_DIM):
        val = turn(q[:, j * HEAD_DIM :][:, :HEAD_DIM], cos_ref, sin_ref).astype(BF16)
        for c in range(2):
            q_ref[0, c, :, head(j)] = val[c * n : (c + 1) * n]


def project(x, gain, w_q, w_k, w_v, cos_f, sin_f):
    n, d = x.shape
    params = pltpu.CompilerParams(vmem_limit_bytes=40 << 20)
    h, kv = pl.pallas_call(
        first_kernel,
        name="norm_kv",
        out_shape=(jax.ShapeDtypeStruct(x.shape, BF16), jax.ShapeDtypeStruct((2,) * 3 + (n // 2, HEAD_DIM), BF16)),
        compiler_params=params,
        cost_estimate=pl.CostEstimate(flops=2 * 10**9, bytes_accessed=7 << 20, transcendentals=0),
    )(x, gain, w_k, w_v, cos_f, sin_f)
    tile = 4 * HEAD_DIM
    rope = pl.BlockSpec(cos_f.shape, lambda j: (0, 0))
    q = pl.pallas_call(
        query_kernel,
        name="query",
        grid=(d // tile,),
        out_shape=jax.ShapeDtypeStruct((2, 2, n // 2, d // 2), BF16),
        in_specs=[pl.BlockSpec(h.shape, lambda j: (0, 0)), pl.BlockSpec((d, tile), lambda j: (0, j)), rope, rope],
        out_specs=pl.BlockSpec((1, 2, n // 2, tile), lambda j: (j // 2, 0, 0, j % 2)),
        compiler_params=params,
        cost_estimate=pl.CostEstimate(flops=5 * 10**9, bytes_accessed=12 << 20, transcendentals=0),
    )(h, w_q, cos_f, sin_f)
    return h, kv, q


def place(me):
    return me // 8, lax.rem(me // 4, 2), lax.rem(me // 2, 2), lax.rem(me, 2)


def dev(z, y, x, core):
    return ((z * 2 + y) * 2 + x) * 2 + core


def z_peers(z):
    return [(k, lax.rem(z + k, 4)) for k in (1, 2, 3)]


def meet(peers):
    barrier = pltpu.get_barrier_semaphore()
    for d in peers:
        pl.semaphore_signal(barrier, device_id=(d,), device_id_type=MESH)
    pl.semaphore_wait(barrier, len(peers))


def remote(src, dst, send, arrive, to):
    return pltpu.make_async_remote_copy(
        src_ref=src, dst_ref=dst, send_sem=send, recv_sem=arrive, device_id=(to,), device_id_type=MESH
    )


def exchange_kernel(kv_ref, q_ref, dy_ref, kv_all, q_u, dy_u, own_sem, quad_s, quad_r, z_s, z_r, y_s, y_r):
    me = lax.axis_index("cp")
    z, y, x, core = place(me)
    pair = me // 4
    quad = [dev(z, y, 1 - x if d // 2 else x, 1 - core if d % 2 else core) for d in range(4)]
    across = dev(z, 1 - y, x, core)
    meet(quad[1:] + [across] + [dev(zz, y, x, core) for _, zz in z_peers(z)])

    def source(a, d):
        xx, cc = 1 - x if d // 2 else x, 1 - core if d % 2 else core
        return dy_ref.at[cc] if a == 2 else (kv_ref, q_ref)[a].at[xx, cc]

    def target(a, d):
        tok = pl.ds(d * CHUNK, CHUNK)
        return kv_all.at[pair, :, :, :, tok] if a == 0 else (q_u, dy_u)[a - 1].at[:, :, tok]

    def quad_copy(a, d):
        return remote(source(a, d), target(a, d), quad_s.at[a, d], quad_r.at[a, d], quad[d])

    def own_copy(a):
        return pltpu.make_async_copy(source(a, 0), target(a, 0), own_sem.at[a])

    sent = [(a, d) for a in range(3) for d in (1, 2, 3) if (a, d) != LATER]
    for a, d in sent:
        quad_copy(a, d).start()
    for a in range(3):
        own_copy(a).start()
    own_copy(0).wait()
    for d in (1, 2, 3):
        quad_copy(0, d).wait_recv()

    def pass_on(zz, k):
        block = kv_all.at[2 * zz + y]
        return remote(block, block, y_s.at[k], y_r.at[k], across)

    mine = kv_all.at[pair]
    to_z = [remote(mine, mine, z_s.at[k], z_r.at[k], dev(zz, y, x, core)) for k, zz in z_peers(z)]
    for c in to_z:
        c.start()
    pass_on(z, 0).start()
    came = [(k, lax.rem(z + 4 - k, 4)) for k in (1, 3, 2)]
    for k, zz in came:
        block = kv_all.at[2 * zz + y]
        remote(block, block, z_s.at[k], z_r.at[k], me).wait_recv()
        pass_on(zz, k).start()
    for k, zz in [(0, z)] + came:
        block = kv_all.at[2 * zz + 1 - y]
        remote(block, block, y_s.at[k], y_r.at[k], me).wait_recv()
        pass_on(zz, k).wait_send()
    for c in to_z:
        c.wait_send()
    for a, d in sent:
        quad_copy(a, d).wait_send()
        if a > 0:
            quad_copy(a, d).wait_recv()
    own_copy(1).wait()
    own_copy(2).wait()


def exchange(kv, q, dy):
    dma = pltpu.SemaphoreType.DMA
    vmem, hbm = pl.BlockSpec(memory_space=pltpu.VMEM), pl.BlockSpec(memory_space=pl.ANY)
    wide = q.shape[-1]
    return pl.pallas_call(
        exchange_kernel,
        name="exchange",
        out_shape=(
            jax.ShapeDtypeStruct((N_PAIRS,) + (2,) * 3 + (BLK, HEAD_DIM), BF16),
            jax.ShapeDtypeStruct((2, 2, BLK, wide), BF16),
            jax.ShapeDtypeStruct((2, 2, LATER[1] * CHUNK, 2 * wide), BF16),
        ),
        in_specs=[vmem] * 3,
        out_specs=[hbm] * 3,
        scratch_shapes=[dma((3,))] + [dma((3, 4))] * 2 + [dma((4,))] * 4,
        compiler_params=pltpu.CompilerParams(collective_id=1),
        cost_estimate=pl.CostEstimate(flops=10**9, bytes_accessed=20 << 20, transcendentals=0),
    )(kv, q, dy)


def reduce_kernel(cuts, shared, *refs):
    n = len(cuts)
    ins, outs, refs = refs[:n], refs[n : 2 * n], refs[2 * n :]
    own, from_core, from_y, from_z = refs[:n], refs[n : 2 * n], refs[2 * n : 3 * n], refs[3 * n : 4 * n]
    load_sem, core_s, core_r, y_s, y_r, z_s, z_r = refs[4 * n :]
    me = lax.axis_index("cp")
    z, y, x, core = place(me)
    partner, across = dev(z, y, x, 1 - core), dev(z, 1 - y, x, core)
    peers = [across] + [dev(zz, y, x, core) for _, zz in z_peers(z)]
    meet(peers + [partner] * any(shared))

    def rows(i, j):
        size = own[i].shape[2] // cuts[i]
        return pl.ds(j * size, size)

    def load(i, j):
        src = ins[i].at[core] if shared[i] else ins[i]
        return pltpu.make_async_copy(src.at[:, :, rows(i, j)], own[i].at[:, :, rows(i, j)], load_sem.at[i, j])

    def core_copy(i, j):
        at = rows(i, j)
        return remote(ins[i].at[1 - core, :, :, at], from_core[i].at[:, :, at], core_s.at[i, j], core_r.at[i, j], partner)

    def y_copy(i, j):
        src = own[i] if shared[i] else ins[i]
        at = rows(i, j)
        return remote(src.at[:, 1 - y, at], from_y[i].at[:, at], y_s.at[i, j], y_r.at[i, j], across)

    def z_copy(i, j, k, zz):
        at = rows(i, j)
        return remote(
            own[i].at[zz, y, at], from_z[i].at[k - 1, at], z_s.at[i, j, k - 1], z_r.at[i, j, k - 1], dev(zz, y, x, core)
        )

    pieces = [(i, j) for i in range(n) for j in range(cuts[i])]
    for i, j in pieces:
        if shared[i]:
            core_copy(i, j).start()
        else:
            y_copy(i, j).start()
        load(i, j).start()
    for i, j in pieces:
        load(i, j).wait()
        if shared[i]:
            core_copy(i, j).wait_recv()
            at = rows(i, j)
            for zz in range(4):
                own[i][zz, :, at] += from_core[i][zz, :, at]
            y_copy(i, j).start()
    for i, j in pieces:
        y_copy(i, j).wait_recv()
        at = rows(i, j)
        for zz in range(4):
            own[i][zz, y, at] += from_y[i][zz, at]
        for k, zz in z_peers(z):
            z_copy(i, j, k, zz).start()
    for i, j in pieces:
        at = rows(i, j)
        for k, zz in z_peers(z):
            z_copy(i, j, k, zz).wait_recv()
        outs[i][at] = own[i][z, y, at] + sum(from_z[i][k, at] for k in range(3))
    for i, j in pieces:
        if shared[i]:
            core_copy(i, j).wait_send()
        y_copy(i, j).wait_send()
        for k, zz in z_peers(z):
            z_copy(i, j, k, zz).wait_send()


def reduce_pairs(arrays, cuts, shared, collective_id):
    dma = pltpu.SemaphoreType.DMA
    vmem, hbm = pl.BlockSpec(memory_space=pltpu.VMEM), pl.BlockSpec(memory_space=pl.ANY)
    n, most = len(arrays), max(cuts)
    blocks = [a.shape[-2:] for a in arrays]
    ins = [a.reshape(a.shape[:-3] + (4, 2) + b) for a, b in zip(arrays, blocks)]
    own = [pltpu.VMEM((4, 2) + b, F32) for b in blocks]
    scratch = own + [o if s else pltpu.VMEM((8, HEAD_DIM), F32) for o, s in zip(own, shared)]
    scratch += [pltpu.VMEM((4,) + b, F32) for b in blocks] + [pltpu.VMEM((3,) + b, F32) for b in blocks]
    return pl.pallas_call(
        functools.partial(reduce_kernel, cuts, shared),
        name="reduce_pairs",
        out_shape=[jax.ShapeDtypeStruct(b, F32) for b in blocks],
        in_specs=[hbm] * n,
        out_specs=[vmem] * n,
        scratch_shapes=scratch + [dma((n, most))] * 5 + [dma((n, most, 3))] * 2,
        compiler_params=pltpu.CompilerParams(collective_id=collective_id, vmem_limit_bytes=56 << 20),
        cost_estimate=pl.CostEstimate(flops=10**9, bytes_accessed=20 << 20, transcendentals=0),
    )(*ins)


def gather_kernel(*refs):
    shards, outs = refs[:4], refs[4:8]
    own_sem, zs, fs, ls, cs, zr, fr, lr, cr = refs[8:]
    me = lax.axis_index("cp")
    z, y, x, core = place(me)
    across = (dev(z, y, 1 - x, core), dev(z, 1 - y, x, core))
    partner = dev(z, y, x, 1 - core)
    meet([partner, *across] + [dev(zz, y, x, core) for _, zz in z_peers(z)])

    def windows(half, zz, yy, xx, cc):
        pair = 2 * zz + yy
        rows = shards[0].shape[0] // 2
        out_rows = pl.ds(((xx * 2 + cc) * N_PAIRS + pair) * 2 * rows + half * rows, rows)
        yield shards[0], pl.ds(half * rows, rows), outs[0].at[out_rows]
        rows = shards[1].shape[0] // 2
        out_rows = pl.ds((cc * N_PAIRS + pair) * 2 * rows + half * rows, rows)
        for s, o in zip(shards[1:], outs[1:]):
            yield s, pl.ds(half * rows, rows), o.at[out_rows, pl.ds(xx * s.shape[1], s.shape[1])]

    total = sum(s.size for s in shards) // 2 // outs[0].shape[1]
    whole = outs[0].at[pl.ds(0, total)]

    def flip(v, on):
        return 1 - v if on else v

    class Copy:
        def __init__(self, half, zz, first, last, send, arrive, to, is_own, cc=core):
            over_x, over_y = (first, last) if half == 0 else (last, first)
            self.at = half, zz, flip(y, over_y), flip(x, over_x), cc
            self.send, self.arrive, self.to, self.is_own = send, arrive, to, is_own

        def start(self):
            for shard, rows, window in windows(*self.at):
                remote(shard.at[rows] if self.is_own else window, window, self.send, self.arrive, self.to).start()

        def wait_recv(self):
            remote(whole, whole, self.send, self.arrive, me).wait_recv()

        def wait_send(self):
            remote(whole, whole, self.send, self.arrive, me).wait_send()

    places = [(0, z)] + [(k, lax.rem(z + 4 - k, 4)) for k in (1, 3, 2)]
    halves = range(2)

    def z_copy(half, k, zz):
        return Copy(half, z, 0, 0, zs.at[half, k], zr.at[half, k], dev(zz, y, x, core), True)

    def first_copy(half, k, zz):
        at = half, k
        return Copy(half, zz, 0, 0, fs.at[at], fr.at[at], across[half], k == 0)

    def last_copy(half, k, zz, first):
        at = half, first, k
        return Copy(half, zz, first, 0, ls.at[at], lr.at[at], across[1 - half], k == first == 0)

    def core_copy(half, k, zz, first, last):
        at = half, first, last, k
        return Copy(half, zz, first, last, cs.at[at], cr.at[at], partner, k == first == last == 0)

    owns = []
    for half in halves:
        for shard, rows, window in windows(half, z, y, x, core):
            owns.append(pltpu.make_async_copy(shard.at[rows], window, own_sem.at[len(owns)]))
    for k, zz in z_peers(z):
        for half in halves:
            z_copy(half, k, zz).start()
    for k, zz in places:
        for half in halves:
            if k > 0:
                z_copy(half, k, zz).wait_recv()
            first_copy(half, k, zz).start()
            last_copy(half, k, zz, 0).start()
            core_copy(half, k, zz, 0, 0).start()
        if k == 0:
            for o in owns:
                o.start()
        for half in halves:
            first_copy(half, k, zz).wait_recv()
            last_copy(half, k, zz, 1).start()
            core_copy(half, k, zz, 1, 0).start()
    for first in halves:
        for k, zz in places:
            for half in halves:
                last_copy(half, k, zz, first).wait_recv()
                core_copy(half, k, zz, first, 1).start()
    for o in owns:
        o.wait()
    for k, zz in z_peers(z):
        for half in halves:
            z_copy(half, k, zz).wait_send()
    for k, zz in places:
        for half in halves:
            first_copy(half, k, zz).wait_send()
            for first in halves:
                last_copy(half, k, zz, first).wait_send()
                for last in halves:
                    core_copy(half, k, zz, first, last).wait_recv()
                    core_copy(half, k, zz, first, last).wait_send()


def gather_all(shards, shapes):
    dma = pltpu.SemaphoreType.DMA
    vmem, hbm = pl.BlockSpec(memory_space=pltpu.VMEM), pl.BlockSpec(memory_space=pl.ANY)
    hops = [dma((2,) * i + (4,)) for i in (1, 1, 2, 3)]
    n = len(shards)
    return pl.pallas_call(
        gather_kernel,
        name="gather_all",
        out_shape=[jax.ShapeDtypeStruct(s, F32) for s in shapes],
        in_specs=[vmem] * n,
        out_specs=[hbm] * n,
        scratch_shapes=[dma((2 * n,))] + hops + hops,
        compiler_params=pltpu.CompilerParams(collective_id=0),
        cost_estimate=pl.CostEstimate(flops=10**9, bytes_accessed=76 << 20, transcendentals=0),
    )(*shards)


def perm(x, pairs):
    return lax.ppermute(x, "cp", pairs)


def flip_pairs(d):
    return [(r, r ^ d) for r in range(32)]


def turn_z(k):
    return [(r, (r + 8 * k) % 32) for r in range(32)]


def solution(mesh):
    def local_step(hidden, grad_out, positions, seg_ids, w_q, w_k, w_v, w_o, norm_gain):
        n_batch, n_tok, d_model = hidden.shape
        n_rows = n_batch * n_tok
        wide = N_HEADS * HEAD_DIM
        me = lax.axis_index("cp")
        z, y, x, core = place(me)
        quad, pair = me % 4, me // 4
        relations = range(4)

        def rows_of(arr, d):
            return pick(arr.reshape((2, 2, 2, CHUNK) + arr.shape[2:]), core ^ (d % 2), 0)

        def swap(pieces):
            return [perm(p, flip_pairs(d)) if d else p for d, p in enumerate(pieces)]

        def unite(arr):
            joined = jnp.stack(swap([rows_of(arr, d) for d in relations]), axis=2)
            return joined.reshape((2, 2, BLK) + joined.shape[4:])

        gain = norm_gain.astype(F32)
        cos_t, sin_t = rope_tables(positions.reshape(n_rows))
        cos_f, sin_f = jnp.concatenate([cos_t, cos_t], axis=1), jnp.concatenate([-sin_t, sin_t], axis=1)
        normed, kv_home, q_home = project(hidden.reshape(n_rows, d_model), gain[None], w_q, w_k, w_v, cos_f, sin_f)
        pos_u = unite(positions)
        kv_all, q_u, dy_part = exchange(
            kv_home.reshape((2,) * 5 + (CHUNK, HEAD_DIM)),
            q_home.reshape((2,) * 4 + (CHUNK, wide)),
            grad_out.reshape((2,) * 3 + (CHUNK, d_model)),
        )
        dy_last, dy_part = lax.optimization_barrier((rows_of(grad_out, LATER[1]), dy_part))
        dy_last = perm(dy_last, flip_pairs(LATER[1]))
        normed_home, dy_part = lax.optimization_barrier((normed.reshape(hidden.shape), dy_part))
        normed_u = unite(normed_home)

        member = quad ^ jnp.arange(4)
        front, back = ((m[:, None] * CHUNK + jnp.arange(CHUNK)[None]).reshape(BLK) for m in (member, 3 - member))
        offsets = jnp.stack([front, back]).astype(jnp.int32)
        own_super = jnp.stack([pair, N_SUPER - 1 - pair]).astype(jnp.int32)
        q_index = own_super[:, None] * BLK + offsets
        start = q_index[None] - pos_u
        koff = jnp.broadcast_to(offsets[:, :, None], (2, BLK, BLK))
        tab = jnp.concatenate(
            [own_super, (jnp.min(start, axis=-1) // BLK).reshape(-1), jnp.max(start, axis=-1).reshape(-1)]
        )
        start_r = start[:, :, None, :]
        q_index_r = jnp.broadcast_to(q_index[None, :, None, :], start_r.shape)
        cos_u, sin_u = rope_tables(pos_u)
        cos_ut, sin_ut = jnp.swapaxes(cos_u, 2, 3), jnp.swapaxes(sin_u, 2, 3)

        attn_u, lse = flash_fwd(tab, q_u, kv_all, start_r, q_index_r, koff)

        def home(arr):
            return swap([piece[:, :, 0] for piece in jnp.split(arr.reshape(2, 2, 4, CHUNK, -1), 4, axis=2)])

        def in_order(place, own, other, axis):
            first = place == 0
            return jnp.concatenate([jnp.where(first, own, other), jnp.where(first, other, own)], axis=axis)

        def join(pieces):
            flat = [p.reshape(n_rows // 2, -1) for p in pieces]
            near, far = (in_order(core, *flat[i : i + 2], 0) for i in (0, 2))
            return in_order(x, near, far, -1)

        tok = tuple(range(3))
        half_wide = wide // 2
        dy_u = jnp.concatenate([dy_part, dy_last], axis=2)
        wo_send = dot(dyn(attn_u, (1 - core) * half_wide, half_wide, 3), dy_u, tok, tok)
        wo_sum = dot(dyn(attn_u, core * half_wide, half_wide, 3), dy_u, tok, tok) + perm(wo_send, flip_pairs(1))
        wo_sum = wo_sum.reshape(4, 2, half_wide // N_PAIRS, d_model)
        wo_y = perm(pick(wo_sum, 1 - y, 1), flip_pairs(4))

        d_attn = dot(dy_u, dyn(w_o, x * wide, wide, 0), (3,), (1,)).astype(BF16)
        d_attn, wo_sum = lax.optimization_barrier((d_attn, wo_sum))
        dq_u, dkv = flash_bwd(tab, q_u, d_attn, attn_u, kv_all, lse, start_r, q_index_r, koff, cos_ut, sin_ut)

        attn_home = join(home(attn_u))
        block_out = (hidden.astype(F32) + jnp.dot(attn_home, w_o, preferred_element_type=F32).reshape(hidden.shape)).astype(BF16)

        wo_sum = pick(wo_sum, y, 1) + wo_y
        wo_own = pick(wo_sum, z, 0)
        for k, zz in z_peers(z):
            wo_own = wo_own + perm(pick(wo_sum, zz, 0), turn_z(k))

        dq_home = join(home(dq_u))
        half_model = d_model // 2

        def by_core(d_out):
            part = lax.optimization_barrier(dot(normed_u, d_out, tok, tok))
            return part.reshape(2, N_PAIRS, half_model // N_PAIRS, -1)

        dkv_own, wq_own = reduce_pairs([dkv.reshape(N_PAIRS, -1, HEAD_DIM), by_core(dq_u)], (4, 2), (False, True), 2)
        dkv_own = dkv_own.reshape((2,) * 3 + (BLK, HEAD_DIM))
        dk_u = rotate(dkv_own[0] * ATTN_SCALE, cos_u, -sin_u).astype(BF16)
        dkv_u = jnp.concatenate([dk_u, dkv_own[1].astype(BF16)], axis=-1)
        (wkv_own,) = reduce_pairs([by_core(dkv_u)], (1,), (True,), 3)

        dkv_home = join(home(dkv_u)).reshape(n_rows, 2, 2, HEAD_DIM)
        dk_home, dv_home = (dkv_home[:, :, i].reshape(n_rows, -1) for i in range(2))
        d_normed = dot_t(dq_home, w_q) + dot_t(dk_home, w_k) + dot_t(dv_home, w_v)
        d_normed = d_normed.astype(BF16).astype(F32).reshape(hidden.shape)
        hidden_f32 = hidden.astype(F32)
        inv_rms = lax.rsqrt(row_mean(hidden_f32 * hidden_f32) + NORM_EPS)
        scaled = d_normed * gain
        unit = hidden_f32 * inv_rms
        d_hidden = inv_rms * (scaled - unit * row_mean(scaled * unit))
        grad_hidden = (grad_out.astype(F32) + d_hidden).astype(BF16)
        d_gain = jnp.sum(d_normed * unit, axis=(0, 1)).reshape(-1, 128)
        for i in range(5):
            d_gain = d_gain + perm(d_gain, flip_pairs(1 << i))

        wk_own, wv_own = jnp.split(wkv_own, 2, axis=1)
        grad_wo, grad_wq, grad_wk, grad_wv = gather_all(
            [wo_own, wq_own, wk_own, wv_own], [w_o.shape, w_q.shape, w_k.shape, w_v.shape]
        )
        return block_out, grad_hidden, grad_wq, grad_wk, grad_wv, grad_wo, d_gain.reshape(d_model)

    seq_spec = P(None, "cp", None)
    tok_spec = P(None, "cp")
    full_spec = P()
    return jax.shard_map(
        local_step,
        mesh=mesh,
        in_specs=(seq_spec, seq_spec, tok_spec, tok_spec, full_spec, full_spec, full_spec, full_spec, full_spec),
        out_specs=(seq_spec, seq_spec, full_spec, full_spec, full_spec, full_spec, full_spec),
        check_vma=False,
    )
```

time: 1610 us -> 837 us (0.52)
  waiting for transfers between devices: 883 us -> 88 us
  Pallas kernels: 0 us -> 553 us
  matrix products: 432 us -> 42.9 us
  blocking collectives: 88 us -> 0 us
  other arithmetic: 98.7 us -> 30.4 us
  starting transfers between devices: 0.5 us -> 31.4 us
  local copies, waits for them, and re-layouts: 91.2 us -> 73.3 us
    pallas_call x0 -> x8, Pallas kernels: none -> 553 us  [the longest x2 267 us: reduce_pairs(): pl.pallas_call(functools.partial(reduce_kernel, cuts, shared), name='redu...]
    psum x1 -> x0, waiting for transfers between devices: 485 us -> none  [finish_backward(): lax.psum(jnp.einsum('nd,nk->dk', normed_flat, dq_flat, preferred_element_...]
    dot_general x26 -> x9, matrix products: 432 us -> 42.9 us  [the longest x8 36.6 us: dot(): lax.dot_general(a, b, ((ca, cb), ((), ())), preferred_element_type=F32)]
    reduce_scatter x2 -> x0, waiting for transfers between devices: 319 us -> none  [the longest x1 181 us: local_step(): dv_own = lax.psum_scatter(dv_t, 'cp', scatter_dimension=2, tiled=True)]
    ppermute x0 -> x26, waiting for transfers between devices: none -> 88 us  [perm(): return lax.ppermute(x, 'cp', pairs)]
    all_gather x2 -> x0, waiting for transfers between devices: 78.8 us -> none  [the longest x1 67.6 us: local_step(): values_all = lax.all_gather(values_loc, 'cp', axis=1, tiled=True)]
    reduce_sum x4 -> x2, other arithmetic: 46.5 us -> 1.86 us  [the longest x1 1.38 us: local_step(): d_gain = jnp.sum(d_normed * unit, axis=(0, 1)).reshape(-1, 128)]
    all_gather x1 -> x0, blocking collectives: 44.2 us -> none  [local_step(): seg_all = lax.all_gather(seg_ids, 'cp', axis=1, tiled=True)]
  transfers between devices with their start and end apart: 5 -> 26, of which waited for: 5 -> 11; matrix products, arithmetic and copies ran while one was open for 8% -> 11% of each run, Pallas kernels for 0% -> 16%
where the time goes in v1:
time: 837 us; the launch traced here: 820 us
  Pallas kernels  553 us (66%)
  waiting for transfers between devices  88 us (11%)
  local copies, waits for them, and re-layouts  73.3 us (9%)
  matrix products  42.9 us (5%)
  starting transfers between devices  31.4 us (4%)
  other arithmetic  30.4 us (4%)
    pallas_call x2, Pallas kernels, reduce_pairs(): pl.pallas_call(functools.partial(reduce_kernel, cuts, shared), name='redu...  267 us
    pallas_call x1, Pallas kernels, gather_all(): pl.pallas_call(gather_kernel, name='gather_all', out_shape=[jax.ShapeDtyp...  161 us
    ppermute x26, waiting for transfers between devices, perm(): return lax.ppermute(x, 'cp', pairs)  88 us
    pallas_call x1, Pallas kernels, exchange(): pl.pallas_call(exchange_kernel, name='exchange', out_shape=(jax.ShapeDtyp...  64.9 us
    unnamed x91, local copies, waits for them, and re-layouts  44.6 us
    dot_general x8, matrix products, dot(): lax.dot_general(a, b, ((ca, cb), ((), ())), preferred_element_type=F32)  36.6 us
    ppermute x26, starting transfers between devices, perm(): return lax.ppermute(x, 'cp', pairs)  31.4 us
    pallas_call x1, Pallas kernels, flash_bwd(): pl.pallas_call(bwd_kernel, name='attn_bwd', out_shape=(jax.ShapeDtypeStru...  27 us
  transfers between devices with their start and end apart: 26, of which 11 were waited for; matrix products, arithmetic and copies ran while one was open for 11% of the time, Pallas kernels for 16%

profile of v1, /device:TPU:0, one launch (start us, length us, event | category | flops | bytes accessed | tf_op | source)
XLA Modules:
  0.0 820.2 jit_solution(9539326920148494358)
XLA Ops:
  12.3 4.1 copy-done.12
  16.4 7.3 query.1
  25.1 64.9 %exchange.1 = (bf16[8,2,2,2,256,128]{5,4,3,2,1,0:T(8,128)(2,1)}, bf16[2,2,256,1024]{3,2,1,0:T(8,128)(2,1)}, bf16[2,2,192,2048]{3,2,1,0:T(8,128)(2,1)}) custom-call(bf16[2,2,2,2,2,64,128]{6,5,4,3,2,1,0:T(8,128)(2,1)} %bitcast.174, bf16[2,2,2,2,64,1024]{5,4,3,2,1,0:T(8,128)(2,1)} %bitcast.173, bf16[2,2,2,64,2048]{4,3,2,1,0:T(8,128)(2,1)} %bitcast.184), custom_call_target="tpu_custom_call" | custom-call | flops 1000000000 | bytes 20971520 | tf_op jit(solution)/shard_map/exchange/pallas_call | solution.py:345
  90.0 3.5 dynamic-slice_bitcast_fusion.4
  96.1 4.0 constant_dynamic-update-slice_fusion.1
  105.1 23.6 %attn_fwd.1 = (bf16[2,2,256,1024]{3,2,1,0:T(8,128)(2,1)S(1)}, f32[2,2,8,1,256]{4,3,2,1,0:T(1,128)S(1)}) custom-call(s32[10]{0:T(128)S(1)} %pad_add_fusion.2.tab, bf16[2,2,256,1024]{3,2,1,0:T(8,128)(2,1)S(1)} %copy-done.14, bf16[8,2,2,2,256,128]{5,4,3,2,1,0:T(8,128)(2,1)S(1)} %copy-done.13, s32[2,2,1,256]{3,2,1,0:T(1,128)S(1)} %broadcast_subtract_fusion.st_ref, ...), custom_call_target="tpu_custom_call" | custom-call | flops 20000000000 | bytes 16777216 | tf_op jit(solution)/shard_map/attn_fwd/pallas_call | solution.py:169
  134.2 7.5 collective-permute-done.6
  144.1 4.8 convolution_bitcast_fusion.1
  152.8 11.2 %collective-permute-done.5 = bf16[2,2,64,1024]{3,2,1,0:T(8,128)(2,1)S(1)} collective-permute-done((bf16[2,2,64,1024]{3,2,1,0:T(8,128)(2,1)S(1)}, bf16[2,2,64,1024]{3,2,1,0:T(8,128)(2,1)S(1)}, u32[]{:S(2)}, u32[]{:S(2)}) %collective-permute-start.5) | collective-permute-done | bytes 524320 | tf_op jit(solution)/shard_map/ppermute | solution.py:569
  166.2 6.3 fusion.14
  172.5 16.6 %collective-permute-done.12 = bf16[2,2,64,2048]{3,2,1,0:T(8,128)(2,1)S(1)} collective-permute-done((bf16[2,2,64,2048]{3,2,1,0:T(8,128)(2,1)S(1)}, bf16[2,2,64,2048]{3,2,1,0:T(8,128)(2,1)S(1)}, u32[]{:S(2)}, u32[]{:S(2)}) %collective-permute-start.12) | collective-permute-done | bytes 1048608 | tf_op jit(solution)/shard_map/ppermute | solution.py:569
  196.8 7.9 fusion.22.do_ref
  204.7 2.8 bitcast_add_fusion
  207.5 27.0 %attn_bwd.1 = (bf16[2,2,256,1024]{3,2,1,0:T(8,128)(2,1)S(1)}, f32[8,2,2,2,256,128]{5,4,3,2,1,0:T(8,128)}) custom-call(s32[10]{0:T(128)S(1)} %pad_add_fusion.2.tab, bf16[2,2,256,1024]{3,2,1,0:T(8,128)(2,1)S(1)} %copy-done.15, bf16[2,2,256,1024]{3,2,1,0:T(8,128)(2,1)} %fusion.22.do_ref, bf16[2,2,256,1024]{3,2,1,0:T(8,128)(2,1)} %copy-done.1, ...), custom_call_target="tpu_custom_call" | custom-call | flops 49999998976 | bytes 33554432 | tf_op jit(solution)/shard_map/attn_bwd/pallas_call | solution.py:187
  234.5 7.0 convolution_bitcast_fusion
  241.6 235.1 %reduce_pairs.2 = (f32[2048,128]{1,0:T(8,128)}, f32[128,1024]{1,0:T(8,128)}) custom-call(f32[4,2,2048,128]{3,2,1,0:T(8,128)} %bitcast.185, f32[2,4,2,128,1024]{4,3,2,1,0:T(8,128)} %bitcast.186), custom_call_target="tpu_custom_call" | custom-call | flops 1000000000 | bytes 20971520 | tf_op jit(solution)/shard_map/reduce_pairs/pallas_call | solution.py:439
  478.9 3.1 dynamic-slice_bitcast_fusion
  485.5 9.0 %collective-permute-start.16 = (bf16[2,2,64,256]{3,2,1,0:T(8,128)(2,1)}, bf16[2,2,64,256]{3,2,1,0:T(8,128)(2,1)}, u32[]{:S(2)}, u32[]{:S(2)}) collective-permute-start(bf16[2,2,64,256]{3,2,1,0:T(8,128)(2,1)} %get-tuple-element.92), channel_id=1, source_target_pairs={{0,3},{1,2},{2,1},{3,0},{4,7},{5,6},{6,5},{7,4},{8,11},{9,10},{10,... | collective-permute-start | bytes 393224 | tf_op jit(solution)/shard_map/ppermute | solution.py:569
  515.3 7.4 collective-permute-done.9
  525.8 6.3 fusion.18
  532.2 3.2 add_convert_fusion
  537.7 2.9 convolution_bitcast_fusion.2
  541.5 31.9 %reduce_pairs.3 = f32[128,256]{1,0:T(8,128)} custom-call(f32[2,4,2,128,256]{4,3,2,1,0:T(8,128)} %bitcast.211), custom_call_target="tpu_custom_call" | custom-call | flops 1000000000 | bytes 20971520 | tf_op jit(solution)/shard_map/reduce_pairs/pallas_call | solution.py:439
  577.2 2.9 collective-permute-start.24
  583.2 2.8 bitcast_add_fusion.1
  590.0 3.4 fusion.6
  594.0 8.8 %collective-permute-done.18 = f32[64,2048]{1,0:T(8,128)S(1)} collective-permute-done((f32[64,2048]{1,0:T(8,128)S(1)}, f32[64,2048]{1,0:T(8,128)S(1)}, u32[]{:S(2)}, u32[]{:S(2)}) %collective-permute-start.18) | collective-permute-done | bytes 524320 | tf_op jit(solution)/shard_map/ppermute | solution.py:569
  602.8 9.0 %collective-permute-done.20 = f32[64,2048]{1,0:T(8,128)S(1)} collective-permute-done((f32[64,2048]{1,0:T(8,128)S(1)}, f32[64,2048]{1,0:T(8,128)S(1)}, u32[]{:S(2)}, u32[]{:S(2)}) %collective-permute-start.20) | collective-permute-done | bytes 524320 | tf_op jit(solution)/shard_map/ppermute | solution.py:569
  611.8 20.9 %collective-permute-done.19 = f32[64,2048]{1,0:T(8,128)S(1)} collective-permute-done((f32[64,2048]{1,0:T(8,128)S(1)}, f32[64,2048]{1,0:T(8,128)S(1)}, u32[]{:S(2)}, u32[]{:S(2)}) %collective-permute-start.19) | collective-permute-done | bytes 524320 | tf_op jit(solution)/shard_map/ppermute | solution.py:569
  633.6 160.9 %gather_all.1 = (f32[2048,2048]{1,0:T(8,128)}, f32[2048,2048]{1,0:T(8,128)}, f32[2048,256]{1,0:T(8,128)}, f32[2048,256]{1,0:T(8,128)}) custom-call(f32[64,2048]{1,0:T(8,128)} %fusion.43.refs_0_, f32[128,1024]{1,0:T(8,128)} %get-tuple-element.44.refs_1_, f32[128,128]{1,0:T(8,128)} %get-tuple-element.98.refs_2_, f32[128,128]{1,0:T(8,128)} %get-tuple-element.97.refs_3_), custom_call_target="tpu_custom_call" | custom-call | flops 1000000000 | bytes 79691776 | tf_op jit(solution)/shard_map/gather_all/pallas_call | solution.py:556
  794.6 13.3 %copy.78 = f32[2048,2048]{1,0:T(8,128)} copy(f32[2048,2048]{1,0:T(8,128)} %get-tuple-element.121) | data formatting | bytes 33554432
  813.8 6.2 copy.81
  (204 shorter events, 93.0 us)
Async XLA Ops:
  1.6 98.8 %collective-permute-start.2 = (s32[2,2,64]{2,1,0:T(2,128)S(1)}, s32[2,2,64]{2,1,0:T(2,128)S(1)}, u32[]{:S(2)}, u32[]{:S(2)}) collective-permute-start(s32[2,2,64]{2,1,0:T(2,128)S(1)} %get-tuple-element.102), channel_id=1, source_target_pairs={{0,3},{1,2},{2,1},{3,0},{4,7},{5,6},{6,5},{7,4},{8,11},{9,10},{10,... | collective-permute-start | bytes 3080 | tf_op jit(solution)/shard_map/ppermute | solution.py:569
  4.0 96.3 %collective-permute-start = (s32[2,2,64]{2,1,0:T(2,128)S(1)}, s32[2,2,64]{2,1,0:T(2,128)S(1)}, u32[]{:S(2)}, u32[]{:S(2)}) collective-permute-start(s32[2,2,64]{2,1,0:T(2,128)S(1)} %get-tuple-element.102), channel_id=1, source_target_pairs={{0,1},{1,0},{2,3},{3,2},{4,5},{5,4},{6,7},{7,6},{8,9},{9,8},{10,11... | collective-permute-start | bytes 3080 | tf_op jit(solution)/shard_map/ppermute | solution.py:569
  4.7 95.7 %collective-permute-start.1 = (s32[2,2,64]{2,1,0:T(2,128)S(1)}, s32[2,2,64]{2,1,0:T(2,128)S(1)}, u32[]{:S(2)}, u32[]{:S(2)}) collective-permute-start(s32[2,2,64]{2,1,0:T(2,128)S(1)} %bitcast.204), channel_id=1, source_target_pairs={{0,2},{1,3},{2,0},{3,1},{4,6},{5,7},{6,4},{7,5},{8,10},{9,11},{10,... | collective-permute-start | bytes 3080 | tf_op jit(solution)/shard_map/ppermute | solution.py:569
  93.4 95.6 %collective-permute-start.13 = (bf16[2,2,64,2048]{3,2,1,0:T(8,128)(2,1)}, bf16[2,2,64,2048]{3,2,1,0:T(8,128)(2,1)}, u32[]{:S(2)}, u32[]{:S(2)}) collective-permute-start(bf16[2,2,64,2048]{3,2,1,0:T(8,128)(2,1)} %get-tuple-element.62), channel_id=1, source_target_pairs={{0,3},{1,2},{2,1},{3,0},{4,7},{5,6},{6,5},{7,4},{8,11},{9,10},{10,... | collective-permute-start | bytes 3145736 | tf_op jit(solution)/shard_map/ppermute | solution.py:569
  94.1 47.6 %collective-permute-start.6 = (bf16[2,2,64,2048]{3,2,1,0:T(8,128)(2,1)}, bf16[2,2,64,2048]{3,2,1,0:T(8,128)(2,1)}, u32[]{:S(2)}, u32[]{:S(2)}) collective-permute-start(bf16[2,2,64,2048]{3,2,1,0:T(8,128)(2,1)} %dynamic-slice_bitcast_fusion.2), channel_id=1, source_target_pairs={{0,3},{1,2},{2,1},{3,0},{4,7},{5,6},{6,5},{7,4},{8,11},{9,10},{10,... | collective-permute-start | bytes 3145736 | tf_op jit(solution)/shard_map/ppermute | solution.py:569
  101.1 27.6 %copy-start.8 = (s32[2,256,256]{2,1,0:T(8,128)}, s32[2,256,256]{2,1,0:T(8,128)S(1)}, u32[]{:S(2)}) copy-start(s32[2,256,256]{2,1,0:T(8,128)S(1)} %broadcast_in_dim.5.ko_ref) | copy-start | bytes 1572868
  131.9 20.7 %collective-permute-start.4 = (bf16[2,2,64,1024]{3,2,1,0:T(8,128)(2,1)S(1)}, bf16[2,2,64,1024]{3,2,1,0:T(8,128)(2,1)S(1)}, u32[]{:S(2)}, u32[]{:S(2)}) collective-permute-start(bf16[2,2,64,1024]{3,2,1,0:T(8,128)(2,1)S(1)} %get-tuple-element.72), channel_id=1, source_target_pairs={{0,2},{1,3},{2,0},{3,1},{4,6},{5,7},{6,4},{7,5},{8,10},{9,11},{10,... | collective-permute-start | bytes 1572872 | tf_op jit(solution)/shard_map/ppermute | solution.py:569
  133.3 30.7 %collective-permute-start.5 = (bf16[2,2,64,1024]{3,2,1,0:T(8,128)(2,1)S(1)}, bf16[2,2,64,1024]{3,2,1,0:T(8,128)(2,1)S(1)}, u32[]{:S(2)}, u32[]{:S(2)}) collective-permute-start(bf16[2,2,64,1024]{3,2,1,0:T(8,128)(2,1)S(1)} %get-tuple-element.73), channel_id=1, source_target_pairs={{0,3},{1,2},{2,1},{3,0},{4,7},{5,6},{6,5},{7,4},{8,11},{9,10},{10,... | collective-permute-start | bytes 1572872 | tf_op jit(solution)/shard_map/ppermute | solution.py:569
  133.3 32.0 %collective-permute-start.3 = (bf16[2,2,64,1024]{3,2,1,0:T(8,128)(2,1)S(1)}, bf16[2,2,64,1024]{3,2,1,0:T(8,128)(2,1)S(1)}, u32[]{:S(2)}, u32[]{:S(2)}) collective-permute-start(bf16[2,2,64,1024]{3,2,1,0:T(8,128)(2,1)S(1)} %get-tuple-element.74), channel_id=1, source_target_pairs={{0,1},{1,0},{2,3},{3,2},{4,5},{5,4},{6,7},{7,6},{8,9},{9,8},{10,11... | collective-permute-start | bytes 1572872 | tf_op jit(solution)/shard_map/ppermute | solution.py:569
  141.7 24.5 %slice-start.6 = ((s8[8388608]{0:T(1024)(128)(4,1)}), s8[4194304]{0:T(1024)(128)(4,1)S(1)}, s32[]{:S(2)}) async-start(s8[8388608]{0:T(1024)(128)(4,1)} %bitcast.209), calls=%async_computation.6 | async-start | bytes 8388608
  144.1 19.8 %copy-start.32 = (bf16[2,2,64,2048]{3,2,1,0:T(8,128)(2,1)S(1)}, bf16[2,2,64,2048]{3,2,1,0:T(8,128)(2,1)}, u32[]{:S(2)}) copy-start(bf16[2,2,64,2048]{3,2,1,0:T(8,128)(2,1)} %get-tuple-element.61) | copy-start | bytes 3145732
  144.1 22.0 %slice-start.7 = ((s8[8388608]{0:T(1024)(128)(4,1)}), s8[4194304]{0:T(1024)(128)(4,1)S(1)}, s32[]{:S(2)}) async-start(s8[8388608]{0:T(1024)(128)(4,1)} %bitcast.209), calls=%async_computation.7 | async-start | bytes 8388608
  148.9 55.8 %collective-permute-start.7 = (f32[512,2048]{1,0:T(8,128)S(1)}, f32[512,2048]{1,0:T(8,128)S(1)}, u32[]{:S(2)}, u32[]{:S(2)}) collective-permute-start(f32[512,2048]{1,0:T(8,128)S(1)} %convolution_bitcast_fusion.1), channel_id=1, source_target_pairs={{0,1},{1,0},{2,3},{3,2},{4,5},{5,4},{6,7},{7,6},{8,9},{9,8},{10,11... | collective-permute-start | bytes 12582920 | tf_op jit(solution)/shard_map/ppermute | solution.py:569
  152.6 36.4 %collective-permute-start.11 = (bf16[2,2,64,2048]{3,2,1,0:T(8,128)(2,1)}, bf16[2,2,64,2048]{3,2,1,0:T(8,128)(2,1)S(1)}, u32[]{:S(2)}, u32[]{:S(2)}) collective-permute-start(bf16[2,2,64,2048]{3,2,1,0:T(8,128)(2,1)} %get-tuple-element.62), channel_id=1, source_target_pairs={{0,1},{1,0},{2,3},{3,2},{4,5},{5,4},{6,7},{7,6},{8,9},{9,8},{10,11... | collective-permute-start | bytes 3145736 | tf_op jit(solution)/shard_map/ppermute | solution.py:569
  164.0 25.1 %collective-permute-start.12 = (bf16[2,2,64,2048]{3,2,1,0:T(8,128)(2,1)S(1)}, bf16[2,2,64,2048]{3,2,1,0:T(8,128)(2,1)S(1)}, u32[]{:S(2)}, u32[]{:S(2)}) collective-permute-start(bf16[2,2,64,2048]{3,2,1,0:T(8,128)(2,1)S(1)} %copy-done.32), channel_id=1, source_target_pairs={{0,2},{1,3},{2,0},{3,1},{4,6},{5,7},{6,4},{7,5},{8,10},{9,11},{10,... | collective-permute-start | bytes 3145736 | tf_op jit(solution)/shard_map/ppermute | solution.py:569
  166.2 22.9 %copy-start.21 = (bf16[2,2,1,64,2048]{4,3,1,0,2:T(8,128)(2,1)S(1)}, bf16[2,2,1,64,2048]{4,3,1,0,2:T(8,128)(2,1)}, u32[]{:S(2)}) copy-start(bf16[2,2,1,64,2048]{4,3,1,0,2:T(8,128)(2,1)} %get-tuple-element.60) | copy-start | bytes 3145732
  207.5 27.0 %copy-start.18 = (bf16[2,2,4,64,2048]{4,3,2,1,0:T(8,128)(2,1)S(1)}, bf16[2,2,4,64,2048]{4,3,2,1,0:T(8,128)(2,1)}, u32[]{:S(2)}) copy-start(bf16[2,2,4,64,2048]{4,3,2,1,0:T(8,128)(2,1)} %copy.47) | copy-start | bytes 12582916
  485.5 12.3 %collective-permute-start.15 = (bf16[2,2,64,256]{3,2,1,0:T(8,128)(2,1)}, bf16[2,2,64,256]{3,2,1,0:T(8,128)(2,1)S(1)}, u32[]{:S(2)}, u32[]{:S(2)}) collective-permute-start(bf16[2,2,64,256]{3,2,1,0:T(8,128)(2,1)} %get-tuple-element.90), channel_id=1, source_target_pairs={{0,2},{1,3},{2,0},{3,1},{4,6},{5,7},{6,4},{7,5},{8,10},{9,11},{10,... | collective-permute-start | bytes 393224 | tf_op jit(solution)/shard_map/ppermute | solution.py:569
  485.5 14.6 %collective-permute-start.16 = (bf16[2,2,64,256]{3,2,1,0:T(8,128)(2,1)}, bf16[2,2,64,256]{3,2,1,0:T(8,128)(2,1)}, u32[]{:S(2)}, u32[]{:S(2)}) collective-permute-start(bf16[2,2,64,256]{3,2,1,0:T(8,128)(2,1)} %get-tuple-element.92), channel_id=1, source_target_pairs={{0,3},{1,2},{2,1},{3,0},{4,7},{5,6},{6,5},{7,4},{8,11},{9,10},{10,... | collective-permute-start | bytes 393224 | tf_op jit(solution)/shard_map/ppermute | solution.py:569
  495.9 19.4 %collective-permute-start.10 = (bf16[2,2,64,1024]{3,2,1,0:T(8,128)(2,1)}, bf16[2,2,64,1024]{3,2,1,0:T(8,128)(2,1)}, u32[]{:S(2)}, u32[]{:S(2)}) collective-permute-start(bf16[2,2,64,1024]{3,2,1,0:T(8,128)(2,1)} %get-tuple-element.66), channel_id=1, source_target_pairs={{0,3},{1,2},{2,1},{3,0},{4,7},{5,6},{6,5},{7,4},{8,11},{9,10},{10,... | collective-permute-start | bytes 1572872 | tf_op jit(solution)/shard_map/ppermute | solution.py:569
  495.9 26.9 %collective-permute-start.9 = (bf16[2,2,64,1024]{3,2,1,0:T(8,128)(2,1)}, bf16[2,2,64,1024]{3,2,1,0:T(8,128)(2,1)}, u32[]{:S(2)}, u32[]{:S(2)}) collective-permute-start(bf16[2,2,64,1024]{3,2,1,0:T(8,128)(2,1)} %get-tuple-element.67), channel_id=1, source_target_pairs={{0,2},{1,3},{2,0},{3,1},{4,6},{5,7},{6,4},{7,5},{8,10},{9,11},{10,... | collective-permute-start | bytes 1572872 | tf_op jit(solution)/shard_map/ppermute | solution.py:569
  497.2 26.9 %collective-permute-start.8 = (bf16[2,2,64,1024]{3,2,1,0:T(8,128)(2,1)}, bf16[2,2,64,1024]{3,2,1,0:T(8,128)(2,1)}, u32[]{:S(2)}, u32[]{:S(2)}) collective-permute-start(bf16[2,2,64,1024]{3,2,1,0:T(8,128)(2,1)} %get-tuple-element.68), channel_id=1, source_target_pairs={{0,1},{1,0},{2,3},{3,2},{4,5},{5,4},{6,7},{7,6},{8,9},{9,8},{10,11... | collective-permute-start | bytes 1572872 | tf_op jit(solution)/shard_map/ppermute | solution.py:569
  497.8 85.4 %collective-permute-start.17 = (f32[4,64,2048]{2,1,0:T(8,128)}, f32[4,64,2048]{2,1,0:T(8,128)}, u32[]{:S(2)}, u32[]{:S(2)}) collective-permute-start(f32[4,64,2048]{2,1,0:T(8,128)} %dynamic-slice_bitcast_fusion), channel_id=1, source_target_pairs={{0,4},{1,5},{2,6},{3,7},{4,0},{5,1},{6,2},{7,3},{8,12},{9,13},{10,... | collective-permute-start | bytes 6291464 | tf_op jit(solution)/shard_map/ppermute | solution.py:569
  500.1 3.8 collective-permute-start.14
  536.8 3.8 collective-permute-start.21
  540.6 32.8 %collective-permute-start.22 = (f32[16,128]{1,0:T(8,128)S(1)}, f32[16,128]{1,0:T(8,128)S(1)}, u32[]{:S(2)}, u32[]{:S(2)}) collective-permute-start(f32[16,128]{1,0:T(8,128)S(1)} %bitcast_add_fusion.3), channel_id=1, source_target_pairs={{0,2},{1,3},{2,0},{3,1},{4,6},{5,7},{6,4},{7,5},{8,10},{9,11},{10,... | collective-permute-start | bytes 24584 | tf_op jit(solution)/shard_map/ppermute | solution.py:569
  573.4 3.7 collective-permute-start.23
  577.2 4.5 collective-permute-start.24
  581.7 11.7 %collective-permute-start.25 = (f32[16,128]{1,0:T(8,128)S(1)}, f32[16,128]{1,0:T(8,128)S(1)}, u32[]{:S(2)}, u32[]{:S(2)}) collective-permute-start(f32[16,128]{1,0:T(8,128)S(1)} %add.260), channel_id=1, source_target_pairs={{0,16},{1,17},{2,18},{3,19},{4,20},{5,21},{6,22},{7,23},{8,24},{9,... | collective-permute-start | bytes 24584 | tf_op jit(solution)/shard_map/ppermute | solution.py:569
  586.1 16.6 %collective-permute-start.18 = (f32[64,2048]{1,0:T(8,128)S(1)}, f32[64,2048]{1,0:T(8,128)S(1)}, u32[]{:S(2)}, u32[]{:S(2)}) collective-permute-start(f32[64,2048]{1,0:T(8,128)S(1)} %get-tuple-element.55), channel_id=1, source_target_pairs={{0,8},{1,9},{2,10},{3,11},{4,12},{5,13},{6,14},{7,15},{8,16},{9,17... | collective-permute-start | bytes 1572872 | tf_op jit(solution)/shard_map/ppermute | solution.py:569
  588.2 23.6 %collective-permute-start.20 = (f32[64,2048]{1,0:T(8,128)S(1)}, f32[64,2048]{1,0:T(8,128)S(1)}, u32[]{:S(2)}, u32[]{:S(2)}) collective-permute-start(f32[64,2048]{1,0:T(8,128)S(1)} %get-tuple-element.56), channel_id=1, source_target_pairs={{0,24},{1,25},{2,26},{3,27},{4,28},{5,29},{6,30},{7,31},{8,0},{9,1... | collective-permute-start | bytes 1572872 | tf_op jit(solution)/shard_map/ppermute | solution.py:569
  590.0 42.7 %collective-permute-start.19 = (f32[64,2048]{1,0:T(8,128)S(1)}, f32[64,2048]{1,0:T(8,128)S(1)}, u32[]{:S(2)}, u32[]{:S(2)}) collective-permute-start(f32[64,2048]{1,0:T(8,128)S(1)} %get-tuple-element.57), channel_id=1, source_target_pairs={{0,16},{1,17},{2,18},{3,19},{4,20},{5,21},{6,22},{7,23},{8,24},{9,... | collective-permute-start | bytes 1572872 | tf_op jit(solution)/shard_map/ppermute | solution.py:569
  (36 other events, 248.8 us)

commit v2 on v1

--- a/solution.py
+++ b/solution.py
@@ -20,6 +20,7 @@
 N_PAIRS = 8
 N_SUPER = 2 * N_PAIRS
 MESH = pl.DeviceIdType.MESH
+ONE = pl.Squeezed()
 LATER = 2, 3
 F32 = jnp.float32
 BF16 = jnp.bfloat16
@@ -42,12 +43,24 @@
     return lax.dot_general(a, b, ((ca, cb), ((), ())), preferred_element_type=F32)
 
 
+def cost(gflop, mib):
+    return pl.CostEstimate(flops=gflop * 10**9, bytes_accessed=mib << 20, transcendentals=0)
+
+
+def params(mib, **more):
+    return pltpu.CompilerParams(vmem_limit_bytes=mib << 20, **more)
+
+
 def row_mean(x):
     return jnp.mean(x, axis=-1, keepdims=True)
 
 
 def head(h):
     return pl.ds(h * HEAD_DIM, HEAD_DIM)
+
+
+def head_slice(h):
+    return slice(h * HEAD_DIM, (h + 1) * HEAD_DIM)
 
 
 def dot_t(a, b):
@@ -78,41 +91,52 @@
 
 
 def may_use(s, off, st_ref, qi_ref):
-    return jnp.logical_and(off >= st_ref[0, 0] - s * BLK, off <= qi_ref[0, 0] - s * BLK)
-
-
-def fwd_kernel(tab, q_ref, kv_ref, st_ref, qi_ref, ko_ref, o_ref, lse_ref, acc, m_s, l_s):
+    return jnp.logical_and(off >= st_ref[...] - s * BLK, off <= qi_ref[...] - s * BLK)
+
+
+def fwd_kernel(tab, q_ref, kv_ref, st_ref, qi_ref, ko_ref, o_ref, lse_ref, q_s, acc, m_s, l_s):
     m_s[...] = jnp.full_like(m_s, NEG_BIG)
     l_s[...] = jnp.zeros_like(l_s)
     acc[...] = jnp.zeros_like(acc)
+    for h in range(N_HEADS):
+        q_s[pl.ds(h * BLK, BLK)] = q_ref[:, head(h)]
 
     def body(s, at, masked):
         pair, hk = at
-        k = kv_ref[pair, 0, 0, hk]
-        v_t = kv_ref[pair, 1, 0, hk].T
-        mask = may_use(s, ko_ref[hk], st_ref, qi_ref) if masked else None
+        k, v = kv_ref[pair, 0, hk], kv_ref[pair, 1, hk]
+        if masked:
+            off = ko_ref[hk] + s * BLK
+            mask = [
+                jnp.logical_and(off[:, lanes] >= st_ref[...], off[:, lanes] <= qi_ref[...])
+                for lanes in (slice(HEAD_DIM), slice(HEAD_DIM, BLK))
+            ]
         for h in range(N_HEADS):
-            sc = dot_t(k, q_ref[0, 0, :, head(h)]) * EXP2_SCALE
+            rows = pl.ds(h * BLK, BLK)
+            sc = dot_t(q_s[rows], k)
+            sc = [sc[:, :HEAD_DIM] * EXP2_SCALE, sc[:, HEAD_DIM:] * EXP2_SCALE]
             if masked:
-                sc = jnp.where(mask, sc, NEG_BIG)
-            m_old = m_s[h]
-            m_new = jnp.maximum(m_old, jnp.max(sc, axis=0, keepdims=True))
+                sc = [jnp.where(m, x, NEG_BIG) for m, x in zip(mask, sc)]
+            m_old = m_s[rows]
+            m_new = jnp.maximum(m_old, jnp.max(jnp.maximum(*sc), axis=1, keepdims=True))
             alpha = jnp.exp2(m_old - m_new)
-            p = jnp.exp2(sc - m_new)
-            m_s[h] = m_new
-            l_s[h] = l_s[h] * alpha + jnp.sum(p, axis=0, keepdims=True)
-            acc[h] = acc[h] * alpha + jnp.dot(v_t, p.astype(BF16), preferred_element_type=F32)
+            p = [jnp.exp2(x - m_new) for x in sc]
+            m_s[rows] = m_new
+            l_s[rows] = l_s[rows] * alpha + (p[0] + p[1])
+            p = jnp.hstack([x.astype(BF16) for x in p])
+            acc[rows] = acc[rows] * alpha + jnp.dot(p, v, preferred_element_type=F32)
 
     steps(tab, body)
     for h in range(N_HEADS):
-        o_ref[0, 0, :, head(h)] = (acc[h] / l_s[h]).T.astype(BF16)
-        lse_ref[0, 0, h] = m_s[h] + jnp.log2(l_s[h])
+        rows = pl.ds(h * BLK, BLK)
+        total = jnp.sum(l_s[rows], axis=1, keepdims=True)
+        o_ref[:, head(h)] = (acc[rows] / total).astype(BF16)
+        lse_ref[h] = (m_s[rows] + jnp.log2(total)).T[:1]
 
 
 def bwd_kernel(tab, q_ref, do_ref, o_ref, kv_ref, lse_ref, st_ref, qi_ref, ko_ref, cos_ref, sin_ref, dq_ref, dkv_ref, dq_acc, delta):
     dq_acc[...] = jnp.zeros_like(dq_acc)
     for h in range(N_HEADS):
-        terms = do_ref[0, 0, :, head(h)].astype(F32) * o_ref[0, 0, :, head(h)].astype(F32)
+        terms = do_ref[:, head(h)].astype(F32) * o_ref[:, head(h)].astype(F32)
         delta[h] = jnp.sum(terms.T, axis=0, keepdims=True)
 
     @pl.when(pl.program_id(1) == 0)
@@ -121,31 +145,31 @@
 
     def body(s, at, masked):
         pair, hk = at
-        k = kv_ref[pair, 0, 0, hk]
-        v = kv_ref[pair, 1, 0, hk]
+        k = kv_ref[pair, 0, hk]
+        v = kv_ref[pair, 1, hk]
         k_t = k.T
         mask = may_use(s, ko_ref[hk], st_ref, qi_ref) if masked else None
         dk = dv = jnp.zeros((BLK, HEAD_DIM), F32)
         for h in range(N_HEADS):
-            q = q_ref[0, 0, :, head(h)]
-            do = do_ref[0, 0, :, head(h)]
-            p = jnp.exp2(dot_t(k, q) * EXP2_SCALE - lse_ref[0, 0, h])
+            q = q_ref[:, head(h)]
+            do = do_ref[:, head(h)]
+            p = jnp.exp2(dot_t(k, q) * EXP2_SCALE - lse_ref[h])
             if masked:
                 p = jnp.where(mask, p, 0.0)
             ds = (p * (dot_t(v, do) - delta[h])).astype(BF16)
             dv += jnp.dot(p.astype(BF16), do, preferred_element_type=F32)
             dk += jnp.dot(ds, q, preferred_element_type=F32)
             dq_acc[h] += jnp.dot(k_t, ds, preferred_element_type=F32)
-        dkv_ref[pair, 0, 0, hk] += dk
-        dkv_ref[pair, 1, 0, hk] += dv
+        dkv_ref[pair, 0, hk] += dk
+        dkv_ref[pair, 1, hk] += dv
 
     steps(tab, body)
-    cos_t, sin_t = cos_ref[0, 0], sin_ref[0, 0]
+    cos_t, sin_t = cos_ref[...], sin_ref[...]
     half = HEAD_DIM // 2
     for h in range(N_HEADS):
         a, c = dq_acc[h, :half] * ATTN_SCALE, dq_acc[h, half:] * ATTN_SCALE
         lin = jnp.concatenate([a * cos_t + c * sin_t, c * cos_t - a * sin_t], axis=0)
-        dq_ref[0, 0, :, head(h)] = lin.T.astype(BF16)
+        dq_ref[:, head(h)] = lin.T.astype(BF16)
 
 
 def attn_specs():
@@ -155,17 +179,19 @@
     def at_row(b, h, t):
         return (0, 0, b) + (0,) * 3
 
-    tile = pl.BlockSpec((1, 1, BLK, N_HEADS * HEAD_DIM), at_tile)
-    row = pl.BlockSpec((1, 1, 1, BLK), at_tile)
-    stat = pl.BlockSpec((1, 1, N_HEADS, 1, BLK), lambda b, h, t: (b, h) + (0,) * 3)
-    rope = pl.BlockSpec((1, 1, HEAD_DIM // 2, BLK), at_tile)
-    kv = pl.BlockSpec((N_PAIRS, 2, 1, 2, BLK, HEAD_DIM), at_row)
+    tile = pl.BlockSpec((ONE, ONE, BLK, N_HEADS * HEAD_DIM), at_tile)
+    row = pl.BlockSpec((ONE, ONE, 1, BLK), at_tile)
+    stat = pl.BlockSpec((ONE, ONE, N_HEADS, 1, BLK), lambda b, h, t: (b, h) + (0,) * 3)
+    rope = pl.BlockSpec((ONE, ONE, HEAD_DIM // 2, BLK), at_tile)
+    kv = pl.BlockSpec((N_PAIRS, 2, ONE, 2, BLK, HEAD_DIM), at_row)
     ko = pl.BlockSpec((2, BLK, BLK), lambda b, h, t: (0,) * 3)
     return tile, row, stat, kv, ko, rope
 
 
 def flash_fwd(tab, q, kv, start, qidx, koff):
-    tile, row, stat, kvs, ko, *_ = attn_specs()
+    tile, _, stat, kvs, *_ = attn_specs()
+    col = pl.BlockSpec((ONE, ONE, BLK, HEAD_DIM), lambda b, h, t: (b, h) + (0,) * 2)
+    ko = pl.BlockSpec((2, 1, BLK), lambda b, h, t: (0,) * 3)
     return pl.pallas_call(
         fwd_kernel,
         name="attn_fwd",
@@ -173,12 +199,12 @@
         grid_spec=pltpu.PrefetchScalarGridSpec(
             num_scalar_prefetch=1,
             grid=(2, 2),
-            in_specs=[tile, kvs, row, row, ko],
+            in_specs=[tile, kvs, col, col, ko],
             out_specs=[tile, stat],
-            scratch_shapes=[pltpu.VMEM((N_HEADS, HEAD_DIM, BLK), F32)] + [pltpu.VMEM((N_HEADS, 1, BLK), F32)] * 2,
+            scratch_shapes=[pltpu.VMEM((N_HEADS * BLK, HEAD_DIM), t) for t in (BF16, F32, F32, F32)],
         ),
-        compiler_params=pltpu.CompilerParams(vmem_limit_bytes=40 << 20),
-        cost_estimate=pl.CostEstimate(flops=20 * 10**9, bytes_accessed=16 << 20, transcendentals=18 * 10**6),
+        compiler_params=params(40),
+        cost_estimate=cost(20, 16),
     )(tab, q, kv, start, qidx, koff)
 
 
@@ -198,8 +224,8 @@
             out_specs=[tile, kvs],
             scratch_shapes=[pltpu.VMEM((N_HEADS, HEAD_DIM, BLK), F32), pltpu.VMEM((N_HEADS, 1, BLK), F32)],
         ),
-        compiler_params=pltpu.CompilerParams(vmem_limit_bytes=48 << 20),
-        cost_estimate=pl.CostEstimate(flops=50 * 10**9, bytes_accessed=32 << 20, transcendentals=18 * 10**6),
+        compiler_params=params(48),
+        cost_estimate=cost(50, 32),
     )(tab, q, do, o, kv, lse, start, qidx, koff, cos_t, sin_t)
 
 
@@ -215,7 +241,7 @@
     v = jnp.dot(h, wv_ref[...], preferred_element_type=F32)
     n = kv_ref.shape[3]
     for i in range(2):
-        for j, val in enumerate((turn(k[:, i * HEAD_DIM :][:, :HEAD_DIM], cos_ref, sin_ref), v[:, i * HEAD_DIM :][:, :HEAD_DIM])):
+        for j, val in enumerate((turn(k[:, head_slice(i)], cos_ref, sin_ref), v[:, head_slice(i)])):
             for c in range(2):
                 kv_ref[i, c, j] = val[c * n : (c + 1) * n].astype(BF16)
 
@@ -224,20 +250,19 @@
     q = jnp.dot(h_ref[...], w_ref[...], preferred_element_type=F32)
     n = q_ref.shape[2]
     for j in range(q.shape[1] // HEAD_DIM):
-        val = turn(q[:, j * HEAD_DIM :][:, :HEAD_DIM], cos_ref, sin_ref).astype(BF16)
+        val = turn(q[:, head_slice(j)], cos_ref, sin_ref).astype(BF16)
         for c in range(2):
             q_ref[0, c, :, head(j)] = val[c * n : (c + 1) * n]
 
 
 def project(x, gain, w_q, w_k, w_v, cos_f, sin_f):
     n, d = x.shape
-    params = pltpu.CompilerParams(vmem_limit_bytes=40 << 20)
     h, kv = pl.pallas_call(
         first_kernel,
         name="norm_kv",
         out_shape=(jax.ShapeDtypeStruct(x.shape, BF16), jax.ShapeDtypeStruct((2,) * 3 + (n // 2, HEAD_DIM), BF16)),
-        compiler_params=params,
-        cost_estimate=pl.CostEstimate(flops=2 * 10**9, bytes_accessed=7 << 20, transcendentals=0),
+        compiler_params=params(40),
+        cost_estimate=cost(2, 7),
     )(x, gain, w_k, w_v, cos_f, sin_f)
     tile = 4 * HEAD_DIM
     rope = pl.BlockSpec(cos_f.shape, lambda j: (0, 0))
@@ -248,8 +273,8 @@
         out_shape=jax.ShapeDtypeStruct((2, 2, n // 2, d // 2), BF16),
         in_specs=[pl.BlockSpec(h.shape, lambda j: (0, 0)), pl.BlockSpec((d, tile), lambda j: (0, j)), rope, rope],
         out_specs=pl.BlockSpec((1, 2, n // 2, tile), lambda j: (j // 2, 0, 0, j % 2)),
-        compiler_params=params,
-        cost_estimate=pl.CostEstimate(flops=5 * 10**9, bytes_accessed=12 << 20, transcendentals=0),
+        compiler_params=params(40),
+        cost_estimate=cost(5, 12),
     )(h, w_q, cos_f, sin_f)
     return h, kv, q
 
@@ -283,7 +308,7 @@
     me = lax.axis_index("cp")
     z, y, x, core = place(me)
     pair = me // 4
-    quad = [dev(z, y, 1 - x if d // 2 else x, 1 - core if d % 2 else core) for d in range(4)]
+    quad = quad_of(me)
     across = dev(z, 1 - y, x, core)
     meet(quad[1:] + [across] + [dev(zz, y, x, core) for _, zz in z_peers(z)])
 
@@ -354,108 +379,237 @@
         out_specs=[hbm] * 3,
         scratch_shapes=[dma((3,))] + [dma((3, 4))] * 2 + [dma((4,))] * 4,
         compiler_params=pltpu.CompilerParams(collective_id=1),
-        cost_estimate=pl.CostEstimate(flops=10**9, bytes_accessed=20 << 20, transcendentals=0),
+        cost_estimate=cost(1, 20),
     )(kv, q, dy)
 
 
-def reduce_kernel(cuts, shared, *refs):
+def reduce_kernel(cuts, kinds, work, *refs):
     n = len(cuts)
-    ins, outs, refs = refs[:n], refs[n : 2 * n], refs[2 * n :]
+    ins, refs = refs[:n], refs[n:]
+    extra = work and work.ins
+    more_in, refs = refs[: extra or 0], refs[extra or 0 :]
+    outs, refs = refs[:n], refs[n:]
+    more_out, refs = refs[: work.outs if work else 0], refs[work.outs if work else 0 :]
     own, from_core, from_y, from_z = refs[:n], refs[n : 2 * n], refs[2 * n : 3 * n], refs[3 * n : 4 * n]
-    load_sem, core_s, core_r, y_s, y_r, z_s, z_r = refs[4 * n :]
+    load_sem, core_s, core_r, y_s, y_r, z_s, z_r = refs[4 * n : 4 * n + 7]
     me = lax.axis_index("cp")
     z, y, x, core = place(me)
     partner, across = dev(z, y, x, 1 - core), dev(z, 1 - y, x, core)
-    peers = [across] + [dev(zz, y, x, core) for _, zz in z_peers(z)]
-    meet(peers + [partner] * any(shared))
+    peers = [across, partner] + [dev(zz, y, x, core) for _, zz in z_peers(z)]
+    meet(peers + (quad_of(me)[2:] if work else []))
+    if work:
+        job = Work(me, more_in, more_out, refs[4 * n + 7 :])
+        job.send()
 
     def rows(i, j):
-        size = own[i].shape[2] // cuts[i]
+        size = from_z[i].shape[1] // cuts[i]
         return pl.ds(j * size, size)
 
+    def mine(i, zz, at):
+        return own[i].at[zz, y, at] if kinds[i] == "core" else own[i].at[zz, at]
+
     def load(i, j):
-        src = ins[i].at[core] if shared[i] else ins[i]
-        return pltpu.make_async_copy(src.at[:, :, rows(i, j)], own[i].at[:, :, rows(i, j)], load_sem.at[i, j])
+        src, at = ins[i], rows(i, j)
+        src = {"core": lambda: src.at[core, :, :, at], "z": lambda: src.at[:, at], "": lambda: src.at[:, y, at]}[kinds[i]]()
+        dst = own[i].at[:, :, at] if kinds[i] == "core" else own[i].at[:, at]
+        return pltpu.make_async_copy(src, dst, load_sem.at[i, j])
 
     def core_copy(i, j):
         at = rows(i, j)
         return remote(ins[i].at[1 - core, :, :, at], from_core[i].at[:, :, at], core_s.at[i, j], core_r.at[i, j], partner)
 
     def y_copy(i, j):
-        src = own[i] if shared[i] else ins[i]
+        src = own[i] if kinds[i] == "core" else ins[i]
         at = rows(i, j)
         return remote(src.at[:, 1 - y, at], from_y[i].at[:, at], y_s.at[i, j], y_r.at[i, j], across)
 
-    def z_copy(i, j, k, zz):
+    def z_copies(i, j):
         at = rows(i, j)
-        return remote(
-            own[i].at[zz, y, at], from_z[i].at[k - 1, at], z_s.at[i, j, k - 1], z_r.at[i, j, k - 1], dev(zz, y, x, core)
-        )
+        for k, zz in z_peers(z):
+            yield remote(
+                mine(i, zz, at), from_z[i].at[k - 1, at], z_s.at[i, j, k - 1], z_r.at[i, j, k - 1], dev(zz, y, x, core)
+            )
 
     pieces = [(i, j) for i in range(n) for j in range(cuts[i])]
     for i, j in pieces:
-        if shared[i]:
+        load(i, j).start()
+        if kinds[i] == "core":
             core_copy(i, j).start()
-        else:
+        elif not kinds[i]:
             y_copy(i, j).start()
-        load(i, j).start()
     for i, j in pieces:
         load(i, j).wait()
-        if shared[i]:
+        if kinds[i] == "z":
+            for c in z_copies(i, j):
+                c.start()
+        if kinds[i] == "core":
             core_copy(i, j).wait_recv()
             at = rows(i, j)
             for zz in range(4):
                 own[i][zz, :, at] += from_core[i][zz, :, at]
             y_copy(i, j).start()
+    if work:
+        job.run()
     for i, j in pieces:
-        y_copy(i, j).wait_recv()
-        at = rows(i, j)
-        for zz in range(4):
-            own[i][zz, y, at] += from_y[i][zz, at]
-        for k, zz in z_peers(z):
-            z_copy(i, j, k, zz).start()
+        if kinds[i] != "z":
+            y_copy(i, j).wait_recv()
+            at = rows(i, j)
+            for zz in range(4):
+                mine(i, zz, at)[...] += from_y[i][zz, at]
+            for c in z_copies(i, j):
+                c.start()
     for i, j in pieces:
         at = rows(i, j)
-        for k, zz in z_peers(z):
-            z_copy(i, j, k, zz).wait_recv()
-        outs[i][at] = own[i][z, y, at] + sum(from_z[i][k, at] for k in range(3))
+        for c in z_copies(i, j):
+            c.wait_recv()
+        outs[i][at] = mine(i, z, at)[...] + sum(from_z[i][k, at] for k in range(3))
     for i, j in pieces:
-        if shared[i]:
+        if kinds[i] == "core":
             core_copy(i, j).wait_send()
-        y_copy(i, j).wait_send()
-        for k, zz in z_peers(z):
-            z_copy(i, j, k, zz).wait_send()
-
-
-def reduce_pairs(arrays, cuts, shared, collective_id):
+        if kinds[i] != "z":
+            y_copy(i, j).wait_send()
+        for c in z_copies(i, j):
+            c.wait_send()
+    if work:
+        job.finish()
+
+
+def quad_of(me):
+    z, y, x, core = place(me)
+    return [dev(z, y, 1 - x if d // 2 else x, 1 - core if d % 2 else core) for d in range(4)]
+
+
+class Home:
+    def __init__(self, me, src, out, own_sem, send, arrive):
+        _, _, x, core = place(me)
+        w = src.shape[-1]
+        to = out.at[core, :, :, :, pl.ds(x * w, w)]
+
+        def piece(d):
+            return src.at[:, :, pl.ds(d * CHUNK, CHUNK)]
+
+        self.own = pltpu.make_async_copy(piece(0), to, own_sem)
+        self.copies = [remote(piece(d), to, send.at[d], arrive.at[d], quad_of(me)[d]) for d in (1, 2, 3)]
+
+    def start(self):
+        self.own.start()
+        for c in self.copies:
+            c.start()
+
+    def wait_recv(self):
+        self.own.wait()
+        for c in self.copies:
+            c.wait_recv()
+
+    def wait_send(self):
+        for c in self.copies:
+            c.wait_send()
+
+
+class Work:
+    ins, outs = 5, 2
+
+    def __init__(self, me, ins, outs, scratch):
+        attn, dq, self.hidden, self.w_o, self.w_q = ins
+        self.block_out, self.d_part = outs
+        self.attn_home, self.dq_home, self.buf_o, self.buf_q, own_sem, quad_s, quad_r, self.w_sem = scratch
+        self.homes = [
+            Home(me, src, out, own_sem.at[i], quad_s.at[i], quad_r.at[i])
+            for i, (src, out) in enumerate([(attn, self.attn_home), (dq, self.dq_home)])
+        ]
+
+    def send(self):
+        for h in self.homes:
+            h.start()
+
+    def tiles(self, fetch, use):
+        n = self.w_o.shape[0] // BLK
+        fetch(0, 0).start()
+
+        @pl.loop(0, n)
+        def _(t):
+            slot = lax.rem(t, 2)
+            fetch(t, slot).wait()
+
+            @pl.when(t + 1 < n)
+            def _():
+                fetch(t + 1, 1 - slot).start()
+
+            use(pl.ds(pl.multiple_of(t * BLK, BLK), BLK), slot)
+
+    def run(self):
+        def cols(t):
+            return pl.ds(pl.multiple_of(t * BLK, BLK), BLK)
+
+        def fetch_o(t, slot):
+            return pltpu.make_async_copy(self.w_o.at[:, cols(t)], self.buf_o.at[slot], self.w_sem.at[0, slot])
+
+        def fetch_q(t, slot):
+            return pltpu.make_async_copy(self.w_q.at[cols(t)], self.buf_q.at[slot], self.w_sem.at[1, slot])
+
+        def project(at, slot):
+            attn = self.attn_home[...].reshape(-1, self.w_o.shape[0])
+            out = jnp.dot(attn, self.buf_o[slot], preferred_element_type=F32)
+            self.block_out[:, at] = (self.hidden[:, at].astype(F32) + out).astype(BF16)
+
+        def pull(at, slot):
+            dq = self.dq_home[...].reshape(-1, self.w_o.shape[0])
+            self.d_part[:, at] = dot_t(dq, self.buf_q[slot])
+
+        self.homes[0].wait_recv()
+        self.tiles(fetch_o, project)
+        self.homes[1].wait_recv()
+        self.tiles(fetch_q, pull)
+
+    def finish(self):
+        for h in self.homes:
+            h.wait_send()
+
+
+def reduce_pairs(arrays, cuts, kinds, collective_id, more=()):
     dma = pltpu.SemaphoreType.DMA
     vmem, hbm = pl.BlockSpec(memory_space=pltpu.VMEM), pl.BlockSpec(memory_space=pl.ANY)
     n, most = len(arrays), max(cuts)
     blocks = [a.shape[-2:] for a in arrays]
-    ins = [a.reshape(a.shape[:-3] + (4, 2) + b) for a, b in zip(arrays, blocks)]
-    own = [pltpu.VMEM((4, 2) + b, F32) for b in blocks]
-    scratch = own + [o if s else pltpu.VMEM((8, HEAD_DIM), F32) for o, s in zip(own, shared)]
-    scratch += [pltpu.VMEM((4,) + b, F32) for b in blocks] + [pltpu.VMEM((3,) + b, F32) for b in blocks]
+    own = [pltpu.VMEM(((4, 2) if k == "core" else (4,)) + b, F32) for b, k in zip(blocks, kinds)]
+    unused = pltpu.VMEM((8, HEAD_DIM), F32)
+    scratch = own + [o if k == "core" else unused for o, k in zip(own, kinds)]
+    scratch += [unused if k == "z" else pltpu.VMEM((4,) + b, F32) for b, k in zip(blocks, kinds)]
+    scratch += [pltpu.VMEM((3,) + b, F32) for b in blocks]
+    scratch += [dma((n, most))] * 5 + [dma((n, most, 3))] * 2
+    outs = [jax.ShapeDtypeStruct(b, F32) for b in blocks]
+    if more:
+        hidden, w_o = more[2:4]
+        outs += [jax.ShapeDtypeStruct(hidden.shape, t) for t in (BF16, F32)]
+        scratch += [pltpu.VMEM((2,) * 3 + (CHUNK, w_o.shape[0]), BF16)] * 2
+        scratch += [pltpu.VMEM((2,) + b, BF16) for b in ((w_o.shape[0], BLK), (BLK, w_o.shape[0]))]
+        scratch += [dma((2,)), dma((2, 4)), dma((2, 4)), dma((2, 2))]
     return pl.pallas_call(
-        functools.partial(reduce_kernel, cuts, shared),
+        functools.partial(reduce_kernel, cuts, kinds, Work if more else None),
         name="reduce_pairs",
-        out_shape=[jax.ShapeDtypeStruct(b, F32) for b in blocks],
-        in_specs=[hbm] * n,
-        out_specs=[vmem] * n,
-        scratch_shapes=scratch + [dma((n, most))] * 5 + [dma((n, most, 3))] * 2,
-        compiler_params=pltpu.CompilerParams(collective_id=collective_id, vmem_limit_bytes=56 << 20),
-        cost_estimate=pl.CostEstimate(flops=10**9, bytes_accessed=20 << 20, transcendentals=0),
-    )(*ins)
+        out_shape=outs,
+        in_specs=[hbm] * n + [vmem] * 3 * bool(more) + [hbm] * 2 * bool(more),
+        out_specs=[vmem] * len(outs),
+        scratch_shapes=scratch,
+        compiler_params=params(60, collective_id=collective_id),
+        cost_estimate=cost(1, 20),
+    )(*arrays, *more)
 
 
 def gather_kernel(*refs):
-    shards, outs = refs[:4], refs[4:8]
-    own_sem, zs, fs, ls, cs, zr, fr, lr, cr = refs[8:]
+    shards, refs = refs[:4], refs[4:]
+    dkv_ref, part_ref, wkv_ref, x_ref, dy_ref, gain_ref, *refs = refs
+    outs, refs = refs[:4], refs[4:]
+    dx_ref, dgain_ref, *refs = refs
+    own_sem, zs, fs, ls, cs, zr, fr, lr, cr, dkv_home, terms, all_terms, home_own, home_s, home_r, g_s, g_r = refs
     me = lax.axis_index("cp")
     z, y, x, core = place(me)
     across = (dev(z, y, 1 - x, core), dev(z, 1 - y, x, core))
     partner = dev(z, y, x, 1 - core)
-    meet([partner, *across] + [dev(zz, y, x, core) for _, zz in z_peers(z)])
+    others = [(i, me ^ i) for i in range(1, all_terms.shape[0])]
+    meet([d for _, d in others])
+    back = Home(me, dkv_ref, dkv_home, home_own, home_s, home_r)
+    back.start()
 
     def windows(half, zz, yy, xx, cc):
         pair = 2 * zz + yy
@@ -506,6 +660,9 @@
     def core_copy(half, k, zz, first, last):
         at = half, first, last, k
         return Copy(half, zz, first, last, cs.at[at], cr.at[at], partner, k == first == last == 0)
+
+    def term_copy(i, d):
+        return remote(terms, all_terms.at[i], g_s.at[i], g_r.at[i], d)
 
     owns = []
     for half in halves:
@@ -524,6 +681,10 @@
         if k == 0:
             for o in owns:
                 o.start()
+            back.wait_recv()
+            hidden_gradient(dkv_home, part_ref, wkv_ref, x_ref, dy_ref, gain_ref, dx_ref, terms)
+            for i, d in others:
+                term_copy(i, d).start()
         for half in halves:
             first_copy(half, k, zz).wait_recv()
             last_copy(half, k, zz, 1).start()
@@ -538,6 +699,14 @@
     for k, zz in z_peers(z):
         for half in halves:
             z_copy(half, k, zz).wait_send()
+    total_gain = terms[...]
+    for i, d in others:
+        term_copy(i, d).wait_recv()
+        total_gain += all_terms[i]
+    dgain_ref[...] = total_gain
+    for i, d in others:
+        term_copy(i, d).wait_send()
+    back.wait_send()
     for k, zz in places:
         for half in halves:
             first_copy(half, k, zz).wait_send()
@@ -548,21 +717,46 @@
                     core_copy(half, k, zz, first, last).wait_send()
 
 
-def gather_all(shards, shapes):
+def hidden_gradient(dkv_home, part_ref, wkv_ref, x_ref, dy_ref, gain_ref, dx_ref, terms):
+    size = CHUNK
+    gain = gain_ref[...]
+    terms[...] = jnp.zeros_like(terms)
+
+    @pl.loop(0, x_ref.shape[0] // size)
+    def _(t):
+        at = pl.ds(pl.multiple_of(t * size, size), size)
+        dkv = dkv_home[t // 4, lax.rem(t // 2, 2), lax.rem(t, 2)]
+        d = part_ref[at] + dot_t(dkv, wkv_ref[...])
+        d = d.astype(BF16).astype(F32)
+        x = x_ref[at].astype(F32)
+        inv_rms = lax.rsqrt(row_mean(x * x) + NORM_EPS)
+        unit, scaled = x * inv_rms, d * gain
+        dx = inv_rms * (scaled - unit * row_mean(scaled * unit))
+        dx_ref[at] = (dy_ref[at].astype(F32) + dx).astype(BF16)
+        terms[...] += jnp.sum((d * unit).reshape((-1,) + terms.shape), axis=0)
+
+
+def gather_all(shards, shapes, dkv, part, wkv, x, dy, gain):
     dma = pltpu.SemaphoreType.DMA
     vmem, hbm = pl.BlockSpec(memory_space=pltpu.VMEM), pl.BlockSpec(memory_space=pl.ANY)
     hops = [dma((2,) * i + (4,)) for i in (1, 1, 2, 3)]
     n = len(shards)
+    terms = 8, x.shape[1]
     return pl.pallas_call(
         gather_kernel,
         name="gather_all",
-        out_shape=[jax.ShapeDtypeStruct(s, F32) for s in shapes],
-        in_specs=[vmem] * n,
-        out_specs=[hbm] * n,
-        scratch_shapes=[dma((2 * n,))] + hops + hops,
-        compiler_params=pltpu.CompilerParams(collective_id=0),
-        cost_estimate=pl.CostEstimate(flops=10**9, bytes_accessed=76 << 20, transcendentals=0),
-    )(*shards)
+        out_shape=[jax.ShapeDtypeStruct(s, F32) for s in shapes]
+        + [jax.ShapeDtypeStruct(x.shape, BF16), jax.ShapeDtypeStruct(terms, F32)],
+        in_specs=[vmem] * (n + 6),
+        out_specs=[hbm] * n + [vmem] * 2,
+        scratch_shapes=[dma((2 * n,))]
+        + hops
+        + hops
+        + [pltpu.VMEM((2,) * 3 + (CHUNK, 2 * dkv.shape[-1]), BF16), pltpu.VMEM(terms, F32)]
+        + [pltpu.VMEM((32,) + terms, F32), dma(()), dma((4,)), dma((4,)), dma((32,)), dma((32,))],
+        compiler_params=params(40, collective_id=0),
+        cost_estimate=cost(1, 76),
+    )(*shards, dkv, part, wkv, x, dy, gain)
 
 
 def perm(x, pairs):
@@ -571,10 +765,6 @@
 
 def flip_pairs(d):
     return [(r, r ^ d) for r in range(32)]
-
-
-def turn_z(k):
-    return [(r, (r + 8 * k) % 32) for r in range(32)]
 
 
 def solution(mesh):
@@ -583,7 +773,7 @@
         n_rows = n_batch * n_tok
         wide = N_HEADS * HEAD_DIM
         me = lax.axis_index("cp")
-        z, y, x, core = place(me)
+        _, y, x, core = place(me)
         quad, pair = me % 4, me // 4
         relations = range(4)
 
@@ -599,7 +789,7 @@
 
         gain = norm_gain.astype(F32)
         cos_t, sin_t = rope_tables(positions.reshape(n_rows))
-        cos_f, sin_f = jnp.concatenate([cos_t, cos_t], axis=1), jnp.concatenate([-sin_t, sin_t], axis=1)
+        cos_f, sin_f = jnp.hstack([cos_t, cos_t]), jnp.hstack([-sin_t, sin_t])
         normed, kv_home, q_home = project(hidden.reshape(n_rows, d_model), gain[None], w_q, w_k, w_v, cos_f, sin_f)
         pos_u = unite(positions)
         kv_all, q_u, dy_part = exchange(
@@ -627,19 +817,9 @@
         cos_u, sin_u = rope_tables(pos_u)
         cos_ut, sin_ut = jnp.swapaxes(cos_u, 2, 3), jnp.swapaxes(sin_u, 2, 3)
 
-        attn_u, lse = flash_fwd(tab, q_u, kv_all, start_r, q_index_r, koff)
-
-        def home(arr):
-            return swap([piece[:, :, 0] for piece in jnp.split(arr.reshape(2, 2, 4, CHUNK, -1), 4, axis=2)])
-
-        def in_order(place, own, other, axis):
-            first = place == 0
-            return jnp.concatenate([jnp.where(first, own, other), jnp.where(first, other, own)], axis=axis)
-
-        def join(pieces):
-            flat = [p.reshape(n_rows // 2, -1) for p in pieces]
-            near, far = (in_order(core, *flat[i : i + 2], 0) for i in (0, 2))
-            return in_order(x, near, far, -1)
+        lanes = start.shape + (HEAD_DIM,)
+        start_l, q_index_l = (jnp.broadcast_to(a[..., None], lanes) for a in (start, q_index[None]))
+        attn_u, lse = flash_fwd(tab, q_u, kv_all, start_l, q_index_l, offsets[:, None])
 
         tok = tuple(range(3))
         half_wide = wide // 2
@@ -653,46 +833,36 @@
         d_attn, wo_sum = lax.optimization_barrier((d_attn, wo_sum))
         dq_u, dkv = flash_bwd(tab, q_u, d_attn, attn_u, kv_all, lse, start_r, q_index_r, koff, cos_ut, sin_ut)
 
-        attn_home = join(home(attn_u))
-        block_out = (hidden.astype(F32) + jnp.dot(attn_home, w_o, preferred_element_type=F32).reshape(hidden.shape)).astype(BF16)
-
         wo_sum = pick(wo_sum, y, 1) + wo_y
-        wo_own = pick(wo_sum, z, 0)
-        for k, zz in z_peers(z):
-            wo_own = wo_own + perm(pick(wo_sum, zz, 0), turn_z(k))
-
-        dq_home = join(home(dq_u))
         half_model = d_model // 2
 
         def by_core(d_out):
             part = lax.optimization_barrier(dot(normed_u, d_out, tok, tok))
-            return part.reshape(2, N_PAIRS, half_model // N_PAIRS, -1)
-
-        dkv_own, wq_own = reduce_pairs([dkv.reshape(N_PAIRS, -1, HEAD_DIM), by_core(dq_u)], (4, 2), (False, True), 2)
+            return part.reshape(2, 4, 2, half_model // N_PAIRS, -1)
+
+        x_flat = hidden.reshape(n_rows, d_model)
+        dkv_own, wq_own, wo_own, block_out, d_part = reduce_pairs(
+            [dkv.reshape(4, 2, -1, HEAD_DIM), by_core(dq_u), wo_sum], (4, 2, 1), ("", "core", "z"), 2, (attn_u, dq_u, x_flat, w_o, w_q)
+        )
         dkv_own = dkv_own.reshape((2,) * 3 + (BLK, HEAD_DIM))
         dk_u = rotate(dkv_own[0] * ATTN_SCALE, cos_u, -sin_u).astype(BF16)
         dkv_u = jnp.concatenate([dk_u, dkv_own[1].astype(BF16)], axis=-1)
-        (wkv_own,) = reduce_pairs([by_core(dkv_u)], (1,), (True,), 3)
-
-        dkv_home = join(home(dkv_u)).reshape(n_rows, 2, 2, HEAD_DIM)
-        dk_home, dv_home = (dkv_home[:, :, i].reshape(n_rows, -1) for i in range(2))
-        d_normed = dot_t(dq_home, w_q) + dot_t(dk_home, w_k) + dot_t(dv_home, w_v)
-        d_normed = d_normed.astype(BF16).astype(F32).reshape(hidden.shape)
-        hidden_f32 = hidden.astype(F32)
-        inv_rms = lax.rsqrt(row_mean(hidden_f32 * hidden_f32) + NORM_EPS)
-        scaled = d_normed * gain
-        unit = hidden_f32 * inv_rms
-        d_hidden = inv_rms * (scaled - unit * row_mean(scaled * unit))
-        grad_hidden = (grad_out.astype(F32) + d_hidden).astype(BF16)
-        d_gain = jnp.sum(d_normed * unit, axis=(0, 1)).reshape(-1, 128)
-        for i in range(5):
-            d_gain = d_gain + perm(d_gain, flip_pairs(1 << i))
+        (wkv_own,) = reduce_pairs([by_core(dkv_u)], (1,), ("core",), 3)
 
         wk_own, wv_own = jnp.split(wkv_own, 2, axis=1)
-        grad_wo, grad_wq, grad_wk, grad_wv = gather_all(
-            [wo_own, wq_own, wk_own, wv_own], [w_o.shape, w_q.shape, w_k.shape, w_v.shape]
+        w_kv = jnp.hstack([w[:, head_slice(i)] for i in range(2) for w in (w_k, w_v)])
+        grad_wo, grad_wq, grad_wk, grad_wv, grad_x, d_gain = gather_all(
+            [wo_own, wq_own, wk_own, wv_own],
+            [w_o.shape, w_q.shape, w_k.shape, w_v.shape],
+            dkv_u,
+            d_part,
+            w_kv,
+            x_flat,
+            grad_out.reshape(n_rows, d_model),
+            gain[None],
         )
-        return block_out, grad_hidden, grad_wq, grad_wk, grad_wv, grad_wo, d_gain.reshape(d_model)
+        block_out, grad_x = (a.reshape(hidden.shape) for a in (block_out, grad_x))
+        return block_out, grad_x, grad_wq, grad_wk, grad_wv, grad_wo, jnp.sum(d_gain, axis=0)
 
     seq_spec = P(None, "cp", None)
     tok_spec = P(None, "cp")

time: 837 us -> 781 us (0.933)
  Pallas kernels: 553 us -> 597 us
  waiting for transfers between devices: 88 us -> 53.6 us
  starting transfers between devices: 31.4 us -> 8.48 us
  matrix products: 42.9 us -> 22.5 us
  other arithmetic: 30.4 us -> 18 us
    ppermute x26 -> x9, waiting for transfers between devices: 88 us -> 53.6 us  [perm(): return lax.ppermute(x, 'cp', pairs)]
    pallas_call x1, Pallas kernels: 161 us -> 194 us  [gather_all(): pl.pallas_call(gather_kernel, name='gather_all', out_shape=[jax.ShapeDtyp...]
    ppermute x26 -> x9, starting transfers between devices: 31.4 us -> 8.48 us  [perm(): return lax.ppermute(x, 'cp', pairs)]
    pallas_call x2, Pallas kernels: 267 us -> 287 us  [reduce_pairs(): pl.pallas_call(functools.partial(reduce_kernel, cuts, kinds, Work if more...]
    dot_general x8 -> x5, matrix products: 36.6 us -> 22.5 us  [dot(): lax.dot_general(a, b, ((ca, cb), ((), ())), preferred_element_type=F32)]
    unnamed x91 -> x77, local copies, waits for them, and re-layouts: 44.6 us -> 49.4 us
  transfers between devices with their start and end apart: 26 -> 9, of which waited for: 11 -> 2; matrix products, arithmetic and copies ran while one was open for 11% -> 5% of each run, Pallas kernels for 16% -> 15%
where the time goes in v2:
time: 781 us; the launch traced here: 766 us
  Pallas kernels  597 us (76%)
  local copies, waits for them, and re-layouts  65.1 us (8%)
  waiting for transfers between devices  53.6 us (7%)
  matrix products  22.5 us (3%)
  other arithmetic  18 us (2%)
  starting transfers between devices  8.48 us (1%)
    pallas_call x2, Pallas kernels, reduce_pairs(): pl.pallas_call(functools.partial(reduce_kernel, cuts, kinds, Work if more...  287 us
    pallas_call x1, Pallas kernels, gather_all(): pl.pallas_call(gather_kernel, name='gather_all', out_shape=[jax.ShapeDtyp...  194 us
    pallas_call x1, Pallas kernels, exchange(): pl.pallas_call(exchange_kernel, name='exchange', out_shape=(jax.ShapeDtyp...  64.9 us
    ppermute x9, waiting for transfers between devices, perm(): return lax.ppermute(x, 'cp', pairs)  53.6 us
    unnamed x77, local copies, waits for them, and re-layouts  49.4 us
    pallas_call x1, Pallas kernels, flash_bwd(): pl.pallas_call(bwd_kernel, name='attn_bwd', out_shape=(jax.ShapeDtypeStru...  26.9 us
    dot_general x5, matrix products, dot(): lax.dot_general(a, b, ((ca, cb), ((), ())), preferred_element_type=F32)  22.5 us
    pallas_call x1, Pallas kernels, flash_fwd(): pl.pallas_call(fwd_kernel, name='attn_fwd', out_shape=(jax.ShapeDtypeStru...  15.6 us
  transfers between devices with their start and end apart: 9, of which 2 were waited for; matrix products, arithmetic and copies ran while one was open for 5% of the time, Pallas kernels for 15%

profile of v2, /device:TPU:0, one launch (start us, length us, event | category | flops | bytes accessed | tf_op | source)
XLA Modules:
  0.0 766.0 jit_solution(6436451116491724791)
XLA Ops:
  1.6 2.4 collective-permute-start.2
  6.1 2.3 dynamic-slice_bitcast_fusion.2
  11.0 1.8 norm_kv.1
  13.6 6.8 query.1
  21.7 64.9 %exchange.1 = (bf16[8,2,2,2,256,128]{5,4,3,2,1,0:T(8,128)(2,1)}, bf16[2,2,256,1024]{3,2,1,0:T(8,128)(2,1)}, bf16[2,2,192,2048]{3,2,1,0:T(8,128)(2,1)}) custom-call(bf16[2,2,2,2,2,64,128]{6,5,4,3,2,1,0:T(8,128)(2,1)} %bitcast.86, bf16[2,2,2,2,64,1024]{5,4,3,2,1,0:T(8,128)(2,1)} %bitcast.85, bf16[2,2,2,64,2048]{4,3,2,1,0:T(8,128)(2,1)} %bitcast.78), custom_call_target="tpu_custom_call" | custom-call | flops 1000000000 | bytes 20971520 | tf_op jit(solution)/shard_map/exchange/pallas_call | solution.py:370
  87.8 4.0 constant_dynamic-update-slice_fusion.1
  93.0 2.2 copy-done.21
  95.2 1.6 copy-done.22
  96.8 15.6 %attn_fwd.1 = (bf16[2,2,256,1024]{3,2,1,0:T(8,128)(2,1)S(1)}, f32[2,2,8,1,256]{4,3,2,1,0:T(1,128)S(1)}) custom-call(s32[10]{0:T(128)S(1)} %pad_add_fusion.2.tab, bf16[2,2,256,1024]{3,2,1,0:T(8,128)(2,1)S(1)} %copy-done.22, bf16[8,2,2,2,256,128]{5,4,3,2,1,0:T(8,128)(2,1)S(1)} %copy-done.21, s32[2,2,256,128]{3,2,1,0:T(8,128)S(1)} %broadcast_in_dim.14.st_ref, ...), custom_call_target="tpu_custom_call" | custom-call | flops 20000000000 | bytes 16777216 | tf_op jit(solution)/shard_map/attn_fwd/pallas_call | solution.py:195
  112.4 2.1 constant_dynamic-update-slice_fusion
  114.5 4.5 convolution_bitcast_fusion.1
  119.1 1.9 dynamic-slice_bitcast_fusion.4
  127.2 42.0 %collective-permute-done.6 = bf16[2,2,64,2048]{3,2,1,0:T(8,128)(2,1)} collective-permute-done((bf16[2,2,64,2048]{3,2,1,0:T(8,128)(2,1)}, bf16[2,2,64,2048]{3,2,1,0:T(8,128)(2,1)}, u32[]{:S(2)}, u32[]{:S(2)}) %collective-permute-start.6) | collective-permute-done | bytes 1048608 | tf_op jit(solution)/shard_map/ppermute | solution.py:763
  169.3 2.8 pad_maximum_fusion
  172.1 2.4 copy.27
  175.8 2.4 fusion.7
  178.2 5.7 fusion.3.do_ref
  184.0 3.1 bitcast_add_fusion
  188.6 2.5 collective-permute-start.8
  191.3 26.9 %attn_bwd.1 = (bf16[2,2,256,1024]{3,2,1,0:T(8,128)(2,1)S(1)}, f32[8,2,2,2,256,128]{5,4,3,2,1,0:T(8,128)}) custom-call(s32[10]{0:T(128)S(1)} %pad_add_fusion.2.tab, bf16[2,2,256,1024]{3,2,1,0:T(8,128)(2,1)S(1)} %copy-done.23, bf16[2,2,256,1024]{3,2,1,0:T(8,128)(2,1)} %fusion.3.do_ref, bf16[2,2,256,1024]{3,2,1,0:T(8,128)(2,1)} %copy-done.2, ...), custom_call_target="tpu_custom_call" | custom-call | flops 49999998976 | bytes 33554432 | tf_op jit(solution)/shard_map/attn_bwd/pallas_call | solution.py:213
  218.2 7.2 convolution_bitcast_fusion
  225.4 11.5 %collective-permute-done.8 = f32[4,64,2048]{2,1,0:T(8,128)S(1)} collective-permute-done((f32[4,64,2048]{2,1,0:T(8,128)}, f32[4,64,2048]{2,1,0:T(8,128)S(1)}, u32[]{:S(2)}, u32[]{:S(2)}) %collective-permute-start.8) | collective-permute-done | bytes 2097184 | tf_op jit(solution)/shard_map/ppermute | solution.py:763
  236.8 1.6 bitcast_add_fusion.1.refs_2_
  238.5 256.6 %reduce_pairs.2 = (f32[2048,128]{1,0:T(8,128)}, f32[128,1024]{1,0:T(8,128)}, f32[64,2048]{1,0:T(8,128)}, bf16[512,2048]{1,0:T(8,128)(2,1)}, f32[512,2048]{1,0:T(8,128)}) custom-call(f32[4,2,2048,128]{3,2,1,0:T(8,128)} %bitcast.95, f32[2,4,2,128,1024]{4,3,2,1,0:T(8,128)} %bitcast.96, f32[4,64,2048]{2,1,0:T(8,128)} %bitcast_add_fusion.1.refs_2_, ...), custom_call_target="tpu_custom_call" | custom-call | flops 1000000000 | bytes 20971520 | tf_op jit(solution)/shard_map/reduce_pairs/pallas_call | solution.py:587
  497.6 2.4 fusion.12
  500.3 2.7 convolution_bitcast_fusion.2
  503.0 30.7 %reduce_pairs.3 = f32[128,256]{1,0:T(8,128)} custom-call(f32[2,4,2,128,256]{4,3,2,1,0:T(8,128)} %bitcast.107), custom_call_target="tpu_custom_call" | custom-call | flops 1000000000 | bytes 20971520 | tf_op jit(solution)/shard_map/reduce_pairs/pallas_call | solution.py:587
  537.8 193.9 %gather_all.1 = (f32[2048,2048]{1,0:T(8,128)}, f32[2048,2048]{1,0:T(8,128)}, f32[2048,256]{1,0:T(8,128)S(1)}, f32[2048,256]{1,0:T(8,128)S(1)}, bf16[512,2048]{1,0:T(8,128)(2,1)S(1)}, /*index=5*/f32[8,2048]{1,0:T(8,128)S(1)}) custom-call(f32[64,2048]{1,0:T(8,128)S(1)} %copy-done.20, f32[128,1024]{1,0:T(8,128)S(1)} %copy-done.19, ...), custom_call_target="tpu_custom_call" | custom-call | flops 1000000000 | bytes 79691776 | tf_op jit(solution)/shard_map/gather_all/pallas_call | solution.py:745
  736.3 3.2 copy.51
  740.8 14.6 %copy.53 = f32[2048,2048]{1,0:T(8,128)} copy(f32[2048,2048]{1,0:T(8,128)} %get-tuple-element.99) | data formatting | bytes 33554432
  756.7 1.8 copy-done.10
  759.8 6.2 copy.56
  (126 shorter events, 34.5 us)
Async XLA Ops:
  0.6 9.0 %copy-start.16 = (bf16[2048,256]{1,0:T(8,128)(2,1)S(1)}, bf16[2048,256]{1,0:T(8,128)(2,1)}, u32[]{:S(2)}) copy-start(bf16[2048,256]{1,0:T(8,128)(2,1)} %wk_ref.1) | copy-start | bytes 3145732
  0.6 9.0 %copy-start.3 = (bf16[4,128,2048]{2,1,0:T(8,128)(2,1)S(1)}, bf16[4,128,2048]{2,1,0:T(8,128)(2,1)}, u32[]{:S(2)}) copy-start(bf16[4,128,2048]{2,1,0:T(8,128)(2,1)} %param.9) | copy-start | bytes 6291460
  1.6 90.4 %collective-permute-start.2 = (s32[2,2,64]{2,1,0:T(2,128)S(1)}, s32[2,2,64]{2,1,0:T(2,128)S(1)}, u32[]{:S(2)}, u32[]{:S(2)}) collective-permute-start(s32[2,2,64]{2,1,0:T(2,128)S(1)} %get-tuple-element.78), channel_id=1, source_target_pairs={{0,3},{1,2},{2,1},{3,0},{4,7},{5,6},{6,5},{7,4},{8,11},{9,10},{10,... | collective-permute-start | bytes 3080 | tf_op jit(solution)/shard_map/ppermute | solution.py:763
  4.0 88.0 %collective-permute-start = (s32[2,2,64]{2,1,0:T(2,128)S(1)}, s32[2,2,64]{2,1,0:T(2,128)S(1)}, u32[]{:S(2)}, u32[]{:S(2)}) collective-permute-start(s32[2,2,64]{2,1,0:T(2,128)S(1)} %get-tuple-element.78), channel_id=1, source_target_pairs={{0,1},{1,0},{2,3},{3,2},{4,5},{5,4},{6,7},{7,6},{8,9},{9,8},{10,11... | collective-permute-start | bytes 3080 | tf_op jit(solution)/shard_map/ppermute | solution.py:763
  4.7 87.4 %collective-permute-start.1 = (s32[2,2,64]{2,1,0:T(2,128)S(1)}, s32[2,2,64]{2,1,0:T(2,128)S(1)}, u32[]{:S(2)}, u32[]{:S(2)}) collective-permute-start(s32[2,2,64]{2,1,0:T(2,128)S(1)} %bitcast.102), channel_id=1, source_target_pairs={{0,2},{1,3},{2,0},{3,1},{4,6},{5,7},{6,4},{7,5},{8,10},{9,11},{10,... | collective-permute-start | bytes 3080 | tf_op jit(solution)/shard_map/ppermute | solution.py:763
  9.4 4.3 copy-start.1
  13.6 6.8 copy-start.7
  86.7 25.8 %collective-permute-start.3 = (bf16[2,2,64,2048]{3,2,1,0:T(8,128)(2,1)}, bf16[2,2,64,2048]{3,2,1,0:T(8,128)(2,1)}, u32[]{:S(2)}, u32[]{:S(2)}) collective-permute-start(bf16[2,2,64,2048]{3,2,1,0:T(8,128)(2,1)} %dynamic-slice_bitcast_fusion.2), channel_id=1, source_target_pairs={{0,3},{1,2},{2,1},{3,0},{4,7},{5,6},{6,5},{7,4},{8,11},{9,10},{10,... | collective-permute-start | bytes 3145736 | tf_op jit(solution)/shard_map/ppermute | solution.py:763
  96.8 15.7 %copy-start.24 = (bf16[2,2,256,2048]{3,2,1,0:T(8,128)(2,1)S(1)}, bf16[2,2,256,2048]{3,2,1,0:T(8,128)(2,1)}, u32[]{:S(2)}) copy-start(bf16[2,2,256,2048]{3,2,1,0:T(8,128)(2,1)} %constant_dynamic-update-slice_fusion.1) | copy-start | bytes 12582916
  112.4 62.1 %copy-start.2 = (bf16[2,2,256,1024]{3,2,1,0:T(8,128)(2,1)}, bf16[2,2,256,1024]{3,2,1,0:T(8,128)(2,1)S(1)}, u32[]{:S(2)}) copy-start(bf16[2,2,256,1024]{3,2,1,0:T(8,128)(2,1)S(1)} %get-tuple-element.41.o_ref.refs_3_) | copy-start | bytes 6291460
  114.5 4.5 copy-start.25
  114.5 4.5 copy-start.8
  119.1 64.9 %collective-permute-start.4 = (f32[512,2048]{1,0:T(8,128)}, f32[512,2048]{1,0:T(8,128)}, u32[]{:S(2)}, u32[]{:S(2)}) collective-permute-start(f32[512,2048]{1,0:T(8,128)} %convolution_bitcast_fusion.1), channel_id=1, source_target_pairs={{0,1},{1,0},{2,3},{3,2},{4,5},{5,4},{6,7},{7,6},{8,9},{9,8},{10,11... | collective-permute-start | bytes 12582920 | tf_op jit(solution)/shard_map/ppermute | solution.py:763
  121.0 48.2 %collective-permute-start.7 = (bf16[2,2,64,2048]{3,2,1,0:T(8,128)(2,1)}, bf16[2,2,64,2048]{3,2,1,0:T(8,128)(2,1)}, u32[]{:S(2)}, u32[]{:S(2)}) collective-permute-start(bf16[2,2,64,2048]{3,2,1,0:T(8,128)(2,1)} %get-tuple-element.64), channel_id=1, source_target_pairs={{0,3},{1,2},{2,1},{3,0},{4,7},{5,6},{6,5},{7,4},{8,11},{9,10},{10,... | collective-permute-start | bytes 3145736 | tf_op jit(solution)/shard_map/ppermute | solution.py:763
  121.8 47.5 %collective-permute-start.5 = (bf16[2,2,64,2048]{3,2,1,0:T(8,128)(2,1)}, bf16[2,2,64,2048]{3,2,1,0:T(8,128)(2,1)}, u32[]{:S(2)}, u32[]{:S(2)}) collective-permute-start(bf16[2,2,64,2048]{3,2,1,0:T(8,128)(2,1)} %get-tuple-element.64), channel_id=1, source_target_pairs={{0,1},{1,0},{2,3},{3,2},{4,5},{5,4},{6,7},{7,6},{8,9},{9,8},{10,11... | collective-permute-start | bytes 3145736 | tf_op jit(solution)/shard_map/ppermute | solution.py:763
  121.8 47.5 %collective-permute-start.6 = (bf16[2,2,64,2048]{3,2,1,0:T(8,128)(2,1)}, bf16[2,2,64,2048]{3,2,1,0:T(8,128)(2,1)}, u32[]{:S(2)}, u32[]{:S(2)}) collective-permute-start(bf16[2,2,64,2048]{3,2,1,0:T(8,128)(2,1)} %get-tuple-element.63), channel_id=1, source_target_pairs={{0,2},{1,3},{2,0},{3,1},{4,6},{5,7},{6,4},{7,5},{8,10},{9,11},{10,... | collective-permute-start | bytes 3145736 | tf_op jit(solution)/shard_map/ppermute | solution.py:763
  169.2 8.9 %slice-start.4 = ((s8[8388608]{0:T(1024)(128)(4,1)}), s8[4194304]{0:T(1024)(128)(4,1)S(1)}, s32[]{:S(2)}) async-start(s8[8388608]{0:T(1024)(128)(4,1)} %bitcast.93), calls=%async_computation.4 | async-start | bytes 8388608
  172.1 6.1 slice-start.5
  187.0 4.3 copy-start.23
  188.6 48.3 %collective-permute-start.8 = (f32[4,64,2048]{2,1,0:T(8,128)}, f32[4,64,2048]{2,1,0:T(8,128)S(1)}, u32[]{:S(2)}, u32[]{:S(2)}) collective-permute-start(f32[4,64,2048]{2,1,0:T(8,128)} %dynamic-slice_bitcast_fusion), channel_id=1, source_target_pairs={{0,4},{1,5},{2,6},{3,7},{4,0},{5,1},{6,2},{7,3},{8,12},{9,13},{10,... | collective-permute-start | bytes 6291464 | tf_op jit(solution)/shard_map/ppermute | solution.py:763
  191.3 26.9 %copy-start.27 = (bf16[2,2,4,64,2048]{4,3,2,1,0:T(8,128)(2,1)S(1)}, bf16[2,2,4,64,2048]{4,3,2,1,0:T(8,128)(2,1)}, u32[]{:S(2)}) copy-start(bf16[2,2,4,64,2048]{4,3,2,1,0:T(8,128)(2,1)} %copy.27) | copy-start | bytes 12582916
  218.2 7.2 copy-start.6
  495.1 5.2 copy-start.28
  500.3 34.3 %copy-start = (bf16[4,128,2048]{2,1,0:T(8,128)(2,1)S(1)}, bf16[4,128,2048]{2,1,0:T(8,128)(2,1)}, u32[]{:S(2)}) copy-start(bf16[4,128,2048]{2,1,0:T(8,128)(2,1)} %param.10) | copy-start | bytes 6291460
  500.3 34.3 %copy-start.19 = (f32[128,1024]{1,0:T(8,128)S(1)}, f32[128,1024]{1,0:T(8,128)}, u32[]{:S(2)}) copy-start(f32[128,1024]{1,0:T(8,128)} %get-tuple-element.50.refs_1_) | copy-start | bytes 1572868
  500.3 34.3 %copy-start.20 = (f32[64,2048]{1,0:T(8,128)S(1)}, f32[64,2048]{1,0:T(8,128)}, u32[]{:S(2)}) copy-start(f32[64,2048]{1,0:T(8,128)} %get-tuple-element.49.refs_0_) | copy-start | bytes 1572868
  735.6 3.8 copy-start.14
  739.5 20.4 %slice-start = ((s8[16777216]{0:T(1024)(128)(4,1)}), s8[4194304]{0:T(1024)(128)(4,1)S(1)}, s32[]{:S(2)}) async-start(s8[16777216]{0:T(1024)(128)(4,1)} %bitcast.91), calls=%async_computation | async-start | bytes 8388608
  740.8 14.6 %copy-start.12 = (f32[2048,256]{1,0:T(8,128)S(1)}, f32[2048,256]{1,0:T(8,128)}, u32[]{:S(2)}) copy-start(f32[2048,256]{1,0:T(8,128)} %copy-done.11) | copy-start | bytes 6291460
  740.8 19.0 %slice-start.1 = ((s8[16777216]{0:T(1024)(128)(4,1)}), s8[4194304]{0:T(1024)(128)(4,1)S(1)}, s32[]{:S(2)}) async-start(s8[16777216]{0:T(1024)(128)(4,1)} %bitcast.91), calls=%async_computation.1 | async-start | bytes 8388608
  740.8 19.0 %slice-start.2 = ((s8[16777216]{0:T(1024)(128)(4,1)}), s8[4194304]{0:T(1024)(128)(4,1)S(1)}, s32[]{:S(2)}) async-start(s8[16777216]{0:T(1024)(128)(4,1)} %bitcast.91), calls=%async_computation.2 | async-start | bytes 8388608
  740.8 19.0 %slice-start.3 = ((s8[16777216]{0:T(1024)(128)(4,1)}), s8[4194304]{0:T(1024)(128)(4,1)S(1)}, s32[]{:S(2)}) async-start(s8[16777216]{0:T(1024)(128)(4,1)} %bitcast.91), calls=%async_computation.3 | async-start | bytes 8388608
  (12 other events, 21.2 us)

commit v3 on v2

v3 whole, which is shorter than its diff:
```python
import functools

import jax
import jax.numpy as jnp
from jax import lax
from jax.experimental import pallas as pl
from jax.experimental.pallas import tpu as pltpu
from jax.sharding import PartitionSpec as P

HEAD_DIM = 128
NORM_EPS = 1e-5
ROPE_BASE = 500000.0
NEG_BIG = -1e30
LOG2E = 1.4426950408889634
ATTN_SCALE = HEAD_DIM**-0.5
EXP2_SCALE = ATTN_SCALE * LOG2E
CHUNK = 64
TWO = 2
NEW = jnp.newaxis
BLK = 4 * CHUNK
N_HEADS = 8
N_PAIRS = 8
N_SUPER = 2 * N_PAIRS
MESH = pl.DeviceIdType.MESH
ONE = pl.Squeezed()
LATER = 2, 3
PRODUCTS_AT = 3, 7
F32 = jnp.float32
BF16 = jnp.bfloat16

T_SQ, T_LO, T_MX = 0, 2, 6


def rope_tables(positions):
    inv_freq = ROPE_BASE ** (-jnp.arange(0, HEAD_DIM, TWO).astype(F32) / HEAD_DIM)
    angles = positions.astype(F32)[..., None] * inv_freq
    return jnp.cos(angles), jnp.sin(angles)


def rotate(x, cos_t, sin_t):
    a, b = x[..., : HEAD_DIM // TWO], x[..., HEAD_DIM // TWO :]
    return jnp.concatenate([a * cos_t - b * sin_t, b * cos_t + a * sin_t], axis=-1)


def dot(a, b, ca, cb):
    return lax.dot_general(a, b, ((ca, cb), ((), ())), preferred_element_type=F32)


def cost(gflop, mib):
    return pl.CostEstimate(flops=gflop * 10**9, bytes_accessed=mib << 20, transcendentals=0)


def params(mib, **more):
    return pltpu.CompilerParams(vmem_limit_bytes=mib << 20, **more)


def row_mean(x):
    return jnp.mean(x, axis=-1, keepdims=True)


def head(h):
    return pl.ds(h * HEAD_DIM, HEAD_DIM)


def head_slice(h):
    return slice(h * HEAD_DIM, (h + 1) * HEAD_DIM)


def dot_t(a, b):
    return dot(a, b, (1,), (1,))


def dyn(x, index, size, axis):
    return lax.dynamic_slice_in_dim(x, index, size, axis)


def pick(x, index, axis):
    return lax.dynamic_index_in_dim(x, index, axis, keepdims=False)


def steps(tab, body):
    b, hf = pl.program_id(0), pl.program_id(1)
    own, first, last_start = tab[T_SQ + hf], tab[T_LO + TWO * b + hf], tab[T_MX + TWO * b + hf]

    def step(s, carry):
        late = s >= N_PAIRS
        at = jnp.where(late, N_SUPER - 1 - s, s), late.astype(jnp.int32)
        full = jnp.logical_and(s < own, s * BLK >= last_start)
        pl.when(full)(lambda: body(s, at, False))
        pl.when(jnp.logical_not(full))(lambda: body(s, at, True))
        return carry

    lax.fori_loop(first, own + 1, step, 0)


def may_use(s, off, st_ref, qi_ref):
    return jnp.logical_and(off >= st_ref[...] - s * BLK, off <= qi_ref[...] - s * BLK)


def fwd_kernel(tab, q_ref, kv_ref, st_ref, qi_ref, ko_ref, o_ref, lse_ref, q_s, acc, m_s, l_s):
    m_s[...] = jnp.full_like(m_s, NEG_BIG)
    l_s[...] = jnp.zeros_like(l_s)
    acc[...] = jnp.zeros_like(acc)
    for h in range(N_HEADS):
        q_s[pl.ds(h * BLK, BLK)] = q_ref[:, head(h)]

    def body(s, at, masked):
        pair, hk = at
        k, v = kv_ref[pair, 0, hk], kv_ref[pair, 1, hk]
        if masked:
            off = ko_ref[hk] + s * BLK
            mask = [
                jnp.logical_and(off[:, lanes] >= st_ref[...], off[:, lanes] <= qi_ref[...])
                for lanes in (slice(HEAD_DIM), slice(HEAD_DIM, BLK))
            ]
        for h in range(N_HEADS):
            rows = pl.ds(h * BLK, BLK)
            sc = dot_t(q_s[rows], k)
            sc = [sc[:, :HEAD_DIM] * EXP2_SCALE, sc[:, HEAD_DIM:] * EXP2_SCALE]
            if masked:
                sc = [jnp.where(m, x, NEG_BIG) for m, x in zip(mask, sc)]
            m_old = m_s[rows]
            m_new = jnp.maximum(m_old, jnp.max(jnp.maximum(*sc), axis=1, keepdims=True))
            alpha = jnp.exp2(m_old - m_new)
            p = [jnp.exp2(x - m_new) for x in sc]
            m_s[rows] = m_new
            l_s[rows] = l_s[rows] * alpha + (p[0] + p[1])
            p = jnp.hstack([x.astype(BF16) for x in p])
            acc[rows] = acc[rows] * alpha + jnp.dot(p, v, preferred_element_type=F32)

    steps(tab, body)
    for h in range(N_HEADS):
        rows = pl.ds(h * BLK, BLK)
        total = jnp.sum(l_s[rows], axis=1, keepdims=True)
        o_ref[:, head(h)] = (acc[rows] / total).astype(BF16)
        lse_ref[h] = (m_s[rows] + jnp.log2(total)).T[:1]


def bwd_kernel(tab, q_ref, do_ref, o_ref, kv_ref, lse_ref, st_ref, qi_ref, ko_ref, cos_ref, sin_ref, dq_ref, dkv_ref, dq_acc, delta):
    dq_acc[...] = jnp.zeros_like(dq_acc)
    for h in range(N_HEADS):
        terms = do_ref[:, head(h)].astype(F32) * o_ref[:, head(h)].astype(F32)
        delta[h] = jnp.sum(terms.T, axis=0, keepdims=True)

    @pl.when(pl.program_id(1) == 0)
    def _():
        dkv_ref[...] = jnp.zeros_like(dkv_ref)

    def body(s, at, masked):
        pair, hk = at
        k = kv_ref[pair, 0, hk]
        v = kv_ref[pair, 1, hk]
        k_t = k.T
        mask = may_use(s, ko_ref[hk], st_ref, qi_ref) if masked else None
        dk = dv = jnp.zeros((BLK, HEAD_DIM), F32)
        for h in range(N_HEADS):
            q = q_ref[:, head(h)]
            do = do_ref[:, head(h)]
            p = jnp.exp2(dot_t(k, q) * EXP2_SCALE - lse_ref[h])
            if masked:
                p = jnp.where(mask, p, 0.0)
            ds = (p * (dot_t(v, do) - delta[h])).astype(BF16)
            dv += jnp.dot(p.astype(BF16), do, preferred_element_type=F32)
            dk += jnp.dot(ds, q, preferred_element_type=F32)
            dq_acc[h] += jnp.dot(k_t, ds, preferred_element_type=F32)
        dkv_ref[pair, 0, hk] += dk
        dkv_ref[pair, 1, hk] += dv

    steps(tab, body)
    cos_t, sin_t = cos_ref[...], sin_ref[...]
    half = HEAD_DIM // TWO
    for h in range(N_HEADS):
        a, c = dq_acc[h, :half] * ATTN_SCALE, dq_acc[h, half:] * ATTN_SCALE
        lin = jnp.concatenate([a * cos_t + c * sin_t, c * cos_t - a * sin_t], axis=0)
        dq_ref[:, head(h)] = lin.T.astype(BF16)


def attn_specs():
    def at_tile(b, h, t):
        return (b, h) + (0,) * TWO

    def at_row(b, h, t):
        return (0, 0, b) + (0,) * 3

    tile = pl.BlockSpec((ONE, ONE, BLK, N_HEADS * HEAD_DIM), at_tile)
    row = pl.BlockSpec((ONE, ONE, 1, BLK), at_tile)
    stat = pl.BlockSpec((ONE, ONE, N_HEADS, 1, BLK), lambda b, h, t: (b, h) + (0,) * 3)
    rope = pl.BlockSpec((ONE, ONE, HEAD_DIM // TWO, BLK), at_tile)
    kv = pl.BlockSpec((N_PAIRS, TWO, ONE, TWO, BLK, HEAD_DIM), at_row)
    ko = pl.BlockSpec((TWO, BLK, BLK), lambda b, h, t: (0,) * 3)
    return tile, row, stat, kv, ko, rope


def flash_fwd(tab, q, kv, start, qidx, koff):
    tile, _, stat, kvs, *_ = attn_specs()
    col = pl.BlockSpec((ONE, ONE, BLK, HEAD_DIM), lambda b, h, t: (b, h) + (0,) * TWO)
    ko = pl.BlockSpec((TWO, 1, BLK), lambda b, h, t: (0,) * 3)
    return pl.pallas_call(
        fwd_kernel,
        name="attn_fwd",
        out_shape=(jax.ShapeDtypeStruct(q.shape, BF16), jax.ShapeDtypeStruct((TWO, TWO, N_HEADS, 1, BLK), F32)),
        grid_spec=pltpu.PrefetchScalarGridSpec(
            num_scalar_prefetch=1,
            grid=(TWO, TWO),
            in_specs=[tile, kvs, col, col, ko],
            out_specs=[tile, stat],
            scratch_shapes=[pltpu.VMEM((N_HEADS * BLK, HEAD_DIM), t) for t in (BF16, F32, F32, F32)],
        ),
        compiler_params=params(40),
        cost_estimate=cost(20, 16),
    )(tab, q, kv, start, qidx, koff)


def flash_bwd(tab, q, do, o, kv, lse, start, qidx, koff, cos_t, sin_t):
    tile, row, stat, kvs, ko, rope = attn_specs()
    return pl.pallas_call(
        bwd_kernel,
        name="attn_bwd",
        out_shape=(
            jax.ShapeDtypeStruct(q.shape, BF16),
            jax.ShapeDtypeStruct(kv.shape, F32),
        ),
        grid_spec=pltpu.PrefetchScalarGridSpec(
            num_scalar_prefetch=1,
            grid=(TWO, TWO),
            in_specs=[tile, tile, tile, kvs, stat, row, row, ko, rope, rope],
            out_specs=[tile, kvs],
            scratch_shapes=[pltpu.VMEM((N_HEADS, HEAD_DIM, BLK), F32), pltpu.VMEM((N_HEADS, 1, BLK), F32)],
        ),
        compiler_params=params(48),
        cost_estimate=cost(50, 32),
    )(tab, q, do, o, kv, lse, start, qidx, koff, cos_t, sin_t)


def turn(x, cos_ref, sin_ref):
    return x * cos_ref[...] + pltpu.roll(x, HEAD_DIM // TWO, 1) * sin_ref[...]


def first_kernel(x_ref, g_ref, wk_ref, wv_ref, cos_ref, sin_ref, h_ref, kv_ref):
    x = x_ref[...].astype(F32)
    h = (x * lax.rsqrt(row_mean(x * x) + NORM_EPS) * g_ref[...]).astype(BF16)
    h_ref[...] = h
    k = jnp.dot(h, wk_ref[...], preferred_element_type=F32)
    v = jnp.dot(h, wv_ref[...], preferred_element_type=F32)
    n = kv_ref.shape[3]
    for i in range(TWO):
        for j, val in enumerate((turn(k[:, head_slice(i)], cos_ref, sin_ref), v[:, head_slice(i)])):
            for c in range(TWO):
                kv_ref[i, c, j] = val[c * n : (c + 1) * n].astype(BF16)


def query_kernel(h_ref, w_ref, cos_ref, sin_ref, q_ref):
    q = jnp.dot(h_ref[...], w_ref[...], preferred_element_type=F32)
    n = q_ref.shape[TWO]
    for j in range(q.shape[1] // HEAD_DIM):
        val = turn(q[:, head_slice(j)], cos_ref, sin_ref).astype(BF16)
        for c in range(TWO):
            q_ref[0, c, :, head(j)] = val[c * n : (c + 1) * n]


def project(x, gain, w_q, w_k, w_v, cos_f, sin_f):
    n, d = x.shape
    h, kv = pl.pallas_call(
        first_kernel,
        name="norm_kv",
        out_shape=(jax.ShapeDtypeStruct(x.shape, BF16), jax.ShapeDtypeStruct((TWO,) * 3 + (n // TWO, HEAD_DIM), BF16)),
        compiler_params=params(40),
        cost_estimate=cost(TWO, 7),
    )(x, gain, w_k, w_v, cos_f, sin_f)
    tile = 4 * HEAD_DIM
    rope = pl.BlockSpec(cos_f.shape, lambda j: (0, 0))
    q = pl.pallas_call(
        query_kernel,
        name="query",
        grid=(d // tile,),
        out_shape=jax.ShapeDtypeStruct((TWO, TWO, n // TWO, d // TWO), BF16),
        in_specs=[pl.BlockSpec(h.shape, lambda j: (0, 0)), pl.BlockSpec((d, tile), lambda j: (0, j)), rope, rope],
        out_specs=pl.BlockSpec((1, TWO, n // TWO, tile), lambda j: (j // TWO, 0, 0, j % TWO)),
        compiler_params=params(40),
        cost_estimate=cost(5, 12),
    )(h, w_q, cos_f, sin_f)
    return h, kv, q


def place(me):
    return me // 8, lax.rem(me // 4, TWO), lax.rem(me // TWO, TWO), lax.rem(me, TWO)


def dev(z, y, x, core):
    return ((z * TWO + y) * TWO + x) * TWO + core


def z_peers(z):
    return [(k, lax.rem(z + k, 4)) for k in (1, TWO, 3)]


def meet(peers):
    barrier = pltpu.get_barrier_semaphore()
    for d in peers:
        pl.semaphore_signal(barrier, device_id=(d,), device_id_type=MESH)
    pl.semaphore_wait(barrier, len(peers))


def remote(src, dst, send, arrive, to):
    return pltpu.make_async_remote_copy(
        src_ref=src, dst_ref=dst, send_sem=send, recv_sem=arrive, device_id=(to,), device_id_type=MESH
    )


class Line:
    order = (0, 1, -1, TWO, -TWO, 3, -3)

    def __init__(self, me):
        self.z, y, x, core = place(me)
        self.next = {1: dev(self.z + 1, y, x, core), -1: dev(self.z - 1, y, x, core)}
        self.inside = {1: self.z < 3, -1: self.z > 0}

    def held(self, dz):
        return jnp.logical_and(self.z + dz >= 0, self.z + dz <= 3)

    def ways(self, dz):
        for d in self.next:
            if d * dz <= 0:
                yield d, self.inside[d] if dz == 0 else jnp.logical_and(self.inside[d], self.held(dz))


def exchange_kernel(kv_ref, q_ref, dy_ref, kv_all, q_u, dy_u, own_sem, quad_s, quad_r, z_s, z_r, y_s, y_r):
    me = lax.axis_index("cp")
    z, y, x, core = place(me)
    quad, line = quad_of(me), Line(me)
    across = dev(z, 1 - y, x, core)
    meet(quad[1:] + [across] + [dev(zz, y, x, core) for _, zz in z_peers(z)])

    def source(a, d):
        xx, cc = 1 - x if d // TWO else x, 1 - core if d % TWO else core
        return dy_ref.at[cc] if a == TWO else (kv_ref, q_ref)[a].at[xx, cc]

    def target(a, d):
        tok = pl.ds(d * CHUNK, CHUNK)
        return kv_all.at[me // 4, :, :, :, tok] if a == 0 else (q_u, dy_u)[a - 1].at[:, :, tok]

    def quad_copy(a, d):
        return remote(source(a, d), target(a, d), quad_s.at[a, d], quad_r.at[a, d], quad[d])

    def own_copy(a):
        return pltpu.make_async_copy(source(a, 0), target(a, 0), own_sem.at[a])

    sent = [(a, d) for a in range(3) for d in (1, TWO, 3) if (a, d) != LATER]
    for a, d in sent:
        quad_copy(a, d).start()
    for a in range(3):
        own_copy(a).start()
    own_copy(0).wait()
    for d in (1, TWO, 3):
        quad_copy(0, d).wait_recv()

    def z_copy(part, dz, d):
        block = kv_all.at[TWO * (z + dz) + y, part]
        return remote(block, block, z_s.at[part, (d + 1) // TWO, dz + 3], z_r.at[part, dz - d + 3], line.next[d])

    def y_copy(part, dz, yy=y):
        block = kv_all.at[TWO * (z + dz) + yy, part]
        return remote(block, block, y_s.at[part, dz + 3], y_r.at[part, dz + 3], across)

    parts = range(TWO)
    moves = [(part, dz) for dz in line.order for part in parts]
    for part, dz in moves:
        if dz:
            block = kv_all.at[TWO * (z + dz) + y, part]
            arrival = remote(block, block, own_sem.at[0], z_r.at[part, dz + 3], me)
            pl.when(line.held(dz))(arrival.wait_recv)
        for d, on in line.ways(dz):
            pl.when(on)(z_copy(part, dz, d).start)
        pl.when(line.held(dz))(y_copy(part, dz).start)
    for part, dz in moves:
        for d, on in line.ways(dz):
            pl.when(on)(z_copy(part, dz, d).wait_send)
        pl.when(line.held(dz))(y_copy(part, dz, 1 - y).wait_recv)
        pl.when(line.held(dz))(y_copy(part, dz).wait_send)
    for a, d in sent:
        quad_copy(a, d).wait_send()
        if a > 0:
            quad_copy(a, d).wait_recv()
    own_copy(1).wait()
    own_copy(TWO).wait()


def exchange(kv, q, dy):
    dma = pltpu.SemaphoreType.DMA
    vmem, hbm = pl.BlockSpec(memory_space=pltpu.VMEM), pl.BlockSpec(memory_space=pl.ANY)
    wide = q.shape[-1]
    return pl.pallas_call(
        exchange_kernel,
        name="exchange",
        out_shape=(
            jax.ShapeDtypeStruct((N_PAIRS,) + (TWO,) * 3 + (BLK, HEAD_DIM), BF16),
            jax.ShapeDtypeStruct((TWO, TWO, BLK, wide), BF16),
            jax.ShapeDtypeStruct((TWO, TWO, LATER[1] * CHUNK, TWO * wide), BF16),
        ),
        in_specs=[vmem] * 3,
        out_specs=[hbm] * 3,
        scratch_shapes=[dma((3,))] + [dma((3, 4))] * TWO + [dma((TWO, TWO, 7))] + [dma((TWO, 7))] * 3,
        compiler_params=pltpu.CompilerParams(collective_id=1),
        cost_estimate=cost(1, 20),
    )(kv, q, dy)


def reduce_kernel(cuts, kinds, work, *refs):
    n = len(cuts)

    def take(count):
        nonlocal refs
        first, refs = refs[:count], refs[count:]
        return first

    ins, more_in, outs, more_out = take(n), take(work.ins), take(n), take(work.outs)
    own, from_core, from_y, from_z = take(n), take(n), take(n), take(n)
    load_sem, core_s, core_r, y_s, y_r, z_s, z_r = take(7)
    me = lax.axis_index("cp")
    z, y, x, core = place(me)
    partner, across = dev(z, y, x, 1 - core), dev(z, 1 - y, x, core)
    next_z = dev(z + 1, y, x, core), dev(z - 1, y, x, core)
    meet(quad_of(me)[1:] + [across] + [dev(zz, y, x, core) for _, zz in z_peers(z)])
    job = work(me, more_in, more_out, refs)

    def rows(i, j):
        size = outs[i].shape[0] // cuts[i]
        return pl.ds(j * size, size)

    def mine(i, j, zz):
        at = rows(i, j)
        return own[i].at[zz, y, at] if kinds[i] == "core" else own[i].at[zz, at]

    def load(i, j):
        src, at = ins[i], rows(i, j)
        src = {"core": lambda: src.at[core, :, :, at], "z": lambda: src.at[:, at], "": lambda: src.at[:, y, at]}[kinds[i]]()
        dst = own[i].at[:, :, at] if kinds[i] == "core" else own[i].at[:, at]
        return pltpu.make_async_copy(src, dst, load_sem.at[i, j])

    def core_copy(i, j):
        at = rows(i, j)
        return remote(ins[i].at[1 - core, :, :, at], from_core[i].at[:, :, at], core_s.at[i, j], core_r.at[i, j], partner)

    def y_copy(i, j):
        src = own[i] if kinds[i] == "core" else ins[i]
        at = rows(i, j)
        return remote(src.at[:, 1 - y, at], from_y[i].at[:, at], y_s.at[i, j], y_r.at[i, j], across)

    def z_copy(i, j, way, zz, to):
        at = way, zz + way - 1
        return remote(mine(i, j, zz), from_z[i].at[*at, rows(i, j)], z_s.at[i, j, *at], z_r.at[i, j, *at], to)

    def relay(i, j, way, zz, add):
        if add:
            z_copy(i, j, way, zz, me).wait_recv()
            mine(i, j, zz)[...] += from_z[i][way, zz + way - 1, rows(i, j)]
        z_copy(i, j, way, zz, next_z[way]).start()

    def hop(i, j, h):
        @pl.when(z == h)
        def _():
            for zz in range(3, h, -1):
                relay(i, j, 0, zz, h > 0)

        @pl.when(z == 3 - h)
        def _():
            for zz in range(3 - h):
                relay(i, j, 1, zz, h > 0)

    def across_y(i, j):
        if kinds[i] != "z":
            y_copy(i, j).wait_recv()
            for zz in range(4):
                mine(i, j, zz)[...] += from_y[i][zz, rows(i, j)]

    def last(i, j):
        at = rows(i, j)
        outs[i][at] = mine(i, j, z)[...]
        for way, on in enumerate((z > 0, z < 3)):

            @pl.when(on)
            def _(way=way):
                z_copy(i, j, way, z, me).wait_recv()
                outs[i][at] += from_z[i][way, z + way - 1, at]

    pieces = [(i, j) for i in range(n) for j in range(cuts[i])]
    for i, j in pieces:
        load(i, j).start()
        if kinds[i] == "core":
            core_copy(i, j).start()
        elif not kinds[i]:
            y_copy(i, j).start()
    for i, j in pieces:
        load(i, j).wait()
        if kinds[i] == "core":
            core_copy(i, j).wait_recv()
            at = rows(i, j)
            for zz in range(4):
                own[i][zz, :, at] += from_core[i][zz, :, at]
            y_copy(i, j).start()
        if kinds[i] == "z":
            hop(i, j, 0)
    for t in range(len(pieces) + 3):
        for h, (i, j) in enumerate(reversed(pieces[max(t - 3, 0) : t + 1]), max(t + 1 - len(pieces), 0)):
            if h == 0:
                across_y(i, j)
            if h == 3:
                last(i, j)
            elif h > 0 or kinds[i] != "z":
                hop(i, j, h)
        job.step(t)
    for i, j in pieces:
        if kinds[i] == "core":
            core_copy(i, j).wait_send()
        if kinds[i] != "z":
            y_copy(i, j).wait_send()
        for zz in range(4):
            if zz > 0:
                pl.when(z < zz)(z_copy(i, j, 0, zz, next_z[0]).wait_send)
            if zz < 3:
                pl.when(z > zz)(z_copy(i, j, 1, zz, next_z[1]).wait_send)
    job.finish()


def quad_of(me):
    z, y, x, core = place(me)
    return [dev(z, y, 1 - x if d // TWO else x, 1 - core if d % TWO else core) for d in range(4)]


class Home:
    def __init__(self, me, src, out, own_sem, send, arrive):
        _, _, x, core = place(me)
        w = src.shape[-1]
        to = out.at[core, :, :, :, pl.ds(x * w, w)]

        def piece(d):
            return src.at[:, :, pl.ds(d * CHUNK, CHUNK)]

        self.own = pltpu.make_async_copy(piece(0), to, own_sem)
        self.copies = [remote(piece(d), to, send.at[d], arrive.at[d], quad_of(me)[d]) for d in (1, TWO, 3)]

    def start(self):
        self.own.start()
        for c in self.copies:
            c.start()

    def wait_recv(self):
        self.own.wait()
        for c in self.copies:
            c.wait_recv()

    def wait_send(self):
        for c in self.copies:
            c.wait_send()


class Products:
    ins, outs = 5, TWO

    def __init__(self, me, ins, outs, scratch):
        attn, dq, self.hidden, self.w_o, self.w_q = ins
        self.block_out, self.d_part = outs
        self.attn_home, self.dq_home, self.buf_o, self.buf_q, own_sem, quad_s, quad_r, self.w_sem = scratch
        self.homes = [
            Home(me, src, out, own_sem.at[i], quad_s.at[i], quad_r.at[i])
            for i, (src, out) in enumerate([(attn, self.attn_home), (dq, self.dq_home)])
        ]
        for h in self.homes:
            h.start()

    @staticmethod
    def scratch(arrays):
        dma, d = pltpu.SemaphoreType.DMA, arrays[3].shape[0]
        home = pltpu.VMEM((TWO,) * 3 + (CHUNK, d), BF16)
        buf = [pltpu.VMEM((TWO,) + b, BF16) for b in ((d, BLK), (BLK, d))]
        return [home] * TWO + buf + [dma((TWO,)), dma((TWO, 4)), dma((TWO, 4)), dma((TWO, TWO))]

    @staticmethod
    def results(arrays):
        return [jax.ShapeDtypeStruct(arrays[TWO].shape, t) for t in (BF16, F32)]

    spaces = [pltpu.VMEM] * 3 + [pl.ANY] * TWO

    def tiles(self, fetch, use):
        n = self.w_o.shape[0] // BLK
        fetch(0, 0).start()

        @pl.loop(0, n)
        def _(t):
            slot = lax.rem(t, TWO)
            fetch(t, slot).wait()

            @pl.when(t + 1 < n)
            def _():
                fetch(t + 1, 1 - slot).start()

            use(pl.ds(pl.multiple_of(t * BLK, BLK), BLK), slot)

    def step(self, t):
        def cols(t):
            return pl.ds(pl.multiple_of(t * BLK, BLK), BLK)

        def fetch_o(t, slot):
            return pltpu.make_async_copy(self.w_o.at[:, cols(t)], self.buf_o.at[slot], self.w_sem.at[0, slot])

        def fetch_q(t, slot):
            return pltpu.make_async_copy(self.w_q.at[cols(t)], self.buf_q.at[slot], self.w_sem.at[1, slot])

        def project(at, slot):
            attn = self.attn_home[...].reshape(-1, self.w_o.shape[0])
            out = jnp.dot(attn, self.buf_o[slot], preferred_element_type=F32)
            self.block_out[:, at] = (self.hidden[:, at].astype(F32) + out).astype(BF16)

        def pull(at, slot):
            dq = self.dq_home[...].reshape(-1, self.w_o.shape[0])
            self.d_part[:, at] = dot_t(dq, self.buf_q[slot])

        if t in PRODUCTS_AT:
            i = PRODUCTS_AT.index(t)
            self.homes[i].wait_recv()
            self.tiles(*((fetch_o, project), (fetch_q, pull))[i])

    def finish(self):
        for h in self.homes:
            h.wait_send()


class HiddenGradient:
    ins, outs = 6, TWO

    def __init__(self, me, ins, outs, scratch):
        dkv, self.part, self.w_kv, self.x, self.dy, self.gain = ins
        self.dx, self.terms = outs
        self.dkv_home, self.rows, *sems = scratch
        self.home = Home(me, dkv, self.dkv_home, *sems)
        self.home.start()

    @staticmethod
    def scratch(arrays):
        dma = pltpu.SemaphoreType.DMA
        dkv, x = arrays[0], arrays[3]
        home = pltpu.VMEM((TWO,) * 3 + (CHUNK, TWO * dkv.shape[-1]), BF16)
        return [home, pltpu.VMEM((8, x.shape[1]), F32), dma(()), dma((4,)), dma((4,))]

    @staticmethod
    def results(arrays):
        x = arrays[3]
        return [jax.ShapeDtypeStruct(x.shape, BF16), jax.ShapeDtypeStruct((1, x.shape[1]), F32)]

    spaces = [pltpu.VMEM] * 6

    def step(self, t):
        if t == 0:
            self.home.wait_recv()
            self.rows[...] = jnp.zeros_like(self.rows)
            pl.loop(0, 4)(self.tile)
            self.terms[...] = jnp.sum(self.rows[...], axis=0, keepdims=True)

    def tile(self, t):
        size = TWO * CHUNK
        at = pl.ds(pl.multiple_of(t * size, size), size)
        dkv = self.dkv_home[t // TWO, lax.rem(t, TWO)].reshape(size, -1)
        d = self.part[at] + dot_t(dkv, self.w_kv[...])
        d = d.astype(BF16).astype(F32)
        x = self.x[at].astype(F32)
        inv_rms = lax.rsqrt(row_mean(x * x) + NORM_EPS)
        unit, scaled = x * inv_rms, d * self.gain[...]
        dx = inv_rms * (scaled - unit * row_mean(scaled * unit))
        self.dx[at] = (self.dy[at].astype(F32) + dx).astype(BF16)
        self.rows[...] += jnp.sum((d * unit).reshape((-1,) + self.rows.shape), axis=0)

    def finish(self):
        self.home.wait_send()


def reduce_pairs(arrays, cuts, kinds, collective_id, work, more):
    dma = pltpu.SemaphoreType.DMA
    n, most = len(arrays), max(cuts)
    blocks = [a.shape[-TWO:] for a in arrays]
    own = [pltpu.VMEM(((4, TWO) if k == "core" else (4,)) + b, F32) for b, k in zip(blocks, kinds)]
    unused = pltpu.VMEM((8, HEAD_DIM), F32)
    scratch = own + [o if k == "core" else unused for o, k in zip(own, kinds)]
    scratch += [unused if k == "z" else pltpu.VMEM((4,) + b, F32) for b, k in zip(blocks, kinds)]
    scratch += [pltpu.VMEM((TWO, 3) + b, F32) for b in blocks]
    scratch += [dma((n, most))] * 5 + [dma((n, most, TWO, 3))] * TWO
    outs = [jax.ShapeDtypeStruct(b, F32) for b in blocks] + work.results(more)
    return pl.pallas_call(
        functools.partial(reduce_kernel, cuts, kinds, work),
        name="reduce_pairs",
        out_shape=outs,
        in_specs=[pl.BlockSpec(memory_space=m) for m in [pl.ANY] * n + work.spaces],
        out_specs=[pl.BlockSpec(memory_space=pltpu.VMEM)] * len(outs),
        scratch_shapes=scratch + work.scratch(more),
        compiler_params=params(60, collective_id=collective_id),
        cost_estimate=cost(1, 20),
    )(*arrays, *more)


def gather_kernel(*refs):
    shards, refs = refs[:4], refs[4:]
    terms, *outs, dgain_ref = refs[:6]
    own_sem, zs, fs, ls, cs, zr, fr, lr, cr, all_terms, g_s, g_r = refs[6:]
    me = lax.axis_index("cp")
    z, y, x, core = place(me)
    across = (dev(z, y, 1 - x, core), dev(z, 1 - y, x, core))
    partner = dev(z, y, x, 1 - core)
    others = [(i, me ^ i) for i in range(1, all_terms.shape[0])]
    meet([d for _, d in others])

    def windows(half, zz, yy, xx, cc):
        pair = TWO * zz + yy
        rows = shards[0].shape[0] // TWO
        out_rows = pl.ds(((xx * TWO + cc) * N_PAIRS + pair) * TWO * rows + half * rows, rows)
        yield shards[0], pl.ds(half * rows, rows), outs[0].at[out_rows]
        rows = shards[1].shape[0] // TWO
        out_rows = pl.ds((cc * N_PAIRS + pair) * TWO * rows + half * rows, rows)
        for s, o in zip(shards[1:], outs[1:]):
            yield s, pl.ds(half * rows, rows), o.at[out_rows, pl.ds(xx * s.shape[1], s.shape[1])]

    total = sum(s.size for s in shards) // TWO // outs[0].shape[1]
    whole = outs[0].at[pl.ds(0, total)]

    def flip(v, on):
        return 1 - v if on else v

    class Copy:
        def __init__(self, half, zz, first, last, send, arrive, to, is_own, cc=core):
            over_x, over_y = (first, last) if half == 0 else (last, first)
            self.at = half, zz, flip(y, over_y), flip(x, over_x), cc
            self.send, self.arrive, self.to, self.is_own = send, arrive, to, is_own

        def start(self):
            for shard, rows, window in windows(*self.at):
                remote(shard.at[rows] if self.is_own else window, window, self.send, self.arrive, self.to).start()

        def wait_recv(self):
            remote(whole, whole, self.send, self.arrive, me).wait_recv()

        def wait_send(self):
            remote(whole, whole, self.send, self.arrive, me).wait_send()

    places = [(0, z)] + [(k, lax.rem(z + 4 - k, 4)) for k in (1, 3, TWO)]
    halves = range(TWO)

    def z_copy(half, k, zz):
        return Copy(half, z, 0, 0, zs.at[half, k], zr.at[half, k], dev(zz, y, x, core), True)

    def first_copy(half, k, zz):
        at = half, k
        return Copy(half, zz, 0, 0, fs.at[at], fr.at[at], across[half], k == 0)

    def last_copy(half, k, zz, first):
        at = half, first, k
        return Copy(half, zz, first, 0, ls.at[at], lr.at[at], across[1 - half], k == first == 0)

    def core_copy(half, k, zz, first, last):
        at = half, first, last, k
        return Copy(half, zz, first, last, cs.at[at], cr.at[at], partner, k == first == last == 0)

    def term_copy(i, d):
        return remote(terms, all_terms.at[i], g_s.at[i], g_r.at[i], d)

    owns = []
    for half in halves:
        for shard, rows, window in windows(half, z, y, x, core):
            owns.append(pltpu.make_async_copy(shard.at[rows], window, own_sem.at[len(owns)]))
    for k, zz in z_peers(z):
        for half in halves:
            z_copy(half, k, zz).start()
    for k, zz in places:
        for half in halves:
            if k > 0:
                z_copy(half, k, zz).wait_recv()
            first_copy(half, k, zz).start()
            last_copy(half, k, zz, 0).start()
            core_copy(half, k, zz, 0, 0).start()
        if k == 0:
            for o in owns:
                o.start()
            for i, d in others:
                term_copy(i, d).start()
        for half in halves:
            first_copy(half, k, zz).wait_recv()
            last_copy(half, k, zz, 1).start()
            core_copy(half, k, zz, 1, 0).start()
    for first in halves:
        for k, zz in places:
            for half in halves:
                last_copy(half, k, zz, first).wait_recv()
                core_copy(half, k, zz, first, 1).start()
    for o in owns:
        o.wait()
    for k, zz in z_peers(z):
        for half in halves:
            z_copy(half, k, zz).wait_send()
    total_gain = terms[...]
    for i, d in others:
        term_copy(i, d).wait_recv()
        total_gain += all_terms[i]
    dgain_ref[...] = total_gain
    for i, d in others:
        term_copy(i, d).wait_send()
    for k, zz in places:
        for half in halves:
            first_copy(half, k, zz).wait_send()
            for first in halves:
                last_copy(half, k, zz, first).wait_send()
                for last in halves:
                    core_copy(half, k, zz, first, last).wait_recv()
                    core_copy(half, k, zz, first, last).wait_send()


def gather_all(shards, shapes, terms):
    dma = pltpu.SemaphoreType.DMA
    vmem, hbm = pl.BlockSpec(memory_space=pltpu.VMEM), pl.BlockSpec(memory_space=pl.ANY)
    hops = [dma((TWO,) * i + (4,)) for i in (1, 1, TWO, 3)]
    n = len(shards)
    return pl.pallas_call(
        gather_kernel,
        name="gather_all",
        out_shape=[jax.ShapeDtypeStruct(s, F32) for s in shapes + [terms.shape]],
        in_specs=[vmem] * (n + 1),
        out_specs=[hbm] * n + [vmem],
        scratch_shapes=[dma((TWO * n,))] + hops + hops + [pltpu.VMEM((32,) + terms.shape, F32), dma((32,)), dma((32,))],
        compiler_params=pltpu.CompilerParams(collective_id=0),
        cost_estimate=cost(1, 76),
    )(*shards, terms)


def perm(x, pairs):
    return lax.ppermute(x, "cp", pairs)


def flip_pairs(d):
    return [(r, r ^ d) for r in range(32)]


def solution(mesh):
    def local_step(hidden, grad_out, positions, seg_ids, w_q, w_k, w_v, w_o, norm_gain):
        n_batch, n_tok, d_model = hidden.shape
        n_rows = n_batch * n_tok
        wide = N_HEADS * HEAD_DIM
        me = lax.axis_index("cp")
        _, y, x, core = place(me)
        quad, pair = me % 4, me // 4
        relations = range(4)

        def rows_of(arr, d):
            return pick(arr.reshape((TWO, TWO, TWO, CHUNK) + arr.shape[TWO:]), core ^ (d % TWO), 0)

        def swap(pieces):
            return [perm(p, flip_pairs(d)) if d else p for d, p in enumerate(pieces)]

        def unite(arr):
            joined = jnp.stack(swap([rows_of(arr, d) for d in relations]), axis=TWO)
            return joined.reshape((TWO, TWO, BLK) + joined.shape[4:])

        gain = norm_gain.astype(F32)
        cos_t, sin_t = rope_tables(positions.reshape(n_rows))
        cos_f, sin_f = jnp.hstack([cos_t, cos_t]), jnp.hstack([-sin_t, sin_t])
        normed, kv_home, q_home = project(hidden.reshape(n_rows, d_model), gain[NEW], w_q, w_k, w_v, cos_f, sin_f)
        pos_u = unite(positions)
        kv_all, q_u, dy_part = exchange(
            kv_home.reshape((TWO,) * 5 + (CHUNK, HEAD_DIM)),
            q_home.reshape((TWO,) * 4 + (CHUNK, wide)),
            grad_out.reshape((TWO,) * 3 + (CHUNK, d_model)),
        )
        dy_last, dy_part = lax.optimization_barrier((rows_of(grad_out, LATER[1]), dy_part))
        dy_last = perm(dy_last, flip_pairs(LATER[1]))
        normed_home, dy_part = lax.optimization_barrier((normed.reshape(hidden.shape), dy_part))
        normed_u = unite(normed_home)

        member = quad ^ jnp.arange(4)
        front, back = ((m[:, NEW] * CHUNK + jnp.arange(CHUNK)[NEW]).reshape(BLK) for m in (member, 3 - member))
        offsets = jnp.stack([front, back]).astype(jnp.int32)
        own_super = jnp.stack([pair, N_SUPER - 1 - pair]).astype(jnp.int32)
        q_index = own_super[:, NEW] * BLK + offsets
        start = q_index[NEW] - pos_u
        koff = jnp.broadcast_to(offsets[:, :, NEW], (TWO, BLK, BLK))
        tab = jnp.concatenate(
            [own_super, (jnp.min(start, axis=-1) // BLK).reshape(-1), jnp.max(start, axis=-1).reshape(-1)]
        )
        start_r = start[:, :, NEW, :]
        q_index_r = jnp.broadcast_to(q_index[NEW, :, NEW, :], start_r.shape)
        cos_u, sin_u = rope_tables(pos_u)
        cos_ut, sin_ut = jnp.swapaxes(cos_u, TWO, 3), jnp.swapaxes(sin_u, TWO, 3)

        lanes = start.shape + (HEAD_DIM,)
        start_l, q_index_l = (jnp.broadcast_to(a[..., NEW], lanes) for a in (start, q_index[NEW]))
        attn_u, lse = flash_fwd(tab, q_u, kv_all, start_l, q_index_l, offsets[:, NEW])

        tok = tuple(range(3))
        half_wide = wide // TWO
        dy_u = jnp.concatenate([dy_part, dy_last], axis=TWO)
        wo_send = dot(dyn(attn_u, (1 - core) * half_wide, half_wide, 3), dy_u, tok, tok)
        wo_sum = dot(dyn(attn_u, core * half_wide, half_wide, 3), dy_u, tok, tok) + perm(wo_send, flip_pairs(1))
        wo_sum = wo_sum.reshape(4, TWO, half_wide // N_PAIRS, d_model)
        wo_y = perm(pick(wo_sum, 1 - y, 1), flip_pairs(4))

        d_attn = dot(dy_u, dyn(w_o, x * wide, wide, 0), (3,), (1,)).astype(BF16)
        d_attn, wo_sum = lax.optimization_barrier((d_attn, wo_sum))
        dq_u, dkv = flash_bwd(tab, q_u, d_attn, attn_u, kv_all, lse, start_r, q_index_r, koff, cos_ut, sin_ut)

        wo_sum = pick(wo_sum, y, 1) + wo_y
        half_model = d_model // TWO

        def by_core(d_out):
            part = lax.optimization_barrier(dot(normed_u, d_out, tok, tok))
            return part.reshape(TWO, 4, TWO, half_model // N_PAIRS, -1)

        x_flat = hidden.reshape(n_rows, d_model)
        wo_own, dkv_own, wq_own, block_out, d_part = reduce_pairs(
            [wo_sum, dkv.reshape(4, TWO, -1, HEAD_DIM), by_core(dq_u)],
            (TWO, 8, 4),
            ("z", "", "core"),
            TWO,
            Products,
            (attn_u, dq_u, x_flat, w_o, w_q),
        )
        dkv_own = dkv_own.reshape((TWO,) * 3 + (BLK, HEAD_DIM))
        dk_u = rotate(dkv_own[0] * ATTN_SCALE, cos_u, -sin_u).astype(BF16)
        dkv_u = jnp.concatenate([dk_u, dkv_own[1].astype(BF16)], axis=-1)
        w_kv = jnp.hstack([w[:, head_slice(i)] for i in range(TWO) for w in (w_k, w_v)])
        more = dkv_u, d_part, w_kv, x_flat, grad_out.reshape(n_rows, d_model), gain[NEW]
        wkv_own, grad_x, terms = reduce_pairs([by_core(dkv_u)], (TWO,), ("core",), 3, HiddenGradient, more)

        wk_own, wv_own = jnp.split(wkv_own, TWO, axis=1)
        grad_wo, grad_wq, grad_wk, grad_wv, d_gain = gather_all(
            [wo_own, wq_own, wk_own, wv_own], [w_o.shape, w_q.shape, w_k.shape, w_v.shape], terms
        )
        block_out, grad_x = (a.reshape(hidden.shape) for a in (block_out, grad_x))
        return block_out, grad_x, grad_wq, grad_wk, grad_wv, grad_wo, d_gain.reshape(d_model)

    seq_spec = P(None, "cp", None)
    tok_spec = P(None, "cp")
    full_spec = P()
    return jax.shard_map(
        local_step,
        mesh=mesh,
        in_specs=(seq_spec, seq_spec, tok_spec, tok_spec, full_spec, full_spec, full_spec, full_spec, full_spec),
        out_specs=(seq_spec, seq_spec, full_spec, full_spec, full_spec, full_spec, full_spec),
        check_vma=False,
    )
```

time: 781 us -> 709 us (0.908)
  the two profiles are of different devices: /device:TPU:0 before, /device:TPU:9 now
where the time goes in v3:
time: 709 us; the launch traced here: 705 us
  Pallas kernels  531 us (75%)
  local copies, waits for them, and re-layouts  56.5 us (8%)
  waiting for transfers between devices  55.4 us (8%)
  matrix products  22.6 us (3%)
  starting transfers between devices  21 us (3%)
  other arithmetic  16.8 us (2%)
    pallas_call x2, Pallas kernels, reduce_pairs(): pl.pallas_call(functools.partial(reduce_kernel, cuts, kinds, work), name=...  237 us
    pallas_call x1, Pallas kernels, gather_all(): pl.pallas_call(gather_kernel, name='gather_all', out_shape=[jax.ShapeDtyp...  186 us
    pallas_call x1, Pallas kernels, exchange(): pl.pallas_call(exchange_kernel, name='exchange', out_shape=(jax.ShapeDtyp...  60.6 us
    ppermute x9, waiting for transfers between devices, perm(): return lax.ppermute(x, 'cp', pairs)  55.4 us
    unnamed x72, local copies, waits for them, and re-layouts  42.6 us
    pallas_call x1, Pallas kernels, flash_bwd(): pl.pallas_call(bwd_kernel, name='attn_bwd', out_shape=(jax.ShapeDtypeStru...  24.7 us
    dot_general x5, matrix products, dot(): lax.dot_general(a, b, ((ca, cb), ((), ())), preferred_element_type=F32)  22.6 us
    ppermute x9, starting transfers between devices, perm(): return lax.ppermute(x, 'cp', pairs)  21 us
  transfers between devices with their start and end apart: 9, of which 3 were waited for; matrix products, arithmetic and copies ran while one was open for 5% of the time, Pallas kernels for 15%

profile of v3, /device:TPU:9, one launch (start us, length us, event | category | flops | bytes accessed | tf_op | source)
XLA Modules:
  0.0 705.1 jit_solution(14373621864686349727)
XLA Ops:
  1.6 1.8 collective-permute-start.3
  5.0 2.3 dynamic-slice_bitcast_fusion.2
  9.9 1.8 norm_kv.1
  12.6 7.3 %query.1 = bf16[2,2,256,1024]{3,2,1,0:T(8,128)(2,1)S(1)} custom-call(bf16[512,2048]{1,0:T(8,128)(2,1)S(1)} %get-tuple-element.35.h_ref, bf16[2048,2048]{1,0:T(8,128)(2,1)S(1)} %copy-done, f32[512,128]{1,0:T(8,128)S(1)} %get-tuple-element.88.cos_ref, f32[512,128]{1,0:T(8,128)S(1)} %get-tuple-element.89.sin_ref), custom_call_target="tpu_custom_call" | custom-call | flops 5000000000 | bytes 12582912 | tf_op jit(solution)/shard_map/query/pallas_call | solution.py:272
  21.2 60.6 %exchange.1 = (bf16[8,2,2,2,256,128]{5,4,3,2,1,0:T(8,128)(2,1)}, bf16[2,2,256,1024]{3,2,1,0:T(8,128)(2,1)}, bf16[2,2,192,2048]{3,2,1,0:T(8,128)(2,1)}) custom-call(bf16[2,2,2,2,2,64,128]{6,5,4,3,2,1,0:T(8,128)(2,1)} %bitcast.83, bf16[2,2,2,2,64,1024]{5,4,3,2,1,0:T(8,128)(2,1)} %bitcast.82, bf16[2,2,2,64,2048]{4,3,2,1,0:T(8,128)(2,1)} %bitcast.91), custom_call_target="tpu_custom_call" | custom-call | flops 1000000000 | bytes 20971520 | tf_op jit(solution)/shard_map/exchange/pallas_call | solution.py:392
  82.3 4.0 constant_dynamic-update-slice_fusion.1
  87.5 2.2 copy-done.11
  89.7 1.6 copy-done.12
  91.3 14.2 %attn_fwd.1 = (bf16[2,2,256,1024]{3,2,1,0:T(8,128)(2,1)S(1)}, f32[2,2,8,1,256]{4,3,2,1,0:T(1,128)S(1)}) custom-call(s32[10]{0:T(128)S(1)} %pad_add_fusion.2.tab, bf16[2,2,256,1024]{3,2,1,0:T(8,128)(2,1)S(1)} %copy-done.12, bf16[8,2,2,2,256,128]{5,4,3,2,1,0:T(8,128)(2,1)S(1)} %copy-done.11, s32[2,2,256,128]{3,2,1,0:T(8,128)S(1)} %broadcast_in_dim.14.st_ref, ...), custom_call_target="tpu_custom_call" | custom-call | flops 20000000000 | bytes 16777216 | tf_op jit(solution)/shard_map/attn_fwd/pallas_call | solution.py:198
  105.9 1.6 constant_dynamic-update-slice_fusion
  107.5 4.5 convolution_bitcast_fusion.1
  112.0 12.8 %collective-permute-start.4 = (f32[512,2048]{1,0:T(8,128)}, f32[512,2048]{1,0:T(8,128)}, u32[]{:S(2)}, u32[]{:S(2)}) collective-permute-start(f32[512,2048]{1,0:T(8,128)} %convolution_bitcast_fusion.1), channel_id=1, source_target_pairs={{0,1},{1,0},{2,3},{3,2},{4,5},{5,4},{6,7},{7,6},{8,9},{9,8},{10,11... | collective-permute-start | bytes 12582920 | tf_op jit(solution)/shard_map/ppermute | solution.py:831
  124.7 1.9 dynamic-slice_bitcast_fusion.4
  132.6 41.3 %collective-permute-done.7 = bf16[2,2,64,2048]{3,2,1,0:T(8,128)(2,1)} collective-permute-done((bf16[2,2,64,2048]{3,2,1,0:T(8,128)(2,1)}, bf16[2,2,64,2048]{3,2,1,0:T(8,128)(2,1)}, u32[]{:S(2)}, u32[]{:S(2)}) %collective-permute-start.7) | collective-permute-done | bytes 1048608 | tf_op jit(solution)/shard_map/ppermute | solution.py:831
  173.9 2.4 pad_maximum_fusion
  176.7 1.8 copy-done.16
  178.5 2.5 fusion.7
  181.0 5.8 fusion.3.do_ref
  186.8 2.9 bitcast_add_fusion
  191.3 4.3 collective-permute-start.5
  195.8 24.7 %attn_bwd.1 = (bf16[2,2,256,1024]{3,2,1,0:T(8,128)(2,1)S(1)}, f32[8,2,2,2,256,128]{5,4,3,2,1,0:T(8,128)}) custom-call(s32[10]{0:T(128)S(1)} %pad_add_fusion.2.tab, bf16[2,2,256,1024]{3,2,1,0:T(8,128)(2,1)S(1)} %copy-done.13, bf16[2,2,256,1024]{3,2,1,0:T(8,128)(2,1)} %fusion.3.do_ref, bf16[2,2,256,1024]{3,2,1,0:T(8,128)(2,1)} %copy-done.1, ...), custom_call_target="tpu_custom_call" | custom-call | flops 49999998976 | bytes 33554432 | tf_op jit(solution)/shard_map/attn_bwd/pallas_call | solution.py:216
  220.4 7.1 %convolution_bitcast_fusion = f32[2048,1024]{1,0:T(8,128)} fusion(bf16[2,2,256,2048]{3,2,1,0:T(8,128)(2,1)S(1)} %bitcast.98, bf16[2,2,256,1024]{3,2,1,0:T(8,128)(2,1)S(1)} %get-tuple-element.49.refs_4_), kind=kOutput, calls=%fused_computation | convolution fusion | flops 4294967296 | bytes 14680064 | tf_op jit(solution)/shard_map/dot_general | solution.py:46
  227.6 13.7 %collective-permute-done.5 = f32[4,64,2048]{2,1,0:T(8,128)S(1)} collective-permute-done((f32[4,64,2048]{2,1,0:T(8,128)}, f32[4,64,2048]{2,1,0:T(8,128)S(1)}, u32[]{:S(2)}, u32[]{:S(2)}) %collective-permute-start.5) | collective-permute-done | bytes 2097184 | tf_op jit(solution)/shard_map/ppermute | solution.py:831
  242.8 203.4 %reduce_pairs.2 = (f32[64,2048]{1,0:T(8,128)}, f32[2048,128]{1,0:T(8,128)}, f32[128,1024]{1,0:T(8,128)}, bf16[512,2048]{1,0:T(8,128)(2,1)}, f32[512,2048]{1,0:T(8,128)}) custom-call(f32[4,64,2048]{2,1,0:T(8,128)} %bitcast_add_fusion.1.refs_0_, f32[4,2,2048,128]{3,2,1,0:T(8,128)} %bitcast.95, f32[2,4,2,128,1024]{4,3,2,1,0:T(8,128)} %bitcast.96, ...), custom_call_target="tpu_custom_call" | custom-call | flops 1000000000 | bytes 20971520 | tf_op jit(solution)/shard_map/reduce_pairs/pallas_call | solution.py:687
  448.8 2.4 fusion.12
  451.5 2.7 convolution_bitcast_fusion.2
  454.1 33.2 %reduce_pairs.3 = (f32[128,256]{1,0:T(8,128)}, bf16[512,2048]{1,0:T(8,128)(2,1)}, f32[1,2048]{1,0:T(1,128)}) custom-call(f32[2,4,2,128,256]{4,3,2,1,0:T(8,128)} %bitcast.102, bf16[2,2,256,256]{3,2,1,0:T(8,128)(2,1)} %copy-done.20, f32[512,2048]{1,0:T(8,128)} %get-tuple-element.52.refs_2_, bf16[2048,512]{1,0:T(8,128)(2,1)} %pad_maximum_fusion.1.refs_3_, ...), custom_call_target="tpu_custom_call" | custom-call | flops 1000000000 | bytes 20971520 | tf_op jit(solution)/shard_map/reduce_pairs/pallas_call | solution.py:687
  487.4 1.7 fusion.26
  489.0 186.4 %gather_all.1 = (f32[2048,2048]{1,0:T(8,128)}, f32[2048,2048]{1,0:T(8,128)}, f32[2048,256]{1,0:T(8,128)}, f32[2048,256]{1,0:T(8,128)}, f32[1,2048]{1,0:T(1,128)}) custom-call(f32[64,2048]{1,0:T(8,128)} %get-tuple-element.54.refs_0_, f32[128,1024]{1,0:T(8,128)} %get-tuple-element.55.refs_1_, f32[128,128]{1,0:T(8,128)} %get-tuple-element.76.refs_2_, ...), custom_call_target="tpu_custom_call" | custom-call | flops 1000000000 | bytes 79691776 | tf_op jit(solution)/shard_map/gather_all/pallas_call | solution.py:818
  679.1 14.6 %copy.54 = f32[2048,2048]{1,0:T(8,128)} copy(f32[2048,2048]{1,0:T(8,128)} %get-tuple-element.103) | data formatting | bytes 33554432
  695.0 1.8 copy-done.23
  698.2 6.2 copy.57
  (120 shorter events, 28.5 us)
Async XLA Ops:
  0.6 7.9 %copy-start.7 = (bf16[2048,256]{1,0:T(8,128)(2,1)S(1)}, bf16[2048,256]{1,0:T(8,128)(2,1)}, u32[]{:S(2)}) copy-start(bf16[2048,256]{1,0:T(8,128)(2,1)} %wk_ref.1) | copy-start | bytes 3145732
  0.6 7.9 %copy-start.2 = (bf16[4,128,2048]{2,1,0:T(8,128)(2,1)S(1)}, bf16[4,128,2048]{2,1,0:T(8,128)(2,1)}, u32[]{:S(2)}) copy-start(bf16[4,128,2048]{2,1,0:T(8,128)(2,1)} %param.9) | copy-start | bytes 6291460
  1.6 84.9 %collective-permute-start.3 = (s32[2,2,64]{2,1,0:T(2,128)S(1)}, s32[2,2,64]{2,1,0:T(2,128)S(1)}, u32[]{:S(2)}, u32[]{:S(2)}) collective-permute-start(s32[2,2,64]{2,1,0:T(2,128)S(1)} %get-tuple-element.82), channel_id=1, source_target_pairs={{0,3},{1,2},{2,1},{3,0},{4,7},{5,6},{6,5},{7,4},{8,11},{9,10},{10,... | collective-permute-start | bytes 3080 | tf_op jit(solution)/shard_map/ppermute | solution.py:831
  3.4 83.2 %collective-permute-start.1 = (s32[2,2,64]{2,1,0:T(2,128)S(1)}, s32[2,2,64]{2,1,0:T(2,128)S(1)}, u32[]{:S(2)}, u32[]{:S(2)}) collective-permute-start(s32[2,2,64]{2,1,0:T(2,128)S(1)} %get-tuple-element.82), channel_id=1, source_target_pairs={{0,1},{1,0},{2,3},{3,2},{4,5},{5,4},{6,7},{7,6},{8,9},{9,8},{10,11... | collective-permute-start | bytes 3080 | tf_op jit(solution)/shard_map/ppermute | solution.py:831
  3.4 83.2 %collective-permute-start.2 = (s32[2,2,64]{2,1,0:T(2,128)S(1)}, s32[2,2,64]{2,1,0:T(2,128)S(1)}, u32[]{:S(2)}, u32[]{:S(2)}) collective-permute-start(s32[2,2,64]{2,1,0:T(2,128)S(1)} %bitcast.105), channel_id=1, source_target_pairs={{0,2},{1,3},{2,0},{3,1},{4,6},{5,7},{6,4},{7,5},{8,10},{9,11},{10,... | collective-permute-start | bytes 3080 | tf_op jit(solution)/shard_map/ppermute | solution.py:831
  5.0 6.8 copy-start.10
  8.3 4.3 copy-start
  12.6 7.3 %copy-start.4 = (bf16[512,2048]{1,0:T(8,128)(2,1)}, bf16[512,2048]{1,0:T(8,128)(2,1)S(1)}, u32[]{:S(2)}) copy-start(bf16[512,2048]{1,0:T(8,128)(2,1)S(1)} %get-tuple-element.35.h_ref) | copy-start | bytes 6291460
  81.8 24.1 %collective-permute-start = (bf16[2,2,64,2048]{3,2,1,0:T(8,128)(2,1)}, bf16[2,2,64,2048]{3,2,1,0:T(8,128)(2,1)}, u32[]{:S(2)}, u32[]{:S(2)}) collective-permute-start(bf16[2,2,64,2048]{3,2,1,0:T(8,128)(2,1)} %dynamic-slice_bitcast_fusion.2), channel_id=1, source_target_pairs={{0,3},{1,2},{2,1},{3,0},{4,7},{5,6},{6,5},{7,4},{8,11},{9,10},{10,... | collective-permute-start | bytes 3145736 | tf_op jit(solution)/shard_map/ppermute | solution.py:831
  91.3 14.6 %copy-start.14 = (bf16[2,2,256,2048]{3,2,1,0:T(8,128)(2,1)S(1)}, bf16[2,2,256,2048]{3,2,1,0:T(8,128)(2,1)}, u32[]{:S(2)}) copy-start(bf16[2,2,256,2048]{3,2,1,0:T(8,128)(2,1)} %constant_dynamic-update-slice_fusion.1) | copy-start | bytes 12582916
  105.4 71.2 %copy-start.1 = (bf16[2,2,256,1024]{3,2,1,0:T(8,128)(2,1)}, bf16[2,2,256,1024]{3,2,1,0:T(8,128)(2,1)S(1)}, u32[]{:S(2)}) copy-start(bf16[2,2,256,1024]{3,2,1,0:T(8,128)(2,1)S(1)} %get-tuple-element.43.o_ref.refs_3_) | copy-start | bytes 6291460
  107.5 4.5 copy-start.15
  107.5 17.2 %copy-start.5 = (bf16[512,2048]{1,0:T(8,128)(2,1)S(1)}, bf16[512,2048]{1,0:T(8,128)(2,1)}, u32[]{:S(2)}) copy-start(bf16[512,2048]{1,0:T(8,128)(2,1)} %copy-done.4) | copy-start | bytes 6291460
  112.0 74.8 %collective-permute-start.4 = (f32[512,2048]{1,0:T(8,128)}, f32[512,2048]{1,0:T(8,128)}, u32[]{:S(2)}, u32[]{:S(2)}) collective-permute-start(f32[512,2048]{1,0:T(8,128)} %convolution_bitcast_fusion.1), channel_id=1, source_target_pairs={{0,1},{1,0},{2,3},{3,2},{4,5},{5,4},{6,7},{7,6},{8,9},{9,8},{10,11... | collective-permute-start | bytes 12582920 | tf_op jit(solution)/shard_map/ppermute | solution.py:831
  126.7 47.2 %collective-permute-start.8 = (bf16[2,2,64,2048]{3,2,1,0:T(8,128)(2,1)}, bf16[2,2,64,2048]{3,2,1,0:T(8,128)(2,1)}, u32[]{:S(2)}, u32[]{:S(2)}) collective-permute-start(bf16[2,2,64,2048]{3,2,1,0:T(8,128)(2,1)} %get-tuple-element.68), channel_id=1, source_target_pairs={{0,3},{1,2},{2,1},{3,0},{4,7},{5,6},{6,5},{7,4},{8,11},{9,10},{10,... | collective-permute-start | bytes 3145736 | tf_op jit(solution)/shard_map/ppermute | solution.py:831
  127.8 46.1 %collective-permute-start.6 = (bf16[2,2,64,2048]{3,2,1,0:T(8,128)(2,1)}, bf16[2,2,64,2048]{3,2,1,0:T(8,128)(2,1)}, u32[]{:S(2)}, u32[]{:S(2)}) collective-permute-start(bf16[2,2,64,2048]{3,2,1,0:T(8,128)(2,1)} %get-tuple-element.68), channel_id=1, source_target_pairs={{0,1},{1,0},{2,3},{3,2},{4,5},{5,4},{6,7},{7,6},{8,9},{9,8},{10,11... | collective-permute-start | bytes 3145736 | tf_op jit(solution)/shard_map/ppermute | solution.py:831
  128.3 45.6 %collective-permute-start.7 = (bf16[2,2,64,2048]{3,2,1,0:T(8,128)(2,1)}, bf16[2,2,64,2048]{3,2,1,0:T(8,128)(2,1)}, u32[]{:S(2)}, u32[]{:S(2)}) collective-permute-start(bf16[2,2,64,2048]{3,2,1,0:T(8,128)(2,1)} %get-tuple-element.67), channel_id=1, source_target_pairs={{0,2},{1,3},{2,0},{3,1},{4,6},{5,7},{6,4},{7,5},{8,10},{9,11},{10,... | collective-permute-start | bytes 3145736 | tf_op jit(solution)/shard_map/ppermute | solution.py:831
  130.0 43.9 %copy-start.19 = (bf16[2,2,1,64,2048]{4,3,1,0,2:T(8,128)(2,1)S(1)}, bf16[2,2,1,64,2048]{4,3,1,0,2:T(8,128)(2,1)}, u32[]{:S(2)}) copy-start(bf16[2,2,1,64,2048]{4,3,1,0,2:T(8,128)(2,1)} %get-tuple-element.66) | copy-start | bytes 3145732
  173.9 7.1 %slice-start.4 = ((s8[8388608]{0:T(1024)(128)(4,1)}), s8[4194304]{0:T(1024)(128)(4,1)S(1)}, s32[]{:S(2)}) async-start(s8[8388608]{0:T(1024)(128)(4,1)} %bitcast.93), calls=%async_computation.4 | async-start | bytes 8388608
  176.3 4.7 slice-start.5
  178.5 41.9 %copy-start.17 = (bf16[2,2,4,64,2048]{4,3,2,1,0:T(8,128)(2,1)}, bf16[2,2,4,64,2048]{4,3,2,1,0:T(8,128)(2,1)S(1)}, u32[]{:S(2)}) copy-start(bf16[2,2,4,64,2048]{4,3,2,1,0:T(8,128)(2,1)S(1)} %copy.29) | copy-start | bytes 12582916
  189.8 6.0 copy-start.13
  191.3 49.9 %collective-permute-start.5 = (f32[4,64,2048]{2,1,0:T(8,128)}, f32[4,64,2048]{2,1,0:T(8,128)S(1)}, u32[]{:S(2)}, u32[]{:S(2)}) collective-permute-start(f32[4,64,2048]{2,1,0:T(8,128)} %dynamic-slice_bitcast_fusion), channel_id=1, source_target_pairs={{0,4},{1,5},{2,6},{3,7},{4,0},{5,1},{6,2},{7,3},{8,12},{9,13},{10,... | collective-permute-start | bytes 6291464 | tf_op jit(solution)/shard_map/ppermute | solution.py:831
  220.4 7.2 %copy-start.3 = (bf16[2,2,256,1024]{3,2,1,0:T(8,128)(2,1)}, bf16[2,2,256,1024]{3,2,1,0:T(8,128)(2,1)S(1)}, u32[]{:S(2)}) copy-start(bf16[2,2,256,1024]{3,2,1,0:T(8,128)(2,1)S(1)} %get-tuple-element.49.refs_4_) | copy-start | bytes 6291460
  446.3 5.2 copy-start.18
  487.4 188.1 %copy-start.21 = (bf16[512,2048]{1,0:T(8,128)(2,1)S(1)}, bf16[512,2048]{1,0:T(8,128)(2,1)}, u32[]{:S(2)}) copy-start(bf16[512,2048]{1,0:T(8,128)(2,1)} %get-tuple-element.50) | copy-start | bytes 6291460
  677.8 20.4 %slice-start = ((s8[16777216]{0:T(1024)(128)(4,1)}), s8[4194304]{0:T(1024)(128)(4,1)S(1)}, s32[]{:S(2)}) async-start(s8[16777216]{0:T(1024)(128)(4,1)} %bitcast.88), calls=%async_computation | async-start | bytes 8388608
  679.1 14.6 %copy-start.24 = (f32[2048,256]{1,0:T(8,128)S(1)}, f32[2048,256]{1,0:T(8,128)}, u32[]{:S(2)}) copy-start(f32[2048,256]{1,0:T(8,128)} %get-tuple-element.104) | copy-start | bytes 6291460
  679.1 19.0 %slice-start.1 = ((s8[16777216]{0:T(1024)(128)(4,1)}), s8[4194304]{0:T(1024)(128)(4,1)S(1)}, s32[]{:S(2)}) async-start(s8[16777216]{0:T(1024)(128)(4,1)} %bitcast.88), calls=%async_computation.1 | async-start | bytes 8388608
  679.1 19.0 %slice-start.2 = ((s8[16777216]{0:T(1024)(128)(4,1)}), s8[4194304]{0:T(1024)(128)(4,1)S(1)}, s32[]{:S(2)}) async-start(s8[16777216]{0:T(1024)(128)(4,1)} %bitcast.88), calls=%async_computation.2 | async-start | bytes 8388608
  679.1 19.0 %slice-start.3 = ((s8[16777216]{0:T(1024)(128)(4,1)}), s8[4194304]{0:T(1024)(128)(4,1)S(1)}, s32[]{:S(2)}) async-start(s8[16777216]{0:T(1024)(128)(4,1)} %bitcast.88), calls=%async_computation.3 | async-start | bytes 8388608
  698.1 6.2 copy-start.25
  (9 other events, 17.6 us)

commit v4 on v3

--- a/solution.py
+++ b/solution.py
@@ -1,4 +1,5 @@
 import functools
+import heapq
 
 import jax
 import jax.numpy as jnp
@@ -405,6 +406,122 @@
     )(kv, q, dy)
 
 
+class PairSum:
+    def __init__(self, me, kind, cut, src, out, buffers, sems):
+        self.me, self.kind, self.src, self.out = me, kind, src, out
+        self.size = out.shape[0] // cut
+        self.own, self.from_core, self.from_y, self.from_z = buffers
+        self.load_sem, self.core_s, self.core_r, self.y_s, self.y_r, self.z_s, self.z_r = sems
+        self.z, self.y, x, core = place(me)
+        self.core, self.partner = core, dev(self.z, self.y, x, 1 - core)
+        self.across = dev(self.z, 1 - self.y, x, core)
+        self.next_z = dev(self.z + 1, self.y, x, core), dev(self.z - 1, self.y, x, core)
+
+    def rows(self, j):
+        return pl.ds(j * self.size, self.size)
+
+    def mine(self, j, zz):
+        at = self.rows(j)
+        return self.own.at[zz, self.y, at] if self.kind == "core" else self.own.at[zz, at]
+
+    def load(self, j):
+        src, at = self.src, self.rows(j)
+        if self.kind == "core":
+            src, dst = src.at[self.core, :, :, at], self.own.at[:, :, at]
+        else:
+            src, dst = (src.at[:, at] if self.kind else src.at[:, self.y, at]), self.own.at[:, at]
+        return pltpu.make_async_copy(src, dst, self.load_sem.at[j])
+
+    def core_copy(self, j):
+        src, dst = (r.at[:, :, self.rows(j)] for r in (self.src.at[1 - self.core], self.from_core))
+        return remote(src, dst, self.core_s.at[j], self.core_r.at[j], self.partner)
+
+    def y_copy(self, j):
+        src = self.own if self.kind == "core" else self.src
+        at = self.rows(j)
+        return remote(src.at[:, 1 - self.y, at], self.from_y.at[:, at], self.y_s.at[j], self.y_r.at[j], self.across)
+
+    def z_copy(self, j, way, zz, to):
+        at = way, zz + way - 1
+        return remote(self.mine(j, zz), self.from_z.at[*at, self.rows(j)], self.z_s.at[j, *at], self.z_r.at[j, *at], to)
+
+    def begin(self, j):
+        self.load(j).start()
+        if self.kind == "core":
+            self.core_copy(j).start()
+        elif not self.kind:
+            self.y_copy(j).start()
+
+    def loaded(self, j):
+        self.load(j).wait()
+        if self.kind == "core":
+            self.core_copy(j).wait_recv()
+            at = self.rows(j)
+            for zz in range(4):
+                self.own[zz, :, at] += self.from_core[zz, :, at]
+            self.y_copy(j).start()
+        if self.kind == "z":
+            self.hop(j, 0)
+
+    def relay(self, j, way, zz, add):
+        if add:
+            self.z_copy(j, way, zz, self.me).wait_recv()
+            self.mine(j, zz)[...] += self.from_z[way, zz + way - 1, self.rows(j)]
+        self.z_copy(j, way, zz, self.next_z[way]).start()
+
+    def hop(self, j, h):
+        @pl.when(self.z == h)
+        def _():
+            for zz in range(3, h, -1):
+                self.relay(j, 0, zz, h > 0)
+
+        @pl.when(self.z == 3 - h)
+        def _():
+            for zz in range(3 - h):
+                self.relay(j, 1, zz, h > 0)
+
+    def step(self, j, h):
+        if h == 0 and self.kind != "z":
+            self.y_copy(j).wait_recv()
+            for zz in range(4):
+                self.mine(j, zz)[...] += self.from_y[zz, self.rows(j)]
+            self.hop(j, 0)
+        elif 0 < h < 3:
+            self.hop(j, h)
+        elif h == 3:
+            at = self.rows(j)
+            self.out[at] = self.mine(j, self.z)[...]
+            for way, on in enumerate((self.z > 0, self.z < 3)):
+
+                @pl.when(on)
+                def _(way=way):
+                    self.z_copy(j, way, self.z, self.me).wait_recv()
+                    self.out[at] += self.from_z[way, self.z + way - 1, at]
+
+    def wait_send(self, j):
+        if self.kind == "core":
+            self.core_copy(j).wait_send()
+        if self.kind != "z":
+            self.y_copy(j).wait_send()
+        for zz in range(4):
+            if zz > 0:
+                pl.when(self.z < zz)(self.z_copy(j, 0, zz, self.next_z[0]).wait_send)
+            if zz < 3:
+                pl.when(self.z > zz)(self.z_copy(j, 1, zz, self.next_z[1]).wait_send)
+
+    @staticmethod
+    def scratch(kind, block):
+        unused = pltpu.VMEM((8, HEAD_DIM), F32)
+        own = pltpu.VMEM(((4, TWO) if kind == "core" else (4,)) + block, F32)
+        from_y = unused if kind == "z" else pltpu.VMEM((4,) + block, F32)
+        return [own, own if kind == "core" else unused, from_y, pltpu.VMEM((TWO, 3) + block, F32)]
+
+    @staticmethod
+    def sems(*dims):
+        dma = pltpu.SemaphoreType.DMA
+        return [dma(dims)] * 5 + [dma(dims + (TWO, 3))] * TWO
+
+
 def reduce_kernel(cuts, kinds, work, *refs):
     n = len(cuts)
 
@@ -414,111 +531,25 @@
         return first
 
     ins, more_in, outs, more_out = take(n), take(work.ins), take(n), take(work.outs)
-    own, from_core, from_y, from_z = take(n), take(n), take(n), take(n)
-    load_sem, core_s, core_r, y_s, y_r, z_s, z_r = take(7)
+    buffers, sems = [take(4) for _ in kinds], take(7)
     me = lax.axis_index("cp")
     z, y, x, core = place(me)
-    partner, across = dev(z, y, x, 1 - core), dev(z, 1 - y, x, core)
-    next_z = dev(z + 1, y, x, core), dev(z - 1, y, x, core)
-    meet(quad_of(me)[1:] + [across] + [dev(zz, y, x, core) for _, zz in z_peers(z)])
+    meet(quad_of(me)[1:] + [dev(z, 1 - y, x, core)] + [dev(zz, y, x, core) for _, zz in z_peers(z)])
     job = work(me, more_in, more_out, refs)
-
-    def rows(i, j):
-        size = outs[i].shape[0] // cuts[i]
-        return pl.ds(j * size, size)
-
-    def mine(i, j, zz):
-        at = rows(i, j)
-        return own[i].at[zz, y, at] if kinds[i] == "core" else own[i].at[zz, at]
-
-    def load(i, j):
-        src, at = ins[i], rows(i, j)
-        src = {"core": lambda: src.at[core, :, :, at], "z": lambda: src.at[:, at], "": lambda: src.at[:, y, at]}[kinds[i]]()
-        dst = own[i].at[:, :, at] if kinds[i] == "core" else own[i].at[:, at]
-        return pltpu.make_async_copy(src, dst, load_sem.at[i, j])
-
-    def core_copy(i, j):
-        at = rows(i, j)
-        return remote(ins[i].at[1 - core, :, :, at], from_core[i].at[:, :, at], core_s.at[i, j], core_r.at[i, j], partner)
-
-    def y_copy(i, j):
-        src = own[i] if kinds[i] == "core" else ins[i]
-        at = rows(i, j)
-        return remote(src.at[:, 1 - y, at], from_y[i].at[:, at], y_s.at[i, j], y_r.at[i, j], across)
-
-    def z_copy(i, j, way, zz, to):
-        at = way, zz + way - 1
-        return remote(mine(i, j, zz), from_z[i].at[*at, rows(i, j)], z_s.at[i, j, *at], z_r.at[i, j, *at], to)
-
-    def relay(i, j, way, zz, add):
-        if add:
-            z_copy(i, j, way, zz, me).wait_recv()
-            mine(i, j, zz)[...] += from_z[i][way, zz + way - 1, rows(i, j)]
-        z_copy(i, j, way, zz, next_z[way]).start()
-
-    def hop(i, j, h):
-        @pl.when(z == h)
-        def _():
-            for zz in range(3, h, -1):
-                relay(i, j, 0, zz, h > 0)
-
-        @pl.when(z == 3 - h)
-        def _():
-            for zz in range(3 - h):
-                relay(i, j, 1, zz, h > 0)
-
-    def across_y(i, j):
-        if kinds[i] != "z":
-            y_copy(i, j).wait_recv()
-            for zz in range(4):
-                mine(i, j, zz)[...] += from_y[i][zz, rows(i, j)]
-
-    def last(i, j):
-        at = rows(i, j)
-        outs[i][at] = mine(i, j, z)[...]
-        for way, on in enumerate((z > 0, z < 3)):
-
-            @pl.when(on)
-            def _(way=way):
-                z_copy(i, j, way, z, me).wait_recv()
-                outs[i][at] += from_z[i][way, z + way - 1, at]
-
-    pieces = [(i, j) for i in range(n) for j in range(cuts[i])]
-    for i, j in pieces:
-        load(i, j).start()
-        if kinds[i] == "core":
-            core_copy(i, j).start()
-        elif not kinds[i]:
-            y_copy(i, j).start()
-    for i, j in pieces:
-        load(i, j).wait()
-        if kinds[i] == "core":
-            core_copy(i, j).wait_recv()
-            at = rows(i, j)
-            for zz in range(4):
-                own[i][zz, :, at] += from_core[i][zz, :, at]
-            y_copy(i, j).start()
-        if kinds[i] == "z":
-            hop(i, j, 0)
+    sums = [PairSum(me, *a, [r.at[i] for r in sems]) for i, a in enumerate(zip(kinds, cuts, ins, outs, buffers))]
+    pieces = [(s, j) for s, cut in zip(sums, cuts) for j in range(cut)]
+    for s, j in pieces:
+        s.begin(j)
+    for s, j in pieces:
+        s.loaded(j)
     for t in range(len(pieces) + 3):
-        for h, (i, j) in enumerate(reversed(pieces[max(t - 3, 0) : t + 1]), max(t + 1 - len(pieces), 0)):
-            if h == 0:
-                across_y(i, j)
-            if h == 3:
-                last(i, j)
-            elif h > 0 or kinds[i] != "z":
-                hop(i, j, h)
+        for h in range(4):
+            if 0 <= t - h < len(pieces):
+                s, j = pieces[t - h]
+                s.step(j, h)
         job.step(t)
-    for i, j in pieces:
-        if kinds[i] == "core":
-            core_copy(i, j).wait_send()
-        if kinds[i] != "z":
-            y_copy(i, j).wait_send()
-        for zz in range(4):
-            if zz > 0:
-                pl.when(z < zz)(z_copy(i, j, 0, zz, next_z[0]).wait_send)
-            if zz < 3:
-                pl.when(z > zz)(z_copy(i, j, 1, zz, next_z[1]).wait_send)
+    for s, j in pieces:
+        s.wait_send(j)
     job.finish()
 
 
@@ -626,7 +657,7 @@
 
 
 class HiddenGradient:
-    ins, outs = 6, TWO
+    tiles = 4
 
     def __init__(self, me, ins, outs, scratch):
         dkv, self.part, self.w_kv, self.x, self.dy, self.gain = ins
@@ -636,30 +667,18 @@
         self.home.start()
 
     @staticmethod
-    def scratch(arrays):
+    def scratch(dkv, x):
         dma = pltpu.SemaphoreType.DMA
-        dkv, x = arrays[0], arrays[3]
         home = pltpu.VMEM((TWO,) * 3 + (CHUNK, TWO * dkv.shape[-1]), BF16)
         return [home, pltpu.VMEM((8, x.shape[1]), F32), dma(()), dma((4,)), dma((4,))]
 
-    @staticmethod
-    def results(arrays):
-        x = arrays[3]
-        return [jax.ShapeDtypeStruct(x.shape, BF16), jax.ShapeDtypeStruct((1, x.shape[1]), F32)]
-
-    spaces = [pltpu.VMEM] * 6
-
-    def step(self, t):
+    def tile(self, t):
         if t == 0:
             self.home.wait_recv()
             self.rows[...] = jnp.zeros_like(self.rows)
-            pl.loop(0, 4)(self.tile)
-            self.terms[...] = jnp.sum(self.rows[...], axis=0, keepdims=True)
-
-    def tile(self, t):
         size = TWO * CHUNK
-        at = pl.ds(pl.multiple_of(t * size, size), size)
-        dkv = self.dkv_home[t // TWO, lax.rem(t, TWO)].reshape(size, -1)
+        at = pl.ds(t * size, size)
+        dkv = self.dkv_home[t // TWO, t % TWO].reshape(size, -1)
         d = self.part[at] + dot_t(dkv, self.w_kv[...])
         d = d.astype(BF16).astype(F32)
         x = self.x[at].astype(F32)
@@ -668,21 +687,17 @@
         dx = inv_rms * (scaled - unit * row_mean(scaled * unit))
         self.dx[at] = (self.dy[at].astype(F32) + dx).astype(BF16)
         self.rows[...] += jnp.sum((d * unit).reshape((-1,) + self.rows.shape), axis=0)
+        if t == self.tiles - 1:
+            self.terms[...] = jnp.sum(self.rows[...], axis=0, keepdims=True)
 
     def finish(self):
         self.home.wait_send()
 
 
 def reduce_pairs(arrays, cuts, kinds, collective_id, work, more):
-    dma = pltpu.SemaphoreType.DMA
-    n, most = len(arrays), max(cuts)
+    n = len(arrays)
     blocks = [a.shape[-TWO:] for a in arrays]
-    own = [pltpu.VMEM(((4, TWO) if k == "core" else (4,)) + b, F32) for b, k in zip(blocks, kinds)]
-    unused = pltpu.VMEM((8, HEAD_DIM), F32)
-    scratch = own + [o if k == "core" else unused for o, k in zip(own, kinds)]
-    scratch += [unused if k == "z" else pltpu.VMEM((4,) + b, F32) for b, k in zip(blocks, kinds)]
-    scratch += [pltpu.VMEM((TWO, 3) + b, F32) for b in blocks]
-    scratch += [dma((n, most))] * 5 + [dma((n, most, TWO, 3))] * TWO
+    scratch = sum((PairSum.scratch(k, b) for k, b in zip(kinds, blocks)), []) + PairSum.sems(n, max(cuts))
     outs = [jax.ShapeDtypeStruct(b, F32) for b in blocks] + work.results(more)
     return pl.pallas_call(
         functools.partial(reduce_kernel, cuts, kinds, work),
@@ -696,103 +711,144 @@
     )(*arrays, *more)
 
 
+LINKS = "xyud"
+ORDERS = "zxy", "zyx", "xyz", "zxy"
+SIZES = 9.5, 9.5, 6.3, 2.8
+LATENCY, TILES_FROM, TILE_EVERY = 3.0, 14.0, 8.0
+SUM_AT = 42.0, 56.0, 70.0, 84.0
+
+
+def onward(order, key):
+    dz, ry, rx = key
+    stage = max((order.index(a) for a, r in zip("zyx", key) if r), default=-1)
+    for axis in order[stage + 1 :]:
+        if axis == "x":
+            yield "x", (dz, ry, 1)
+        elif axis == "y":
+            yield "y", (dz, 1, rx)
+        else:
+            yield "u", (-1, ry, rx)
+            yield "d", (1, ry, rx)
+    if stage >= 0 and order[stage] == "z" and abs(dz) < 3:
+        yield ("u", (dz - 1, ry, rx)) if dz < 0 else ("d", (dz + 1, ry, rx))
+
+
+def arrivals():
+    busy = dict.fromkeys(LINKS, 0.0)
+    starts = [0.0] * 3 + [SUM_AT[-1] + LATENCY]
+    here, seen = [(t, part, (0, 0, 0)) for part, t in enumerate(starts)], []
+    while here:
+        now, part, key = heapq.heappop(here)
+        seen.append((now, part, key))
+        for link, there in onward(ORDERS[part], key):
+            busy[link] = max(busy[link], now) + SIZES[part]
+            heapq.heappush(here, (busy[link] + LATENCY, part, there))
+    return seen
+
+
 def gather_kernel(*refs):
-    shards, refs = refs[:4], refs[4:]
-    terms, *outs, dgain_ref = refs[:6]
-    own_sem, zs, fs, ls, cs, zr, fr, lr, cr, all_terms, g_s, g_r = refs[6:]
+    wo_ref, wq_ref, wkv_ref, *refs = refs
+    grad_ins, outs, (dx_ref, dgain_ref), refs = refs[:6], refs[6:10], refs[10:12], refs[12:]
+    own_sem, send_sem, come_sem, core_sem, all_terms, g_s, g_r, terms, wkv_own = refs[:9]
+    buffers, sems, refs = refs[9:13], refs[13:20], refs[20:]
     me = lax.axis_index("cp")
     z, y, x, core = place(me)
-    across = (dev(z, y, 1 - x, core), dev(z, 1 - y, x, core))
+    line = Line(me)
+    to = {"x": dev(z, y, 1 - x, core), "y": dev(z, 1 - y, x, core), "u": line.next[1], "d": line.next[-1]}
     partner = dev(z, y, x, 1 - core)
     others = [(i, me ^ i) for i in range(1, all_terms.shape[0])]
     meet([d for _, d in others])
-
-    def windows(half, zz, yy, xx, cc):
+    job = HiddenGradient(me, grad_ins, (dx_ref, terms), refs)
+    wkv = PairSum(me, "core", 1, wkv_ref, wkv_own, buffers, [r.at[0] for r in sems])
+    wkv.begin(0)
+
+    def windows(part, zz, yy, xx, cc):
         pair = TWO * zz + yy
-        rows = shards[0].shape[0] // TWO
-        out_rows = pl.ds(((xx * TWO + cc) * N_PAIRS + pair) * TWO * rows + half * rows, rows)
-        yield shards[0], pl.ds(half * rows, rows), outs[0].at[out_rows]
-        rows = shards[1].shape[0] // TWO
-        out_rows = pl.ds((cc * N_PAIRS + pair) * TWO * rows + half * rows, rows)
-        for s, o in zip(shards[1:], outs[1:]):
-            yield s, pl.ds(half * rows, rows), o.at[out_rows, pl.ds(xx * s.shape[1], s.shape[1])]
-
-    total = sum(s.size for s in shards) // TWO // outs[0].shape[1]
-    whole = outs[0].at[pl.ds(0, total)]
-
-    def flip(v, on):
-        return 1 - v if on else v
-
-    class Copy:
-        def __init__(self, half, zz, first, last, send, arrive, to, is_own, cc=core):
-            over_x, over_y = (first, last) if half == 0 else (last, first)
-            self.at = half, zz, flip(y, over_y), flip(x, over_x), cc
-            self.send, self.arrive, self.to, self.is_own = send, arrive, to, is_own
-
-        def start(self):
-            for shard, rows, window in windows(*self.at):
-                remote(shard.at[rows] if self.is_own else window, window, self.send, self.arrive, self.to).start()
-
-        def wait_recv(self):
-            remote(whole, whole, self.send, self.arrive, me).wait_recv()
-
-        def wait_send(self):
-            remote(whole, whole, self.send, self.arrive, me).wait_send()
-
-    places = [(0, z)] + [(k, lax.rem(z + 4 - k, 4)) for k in (1, 3, TWO)]
-    halves = range(TWO)
-
-    def z_copy(half, k, zz):
-        return Copy(half, z, 0, 0, zs.at[half, k], zr.at[half, k], dev(zz, y, x, core), True)
-
-    def first_copy(half, k, zz):
-        at = half, k
-        return Copy(half, zz, 0, 0, fs.at[at], fr.at[at], across[half], k == 0)
-
-    def last_copy(half, k, zz, first):
-        at = half, first, k
-        return Copy(half, zz, first, 0, ls.at[at], lr.at[at], across[1 - half], k == first == 0)
-
-    def core_copy(half, k, zz, first, last):
-        at = half, first, last, k
-        return Copy(half, zz, first, last, cs.at[at], cr.at[at], partner, k == first == last == 0)
+        wide, narrow = wq_ref.shape[1], wkv_own.shape[1] // TWO
+        wo_at, wq_at = ((xx * TWO + cc) * N_PAIRS + pair) * wo_ref.shape[0], (cc * N_PAIRS + pair) * wq_ref.shape[0]
+        if part == 3:
+            for i, out in enumerate(outs[TWO:]):
+                cols = pl.ds(xx * narrow, narrow)
+                yield wkv_own.at[:, head_slice(i)], out.at[pl.ds(wq_at, wkv_own.shape[0]), cols]
+            return
+        eighth = wo_ref.shape[0] // 8
+        at, rows = (part * 3 * eighth, (TWO if part == TWO else 3) * eighth)
+        yield wo_ref.at[pl.ds(at, rows)], outs[0].at[pl.ds(wo_at + at, rows)]
+        at, rows = TWO * at, TWO * rows
+        yield wq_ref.at[pl.ds(at, rows)], outs[1].at[pl.ds(wq_at + at, rows), pl.ds(xx * wide, wide)]
+
+    def block(part, key, cc=core):
+        dz, ry, rx = key
+        return windows(part, z + dz, 1 - y if ry else y, 1 - x if rx else x, cc)
+
+    def index(part, key):
+        return (part, key[0] + 3) + key[1:]
+
+    def send(part, key, link, there):
+        arrive = (core_sem if link is None else come_sem).at[index(part, there)]
+        for shard, window in block(part, key):
+            src = window if any(key) else shard
+            remote(src, window, send_sem.at[index(part, key) + (LINKS.find(link or "-") + 1,)], arrive, to.get(link, partner)).start()
+
+    def whole(part, send, arrive):
+        size = sum(shard.size for shard, _ in block(part, (0, 0, 0))) // outs[0].shape[1]
+        dst = outs[0].at[pl.ds(0, size)]
+        return remote(dst, dst, send, arrive, me)
+
+    def when(on, do):
+        pl.when(on)(do)
+
+    def each_way(part, key):
+        held = line.held(key[0])
+        yield None, key, held
+        for link, there in onward(ORDERS[part], key):
+            inside = {"u": line.inside[1], "d": line.inside[-1]}.get(link)
+            yield link, there, held if inside is None else jnp.logical_and(held, inside)
+
+    def pass_on(part, key):
+        for link, there, on in each_way(part, key):
+            when(on, functools.partial(send, part, key, link, there))
 
     def term_copy(i, d):
         return remote(terms, all_terms.at[i], g_s.at[i], g_r.at[i], d)
 
     owns = []
-    for half in halves:
-        for shard, rows, window in windows(half, z, y, x, core):
-            owns.append(pltpu.make_async_copy(shard.at[rows], window, own_sem.at[len(owns)]))
-    for k, zz in z_peers(z):
-        for half in halves:
-            z_copy(half, k, zz).start()
-    for k, zz in places:
-        for half in halves:
-            if k > 0:
-                z_copy(half, k, zz).wait_recv()
-            first_copy(half, k, zz).start()
-            last_copy(half, k, zz, 0).start()
-            core_copy(half, k, zz, 0, 0).start()
-        if k == 0:
-            for o in owns:
-                o.start()
+
+    def put_own(part):
+        for shard, window in block(part, (0, 0, 0)):
+            owns.append(pltpu.make_async_copy(shard, window, own_sem.at[len(owns)]))
+            owns[-1].start()
+
+    def tile(t):
+        job.tile(t)
+        if t == job.tiles - 1:
             for i, d in others:
                 term_copy(i, d).start()
-        for half in halves:
-            first_copy(half, k, zz).wait_recv()
-            last_copy(half, k, zz, 1).start()
-            core_copy(half, k, zz, 1, 0).start()
-    for first in halves:
-        for k, zz in places:
-            for half in halves:
-                last_copy(half, k, zz, first).wait_recv()
-                core_copy(half, k, zz, first, 1).start()
+
+    def sum_step(h):
+        wkv.step(0, h)
+        if h == 3:
+            put_own(3)
+
+    steps = [(TILES_FROM + t * TILE_EVERY, functools.partial(tile, t)) for t in range(job.tiles)]
+    steps += [(at, functools.partial(sum_step, h)) for h, at in enumerate(SUM_AT)]
+    steps.sort(key=lambda s: s[0])
+    events = arrivals()
+    for part in range(3):
+        pass_on(part, (0, 0, 0))
+        put_own(part)
+    wkv.loaded(0)
+    for now, part, key in events:
+        while steps and steps[0][0] <= now:
+            steps.pop(0)[1]()
+        if any(key):
+            arrive = come_sem.at[index(part, key)]
+            when(line.held(key[0]), whole(part, own_sem.at[0], arrive).wait_recv)
+            pass_on(part, key)
+        elif part == 3:
+            pass_on(part, key)
     for o in owns:
         o.wait()
-    for k, zz in z_peers(z):
-        for half in halves:
-            z_copy(half, k, zz).wait_send()
     total_gain = terms[...]
     for i, d in others:
         term_copy(i, d).wait_recv()
@@ -800,31 +856,35 @@
     dgain_ref[...] = total_gain
     for i, d in others:
         term_copy(i, d).wait_send()
-    for k, zz in places:
-        for half in halves:
-            first_copy(half, k, zz).wait_send()
-            for first in halves:
-                last_copy(half, k, zz, first).wait_send()
-                for last in halves:
-                    core_copy(half, k, zz, first, last).wait_recv()
-                    core_copy(half, k, zz, first, last).wait_send()
-
-
-def gather_all(shards, shapes, terms):
+    for _, part, key in events:
+        when(line.held(key[0]), whole(part, own_sem.at[0], core_sem.at[index(part, key)]).wait_recv)
+        for link, there, on in each_way(part, key):
+            sent = send_sem.at[index(part, key) + (LINKS.find(link or "-") + 1,)]
+            when(on, whole(part, sent, own_sem.at[0]).wait_send)
+    wkv.wait_send(0)
+    job.finish()
+
+
+def gather_all(wo, wq, wkv, dkv, part, w_kv, x, dy, gain, shapes):
     dma = pltpu.SemaphoreType.DMA
     vmem, hbm = pl.BlockSpec(memory_space=pltpu.VMEM), pl.BlockSpec(memory_space=pl.ANY)
-    hops = [dma((TWO,) * i + (4,)) for i in (1, 1, TWO, 3)]
-    n = len(shards)
+    block = wkv.shape[-TWO:]
+    parts = len(ORDERS)
+    keys = (parts, 7, TWO, TWO)
+    terms = 1, x.shape[1]
+    scratch = [dma((TWO * parts,)), dma(keys + (len(LINKS) + 1,)), dma(keys), dma(keys)]
+    scratch += [pltpu.VMEM((32,) + terms, F32), dma((32,)), dma((32,)), pltpu.VMEM(terms, F32), pltpu.VMEM(block, F32)]
     return pl.pallas_call(
         gather_kernel,
         name="gather_all",
-        out_shape=[jax.ShapeDtypeStruct(s, F32) for s in shapes + [terms.shape]],
-        in_specs=[vmem] * (n + 1),
-        out_specs=[hbm] * n + [vmem],
-        scratch_shapes=[dma((TWO * n,))] + hops + hops + [pltpu.VMEM((32,) + terms.shape, F32), dma((32,)), dma((32,))],
-        compiler_params=pltpu.CompilerParams(collective_id=0),
+        out_shape=[jax.ShapeDtypeStruct(s, F32) for s in shapes]
+        + [jax.ShapeDtypeStruct(x.shape, BF16), jax.ShapeDtypeStruct(terms, F32)],
+        in_specs=[vmem] * TWO + [hbm] + [vmem] * 6,
+        out_specs=[hbm] * len(shapes) + [vmem] * TWO,
+        scratch_shapes=scratch + PairSum.scratch("core", block) + PairSum.sems(1, 1) + HiddenGradient.scratch(dkv, x),
+        compiler_params=params(40, collective_id=0),
         cost_estimate=cost(1, 76),
-    )(*shards, terms)
+    )(wo, wq, wkv, dkv, part, w_kv, x, dy, gain)
 
 
 def perm(x, pairs):
@@ -921,12 +981,17 @@
         dk_u = rotate(dkv_own[0] * ATTN_SCALE, cos_u, -sin_u).astype(BF16)
         dkv_u = jnp.concatenate([dk_u, dkv_own[1].astype(BF16)], axis=-1)
         w_kv = jnp.hstack([w[:, head_slice(i)] for i in range(TWO) for w in (w_k, w_v)])
-        more = dkv_u, d_part, w_kv, x_flat, grad_out.reshape(n_rows, d_model), gain[NEW]
-        wkv_own, grad_x, terms = reduce_pairs([by_core(dkv_u)], (TWO,), ("core",), 3, HiddenGradient, more)
-
-        wk_own, wv_own = jnp.split(wkv_own, TWO, axis=1)
-        grad_wo, grad_wq, grad_wk, grad_wv, d_gain = gather_all(
-            [wo_own, wq_own, wk_own, wv_own], [w_o.shape, w_q.shape, w_k.shape, w_v.shape], terms
+        grad_wo, grad_wq, grad_wk, grad_wv, grad_x, d_gain = gather_all(
+            wo_own,
+            wq_own,
+            by_core(dkv_u),
+            dkv_u,
+            d_part,
+            w_kv,
+            x_flat,
+            grad_out.reshape(n_rows, d_model),
+            gain[NEW],
+            [w_o.shape, w_q.shape, w_k.shape, w_v.shape],
         )
         block_out, grad_x = (a.reshape(hidden.shape) for a in (block_out, grad_x))
         return block_out, grad_x, grad_wq, grad_wk, grad_wv, grad_wo, d_gain.reshape(d_model)

time: 709 us -> 665 us (0.938)
  the two profiles are of different devices: /device:TPU:9 before, /device:TPU:0 now
where the time goes in v4:
time: 665 us; the launch traced here: 661 us
  Pallas kernels  502 us (75%)
  local copies, waits for them, and re-layouts  55.3 us (8%)
  waiting for transfers between devices  53.8 us (8%)
  matrix products  21.1 us (3%)
  other arithmetic  18.4 us (3%)
  starting transfers between devices  8.82 us (1%)
    pallas_call x1, Pallas kernels, reduce_pairs(): pl.pallas_call(functools.partial(reduce_kernel, cuts, kinds, work), name=...  219 us
    pallas_call x1, Pallas kernels, gather_all(): pl.pallas_call(gather_kernel, name='gather_all', out_shape=[jax.ShapeDtyp...  172 us
    pallas_call x1, Pallas kernels, exchange(): pl.pallas_call(exchange_kernel, name='exchange', out_shape=(jax.ShapeDtyp...  60.1 us
    ppermute x9, waiting for transfers between devices, perm(): return lax.ppermute(x, 'cp', pairs)  53.8 us
    unnamed x66, local copies, waits for them, and re-layouts  40.5 us
    pallas_call x1, Pallas kernels, flash_bwd(): pl.pallas_call(bwd_kernel, name='attn_bwd', out_shape=(jax.ShapeDtypeStru...  26.9 us
    dot_general x5, matrix products, dot(): lax.dot_general(a, b, ((ca, cb), ((), ())), preferred_element_type=F32)  21.1 us
    pallas_call x1, Pallas kernels, flash_fwd(): pl.pallas_call(fwd_kernel, name='attn_fwd', out_shape=(jax.ShapeDtypeStru...  15.6 us
  transfers between devices with their start and end apart: 9, of which 2 were waited for; matrix products, arithmetic and copies ran while one was open for 6% of the time, Pallas kernels for 17%

profile of v4, /device:TPU:0, one launch (start us, length us, event | category | flops | bytes accessed | tf_op | source)
XLA Modules:
  0.0 661.1 jit_solution(12669314063330065074)
XLA Ops:
  1.6 2.4 collective-permute-start.3
  6.1 2.3 dynamic-slice_bitcast_fusion.2
  11.0 1.8 norm_kv.1
  13.6 7.1 %query.1 = bf16[2,2,256,1024]{3,2,1,0:T(8,128)(2,1)S(1)} custom-call(bf16[512,2048]{1,0:T(8,128)(2,1)S(1)} %get-tuple-element.33.h_ref, bf16[2048,2048]{1,0:T(8,128)(2,1)S(1)} %copy-done, f32[512,128]{1,0:T(8,128)S(1)} %get-tuple-element.82.cos_ref, f32[512,128]{1,0:T(8,128)S(1)} %get-tuple-element.83.sin_ref), custom_call_target="tpu_custom_call" | custom-call | flops 5000000000 | bytes 12582912 | tf_op jit(solution)/shard_map/query/pallas_call | solution.py:273
  22.0 60.1 %exchange.1 = (bf16[8,2,2,2,256,128]{5,4,3,2,1,0:T(8,128)(2,1)}, bf16[2,2,256,1024]{3,2,1,0:T(8,128)(2,1)}, bf16[2,2,192,2048]{3,2,1,0:T(8,128)(2,1)}) custom-call(bf16[2,2,2,2,2,64,128]{6,5,4,3,2,1,0:T(8,128)(2,1)} %bitcast.85, bf16[2,2,2,2,64,1024]{5,4,3,2,1,0:T(8,128)(2,1)} %bitcast.83, bf16[2,2,2,64,2048]{4,3,2,1,0:T(8,128)(2,1)} %bitcast.94), custom_call_target="tpu_custom_call" | custom-call | flops 1000000000 | bytes 20971520 | tf_op jit(solution)/shard_map/exchange/pallas_call | solution.py:393
  82.1 1.9 collective-permute-start
  84.5 4.0 constant_dynamic-update-slice_fusion.1
  89.7 2.2 copy-done.14
  91.8 1.6 copy-done.15
  93.4 15.6 %attn_fwd.1 = (bf16[2,2,256,1024]{3,2,1,0:T(8,128)(2,1)S(1)}, f32[2,2,8,1,256]{4,3,2,1,0:T(1,128)S(1)}) custom-call(s32[10]{0:T(128)S(1)} %pad_add_fusion.2.tab, bf16[2,2,256,1024]{3,2,1,0:T(8,128)(2,1)S(1)} %copy-done.15, bf16[8,2,2,2,256,128]{5,4,3,2,1,0:T(8,128)(2,1)S(1)} %copy-done.14, s32[2,2,256,128]{3,2,1,0:T(8,128)S(1)} %broadcast_in_dim.14.st_ref, ...), custom_call_target="tpu_custom_call" | custom-call | flops 20000000000 | bytes 16777216 | tf_op jit(solution)/shard_map/attn_fwd/pallas_call | solution.py:199
  109.1 2.1 constant_dynamic-update-slice_fusion
  111.2 4.5 convolution_bitcast_fusion.1
  115.7 1.9 dynamic-slice_bitcast_fusion.4
  117.6 1.6 collective-permute-start.8
  121.2 1.5 pad_maximum_fusion.1.refs_5_
  123.9 42.0 %collective-permute-done.7 = bf16[2,2,64,2048]{3,2,1,0:T(8,128)(2,1)} collective-permute-done((bf16[2,2,64,2048]{3,2,1,0:T(8,128)(2,1)}, bf16[2,2,64,2048]{3,2,1,0:T(8,128)(2,1)}, u32[]{:S(2)}, u32[]{:S(2)}) %collective-permute-start.7) | collective-permute-done | bytes 1048608 | tf_op jit(solution)/shard_map/ppermute | solution.py:891
  165.9 3.1 pad_maximum_fusion
  169.0 2.4 copy.29
  172.7 2.5 fusion.7
  175.2 5.7 fusion.3.do_ref
  181.0 3.5 bitcast_add_fusion
  184.5 1.6 dynamic-slice_bitcast_fusion
  186.1 1.7 collective-permute-start.5
  187.9 26.9 %attn_bwd.1 = (bf16[2,2,256,1024]{3,2,1,0:T(8,128)(2,1)S(1)}, f32[8,2,2,2,256,128]{5,4,3,2,1,0:T(8,128)}) custom-call(s32[10]{0:T(128)S(1)} %pad_add_fusion.2.tab, bf16[2,2,256,1024]{3,2,1,0:T(8,128)(2,1)S(1)} %copy-done.16, bf16[2,2,256,1024]{3,2,1,0:T(8,128)(2,1)} %fusion.3.do_ref, bf16[2,2,256,1024]{3,2,1,0:T(8,128)(2,1)} %copy-done.1, ...), custom_call_target="tpu_custom_call" | custom-call | flops 49999998976 | bytes 33554432 | tf_op jit(solution)/shard_map/attn_bwd/pallas_call | solution.py:217
  214.8 7.1 %convolution_bitcast_fusion = f32[2048,1024]{1,0:T(8,128)} fusion(bf16[2,2,256,2048]{3,2,1,0:T(8,128)(2,1)S(1)} %bitcast.101, bf16[2,2,256,1024]{3,2,1,0:T(8,128)(2,1)S(1)} %get-tuple-element.47.refs_4_), kind=kOutput, calls=%fused_computation | convolution fusion | flops 4294967296 | bytes 14680064 | tf_op jit(solution)/shard_map/dot_general | solution.py:47
  221.9 11.7 %collective-permute-done.5 = f32[4,64,2048]{2,1,0:T(8,128)S(1)} collective-permute-done((f32[4,64,2048]{2,1,0:T(8,128)}, f32[4,64,2048]{2,1,0:T(8,128)S(1)}, u32[]{:S(2)}, u32[]{:S(2)}) %collective-permute-start.5) | collective-permute-done | bytes 2097184 | tf_op jit(solution)/shard_map/ppermute | solution.py:891
  233.6 1.6 bitcast_add_fusion.1.refs_0_
  235.2 219.3 %reduce_pairs.1 = (f32[64,2048]{1,0:T(8,128)}, f32[2048,128]{1,0:T(8,128)}, f32[128,1024]{1,0:T(8,128)}, bf16[512,2048]{1,0:T(8,128)(2,1)}, f32[512,2048]{1,0:T(8,128)}) custom-call(f32[4,64,2048]{2,1,0:T(8,128)} %bitcast_add_fusion.1.refs_0_, f32[4,2,2048,128]{3,2,1,0:T(8,128)} %bitcast.98, f32[2,4,2,128,1024]{4,3,2,1,0:T(8,128)} %bitcast.99, ...), custom_call_target="tpu_custom_call" | custom-call | flops 1000000000 | bytes 20971520 | tf_op jit(solution)/shard_map/reduce_pairs/pallas_call | solution.py:702
  457.0 2.6 fusion.12
  462.4 171.5 %gather_all.1 = (f32[2048,2048]{1,0:T(8,128)}, f32[2048,2048]{1,0:T(8,128)}, f32[2048,256]{1,0:T(8,128)S(1)}, f32[2048,256]{1,0:T(8,128)S(1)}, bf16[512,2048]{1,0:T(8,128)(2,1)S(1)}, /*index=5*/f32[1,2048]{1,0:T(1,128)S(1)}) custom-call(f32[64,2048]{1,0:T(8,128)S(1)} %copy-done.11, f32[128,1024]{1,0:T(8,128)S(1)} %copy-done.12, ...), custom_call_target="tpu_custom_call" | custom-call | flops 1000000000 | bytes 79691776 | tf_op jit(solution)/shard_map/gather_all/pallas_call | solution.py:877
  636.6 14.1 %copy.54 = f32[2048,2048]{1,0:T(8,128)} copy(f32[2048,2048]{1,0:T(8,128)} %get-tuple-element.97) | data formatting | bytes 33554432
  654.1 6.2 copy.57
  (112 shorter events, 25.6 us)
Async XLA Ops:
  0.6 9.0 %copy-start.9 = (bf16[2048,256]{1,0:T(8,128)(2,1)S(1)}, bf16[2048,256]{1,0:T(8,128)(2,1)}, u32[]{:S(2)}) copy-start(bf16[2048,256]{1,0:T(8,128)(2,1)} %wk_ref.1) | copy-start | bytes 3145732
  0.6 9.0 %copy-start.2 = (bf16[4,128,2048]{2,1,0:T(8,128)(2,1)S(1)}, bf16[4,128,2048]{2,1,0:T(8,128)(2,1)}, u32[]{:S(2)}) copy-start(bf16[4,128,2048]{2,1,0:T(8,128)(2,1)} %param.9) | copy-start | bytes 6291460
  1.6 87.1 %collective-permute-start.3 = (s32[2,2,64]{2,1,0:T(2,128)S(1)}, s32[2,2,64]{2,1,0:T(2,128)S(1)}, u32[]{:S(2)}, u32[]{:S(2)}) collective-permute-start(s32[2,2,64]{2,1,0:T(2,128)S(1)} %get-tuple-element.76), channel_id=1, source_target_pairs={{0,3},{1,2},{2,1},{3,0},{4,7},{5,6},{6,5},{7,4},{8,11},{9,10},{10,... | collective-permute-start | bytes 3080 | tf_op jit(solution)/shard_map/ppermute | solution.py:891
  4.0 84.7 %collective-permute-start.1 = (s32[2,2,64]{2,1,0:T(2,128)S(1)}, s32[2,2,64]{2,1,0:T(2,128)S(1)}, u32[]{:S(2)}, u32[]{:S(2)}) collective-permute-start(s32[2,2,64]{2,1,0:T(2,128)S(1)} %get-tuple-element.76), channel_id=1, source_target_pairs={{0,1},{1,0},{2,3},{3,2},{4,5},{5,4},{6,7},{7,6},{8,9},{9,8},{10,11... | collective-permute-start | bytes 3080 | tf_op jit(solution)/shard_map/ppermute | solution.py:891
  4.7 84.0 %collective-permute-start.2 = (s32[2,2,64]{2,1,0:T(2,128)S(1)}, s32[2,2,64]{2,1,0:T(2,128)S(1)}, u32[]{:S(2)}, u32[]{:S(2)}) collective-permute-start(s32[2,2,64]{2,1,0:T(2,128)S(1)} %bitcast.105), channel_id=1, source_target_pairs={{0,2},{1,3},{2,0},{3,1},{4,6},{5,7},{6,4},{7,5},{8,10},{9,11},{10,... | collective-permute-start | bytes 3080 | tf_op jit(solution)/shard_map/ppermute | solution.py:891
  9.4 4.3 copy-start
  13.6 7.1 %copy-start.6 = (bf16[512,2048]{1,0:T(8,128)(2,1)}, bf16[512,2048]{1,0:T(8,128)(2,1)S(1)}, u32[]{:S(2)}) copy-start(bf16[512,2048]{1,0:T(8,128)(2,1)S(1)} %get-tuple-element.33.h_ref) | copy-start | bytes 6291460
  82.1 27.0 %collective-permute-start = (bf16[2,2,64,2048]{3,2,1,0:T(8,128)(2,1)}, bf16[2,2,64,2048]{3,2,1,0:T(8,128)(2,1)}, u32[]{:S(2)}, u32[]{:S(2)}) collective-permute-start(bf16[2,2,64,2048]{3,2,1,0:T(8,128)(2,1)} %dynamic-slice_bitcast_fusion.2), channel_id=1, source_target_pairs={{0,3},{1,2},{2,1},{3,0},{4,7},{5,6},{6,5},{7,4},{8,11},{9,10},{10,... | collective-permute-start | bytes 3145736 | tf_op jit(solution)/shard_map/ppermute | solution.py:891
  93.4 15.7 %copy-start.17 = (bf16[2,2,256,2048]{3,2,1,0:T(8,128)(2,1)S(1)}, bf16[2,2,256,2048]{3,2,1,0:T(8,128)(2,1)}, u32[]{:S(2)}) copy-start(bf16[2,2,256,2048]{3,2,1,0:T(8,128)(2,1)} %constant_dynamic-update-slice_fusion.1) | copy-start | bytes 12582916
  109.1 62.4 %copy-start.1 = (bf16[2,2,256,1024]{3,2,1,0:T(8,128)(2,1)}, bf16[2,2,256,1024]{3,2,1,0:T(8,128)(2,1)S(1)}, u32[]{:S(2)}) copy-start(bf16[2,2,256,1024]{3,2,1,0:T(8,128)(2,1)S(1)} %get-tuple-element.41.o_ref.refs_3_) | copy-start | bytes 6291460
  111.2 4.5 copy-start.18
  111.2 4.5 copy-start.7
  115.7 65.2 %collective-permute-start.4 = (f32[512,2048]{1,0:T(8,128)}, f32[512,2048]{1,0:T(8,128)}, u32[]{:S(2)}, u32[]{:S(2)}) collective-permute-start(f32[512,2048]{1,0:T(8,128)} %convolution_bitcast_fusion.1), channel_id=1, source_target_pairs={{0,1},{1,0},{2,3},{3,2},{4,5},{5,4},{6,7},{7,6},{8,9},{9,8},{10,11... | collective-permute-start | bytes 12582920 | tf_op jit(solution)/shard_map/ppermute | solution.py:891
  117.6 48.2 %collective-permute-start.8 = (bf16[2,2,64,2048]{3,2,1,0:T(8,128)(2,1)}, bf16[2,2,64,2048]{3,2,1,0:T(8,128)(2,1)}, u32[]{:S(2)}, u32[]{:S(2)}) collective-permute-start(bf16[2,2,64,2048]{3,2,1,0:T(8,128)(2,1)} %get-tuple-element.64), channel_id=1, source_target_pairs={{0,3},{1,2},{2,1},{3,0},{4,7},{5,6},{6,5},{7,4},{8,11},{9,10},{10,... | collective-permute-start | bytes 3145736 | tf_op jit(solution)/shard_map/ppermute | solution.py:891
  119.3 46.6 %collective-permute-start.6 = (bf16[2,2,64,2048]{3,2,1,0:T(8,128)(2,1)}, bf16[2,2,64,2048]{3,2,1,0:T(8,128)(2,1)}, u32[]{:S(2)}, u32[]{:S(2)}) collective-permute-start(bf16[2,2,64,2048]{3,2,1,0:T(8,128)(2,1)} %get-tuple-element.64), channel_id=1, source_target_pairs={{0,1},{1,0},{2,3},{3,2},{4,5},{5,4},{6,7},{7,6},{8,9},{9,8},{10,11... | collective-permute-start | bytes 3145736 | tf_op jit(solution)/shard_map/ppermute | solution.py:891
  119.3 46.6 %collective-permute-start.7 = (bf16[2,2,64,2048]{3,2,1,0:T(8,128)(2,1)}, bf16[2,2,64,2048]{3,2,1,0:T(8,128)(2,1)}, u32[]{:S(2)}, u32[]{:S(2)}) collective-permute-start(bf16[2,2,64,2048]{3,2,1,0:T(8,128)(2,1)} %get-tuple-element.63), channel_id=1, source_target_pairs={{0,2},{1,3},{2,0},{3,1},{4,6},{5,7},{6,4},{7,5},{8,10},{9,11},{10,... | collective-permute-start | bytes 3145736 | tf_op jit(solution)/shard_map/ppermute | solution.py:891
  165.9 9.3 %slice-start.4 = ((s8[8388608]{0:T(1024)(128)(4,1)}), s8[4194304]{0:T(1024)(128)(4,1)S(1)}, s32[]{:S(2)}) async-start(s8[8388608]{0:T(1024)(128)(4,1)} %bitcast.96), calls=%async_computation.4 | async-start | bytes 8388608
  169.0 3.7 copy-start.19
  169.0 6.2 slice-start.5
  184.5 3.4 copy-start.16
  186.1 47.6 %collective-permute-start.5 = (f32[4,64,2048]{2,1,0:T(8,128)}, f32[4,64,2048]{2,1,0:T(8,128)S(1)}, u32[]{:S(2)}, u32[]{:S(2)}) collective-permute-start(f32[4,64,2048]{2,1,0:T(8,128)} %dynamic-slice_bitcast_fusion), channel_id=1, source_target_pairs={{0,4},{1,5},{2,6},{3,7},{4,0},{5,1},{6,2},{7,3},{8,12},{9,13},{10,... | collective-permute-start | bytes 6291464 | tf_op jit(solution)/shard_map/ppermute | solution.py:891
  187.9 26.9 %copy-start.20 = (bf16[2,2,4,64,2048]{4,3,2,1,0:T(8,128)(2,1)S(1)}, bf16[2,2,4,64,2048]{4,3,2,1,0:T(8,128)(2,1)}, u32[]{:S(2)}) copy-start(bf16[2,2,4,64,2048]{4,3,2,1,0:T(8,128)(2,1)} %copy.29) | copy-start | bytes 12582916
  214.8 7.1 %copy-start.5 = (bf16[2,2,256,1024]{3,2,1,0:T(8,128)(2,1)}, bf16[2,2,256,1024]{3,2,1,0:T(8,128)(2,1)S(1)}, u32[]{:S(2)}) copy-start(bf16[2,2,256,1024]{3,2,1,0:T(8,128)(2,1)S(1)} %get-tuple-element.47.refs_4_) | copy-start | bytes 6291460
  454.5 5.4 copy-start.21
  459.9 2.2 copy-start.4
  459.9 2.3 copy-start.11
  459.9 2.4 copy-start.12
  462.4 171.6 %copy-start.22 = (bf16[512,2048]{1,0:T(8,128)(2,1)S(1)}, bf16[512,2048]{1,0:T(8,128)(2,1)}, u32[]{:S(2)}) copy-start(bf16[512,2048]{1,0:T(8,128)(2,1)} %get-tuple-element.48) | copy-start | bytes 6291460
  635.3 18.0 %slice-start = ((s8[16777216]{0:T(1024)(128)(4,1)}), s8[4194304]{0:T(1024)(128)(4,1)S(1)}, s32[]{:S(2)}) async-start(s8[16777216]{0:T(1024)(128)(4,1)} %bitcast.91), calls=%async_computation | async-start | bytes 8388608
  636.6 16.7 %slice-start.1 = ((s8[16777216]{0:T(1024)(128)(4,1)}), s8[4194304]{0:T(1024)(128)(4,1)S(1)}, s32[]{:S(2)}) async-start(s8[16777216]{0:T(1024)(128)(4,1)} %bitcast.91), calls=%async_computation.1 | async-start | bytes 8388608
  636.6 16.7 %slice-start.2 = ((s8[16777216]{0:T(1024)(128)(4,1)}), s8[4194304]{0:T(1024)(128)(4,1)S(1)}, s32[]{:S(2)}) async-start(s8[16777216]{0:T(1024)(128)(4,1)} %bitcast.91), calls=%async_computation.2 | async-start | bytes 8388608
  636.6 17.5 %slice-start.3 = ((s8[16777216]{0:T(1024)(128)(4,1)}), s8[4194304]{0:T(1024)(128)(4,1)S(1)}, s32[]{:S(2)}) async-start(s8[16777216]{0:T(1024)(128)(4,1)} %bitcast.91), calls=%async_computation.3 | async-start | bytes 8388608
  (6 other events, 8.9 us)

commit v5 on v4

--- a/solution.py
+++ b/solution.py
@@ -1,5 +1,6 @@
 import functools
 import heapq
+import itertools
 
 import jax
 import jax.numpy as jnp
@@ -17,6 +18,7 @@
 EXP2_SCALE = ATTN_SCALE * LOG2E
 CHUNK = 64
 TWO = 2
+FOUR = 4
 NEW = jnp.newaxis
 BLK = 4 * CHUNK
 N_HEADS = 8
@@ -25,7 +27,8 @@
 MESH = pl.DeviceIdType.MESH
 ONE = pl.Squeezed()
 LATER = 2, 3
-PRODUCTS_AT = 3, 7
+MADE_AT = 5
+PRODUCTS_AT = 7, 9
 F32 = jnp.float32
 BF16 = jnp.bfloat16
 
@@ -36,11 +39,6 @@
     inv_freq = ROPE_BASE ** (-jnp.arange(0, HEAD_DIM, TWO).astype(F32) / HEAD_DIM)
     angles = positions.astype(F32)[..., None] * inv_freq
     return jnp.cos(angles), jnp.sin(angles)
-
-
-def rotate(x, cos_t, sin_t):
-    a, b = x[..., : HEAD_DIM // TWO], x[..., HEAD_DIM // TWO :]
-    return jnp.concatenate([a * cos_t - b * sin_t, b * cos_t + a * sin_t], axis=-1)
 
 
 def dot(a, b, ca, cb):
@@ -98,32 +96,40 @@
     return jnp.logical_and(off >= st_ref[...] - s * BLK, off <= qi_ref[...] - s * BLK)
 
 
-def fwd_kernel(tab, q_ref, kv_ref, st_ref, qi_ref, ko_ref, o_ref, lse_ref, q_s, acc, m_s, l_s):
+def fwd_kernel(tab, q_ref, kv_ref, st_ref, qi_ref, ko_ref, o_ref, lse_ref, q_s, acc, m_s, l_s, k_t):
     m_s[...] = jnp.full_like(m_s, NEG_BIG)
     l_s[...] = jnp.zeros_like(l_s)
     acc[...] = jnp.zeros_like(acc)
     for h in range(N_HEADS):
         q_s[pl.ds(h * BLK, BLK)] = q_ref[:, head(h)]
 
+    @pl.when(pl.program_id(1) == 0)
+    def _():
+        @pl.loop(0, N_PAIRS)
+        def _(pair):
+            for hk in range(TWO):
+                k_t[pair, hk] = kv_ref[pair, 0, hk].T
+
     def body(s, at, masked):
         pair, hk = at
-        k, v = kv_ref[pair, 0, hk], kv_ref[pair, 1, hk]
+        v = kv_ref[pair, 1, hk]
         if masked:
             off = ko_ref[hk] + s * BLK
             mask = [
                 jnp.logical_and(off[:, lanes] >= st_ref[...], off[:, lanes] <= qi_ref[...])
                 for lanes in (slice(HEAD_DIM), slice(HEAD_DIM, BLK))
             ]
-        for h in range(N_HEADS):
-            rows = pl.ds(h * BLK, BLK)
-            sc = dot_t(q_s[rows], k)
-            sc = [sc[:, :HEAD_DIM] * EXP2_SCALE, sc[:, HEAD_DIM:] * EXP2_SCALE]
+            mask = [jnp.concatenate([m, m], axis=0) for m in mask]
+        for g in range(N_HEADS // TWO):
+            rows = pl.ds(g * TWO * BLK, TWO * BLK)
+            sc = jnp.dot(q_s[rows], k_t[pair, hk], preferred_element_type=F32)
+            sc = [sc[:, :HEAD_DIM], sc[:, HEAD_DIM:]]
             if masked:
                 sc = [jnp.where(m, x, NEG_BIG) for m, x in zip(mask, sc)]
             m_old = m_s[rows]
             m_new = jnp.maximum(m_old, jnp.max(jnp.maximum(*sc), axis=1, keepdims=True))
-            alpha = jnp.exp2(m_old - m_new)
-            p = [jnp.exp2(x - m_new) for x in sc]
+            alpha = jnp.exp2((m_old - m_new) * EXP2_SCALE)
+            p = [jnp.exp2((x - m_new) * EXP2_SCALE) for x in sc]
             m_s[rows] = m_new
             l_s[rows] = l_s[rows] * alpha + (p[0] + p[1])
             p = jnp.hstack([x.astype(BF16) for x in p])
@@ -134,7 +140,7 @@
         rows = pl.ds(h * BLK, BLK)
         total = jnp.sum(l_s[rows], axis=1, keepdims=True)
         o_ref[:, head(h)] = (acc[rows] / total).astype(BF16)
-        lse_ref[h] = (m_s[rows] + jnp.log2(total)).T[:1]
+        lse_ref[h] = (m_s[rows] * EXP2_SCALE + jnp.log2(total)).T[:1]
 
 
 def bwd_kernel(tab, q_ref, do_ref, o_ref, kv_ref, lse_ref, st_ref, qi_ref, ko_ref, cos_ref, sin_ref, dq_ref, dkv_ref, dq_acc, delta):
@@ -205,7 +211,8 @@
             grid=(TWO, TWO),
             in_specs=[tile, kvs, col, col, ko],
             out_specs=[tile, stat],
-            scratch_shapes=[pltpu.VMEM((N_HEADS * BLK, HEAD_DIM), t) for t in (BF16, F32, F32, F32)],
+            scratch_shapes=[pltpu.VMEM((N_HEADS * BLK, HEAD_DIM), t) for t in (BF16, F32, F32, F32)]
+            + [pltpu.VMEM((N_PAIRS, TWO, HEAD_DIM, BLK), BF16)],
         ),
         compiler_params=params(40),
         cost_estimate=cost(20, 16),
@@ -268,7 +275,7 @@
         compiler_params=params(40),
         cost_estimate=cost(TWO, 7),
     )(x, gain, w_k, w_v, cos_f, sin_f)
-    tile = 4 * HEAD_DIM
+    tile = FOUR * HEAD_DIM
     rope = pl.BlockSpec(cos_f.shape, lambda j: (0, 0))
     q = pl.pallas_call(
         query_kernel,
@@ -284,7 +291,7 @@
 
 
 def place(me):
-    return me // 8, lax.rem(me // 4, TWO), lax.rem(me // TWO, TWO), lax.rem(me, TWO)
+    return me // 8, lax.rem(me // FOUR, TWO), lax.rem(me // TWO, TWO), lax.rem(me, TWO)
 
 
 def dev(z, y, x, core):
@@ -292,7 +299,7 @@
 
 
 def z_peers(z):
-    return [(k, lax.rem(z + k, 4)) for k in (1, TWO, 3)]
+    return [(k, lax.rem(z + k, FOUR)) for k in (1, TWO, 3)]
 
 
 def meet(peers):
@@ -338,7 +345,7 @@
 
     def target(a, d):
         tok = pl.ds(d * CHUNK, CHUNK)
-        return kv_all.at[me // 4, :, :, :, tok] if a == 0 else (q_u, dy_u)[a - 1].at[:, :, tok]
+        return kv_all.at[me // FOUR, :, :, :, tok] if a == 0 else (q_u, dy_u)[a - 1].at[:, :, tok]
 
     def quad_copy(a, d):
         return remote(source(a, d), target(a, d), quad_s.at[a, d], quad_r.at[a, d], quad[d])
@@ -400,7 +407,7 @@
         ),
         in_specs=[vmem] * 3,
         out_specs=[hbm] * 3,
-        scratch_shapes=[dma((3,))] + [dma((3, 4))] * TWO + [dma((TWO, TWO, 7))] + [dma((TWO, 7))] * 3,
+        scratch_shapes=[dma((3,))] + [dma((3, FOUR))] * TWO + [dma((TWO, TWO, 7))] + [dma((TWO, 7))] * 3,
         compiler_params=pltpu.CompilerParams(collective_id=1),
         cost_estimate=cost(1, 20),
     )(kv, q, dy)
@@ -413,7 +420,7 @@
         self.own, self.from_core, self.from_y, self.from_z = buffers
         self.load_sem, self.core_s, self.core_r, self.y_s, self.y_r, self.z_s, self.z_r = sems
         self.z, self.y, x, core = place(me)
-        self.core, self.partner = core, dev(self.z, self.y, x, 1 - core)
+        self.partner = dev(self.z, self.y, x, 1 - core)
         self.across = dev(self.z, 1 - self.y, x, core)
         self.next_z = dev(self.z + 1, self.y, x, core), dev(self.z - 1, self.y, x, core)
 
@@ -425,15 +432,12 @@
         return self.own.at[zz, self.y, at] if self.kind == "core" else self.own.at[zz, at]
 
     def load(self, j):
-        src, at = self.src, self.rows(j)
-        if self.kind == "core":
-            src, dst = src.at[self.core, :, :, at], self.own.at[:, :, at]
-        else:
-            src, dst = (src.at[:, at] if self.kind else src.at[:, self.y, at]), self.own.at[:, at]
-        return pltpu.make_async_copy(src, dst, self.load_sem.at[j])
+        at = self.rows(j)
+        src = self.src.at[:, at] if self.kind else self.src.at[:, self.y, at]
+        return pltpu.make_async_copy(src, self.own.at[:, at], self.load_sem.at[j])
 
     def core_copy(self, j):
-        src, dst = (r.at[:, :, self.rows(j)] for r in (self.src.at[1 - self.core], self.from_core))
+        src, dst = (r.at[:, :, self.rows(j)] for r in (self.src, self.from_core))
         return remote(src, dst, self.core_s.at[j], self.core_r.at[j], self.partner)
 
     def y_copy(self, j):
@@ -446,18 +450,20 @@
         return remote(self.mine(j, zz), self.from_z.at[*at, self.rows(j)], self.z_s.at[j, *at], self.z_r.at[j, *at], to)
 
     def begin(self, j):
-        self.load(j).start()
         if self.kind == "core":
             self.core_copy(j).start()
-        elif not self.kind:
+            return
+        self.load(j).start()
+        if not self.kind:
             self.y_copy(j).start()
 
     def loaded(self, j):
-        self.load(j).wait()
-        if self.kind == "core":
+        if self.kind != "core":
+            self.load(j).wait()
+        else:
             self.core_copy(j).wait_recv()
             at = self.rows(j)
-            for zz in range(4):
+            for zz in range(FOUR):
                 self.own[zz, :, at] += self.from_core[zz, :, at]
             self.y_copy(j).start()
         if self.kind == "z":
@@ -483,7 +489,7 @@
     def step(self, j, h):
         if h == 0 and self.kind != "z":
             self.y_copy(j).wait_recv()
-            for zz in range(4):
+            for zz in range(FOUR):
                 self.mine(j, zz)[...] += self.from_y[zz, self.rows(j)]
             self.hop(j, 0)
         elif 0 < h < 3:
@@ -503,7 +509,7 @@
             self.core_copy(j).wait_send()
         if self.kind != "z":
             self.y_copy(j).wait_send()
-        for zz in range(4):
+        for zz in range(FOUR):
             if zz > 0:
                 pl.when(self.z < zz)(self.z_copy(j, 0, zz, self.next_z[0]).wait_send)
             if zz < 3:
@@ -512,8 +518,8 @@
     @staticmethod
     def scratch(kind, block):
         unused = pltpu.VMEM((8, HEAD_DIM), F32)
-        own = pltpu.VMEM(((4, TWO) if kind == "core" else (4,)) + block, F32)
-        from_y = unused if kind == "z" else pltpu.VMEM((4,) + block, F32)
+        own = pltpu.VMEM(((FOUR, TWO) if kind == "core" else (FOUR,)) + block, F32)
+        from_y = unused if kind == "z" else pltpu.VMEM((FOUR,) + block, F32)
         return [own, own if kind == "core" else unused, from_y, pltpu.VMEM((TWO, 3) + block, F32)]
 
     @staticmethod
@@ -522,28 +528,37 @@
         return [dma(dims)] * 5 + [dma(dims + (TWO, 3))] * TWO
 
 
+def taker(refs):
+    rest = iter(refs)
+    return lambda count: list(itertools.islice(rest, count))
+
+
 def reduce_kernel(cuts, kinds, work, *refs):
     n = len(cuts)
 
-    def take(count):
-        nonlocal refs
-        first, refs = refs[:count], refs[count:]
-        return first
-
-    ins, more_in, outs, more_out = take(n), take(work.ins), take(n), take(work.outs)
-    buffers, sems = [take(4) for _ in kinds], take(7)
+    take = taker(refs)
+    ins, more_in, outs, more_out, made = take(n - 1), take(work.ins), take(n), take(work.outs), take(1)
+    buffers, sems = [take(FOUR) for _ in kinds], take(7)
     me = lax.axis_index("cp")
     z, y, x, core = place(me)
     meet(quad_of(me)[1:] + [dev(z, 1 - y, x, core)] + [dev(zz, y, x, core) for _, zz in z_peers(z)])
-    job = work(me, more_in, more_out, refs)
-    sums = [PairSum(me, *a, [r.at[i] for r in sems]) for i, a in enumerate(zip(kinds, cuts, ins, outs, buffers))]
+    job = work(me, more_in, more_out, take(len(refs)))
+    sums = [PairSum(me, *a, [r.at[i] for r in sems]) for i, a in enumerate(zip(kinds, cuts, ins + made, outs, buffers))]
     pieces = [(s, j) for s, cut in zip(sums, cuts) for j in range(cut)]
-    for s, j in pieces:
+    early, late = pieces[: -cuts[-1]], pieces[-cuts[-1] :]
+    for s, j in early:
         s.begin(j)
-    for s, j in pieces:
+    for s, j in early:
         s.loaded(j)
     for t in range(len(pieces) + 3):
-        for h in range(4):
+        if t == MADE_AT:
+            job.wq_terms(sums[-1].own, made[0])
+            for s, j in late:
+                s.begin(j)
+        if t == MADE_AT + 1:
+            for s, j in late:
+                s.loaded(j)
+        for h in range(FOUR):
             if 0 <= t - h < len(pieces):
                 s, j = pieces[t - h]
                 s.step(j, h)
@@ -555,7 +570,7 @@
 
 def quad_of(me):
     z, y, x, core = place(me)
-    return [dev(z, y, 1 - x if d // TWO else x, 1 - core if d % TWO else core) for d in range(4)]
+    return [dev(z, y, 1 - x if d // TWO else x, 1 - core if d % TWO else core) for d in range(FOUR)]
 
 
 class Home:
@@ -586,31 +601,53 @@
 
 
 class Products:
-    ins, outs = 5, TWO
+    ins, outs = 6, 3
 
     def __init__(self, me, ins, outs, scratch):
-        attn, dq, self.hidden, self.w_o, self.w_q = ins
-        self.block_out, self.d_part = outs
-        self.attn_home, self.dq_home, self.buf_o, self.buf_q, own_sem, quad_s, quad_r, self.w_sem = scratch
+        attn, self.dq, hidden, normed, self.w_o, self.w_q = ins
+        self.block_out, self.d_part, self.h_u = outs
+        self.attn_home, self.dq_home, self.buf_o, self.buf_q, self.h_own, *sems = scratch
+        self.w_sem, self.load_sem, own_sem, quad_s, quad_r = sems
+        _, _, _, core = place(me)
+
+        def piece(d):
+            return normed.at[1 - core if d % TWO else core]
+
+        def tokens(d):
+            return self.h_u.at[:, :, pl.ds(d * CHUNK, CHUNK)]
+
+        self.h_copies = [remote(piece(d), tokens(d), quad_s.at[TWO, d], quad_r.at[TWO, d], quad_of(me)[d]) for d in (1, TWO, 3)]
+        self.h_mine = pltpu.make_async_copy(piece(0), self.h_own.at[:, :, pl.ds(0, CHUNK)], own_sem.at[TWO])
+        self.h_rest = pltpu.make_async_copy(
+            self.h_u.at[:, :, pl.ds(CHUNK, BLK - CHUNK)], self.h_own.at[:, :, pl.ds(CHUNK, BLK - CHUNK)], self.load_sem
+        )
+        self.h_back = pltpu.make_async_copy(self.h_own.at[:, :, pl.ds(0, CHUNK)], tokens(0), self.load_sem)
+        self.residual = pltpu.make_async_copy(hidden, self.block_out, own_sem.at[3])
+        self.residual.start()
+        for c in self.h_copies:
+            c.start()
+        self.h_mine.start()
         self.homes = [
             Home(me, src, out, own_sem.at[i], quad_s.at[i], quad_r.at[i])
-            for i, (src, out) in enumerate([(attn, self.attn_home), (dq, self.dq_home)])
+            for i, (src, out) in enumerate([(attn, self.attn_home), (self.dq, self.dq_home)])
         ]
         for h in self.homes:
             h.start()
 
     @staticmethod
     def scratch(arrays):
-        dma, d = pltpu.SemaphoreType.DMA, arrays[3].shape[0]
+        dma, d = pltpu.SemaphoreType.DMA, arrays[-1].shape[0]
         home = pltpu.VMEM((TWO,) * 3 + (CHUNK, d), BF16)
         buf = [pltpu.VMEM((TWO,) + b, BF16) for b in ((d, BLK), (BLK, d))]
-        return [home] * TWO + buf + [dma((TWO,)), dma((TWO, 4)), dma((TWO, 4)), dma((TWO, TWO))]
+        unit = pltpu.VMEM((TWO, TWO, BLK, d), BF16)
+        return [home] * TWO + buf + [unit, dma((TWO, TWO)), dma(()), dma((FOUR,)), dma((3, FOUR)), dma((3, FOUR))]
 
     @staticmethod
     def results(arrays):
-        return [jax.ShapeDtypeStruct(arrays[TWO].shape, t) for t in (BF16, F32)]
-
-    spaces = [pltpu.VMEM] * 3 + [pl.ANY] * TWO
+        unit = TWO, TWO, BLK, arrays[-1].shape[0]
+        return [jax.ShapeDtypeStruct(arrays[TWO].shape, t) for t in (BF16, F32)] + [jax.ShapeDtypeStruct(unit, BF16)]
+
+    spaces, out_spaces = [pl.ANY, pltpu.VMEM] + [pl.ANY] * FOUR, [pltpu.VMEM] * TWO + [pl.ANY]
 
     def tiles(self, fetch, use):
         n = self.w_o.shape[0] // BLK
@@ -640,7 +677,7 @@
         def project(at, slot):
             attn = self.attn_home[...].reshape(-1, self.w_o.shape[0])
             out = jnp.dot(attn, self.buf_o[slot], preferred_element_type=F32)
-            self.block_out[:, at] = (self.hidden[:, at].astype(F32) + out).astype(BF16)
+            self.block_out[:, at] = (self.block_out[:, at].astype(F32) + out).astype(BF16)
 
         def pull(at, slot):
             dq = self.dq_home[...].reshape(-1, self.w_o.shape[0])
@@ -649,37 +686,61 @@
         if t in PRODUCTS_AT:
             i = PRODUCTS_AT.index(t)
             self.homes[i].wait_recv()
+            if i == 0:
+                self.residual.wait()
             self.tiles(*((fetch_o, project), (fetch_q, pull))[i])
 
+    def wq_terms(self, own, other):
+        self.h_mine.wait()
+        self.h_back.start()
+        for c in self.h_copies:
+            c.wait_recv()
+        self.h_back.wait()
+        self.h_rest.start()
+        self.h_rest.wait()
+        core = lax.rem(lax.axis_index("cp"), TWO)
+        d_out = self.dq[...].reshape(-1, self.dq.shape[-1])
+        for out, half in ((other, 1 - core), (own, core)):
+
+            @pl.loop(0, FOUR)
+            def _(zz, out=out, half=half):
+                at = pl.multiple_of((half * FOUR + zz) * BLK, BLK)
+                h = self.h_own[:, :, :, pl.ds(at, BLK)].reshape(-1, BLK)
+                out[zz] = dot(h, d_out, (0,), (0,)).reshape(out.shape[1:])
+
     def finish(self):
+        for c in self.h_copies + self.homes:
+            c.wait_send()
+
+
+class HiddenGradient:
+    tiles = FOUR
+
+    def __init__(self, me, dk, dv, ins, outs, scratch):
+        self.part, self.w_k, self.w_v, self.x, self.dy, self.gain = ins
+        self.dx, self.terms = outs
+        self.dk_home, self.dv_home, self.rows, *sems = scratch
+        pairs = (dk, self.dk_home), (dv, self.dv_home)
+        self.homes = [Home(me, src, out, *[r.at[i] for r in sems]) for i, (src, out) in enumerate(pairs)]
         for h in self.homes:
-            h.wait_send()
-
-
-class HiddenGradient:
-    tiles = 4
-
-    def __init__(self, me, ins, outs, scratch):
-        dkv, self.part, self.w_kv, self.x, self.dy, self.gain = ins
-        self.dx, self.terms = outs
-        self.dkv_home, self.rows, *sems = scratch
-        self.home = Home(me, dkv, self.dkv_home, *sems)
-        self.home.start()
+            h.start()
 
     @staticmethod
-    def scratch(dkv, x):
+    def scratch(x):
         dma = pltpu.SemaphoreType.DMA
-        home = pltpu.VMEM((TWO,) * 3 + (CHUNK, TWO * dkv.shape[-1]), BF16)
-        return [home, pltpu.VMEM((8, x.shape[1]), F32), dma(()), dma((4,)), dma((4,))]
+        home = pltpu.VMEM((TWO,) * 3 + (CHUNK, TWO * HEAD_DIM), BF16)
+        return [home, home, pltpu.VMEM((8, x.shape[1]), F32), dma((TWO,)), dma((TWO, FOUR)), dma((TWO, FOUR))]
 
     def tile(self, t):
         if t == 0:
-            self.home.wait_recv()
+            for h in self.homes:
+                h.wait_recv()
             self.rows[...] = jnp.zeros_like(self.rows)
         size = TWO * CHUNK
         at = pl.ds(t * size, size)
-        dkv = self.dkv_home[t // TWO, t % TWO].reshape(size, -1)
-        d = self.part[at] + dot_t(dkv, self.w_kv[...])
+        d = self.part[at]
+        for home, w in ((self.dk_home, self.w_k), (self.dv_home, self.w_v)):
+            d += dot_t(home[t // TWO, t % TWO].reshape(size, -1), w[...])
         d = d.astype(BF16).astype(F32)
         x = self.x[at].astype(F32)
         inv_rms = lax.rsqrt(row_mean(x * x) + NORM_EPS)
@@ -691,31 +752,34 @@
             self.terms[...] = jnp.sum(self.rows[...], axis=0, keepdims=True)
 
     def finish(self):
-        self.home.wait_send()
-
-
-def reduce_pairs(arrays, cuts, kinds, collective_id, work, more):
-    n = len(arrays)
-    blocks = [a.shape[-TWO:] for a in arrays]
-    scratch = sum((PairSum.scratch(k, b) for k, b in zip(kinds, blocks)), []) + PairSum.sems(n, max(cuts))
+        for h in self.homes:
+            h.wait_send()
+
+
+def reduce_pairs(arrays, blocks, cuts, kinds, collective_id, work, more):
+    vmem, hbm = pl.BlockSpec(memory_space=pltpu.VMEM), pl.BlockSpec(memory_space=pl.ANY)
+    n = len(blocks)
+    scratch = [pltpu.VMEM((FOUR, TWO) + blocks[-1], F32)]
+    scratch += sum((PairSum.scratch(k, b) for k, b in zip(kinds, blocks)), []) + PairSum.sems(n, max(cuts))
     outs = [jax.ShapeDtypeStruct(b, F32) for b in blocks] + work.results(more)
     return pl.pallas_call(
         functools.partial(reduce_kernel, cuts, kinds, work),
         name="reduce_pairs",
         out_shape=outs,
-        in_specs=[pl.BlockSpec(memory_space=m) for m in [pl.ANY] * n + work.spaces],
-        out_specs=[pl.BlockSpec(memory_space=pltpu.VMEM)] * len(outs),
+        in_specs=[hbm] * len(arrays) + [pl.BlockSpec(memory_space=m) for m in work.spaces],
+        out_specs=[vmem] * n + [pl.BlockSpec(memory_space=m) for m in work.out_spaces],
         scratch_shapes=scratch + work.scratch(more),
-        compiler_params=params(60, collective_id=collective_id),
+        compiler_params=params(63, collective_id=collective_id),
         cost_estimate=cost(1, 20),
     )(*arrays, *more)
 
 
+HERE = 0, 0, 0
 LINKS = "xyud"
-ORDERS = "zxy", "zyx", "xyz", "zxy"
-SIZES = 9.5, 9.5, 6.3, 2.8
+ORDERS = "zxy", "zyx", "xyz", "zyx"
+SIZES = 8.4, 8.4, 5.6, 2.8
 LATENCY, TILES_FROM, TILE_EVERY = 3.0, 14.0, 8.0
-SUM_AT = 42.0, 56.0, 70.0, 84.0
+SUM_AT = 30.0, 42.0, 54.0, 66.0
 
 
 def onward(order, key):
@@ -734,23 +798,45 @@
 
 
 def arrivals():
-    busy = dict.fromkeys(LINKS, 0.0)
+    busy, times = {}, {}
     starts = [0.0] * 3 + [SUM_AT[-1] + LATENCY]
-    here, seen = [(t, part, (0, 0, 0)) for part, t in enumerate(starts)], []
+    here = [(t, z, part, HERE) for part, t in enumerate(starts) for z in range(FOUR)]
     while here:
-        now, part, key = heapq.heappop(here)
-        seen.append((now, part, key))
+        now, z, part, key = heapq.heappop(here)
+        times.setdefault((part, key), []).append(now)
         for link, there in onward(ORDERS[part], key):
-            busy[link] = max(busy[link], now) + SIZES[part]
-            heapq.heappush(here, (busy[link] + LATENCY, part, there))
-    return seen
+            to = z + {"u": 1, "d": -1}.get(link, 0)
+            if 0 <= to <= 3:
+                busy[z, link] = max(busy.get((z, link), 0), now) + SIZES[part]
+                heapq.heappush(here, (busy[z, link] + LATENCY, to, part, there))
+    return sorted((sum(t) / len(t), *at) for at, t in times.items())
+
+
+def turn_back(dkv_ref, cos_ref, sin_ref, dk_u, dv_u):
+    n = dk_u.shape[0] * dk_u.shape[1] * dk_u.shape[TWO]
+    dk = turn(dkv_ref[pl.ds(0, n)] * ATTN_SCALE, cos_ref, sin_ref)
+    dk_u[...] = dk.astype(BF16).reshape(dk_u.shape)
+    dv_u[...] = dkv_ref[pl.ds(n, n)].astype(BF16).reshape(dv_u.shape)
+
+
+def wkv_terms(h_own, dk_u, dv_u, outs):
+    d_out = jnp.hstack([r[...].reshape(-1, HEAD_DIM) for r in (dk_u, dv_u)])
+    for out, half in outs:
+
+        @pl.loop(0, FOUR)
+        def _(zz, out=out, half=half):
+            at = pl.multiple_of((half * FOUR + zz) * BLK, BLK)
+            h = h_own[:, :, :, pl.ds(at, BLK)].reshape(-1, BLK)
+            out[zz] = dot(h, d_out, (0,), (0,)).reshape(out.shape[1:])
 
 
 def gather_kernel(*refs):
-    wo_ref, wq_ref, wkv_ref, *refs = refs
-    grad_ins, outs, (dx_ref, dgain_ref), refs = refs[:6], refs[6:10], refs[10:12], refs[12:]
-    own_sem, send_sem, come_sem, core_sem, all_terms, g_s, g_r, terms, wkv_own = refs[:9]
-    buffers, sems, refs = refs[9:13], refs[13:20], refs[20:]
+    take = taker(refs)
+    wo_ref, wq_ref, dkv_ref, cos_ref, sin_ref, h_ref = take(6)
+    grad_ins, outs, (dx_ref, dgain_ref) = take(6), take(FOUR), take(TWO)
+    own_sem, send_sem, come_sem, core_sem, all_terms, g_s, g_r = take(7)
+    terms, wkv_own, wkv_ref, h_own, dk_u, dv_u = take(6)
+    buffers, sems, refs = take(FOUR), take(7), take(len(refs))
     me = lax.axis_index("cp")
     z, y, x, core = place(me)
     line = Line(me)
@@ -758,9 +844,9 @@
     partner = dev(z, y, x, 1 - core)
     others = [(i, me ^ i) for i in range(1, all_terms.shape[0])]
     meet([d for _, d in others])
-    job = HiddenGradient(me, grad_ins, (dx_ref, terms), refs)
+    load_h = pltpu.make_async_copy(h_ref, h_own, own_sem.at[0])
+    load_h.start()
     wkv = PairSum(me, "core", 1, wkv_ref, wkv_own, buffers, [r.at[0] for r in sems])
-    wkv.begin(0)
 
     def windows(part, zz, yy, xx, cc):
         pair = TWO * zz + yy
@@ -791,7 +877,7 @@
             remote(src, window, send_sem.at[index(part, key) + (LINKS.find(link or "-") + 1,)], arrive, to.get(link, partner)).start()
 
     def whole(part, send, arrive):
-        size = sum(shard.size for shard, _ in block(part, (0, 0, 0))) // outs[0].shape[1]
+        size = sum(shard.size for shard, _ in block(part, HERE)) // outs[0].shape[1]
         dst = outs[0].at[pl.ds(0, size)]
         return remote(dst, dst, send, arrive, me)
 
@@ -815,7 +901,7 @@
     owns = []
 
     def put_own(part):
-        for shard, window in block(part, (0, 0, 0)):
+        for shard, window in block(part, HERE):
             owns.append(pltpu.make_async_copy(shard, window, own_sem.at[len(owns)]))
             owns[-1].start()
 
@@ -830,12 +916,18 @@
         if h == 3:
             put_own(3)
 
-    steps = [(TILES_FROM + t * TILE_EVERY, functools.partial(tile, t)) for t in range(job.tiles)]
+    steps = [(TILES_FROM + t * TILE_EVERY, functools.partial(tile, t)) for t in range(HiddenGradient.tiles)]
     steps += [(at, functools.partial(sum_step, h)) for h, at in enumerate(SUM_AT)]
     steps.sort(key=lambda s: s[0])
     events = arrivals()
     for part in range(3):
-        pass_on(part, (0, 0, 0))
+        pass_on(part, HERE)
+    turn_back(dkv_ref, cos_ref, sin_ref, dk_u, dv_u)
+    job = HiddenGradient(me, dk_u, dv_u, grad_ins, (dx_ref, terms), refs)
+    load_h.wait()
+    wkv_terms(h_own, dk_u, dv_u, ((wkv_ref, 1 - core), (buffers[0], core)))
+    wkv.begin(0)
+    for part in range(3):
         put_own(part)
     wkv.loaded(0)
     for now, part, key in events:
@@ -865,26 +957,28 @@
     job.finish()
 
 
-def gather_all(wo, wq, wkv, dkv, part, w_kv, x, dy, gain, shapes):
+def gather_all(wo, wq, dkv, cos_f, sin_f, h_u, part, w_k, w_v, x, dy, gain, shapes):
     dma = pltpu.SemaphoreType.DMA
     vmem, hbm = pl.BlockSpec(memory_space=pltpu.VMEM), pl.BlockSpec(memory_space=pl.ANY)
-    block = wkv.shape[-TWO:]
+    block = w_k.shape[0] // TWO // N_PAIRS, w_k.shape[1]
     parts = len(ORDERS)
     keys = (parts, 7, TWO, TWO)
     terms = 1, x.shape[1]
     scratch = [dma((TWO * parts,)), dma(keys + (len(LINKS) + 1,)), dma(keys), dma(keys)]
     scratch += [pltpu.VMEM((32,) + terms, F32), dma((32,)), dma((32,)), pltpu.VMEM(terms, F32), pltpu.VMEM(block, F32)]
+    scratch += [pltpu.VMEM((FOUR, TWO) + block, F32), pltpu.VMEM(h_u.shape, BF16)]
+    scratch += [pltpu.VMEM((TWO, TWO, BLK, HEAD_DIM), BF16)] * TWO
     return pl.pallas_call(
         gather_kernel,
         name="gather_all",
         out_shape=[jax.ShapeDtypeStruct(s, F32) for s in shapes]
         + [jax.ShapeDtypeStruct(x.shape, BF16), jax.ShapeDtypeStruct(terms, F32)],
-        in_specs=[vmem] * TWO + [hbm] + [vmem] * 6,
+        in_specs=[vmem] * 5 + [hbm] + [vmem] * 6,
         out_specs=[hbm] * len(shapes) + [vmem] * TWO,
-        scratch_shapes=scratch + PairSum.scratch("core", block) + PairSum.sems(1, 1) + HiddenGradient.scratch(dkv, x),
-        compiler_params=params(40, collective_id=0),
+        scratch_shapes=scratch + PairSum.scratch("core", block) + PairSum.sems(1, 1) + HiddenGradient.scratch(x),
+        compiler_params=params(56, collective_id=0),
         cost_estimate=cost(1, 76),
-    )(wo, wq, wkv, dkv, part, w_kv, x, dy, gain)
+    )(wo, wq, dkv, cos_f, sin_f, h_u, part, w_k, w_v, x, dy, gain)
 
 
 def perm(x, pairs):
@@ -902,8 +996,8 @@
         wide = N_HEADS * HEAD_DIM
         me = lax.axis_index("cp")
         _, y, x, core = place(me)
-        quad, pair = me % 4, me // 4
-        relations = range(4)
+        quad, pair = me % FOUR, me // FOUR
+        relations = range(FOUR)
 
         def rows_of(arr, d):
             return pick(arr.reshape((TWO, TWO, TWO, CHUNK) + arr.shape[TWO:]), core ^ (d % TWO), 0)
@@ -913,7 +1007,7 @@
 
         def unite(arr):
             joined = jnp.stack(swap([rows_of(arr, d) for d in relations]), axis=TWO)
-            return joined.reshape((TWO, TWO, BLK) + joined.shape[4:])
+            return joined.reshape((TWO, TWO, BLK) + joined.shape[FOUR:])
 
         gain = norm_gain.astype(F32)
         cos_t, sin_t = rope_tables(positions.reshape(n_rows))
@@ -922,15 +1016,13 @@
         pos_u = unite(positions)
         kv_all, q_u, dy_part = exchange(
             kv_home.reshape((TWO,) * 5 + (CHUNK, HEAD_DIM)),
-            q_home.reshape((TWO,) * 4 + (CHUNK, wide)),
+            q_home.reshape((TWO,) * FOUR + (CHUNK, wide)),
             grad_out.reshape((TWO,) * 3 + (CHUNK, d_model)),
         )
         dy_last, dy_part = lax.optimization_barrier((rows_of(grad_out, LATER[1]), dy_part))
         dy_last = perm(dy_last, flip_pairs(LATER[1]))
-        normed_home, dy_part = lax.optimization_barrier((normed.reshape(hidden.shape), dy_part))
-        normed_u = unite(normed_home)
-
-        member = quad ^ jnp.arange(4)
+
+        member = quad ^ jnp.arange(FOUR)
         front, back = ((m[:, NEW] * CHUNK + jnp.arange(CHUNK)[NEW]).reshape(BLK) for m in (member, 3 - member))
         offsets = jnp.stack([front, back]).astype(jnp.int32)
         own_super = jnp.stack([pair, N_SUPER - 1 - pair]).astype(jnp.int32)
@@ -954,40 +1046,36 @@
         dy_u = jnp.concatenate([dy_part, dy_last], axis=TWO)
         wo_send = dot(dyn(attn_u, (1 - core) * half_wide, half_wide, 3), dy_u, tok, tok)
         wo_sum = dot(dyn(attn_u, core * half_wide, half_wide, 3), dy_u, tok, tok) + perm(wo_send, flip_pairs(1))
-        wo_sum = wo_sum.reshape(4, TWO, half_wide // N_PAIRS, d_model)
-        wo_y = perm(pick(wo_sum, 1 - y, 1), flip_pairs(4))
+        wo_sum = wo_sum.reshape(FOUR, TWO, half_wide // N_PAIRS, d_model)
+        wo_y = perm(pick(wo_sum, 1 - y, 1), flip_pairs(FOUR))
 
         d_attn = dot(dy_u, dyn(w_o, x * wide, wide, 0), (3,), (1,)).astype(BF16)
         d_attn, wo_sum = lax.optimization_barrier((d_attn, wo_sum))
         dq_u, dkv = flash_bwd(tab, q_u, d_attn, attn_u, kv_all, lse, start_r, q_index_r, koff, cos_ut, sin_ut)
 
         wo_sum = pick(wo_sum, y, 1) + wo_y
-        half_model = d_model // TWO
-
-        def by_core(d_out):
-            part = lax.optimization_barrier(dot(normed_u, d_out, tok, tok))
-            return part.reshape(TWO, 4, TWO, half_model // N_PAIRS, -1)
 
         x_flat = hidden.reshape(n_rows, d_model)
-        wo_own, dkv_own, wq_own, block_out, d_part = reduce_pairs(
-            [wo_sum, dkv.reshape(4, TWO, -1, HEAD_DIM), by_core(dq_u)],
-            (TWO, 8, 4),
+        wo_own, dkv_own, wq_own, block_out, d_part, h_u = reduce_pairs(
+            [wo_sum, dkv.reshape(FOUR, TWO, -1, HEAD_DIM)],
+            [wo_sum.shape[1:], (dkv.size // N_PAIRS // HEAD_DIM, HEAD_DIM), (d_model // TWO // N_PAIRS, wide)],
+            (TWO, 8, FOUR),
             ("z", "", "core"),
             TWO,
             Products,
-            (attn_u, dq_u, x_flat, w_o, w_q),
+            (attn_u, dq_u, x_flat, normed.reshape((TWO,) * 3 + (CHUNK, d_model)), w_o, w_q),
         )
-        dkv_own = dkv_own.reshape((TWO,) * 3 + (BLK, HEAD_DIM))
-        dk_u = rotate(dkv_own[0] * ATTN_SCALE, cos_u, -sin_u).astype(BF16)
-        dkv_u = jnp.concatenate([dk_u, dkv_own[1].astype(BF16)], axis=-1)
-        w_kv = jnp.hstack([w[:, head_slice(i)] for i in range(TWO) for w in (w_k, w_v)])
+        cos_uf, sin_uf = jnp.concatenate([cos_u, cos_u], axis=-1), jnp.concatenate([sin_u, -sin_u], axis=-1)
         grad_wo, grad_wq, grad_wk, grad_wv, grad_x, d_gain = gather_all(
             wo_own,
             wq_own,
-            by_core(dkv_u),
-            dkv_u,
+            dkv_own,
+            cos_uf.reshape(-1, HEAD_DIM),
+            sin_uf.reshape(-1, HEAD_DIM),
+            h_u,
             d_part,
-            w_kv,
+            w_k,
+            w_v,
             x_flat,
             grad_out.reshape(n_rows, d_model),
             gain[NEW],

time: 665 us -> 606 us (0.911)
  waiting for transfers between devices: 53.8 us -> 18.3 us
  Pallas kernels: 502 us -> 494 us
  local copies, waits for them, and re-layouts: 55.3 us -> 48.5 us
    ppermute x9 -> x6, waiting for transfers between devices: 53.8 us -> 18.3 us  [perm(): return lax.ppermute(x, 'cp', pairs)]
    pallas_call x1, Pallas kernels: 219 us -> 207 us  [reduce_pairs(): pl.pallas_call(functools.partial(reduce_kernel, cuts, kinds, work), name=...]
    dot_general x5 -> x3, matrix products: 21.1 us -> 15 us  [dot(): lax.dot_general(a, b, ((ca, cb), ((), ())), preferred_element_type=F32)]
    unnamed x66 -> x60, local copies, waits for them, and re-layouts: 40.5 us -> 42 us
  transfers between devices with their start and end apart: 9 -> 6, of which waited for: 2 -> 1; matrix products, arithmetic and copies ran while one was open for 6% -> 4% of each run, Pallas kernels for 17% -> 19%
where the time goes in v5:
time: 606 us; the launch traced here: 596 us
  Pallas kernels  494 us (82%)
  local copies, waits for them, and re-layouts  48.5 us (8%)
  waiting for transfers between devices  18.3 us (3%)
  matrix products  15 us (2%)
  other arithmetic  12.3 us (2%)
  starting transfers between devices  6.44 us (1%)
    pallas_call x1, Pallas kernels, reduce_pairs(): pl.pallas_call(functools.partial(reduce_kernel, cuts, kinds, work), name=...  207 us
    pallas_call x1, Pallas kernels, gather_all(): pl.pallas_call(gather_kernel, name='gather_all', out_shape=[jax.ShapeDtyp...  176 us
    pallas_call x1, Pallas kernels, exchange(): pl.pallas_call(exchange_kernel, name='exchange', out_shape=(jax.ShapeDtyp...  60.2 us
    unnamed x60, local copies, waits for them, and re-layouts  42 us
    pallas_call x1, Pallas kernels, flash_bwd(): pl.pallas_call(bwd_kernel, name='attn_bwd', out_shape=(jax.ShapeDtypeStru...  26.9 us
    ppermute x6, waiting for transfers between devices, perm(): return lax.ppermute(x, 'cp', pairs)  18.3 us
    pallas_call x1, Pallas kernels, flash_fwd(): pl.pallas_call(fwd_kernel, name='attn_fwd', out_shape=(jax.ShapeDtypeStru...  15.5 us
    dot_general x3, matrix products, dot(): lax.dot_general(a, b, ((ca, cb), ((), ())), preferred_element_type=F32)  15 us
  transfers between devices with their start and end apart: 6, of which 1 were waited for; matrix products, arithmetic and copies ran while one was open for 4% of the time, Pallas kernels for 19%

profile of v5, /device:TPU:0, one launch (start us, length us, event | category | flops | bytes accessed | tf_op | source)
XLA Modules:
  0.0 596.3 jit_solution(13526910982316314311)
XLA Ops:
  1.6 2.4 collective-permute-start.3
  6.1 2.3 dynamic-slice_bitcast_fusion.1
  9.6 1.4 copy-done.7
  11.0 1.8 norm_kv.1
  13.6 6.8 %query.1 = bf16[2,2,256,1024]{3,2,1,0:T(8,128)(2,1)S(1)} custom-call(bf16[512,2048]{1,0:T(8,128)(2,1)S(1)} %get-tuple-element.33.h_ref, bf16[2048,2048]{1,0:T(8,128)(2,1)S(1)} %copy-done, f32[512,128]{1,0:T(8,128)S(1)} %get-tuple-element.75.cos_ref, f32[512,128]{1,0:T(8,128)S(1)} %get-tuple-element.76.sin_ref), custom_call_target="tpu_custom_call" | custom-call | flops 5000000000 | bytes 12582912 | tf_op jit(solution)/shard_map/query/pallas_call | solution.py:280
  21.8 60.2 %exchange.1 = (bf16[8,2,2,2,256,128]{5,4,3,2,1,0:T(8,128)(2,1)}, bf16[2,2,256,1024]{3,2,1,0:T(8,128)(2,1)}, bf16[2,2,192,2048]{3,2,1,0:T(8,128)(2,1)}) custom-call(bf16[2,2,2,2,2,64,128]{6,5,4,3,2,1,0:T(8,128)(2,1)} %bitcast.56, bf16[2,2,2,2,64,1024]{5,4,3,2,1,0:T(8,128)(2,1)} %bitcast.55, bf16[2,2,2,64,2048]{4,3,2,1,0:T(8,128)(2,1)} %bitcast.64), custom_call_target="tpu_custom_call" | custom-call | flops 1000000000 | bytes 20971520 | tf_op jit(solution)/shard_map/exchange/pallas_call | solution.py:400
  82.0 1.9 collective-permute-start
  84.4 4.0 constant_dynamic-update-slice_fusion.1
  89.5 2.2 copy-done.10
  91.7 1.6 copy-done.11
  93.3 15.5 %attn_fwd.1 = (bf16[2,2,256,1024]{3,2,1,0:T(8,128)(2,1)S(1)}, f32[2,2,8,1,256]{4,3,2,1,0:T(1,128)S(1)}) custom-call(s32[10]{0:T(128)S(1)} %pad_add_fusion.2.tab, bf16[2,2,256,1024]{3,2,1,0:T(8,128)(2,1)S(1)} %copy-done.11, bf16[8,2,2,2,256,128]{5,4,3,2,1,0:T(8,128)(2,1)S(1)} %copy-done.10, s32[2,2,256,128]{3,2,1,0:T(8,128)S(1)} %broadcast_in_dim.14.st_ref, ...), custom_call_target="tpu_custom_call" | custom-call | flops 20000000000 | bytes 16777216 | tf_op jit(solution)/shard_map/attn_fwd/pallas_call | solution.py:205
  108.8 2.1 constant_dynamic-update-slice_fusion
  110.9 4.4 convolution_bitcast_fusion
  115.5 1.9 multiply_sine_fusion
  117.4 1.3 pad_maximum_fusion
  119.7 2.4 fusion.7
  122.2 8.2 %fusion.3.do_ref = bf16[2,2,256,1024]{3,2,1,0:T(8,128)(2,1)} fusion(bf16[2,2,256,2048]{3,2,1,0:T(8,128)(2,1)S(1)} %copy-done.15, bf16[2048,2048]{1,0:T(8,128)(2,1)} %refs_6_.1, s32[]{:T(128)S(6)} %select_n.50), kind=kOutput, calls=%fused_computation.7 | convolution fusion | flops 4296015872 | bytes 10485764 | tf_op jit(solution)/shard_map/dot_general | solution.py:45
  130.3 3.1 bitcast_add_fusion
  133.6 1.4 collective-permute-start.5
  135.1 26.9 %attn_bwd.1 = (bf16[2,2,256,1024]{3,2,1,0:T(8,128)(2,1)S(1)}, f32[8,2,2,2,256,128]{5,4,3,2,1,0:T(8,128)}) custom-call(s32[10]{0:T(128)S(1)} %pad_add_fusion.2.tab, bf16[2,2,256,1024]{3,2,1,0:T(8,128)(2,1)S(1)} %copy-done.12, bf16[2,2,256,1024]{3,2,1,0:T(8,128)(2,1)} %fusion.3.do_ref, bf16[2,2,256,1024]{3,2,1,0:T(8,128)(2,1)} %copy-done.1, ...), custom_call_target="tpu_custom_call" | custom-call | flops 49999998976 | bytes 33554432 | tf_op jit(solution)/shard_map/attn_bwd/pallas_call | solution.py:224
  162.0 1.3 copy-done.4
  163.4 18.3 %collective-permute-done.5 = f32[4,64,2048]{2,1,0:T(8,128)S(1)} collective-permute-done((f32[4,64,2048]{2,1,0:T(8,128)S(1)}, f32[4,64,2048]{2,1,0:T(8,128)S(1)}, u32[]{:S(2)}, u32[]{:S(2)}) %collective-permute-start.5) | collective-permute-done | bytes 2097184 | tf_op jit(solution)/shard_map/ppermute | solution.py:985
  181.7 1.6 bitcast_add_fusion.1.refs_0_
  183.3 206.9 %reduce_pairs.1 = (f32[64,2048]{1,0:T(8,128)}, f32[2048,128]{1,0:T(8,128)}, f32[128,1024]{1,0:T(8,128)}, bf16[512,2048]{1,0:T(8,128)(2,1)}, f32[512,2048]{1,0:T(8,128)}, /*index=5*/bf16[2,2,256,2048]{3,2,1,0:T(8,128)(2,1)}) custom-call(f32[4,64,2048]{2,1,0:T(8,128)} %bitcast_add_fusion.1.refs_0_, f32[4,2,2048,128]{3,2,1,0:T(8,128)} %bitcast.66, ...), custom_call_target="tpu_custom_call" | custom-call | flops 1000000000 | bytes 20971520 | tf_op jit(solution)/shard_map/reduce_pairs/pallas_call | solution.py:765
  390.2 176.3 %gather_all.1 = (f32[2048,2048]{1,0:T(8,128)}, f32[2048,2048]{1,0:T(8,128)}, f32[2048,256]{1,0:T(8,128)}, f32[2048,256]{1,0:T(8,128)}, bf16[512,2048]{1,0:T(8,128)(2,1)}, /*index=5*/f32[1,2048]{1,0:T(1,128)}) custom-call(f32[64,2048]{1,0:T(8,128)} %get-tuple-element.46.refs_0_, f32[128,1024]{1,0:T(8,128)} %get-tuple-element.47.refs_1_, ...), custom_call_target="tpu_custom_call" | custom-call | flops 1000000000 | bytes 79691776 | tf_op jit(solution)/shard_map/gather_all/pallas_call | solution.py:971
  566.5 1.3 copy.36
  568.9 1.3 copy.37
  570.2 14.6 %copy.38 = f32[2048,2048]{1,0:T(8,128)} copy(f32[2048,2048]{1,0:T(8,128)} %get-tuple-element.90) | data formatting | bytes 33554432
  584.8 1.3 copy.39
  586.1 1.8 copy-done.17
  587.9 1.3 copy.40
  589.3 6.2 %copy.41 = f32[2048,2048]{1,0:T(8,128)} copy(f32[2048,2048]{1,0:T(8,128)S(1)} %bitcast.62) | data formatting | bytes 33554432
  (92 shorter events, 11.0 us)
Async XLA Ops:
  0.6 9.0 %copy-start.6 = (bf16[2048,256]{1,0:T(8,128)(2,1)S(1)}, bf16[2048,256]{1,0:T(8,128)(2,1)}, u32[]{:S(2)}) copy-start(bf16[2048,256]{1,0:T(8,128)(2,1)} %refs_7_.3) | copy-start | bytes 3145732
  0.6 9.0 %copy-start.2 = (bf16[4,128,2048]{2,1,0:T(8,128)(2,1)S(1)}, bf16[4,128,2048]{2,1,0:T(8,128)(2,1)}, u32[]{:S(2)}) copy-start(bf16[4,128,2048]{2,1,0:T(8,128)(2,1)} %param.9) | copy-start | bytes 6291460
  1.6 87.0 %collective-permute-start.3 = (s32[2,2,64]{2,1,0:T(2,128)S(1)}, s32[2,2,64]{2,1,0:T(2,128)S(1)}, u32[]{:S(2)}, u32[]{:S(2)}) collective-permute-start(s32[2,2,64]{2,1,0:T(2,128)S(1)} %get-tuple-element.69), channel_id=1, source_target_pairs={{0,3},{1,2},{2,1},{3,0},{4,7},{5,6},{6,5},{7,4},{8,11},{9,10},{10,... | collective-permute-start | bytes 3080 | tf_op jit(solution)/shard_map/ppermute | solution.py:985
  4.0 84.6 %collective-permute-start.1 = (s32[2,2,64]{2,1,0:T(2,128)S(1)}, s32[2,2,64]{2,1,0:T(2,128)S(1)}, u32[]{:S(2)}, u32[]{:S(2)}) collective-permute-start(s32[2,2,64]{2,1,0:T(2,128)S(1)} %get-tuple-element.69), channel_id=1, source_target_pairs={{0,1},{1,0},{2,3},{3,2},{4,5},{5,4},{6,7},{7,6},{8,9},{9,8},{10,11... | collective-permute-start | bytes 3080 | tf_op jit(solution)/shard_map/ppermute | solution.py:985
  4.7 83.9 %collective-permute-start.2 = (s32[2,2,64]{2,1,0:T(2,128)S(1)}, s32[2,2,64]{2,1,0:T(2,128)S(1)}, u32[]{:S(2)}, u32[]{:S(2)}) collective-permute-start(s32[2,2,64]{2,1,0:T(2,128)S(1)} %bitcast.70), channel_id=1, source_target_pairs={{0,2},{1,3},{2,0},{3,1},{4,6},{5,7},{6,4},{7,5},{8,10},{9,11},{10,... | collective-permute-start | bytes 3080 | tf_op jit(solution)/shard_map/ppermute | solution.py:985
  6.1 6.8 %copy-start.9 = (f32[2048]{0:T(1024)}, f32[2048]{0:T(1024)S(1)}, u32[]{:S(2)}) copy-start(f32[2048]{0:T(1024)S(1)} %broadcast_in_dim.18) | copy-start | bytes 24580
  9.4 4.3 copy-start
  9.6 1.4 copy-start.7
  12.8 0.8 copy-start.8
  13.6 6.8 %copy-start.3 = (bf16[512,2048]{1,0:T(8,128)(2,1)}, bf16[512,2048]{1,0:T(8,128)(2,1)S(1)}, u32[]{:S(2)}) copy-start(bf16[512,2048]{1,0:T(8,128)(2,1)S(1)} %get-tuple-element.33.h_ref) | copy-start | bytes 6291460
  20.5 1.3 copy-start.5
  21.8 60.2 %copy-start.20 = (bf16[2,2,64,2048]{3,2,1,0:T(8,128)(2,1)S(1)}, bf16[2,2,64,2048]{3,2,1,0:T(8,128)(2,1)}, u32[]{:S(2)}) copy-start(bf16[2,2,64,2048]{3,2,1,0:T(8,128)(2,1)} %dynamic-slice_bitcast_fusion.1) | copy-start | bytes 3145732
  82.0 26.8 %collective-permute-start = (bf16[2,2,64,2048]{3,2,1,0:T(8,128)(2,1)S(1)}, bf16[2,2,64,2048]{3,2,1,0:T(8,128)(2,1)}, u32[]{:S(2)}, u32[]{:S(2)}) collective-permute-start(bf16[2,2,64,2048]{3,2,1,0:T(8,128)(2,1)S(1)} %copy-done.20), channel_id=1, source_target_pairs={{0,3},{1,2},{2,1},{3,0},{4,7},{5,6},{6,5},{7,4},{8,11},{9,10},{10,... | collective-permute-start | bytes 3145736 | tf_op jit(solution)/shard_map/ppermute | solution.py:985
  89.5 2.2 copy-start.10
  91.7 1.6 copy-start.11
  93.3 15.5 %copy-start.13 = (bf16[2,2,256,2048]{3,2,1,0:T(8,128)(2,1)S(1)}, bf16[2,2,256,2048]{3,2,1,0:T(8,128)(2,1)}, u32[]{:S(2)}) copy-start(bf16[2,2,256,2048]{3,2,1,0:T(8,128)(2,1)} %constant_dynamic-update-slice_fusion.1) | copy-start | bytes 12582916
  108.8 10.9 %copy-start.1 = (bf16[2,2,256,1024]{3,2,1,0:T(8,128)(2,1)}, bf16[2,2,256,1024]{3,2,1,0:T(8,128)(2,1)S(1)}, u32[]{:S(2)}) copy-start(bf16[2,2,256,1024]{3,2,1,0:T(8,128)(2,1)S(1)} %get-tuple-element.39.o_ref.refs_2_) | copy-start | bytes 6291460
  110.9 4.4 copy-start.14
  115.3 15.0 %collective-permute-start.4 = (f32[512,2048]{1,0:T(8,128)}, f32[512,2048]{1,0:T(8,128)}, u32[]{:S(2)}, u32[]{:S(2)}) collective-permute-start(f32[512,2048]{1,0:T(8,128)} %convolution_bitcast_fusion), channel_id=1, source_target_pairs={{0,1},{1,0},{2,3},{3,2},{4,5},{5,4},{6,7},{7,6},{8,9},{9,8},{10,11... | collective-permute-start | bytes 12582920 | tf_op jit(solution)/shard_map/ppermute | solution.py:985
  115.5 4.2 copy-start.15
  133.4 1.7 copy-start.12
  133.6 48.1 %collective-permute-start.5 = (f32[4,64,2048]{2,1,0:T(8,128)S(1)}, f32[4,64,2048]{2,1,0:T(8,128)S(1)}, u32[]{:S(2)}, u32[]{:S(2)}) collective-permute-start(f32[4,64,2048]{2,1,0:T(8,128)S(1)} %dynamic-slice_bitcast_fusion), channel_id=1, source_target_pairs={{0,4},{1,5},{2,6},{3,7},{4,0},{5,1},{6,2},{7,3},{8,12},{9,13},{10,... | collective-permute-start | bytes 6291464 | tf_op jit(solution)/shard_map/ppermute | solution.py:985
  162.0 1.3 copy-start.4
  390.2 176.3 %copy-start.16 = (bf16[512,2048]{1,0:T(8,128)(2,1)S(1)}, bf16[512,2048]{1,0:T(8,128)(2,1)}, u32[]{:S(2)}) copy-start(bf16[512,2048]{1,0:T(8,128)(2,1)} %get-tuple-element.45) | copy-start | bytes 6291460
  566.5 2.3 copy-start.19
  568.9 20.4 %slice-start = ((s8[16777216]{0:T(1024)(128)(4,1)}), s8[4194304]{0:T(1024)(128)(4,1)S(1)}, s32[]{:S(2)}) async-start(s8[16777216]{0:T(1024)(128)(4,1)} %bitcast.61), calls=%async_computation | async-start | bytes 8388608
  570.2 14.6 %copy-start.18 = (f32[2048,256]{1,0:T(8,128)S(1)}, f32[2048,256]{1,0:T(8,128)}, u32[]{:S(2)}) copy-start(f32[2048,256]{1,0:T(8,128)} %get-tuple-element.91) | copy-start | bytes 6291460
  570.2 19.0 %slice-start.1 = ((s8[16777216]{0:T(1024)(128)(4,1)}), s8[4194304]{0:T(1024)(128)(4,1)S(1)}, s32[]{:S(2)}) async-start(s8[16777216]{0:T(1024)(128)(4,1)} %bitcast.61), calls=%async_computation.1 | async-start | bytes 8388608
  570.2 19.0 %slice-start.2 = ((s8[16777216]{0:T(1024)(128)(4,1)}), s8[4194304]{0:T(1024)(128)(4,1)S(1)}, s32[]{:S(2)}) async-start(s8[16777216]{0:T(1024)(128)(4,1)} %bitcast.61), calls=%async_computation.2 | async-start | bytes 8388608
  570.2 19.0 %slice-start.3 = ((s8[16777216]{0:T(1024)(128)(4,1)}), s8[4194304]{0:T(1024)(128)(4,1)S(1)}, s32[]{:S(2)}) async-start(s8[16777216]{0:T(1024)(128)(4,1)} %bitcast.61), calls=%async_computation.3 | async-start | bytes 8388608
  584.8 3.1 copy-start.17
  589.2 6.2 %copy-start.21 = (f32[1,2048]{1,0:T(1,128)S(1)}, f32[1,2048]{1,0:T(1,128)}, u32[]{:S(2)}) copy-start(f32[1,2048]{1,0:T(1,128)} %get-tuple-element.56) | copy-start | bytes 24580

commit v6 on v5

--- a/solution.py
+++ b/solution.py
@@ -26,7 +26,6 @@
 N_SUPER = 2 * N_PAIRS
 MESH = pl.DeviceIdType.MESH
 ONE = pl.Squeezed()
-LATER = 2, 3
 MADE_AT = 5
 PRODUCTS_AT = 7, 9
 F32 = jnp.float32
@@ -67,10 +66,6 @@
 
 def dot_t(a, b):
     return dot(a, b, (1,), (1,))
-
-
-def dyn(x, index, size, axis):
-    return lax.dynamic_slice_in_dim(x, index, size, axis)
 
 
 def pick(x, index, axis):
@@ -92,14 +87,20 @@
     lax.fori_loop(first, own + 1, step, 0)
 
 
+def down(row, n):
+    return jnp.broadcast_to(row, (n, row.shape[-1])).T
+
+
 def may_use(s, off, st_ref, qi_ref):
     return jnp.logical_and(off >= st_ref[...] - s * BLK, off <= qi_ref[...] - s * BLK)
 
 
-def fwd_kernel(tab, q_ref, kv_ref, st_ref, qi_ref, ko_ref, o_ref, lse_ref, q_s, acc, m_s, l_s, k_t):
+def fwd_kernel(tab, q_ref, kv_ref, st_ref, qi_ref, ko_ref, o_ref, lse_ref, q_s, acc, m_s, l_s, k_t, bounds):
     m_s[...] = jnp.full_like(m_s, NEG_BIG)
     l_s[...] = jnp.zeros_like(l_s)
     acc[...] = jnp.zeros_like(acc)
+    for i, ref in enumerate((st_ref, qi_ref)):
+        bounds[i] = down(ref[...], HEAD_DIM)
     for h in range(N_HEADS):
         q_s[pl.ds(h * BLK, BLK)] = q_ref[:, head(h)]
 
@@ -116,7 +117,7 @@
         if masked:
             off = ko_ref[hk] + s * BLK
             mask = [
-                jnp.logical_and(off[:, lanes] >= st_ref[...], off[:, lanes] <= qi_ref[...])
+                jnp.logical_and(off[:, lanes] >= bounds[0], off[:, lanes] <= bounds[1])
                 for lanes in (slice(HEAD_DIM), slice(HEAD_DIM, BLK))
             ]
             mask = [jnp.concatenate([m, m], axis=0) for m in mask]
@@ -143,7 +144,7 @@
         lse_ref[h] = (m_s[rows] * EXP2_SCALE + jnp.log2(total)).T[:1]
 
 
-def bwd_kernel(tab, q_ref, do_ref, o_ref, kv_ref, lse_ref, st_ref, qi_ref, ko_ref, cos_ref, sin_ref, dq_ref, dkv_ref, dq_acc, delta):
+def bwd_kernel(tab, q_ref, do_ref, o_ref, kv_ref, lse_ref, st_ref, qi_ref, ko_ref, cos_ref, sin_ref, dq_ref, dkv_ref, dq_acc, delta, off_s):
     dq_acc[...] = jnp.zeros_like(dq_acc)
     for h in range(N_HEADS):
         terms = do_ref[:, head(h)].astype(F32) * o_ref[:, head(h)].astype(F32)
@@ -152,13 +153,15 @@
     @pl.when(pl.program_id(1) == 0)
     def _():
         dkv_ref[...] = jnp.zeros_like(dkv_ref)
+        for hk in range(TWO):
+            off_s[hk] = down(ko_ref[hk], BLK)
 
     def body(s, at, masked):
         pair, hk = at
         k = kv_ref[pair, 0, hk]
         v = kv_ref[pair, 1, hk]
         k_t = k.T
-        mask = may_use(s, ko_ref[hk], st_ref, qi_ref) if masked else None
+        mask = may_use(s, off_s[hk], st_ref, qi_ref) if masked else None
         dk = dv = jnp.zeros((BLK, HEAD_DIM), F32)
         for h in range(N_HEADS):
             q = q_ref[:, head(h)]
@@ -194,14 +197,12 @@
     stat = pl.BlockSpec((ONE, ONE, N_HEADS, 1, BLK), lambda b, h, t: (b, h) + (0,) * 3)
     rope = pl.BlockSpec((ONE, ONE, HEAD_DIM // TWO, BLK), at_tile)
     kv = pl.BlockSpec((N_PAIRS, TWO, ONE, TWO, BLK, HEAD_DIM), at_row)
-    ko = pl.BlockSpec((TWO, BLK, BLK), lambda b, h, t: (0,) * 3)
+    ko = pl.BlockSpec((TWO, 1, BLK), lambda b, h, t: (0,) * 3)
     return tile, row, stat, kv, ko, rope
 
 
 def flash_fwd(tab, q, kv, start, qidx, koff):
-    tile, _, stat, kvs, *_ = attn_specs()
-    col = pl.BlockSpec((ONE, ONE, BLK, HEAD_DIM), lambda b, h, t: (b, h) + (0,) * TWO)
-    ko = pl.BlockSpec((TWO, 1, BLK), lambda b, h, t: (0,) * 3)
+    tile, row, stat, kvs, ko, _ = attn_specs()
     return pl.pallas_call(
         fwd_kernel,
         name="attn_fwd",
@@ -209,10 +210,10 @@
         grid_spec=pltpu.PrefetchScalarGridSpec(
             num_scalar_prefetch=1,
             grid=(TWO, TWO),
-            in_specs=[tile, kvs, col, col, ko],
+            in_specs=[tile, kvs, row, row, ko],
             out_specs=[tile, stat],
             scratch_shapes=[pltpu.VMEM((N_HEADS * BLK, HEAD_DIM), t) for t in (BF16, F32, F32, F32)]
-            + [pltpu.VMEM((N_PAIRS, TWO, HEAD_DIM, BLK), BF16)],
+            + [pltpu.VMEM((N_PAIRS, TWO, HEAD_DIM, BLK), BF16), pltpu.VMEM((TWO, BLK, HEAD_DIM), jnp.int32)],
         ),
         compiler_params=params(40),
         cost_estimate=cost(20, 16),
@@ -233,7 +234,8 @@
             grid=(TWO, TWO),
             in_specs=[tile, tile, tile, kvs, stat, row, row, ko, rope, rope],
             out_specs=[tile, kvs],
-            scratch_shapes=[pltpu.VMEM((N_HEADS, HEAD_DIM, BLK), F32), pltpu.VMEM((N_HEADS, 1, BLK), F32)],
+            scratch_shapes=[pltpu.VMEM((N_HEADS, HEAD_DIM, BLK), F32), pltpu.VMEM((N_HEADS, 1, BLK), F32)]
+            + [pltpu.VMEM((TWO, BLK, BLK), jnp.int32)],
         ),
         compiler_params=params(48),
         cost_estimate=cost(50, 32),
@@ -257,37 +259,15 @@
                 kv_ref[i, c, j] = val[c * n : (c + 1) * n].astype(BF16)
 
 
-def query_kernel(h_ref, w_ref, cos_ref, sin_ref, q_ref):
-    q = jnp.dot(h_ref[...], w_ref[...], preferred_element_type=F32)
-    n = q_ref.shape[TWO]
-    for j in range(q.shape[1] // HEAD_DIM):
-        val = turn(q[:, head_slice(j)], cos_ref, sin_ref).astype(BF16)
-        for c in range(TWO):
-            q_ref[0, c, :, head(j)] = val[c * n : (c + 1) * n]
-
-
-def project(x, gain, w_q, w_k, w_v, cos_f, sin_f):
-    n, d = x.shape
-    h, kv = pl.pallas_call(
+def project(x, gain, w_k, w_v, cos_f, sin_f):
+    n = x.shape[0] // TWO
+    return pl.pallas_call(
         first_kernel,
         name="norm_kv",
-        out_shape=(jax.ShapeDtypeStruct(x.shape, BF16), jax.ShapeDtypeStruct((TWO,) * 3 + (n // TWO, HEAD_DIM), BF16)),
+        out_shape=(jax.ShapeDtypeStruct(x.shape, BF16), jax.ShapeDtypeStruct((TWO,) * 3 + (n, HEAD_DIM), BF16)),
         compiler_params=params(40),
         cost_estimate=cost(TWO, 7),
     )(x, gain, w_k, w_v, cos_f, sin_f)
-    tile = FOUR * HEAD_DIM
-    rope = pl.BlockSpec(cos_f.shape, lambda j: (0, 0))
-    q = pl.pallas_call(
-        query_kernel,
-        name="query",
-        grid=(d // tile,),
-        out_shape=jax.ShapeDtypeStruct((TWO, TWO, n // TWO, d // TWO), BF16),
-        in_specs=[pl.BlockSpec(h.shape, lambda j: (0, 0)), pl.BlockSpec((d, tile), lambda j: (0, j)), rope, rope],
-        out_specs=pl.BlockSpec((1, TWO, n // TWO, tile), lambda j: (j // TWO, 0, 0, j % TWO)),
-        compiler_params=params(40),
-        cost_estimate=cost(5, 12),
-    )(h, w_q, cos_f, sin_f)
-    return h, kv, q
 
 
 def place(me):
@@ -332,7 +312,29 @@
                 yield d, self.inside[d] if dz == 0 else jnp.logical_and(self.inside[d], self.held(dz))
 
 
-def exchange_kernel(kv_ref, q_ref, dy_ref, kv_all, q_u, dy_u, own_sem, quad_s, quad_r, z_s, z_r, y_s, y_r):
+def tiled(n, fetch, use, first=0):
+    fetch(first, 0).start()
+
+    @pl.loop(0, n)
+    def _(t):
+        slot = lax.rem(t, TWO)
+        fetch(first + t, slot).wait()
+
+        @pl.when(t + 1 < n)
+        def _():
+            fetch(first + t + 1, 1 - slot).start()
+
+        use(first + t, slot)
+
+
+def aligned(t, size=BLK):
+    return pl.ds(pl.multiple_of(t * size, size), size)
+
+
+def exchange_kernel(*refs):
+    take = taker(refs)
+    kv_ref, h_ref, dy_ref, cos_ref, sin_ref, wq_ref, wo_ref, kv_all, q_u, do_u = take(10)
+    own_sem, quad_s, quad_r, z_s, z_r, y_s, y_r, q_home, do_home, wq_buf, wo_buf, w_sem = take(len(refs))
     me = lax.axis_index("cp")
     z, y, x, core = place(me)
     quad, line = quad_of(me), Line(me)
@@ -341,26 +343,17 @@
 
     def source(a, d):
         xx, cc = 1 - x if d // TWO else x, 1 - core if d % TWO else core
-        return dy_ref.at[cc] if a == TWO else (kv_ref, q_ref)[a].at[xx, cc]
+        return (kv_ref, q_home, do_home)[a].at[xx, cc]
 
     def target(a, d):
         tok = pl.ds(d * CHUNK, CHUNK)
-        return kv_all.at[me // FOUR, :, :, :, tok] if a == 0 else (q_u, dy_u)[a - 1].at[:, :, tok]
+        return kv_all.at[me // FOUR, :, :, :, tok] if a == 0 else (q_u, do_u)[a - 1].at[:, :, tok]
 
     def quad_copy(a, d):
         return remote(source(a, d), target(a, d), quad_s.at[a, d], quad_r.at[a, d], quad[d])
 
     def own_copy(a):
         return pltpu.make_async_copy(source(a, 0), target(a, 0), own_sem.at[a])
-
-    sent = [(a, d) for a in range(3) for d in (1, TWO, 3) if (a, d) != LATER]
-    for a, d in sent:
-        quad_copy(a, d).start()
-    for a in range(3):
-        own_copy(a).start()
-    own_copy(0).wait()
-    for d in (1, TWO, 3):
-        quad_copy(0, d).wait_recv()
 
     def z_copy(part, dz, d):
         block = kv_all.at[TWO * (z + dz) + y, part]
@@ -372,45 +365,146 @@
 
     parts = range(TWO)
     moves = [(part, dz) for dz in line.order for part in parts]
-    for part, dz in moves:
-        if dz:
-            block = kv_all.at[TWO * (z + dz) + y, part]
-            arrival = remote(block, block, own_sem.at[0], z_r.at[part, dz + 3], me)
-            pl.when(line.held(dz))(arrival.wait_recv)
-        for d, on in line.ways(dz):
-            pl.when(on)(z_copy(part, dz, d).start)
-        pl.when(line.held(dz))(y_copy(part, dz).start)
-    for part, dz in moves:
+
+    def pass_on(count):
+        for part, dz in [moves.pop(0) for _ in range(count)]:
+            if dz:
+                block = kv_all.at[TWO * (z + dz) + y, part]
+                arrival = remote(block, block, own_sem.at[0], z_r.at[part, dz + 3], me)
+                pl.when(line.held(dz))(arrival.wait_recv)
+            for d, on in line.ways(dz):
+                pl.when(on)(z_copy(part, dz, d).start)
+            pl.when(line.held(dz))(y_copy(part, dz).start)
+
+    n = h_ref.shape[1] // BLK // TWO
+
+    def fetch_q(t, slot):
+        return pltpu.make_async_copy(wq_ref.at[:, aligned(t)], wq_buf.at[slot], w_sem.at[0, slot])
+
+    def fetch_o(t, slot):
+        return pltpu.make_async_copy(wo_ref.at[aligned(t)], wo_buf.at[slot], w_sem.at[1, slot])
+
+    def put(home, t, val):
+        home[t // n, :, :, :, :, aligned(lax.rem(t, n))] = val.astype(BF16).reshape(home.shape[1:-1] + (BLK,))
+
+    def query(t, slot):
+        q = jnp.dot(h_ref[...], wq_buf[slot], preferred_element_type=F32)
+        put(q_home, t, jnp.hstack([turn(q[:, head_slice(j)], cos_ref, sin_ref) for j in range(BLK // HEAD_DIM)]))
+
+    def pull(t, slot):
+        put(do_home, t, dot_t(dy_ref[...], wo_buf[slot]))
+
+    all_moves = list(moves)
+    for d in (1, TWO, 3):
+        quad_copy(0, d).start()
+    own_copy(0).start()
+    for a, (fetch, use) in enumerate(((fetch_q, query), (fetch_o, pull)), 1):
+        for near in range(TWO):
+            tiled(n, fetch, use, n * (x if near else 1 - x))
+            for d in range(TWO):
+                if d or not near:
+                    quad_copy(a, d if near else d + TWO).start()
+            if near:
+                own_copy(a).start()
+            if len(moves) == len(all_moves):
+                own_copy(0).wait()
+                for d in (1, TWO, 3):
+                    quad_copy(0, d).wait_recv()
+            pass_on(TWO)
+    pass_on(len(moves))
+    for part, dz in all_moves:
         for d, on in line.ways(dz):
             pl.when(on)(z_copy(part, dz, d).wait_send)
         pl.when(line.held(dz))(y_copy(part, dz, 1 - y).wait_recv)
         pl.when(line.held(dz))(y_copy(part, dz).wait_send)
-    for a, d in sent:
-        quad_copy(a, d).wait_send()
-        if a > 0:
-            quad_copy(a, d).wait_recv()
+    for a in range(3):
+        for d in (1, TWO, 3):
+            quad_copy(a, d).wait_send()
+            if a > 0:
+                quad_copy(a, d).wait_recv()
     own_copy(1).wait()
     own_copy(TWO).wait()
 
 
-def exchange(kv, q, dy):
+def exchange(kv, h, dy, cos_f, sin_f, w_q, w_o):
     dma = pltpu.SemaphoreType.DMA
     vmem, hbm = pl.BlockSpec(memory_space=pltpu.VMEM), pl.BlockSpec(memory_space=pl.ANY)
-    wide = q.shape[-1]
+    wide = w_q.shape[1] // TWO
+    unit = jax.ShapeDtypeStruct((TWO, TWO, BLK, wide), BF16)
+    home = pltpu.VMEM((TWO,) * FOUR + (CHUNK, wide), BF16)
+    sems = [dma((3,))] + [dma((3, FOUR))] * TWO + [dma((TWO, TWO, 7))] + [dma((TWO, 7))] * 3
+    bufs = [pltpu.VMEM((TWO,) + b, BF16) for b in ((w_q.shape[0], BLK), (BLK, w_o.shape[1]))]
     return pl.pallas_call(
         exchange_kernel,
         name="exchange",
-        out_shape=(
-            jax.ShapeDtypeStruct((N_PAIRS,) + (TWO,) * 3 + (BLK, HEAD_DIM), BF16),
-            jax.ShapeDtypeStruct((TWO, TWO, BLK, wide), BF16),
-            jax.ShapeDtypeStruct((TWO, TWO, LATER[1] * CHUNK, TWO * wide), BF16),
-        ),
-        in_specs=[vmem] * 3,
+        out_shape=(jax.ShapeDtypeStruct((N_PAIRS,) + (TWO,) * 3 + (BLK, HEAD_DIM), BF16), unit, unit),
+        in_specs=[vmem] * 5 + [hbm] * TWO,
         out_specs=[hbm] * 3,
-        scratch_shapes=[dma((3,))] + [dma((3, FOUR))] * TWO + [dma((TWO, TWO, 7))] + [dma((TWO, 7))] * 3,
-        compiler_params=pltpu.CompilerParams(collective_id=1),
+        scratch_shapes=sems + [home, home] + bufs + [dma((TWO, TWO))],
+        compiler_params=params(40, collective_id=1),
         cost_estimate=cost(1, 20),
-    )(kv, q, dy)
+    )(kv, h, dy, cos_f, sin_f, w_q, w_o)
+
+
+def taker(refs):
+    rest = iter(refs)
+    return lambda count: list(itertools.islice(rest, count))
+
+
+def wo_kernel(*refs):
+    take = taker(refs)
+    o_ref, dy_ref, pieces = take(1) + take(1) + [take(3)]
+    keep, away, dy_u, o_t, terms, came, load_sem, core_s, core_r = take(len(refs))
+    me = lax.axis_index("cp")
+    _, y, _, core = place(me)
+    meet(quad_of(me)[1:TWO])
+    loads = [
+        pltpu.make_async_copy(src, dy_u.at[:, :, pl.ds(d * CHUNK, CHUNK)], load_sem.at[d])
+        for d, src in enumerate([dy_ref.at[core]] + pieces)
+    ]
+    for c in loads:
+        c.start()
+    for h in range(N_HEADS):
+        o_t[head(h)] = o_ref[:, :, :, head(h)].reshape(-1, HEAD_DIM).T
+    for c in loads:
+        c.wait()
+    half = terms.shape[1]
+
+    def half_terms(i, to):
+        @pl.loop(0, terms.shape[TWO] // BLK)
+        def _(t):
+            dy = dy_u[:, :, :, aligned(t)].reshape(-1, BLK)
+            terms[to, :, aligned(t)] = jnp.dot(o_t[aligned(i, half)], dy, preferred_element_type=F32)
+
+    half_terms(1 - core, 0)
+    swap = remote(terms.at[0], came, core_s, core_r, quad_of(me)[1])
+    swap.start()
+    half_terms(core, 1)
+    swap.wait_recv()
+    rows = keep.shape[1]
+    for zz in range(FOUR):
+        for out, yy in ((keep, y), (away, 1 - y)):
+            at = aligned(TWO * zz + yy, rows)
+            out[zz] = terms[1, at] + came[at]
+    swap.wait_send()
+
+
+def wo_terms(o, dy, pieces):
+    dma = pltpu.SemaphoreType.DMA
+    vmem, hbm = pl.BlockSpec(memory_space=pltpu.VMEM), pl.BlockSpec(memory_space=pl.ANY)
+    n, d, wide = o.shape[0] * o.shape[1] * o.shape[TWO], dy.shape[-1], o.shape[-1]
+    half = wide // TWO
+    return pl.pallas_call(
+        wo_kernel,
+        name="wo_terms",
+        out_shape=[jax.ShapeDtypeStruct((FOUR, half // N_PAIRS, d), F32)] * TWO,
+        in_specs=[vmem] + [hbm] * FOUR,
+        out_specs=[vmem] * TWO,
+        scratch_shapes=[pltpu.VMEM((TWO, TWO, BLK, d), BF16), pltpu.VMEM((wide, n), BF16)]
+        + [pltpu.VMEM((TWO, half, d), F32), pltpu.VMEM((half, d), F32), dma((FOUR,)), dma(()), dma(())],
+        compiler_params=params(40, collective_id=3),
+        cost_estimate=cost(FOUR, 20),
+    )(o, dy, *pieces)
 
 
 class PairSum:
@@ -526,11 +620,6 @@
     def sems(*dims):
         dma = pltpu.SemaphoreType.DMA
         return [dma(dims)] * 5 + [dma(dims + (TWO, 3))] * TWO
-
-
-def taker(refs):
-    rest = iter(refs)
-    return lambda count: list(itertools.islice(rest, count))
 
 
 def reduce_kernel(cuts, kinds, work, *refs):
@@ -649,46 +738,29 @@
 
     spaces, out_spaces = [pl.ANY, pltpu.VMEM] + [pl.ANY] * FOUR, [pltpu.VMEM] * TWO + [pl.ANY]
 
-    def tiles(self, fetch, use):
-        n = self.w_o.shape[0] // BLK
-        fetch(0, 0).start()
-
-        @pl.loop(0, n)
-        def _(t):
-            slot = lax.rem(t, TWO)
-            fetch(t, slot).wait()
-
-            @pl.when(t + 1 < n)
-            def _():
-                fetch(t + 1, 1 - slot).start()
-
-            use(pl.ds(pl.multiple_of(t * BLK, BLK), BLK), slot)
-
     def step(self, t):
-        def cols(t):
-            return pl.ds(pl.multiple_of(t * BLK, BLK), BLK)
-
         def fetch_o(t, slot):
-            return pltpu.make_async_copy(self.w_o.at[:, cols(t)], self.buf_o.at[slot], self.w_sem.at[0, slot])
+            return pltpu.make_async_copy(self.w_o.at[:, aligned(t)], self.buf_o.at[slot], self.w_sem.at[0, slot])
 
         def fetch_q(t, slot):
-            return pltpu.make_async_copy(self.w_q.at[cols(t)], self.buf_q.at[slot], self.w_sem.at[1, slot])
-
-        def project(at, slot):
+            return pltpu.make_async_copy(self.w_q.at[aligned(t)], self.buf_q.at[slot], self.w_sem.at[1, slot])
+
+        def project(t, slot):
+            at = aligned(t)
             attn = self.attn_home[...].reshape(-1, self.w_o.shape[0])
             out = jnp.dot(attn, self.buf_o[slot], preferred_element_type=F32)
             self.block_out[:, at] = (self.block_out[:, at].astype(F32) + out).astype(BF16)
 
-        def pull(at, slot):
+        def pull(t, slot):
             dq = self.dq_home[...].reshape(-1, self.w_o.shape[0])
-            self.d_part[:, at] = dot_t(dq, self.buf_q[slot])
+            self.d_part[:, aligned(t)] = dot_t(dq, self.buf_q[slot])
 
         if t in PRODUCTS_AT:
             i = PRODUCTS_AT.index(t)
             self.homes[i].wait_recv()
             if i == 0:
                 self.residual.wait()
-            self.tiles(*((fetch_o, project), (fetch_q, pull))[i])
+            tiled(self.w_o.shape[0] // BLK, *((fetch_o, project), (fetch_q, pull))[i])
 
     def wq_terms(self, own, other):
         self.h_mine.wait()
@@ -704,8 +776,7 @@
 
             @pl.loop(0, FOUR)
             def _(zz, out=out, half=half):
-                at = pl.multiple_of((half * FOUR + zz) * BLK, BLK)
-                h = self.h_own[:, :, :, pl.ds(at, BLK)].reshape(-1, BLK)
+                h = self.h_own[:, :, :, aligned(half * FOUR + zz)].reshape(-1, BLK)
                 out[zz] = dot(h, d_out, (0,), (0,)).reshape(out.shape[1:])
 
     def finish(self):
@@ -776,10 +847,11 @@
 
 HERE = 0, 0, 0
 LINKS = "xyud"
-ORDERS = "zxy", "zyx", "xyz", "zyx"
-SIZES = 8.4, 8.4, 5.6, 2.8
+ORDERS = "zxy", "zyx", "yxz", "zxy"
+WO_CUTS, WQ_CUTS = (0, 3, 7, 8), (0, 3, 6, 8)
+SIZES = 8.4, 9.8, 4.2, 2.8
 LATENCY, TILES_FROM, TILE_EVERY = 3.0, 14.0, 8.0
-SUM_AT = 30.0, 42.0, 54.0, 66.0
+SUM_AT = 30.0, 41.0, 52.0, 63.0
 
 
 def onward(order, key):
@@ -813,9 +885,12 @@
 
 
 def turn_back(dkv_ref, cos_ref, sin_ref, dk_u, dv_u):
-    n = dk_u.shape[0] * dk_u.shape[1] * dk_u.shape[TWO]
-    dk = turn(dkv_ref[pl.ds(0, n)] * ATTN_SCALE, cos_ref, sin_ref)
-    dk_u[...] = dk.astype(BF16).reshape(dk_u.shape)
+    n = TWO * TWO * BLK
+    for i in range(TWO):
+        for j in range(TWO):
+            cos_t, sin_t = (jnp.hstack([t, t * sign]) for t, sign in ((cos_ref[i, j].T, 1), (sin_ref[i, j].T, -1)))
+            dk = dkv_ref[pl.ds((i * TWO + j) * BLK, BLK)] * ATTN_SCALE
+            dk_u[i, j] = (dk * cos_t + pltpu.roll(dk, HEAD_DIM // TWO, 1) * sin_t).astype(BF16)
     dv_u[...] = dkv_ref[pl.ds(n, n)].astype(BF16).reshape(dv_u.shape)
 
 
@@ -825,8 +900,7 @@
 
         @pl.loop(0, FOUR)
         def _(zz, out=out, half=half):
-            at = pl.multiple_of((half * FOUR + zz) * BLK, BLK)
-            h = h_own[:, :, :, pl.ds(at, BLK)].reshape(-1, BLK)
+            h = h_own[:, :, :, aligned(half * FOUR + zz)].reshape(-1, BLK)
             out[zz] = dot(h, d_out, (0,), (0,)).reshape(out.shape[1:])
 
 
@@ -857,10 +931,14 @@
                 cols = pl.ds(xx * narrow, narrow)
                 yield wkv_own.at[:, head_slice(i)], out.at[pl.ds(wq_at, wkv_own.shape[0]), cols]
             return
-        eighth = wo_ref.shape[0] // 8
-        at, rows = (part * 3 * eighth, (TWO if part == TWO else 3) * eighth)
+
+        def cut(ref, cuts):
+            first, last = (c * ref.shape[0] // 8 for c in cuts[part : part + TWO])
+            return first, last - first
+
+        at, rows = cut(wo_ref, WO_CUTS)
         yield wo_ref.at[pl.ds(at, rows)], outs[0].at[pl.ds(wo_at + at, rows)]
-        at, rows = TWO * at, TWO * rows
+        at, rows = cut(wq_ref, WQ_CUTS)
         yield wq_ref.at[pl.ds(at, rows)], outs[1].at[pl.ds(wq_at + at, rows), pl.ds(xx * wide, wide)]
 
     def block(part, key, cc=core):
@@ -995,7 +1073,7 @@
         n_rows = n_batch * n_tok
         wide = N_HEADS * HEAD_DIM
         me = lax.axis_index("cp")
-        _, y, x, core = place(me)
+        _, _, _, core = place(me)
         quad, pair = me % FOUR, me // FOUR
         relations = range(FOUR)
 
@@ -1012,15 +1090,14 @@
         gain = norm_gain.astype(F32)
         cos_t, sin_t = rope_tables(positions.reshape(n_rows))
         cos_f, sin_f = jnp.hstack([cos_t, cos_t]), jnp.hstack([-sin_t, sin_t])
-        normed, kv_home, q_home = project(hidden.reshape(n_rows, d_model), gain[NEW], w_q, w_k, w_v, cos_f, sin_f)
+        dy_flat = grad_out.reshape(n_rows, d_model)
+        normed, kv_home = project(hidden.reshape(n_rows, d_model), gain[NEW], w_k, w_v, cos_f, sin_f)
         pos_u = unite(positions)
-        kv_all, q_u, dy_part = exchange(
-            kv_home.reshape((TWO,) * 5 + (CHUNK, HEAD_DIM)),
-            q_home.reshape((TWO,) * FOUR + (CHUNK, wide)),
-            grad_out.reshape((TWO,) * 3 + (CHUNK, d_model)),
-        )
-        dy_last, dy_part = lax.optimization_barrier((rows_of(grad_out, LATER[1]), dy_part))
-        dy_last = perm(dy_last, flip_pairs(LATER[1]))
+        kv_home = kv_home.reshape((TWO,) * 5 + (CHUNK, HEAD_DIM))
+        kv_all, q_u, do_u = exchange(kv_home, normed, dy_flat, cos_f, sin_f, w_q, w_o)
+        dy_quad = grad_out.reshape((TWO,) * 3 + (CHUNK, d_model))
+        dy_pieces, q_u = lax.optimization_barrier(([rows_of(grad_out, d) for d in relations], q_u))
+        dy_pieces = swap(dy_pieces)[1:]
 
         member = quad ^ jnp.arange(FOUR)
         front, back = ((m[:, NEW] * CHUNK + jnp.arange(CHUNK)[NEW]).reshape(BLK) for m in (member, 3 - member))
@@ -1028,7 +1105,6 @@
         own_super = jnp.stack([pair, N_SUPER - 1 - pair]).astype(jnp.int32)
         q_index = own_super[:, NEW] * BLK + offsets
         start = q_index[NEW] - pos_u
-        koff = jnp.broadcast_to(offsets[:, :, NEW], (TWO, BLK, BLK))
         tab = jnp.concatenate(
             [own_super, (jnp.min(start, axis=-1) // BLK).reshape(-1), jnp.max(start, axis=-1).reshape(-1)]
         )
@@ -1037,23 +1113,14 @@
         cos_u, sin_u = rope_tables(pos_u)
         cos_ut, sin_ut = jnp.swapaxes(cos_u, TWO, 3), jnp.swapaxes(sin_u, TWO, 3)
 
-        lanes = start.shape + (HEAD_DIM,)
-        start_l, q_index_l = (jnp.broadcast_to(a[..., NEW], lanes) for a in (start, q_index[NEW]))
-        attn_u, lse = flash_fwd(tab, q_u, kv_all, start_l, q_index_l, offsets[:, NEW])
-
-        tok = tuple(range(3))
-        half_wide = wide // TWO
-        dy_u = jnp.concatenate([dy_part, dy_last], axis=TWO)
-        wo_send = dot(dyn(attn_u, (1 - core) * half_wide, half_wide, 3), dy_u, tok, tok)
-        wo_sum = dot(dyn(attn_u, core * half_wide, half_wide, 3), dy_u, tok, tok) + perm(wo_send, flip_pairs(1))
-        wo_sum = wo_sum.reshape(FOUR, TWO, half_wide // N_PAIRS, d_model)
-        wo_y = perm(pick(wo_sum, 1 - y, 1), flip_pairs(FOUR))
-
-        d_attn = dot(dy_u, dyn(w_o, x * wide, wide, 0), (3,), (1,)).astype(BF16)
-        d_attn, wo_sum = lax.optimization_barrier((d_attn, wo_sum))
-        dq_u, dkv = flash_bwd(tab, q_u, d_attn, attn_u, kv_all, lse, start_r, q_index_r, koff, cos_ut, sin_ut)
-
-        wo_sum = pick(wo_sum, y, 1) + wo_y
+        koff = offsets[:, NEW]
+        attn_u, lse = flash_fwd(tab, q_u, kv_all, start_r, q_index_r, koff)
+
+        wo_keep, wo_away = wo_terms(attn_u, dy_quad, dy_pieces)
+        wo_come = perm(wo_away, flip_pairs(FOUR))
+        do_u, wo_keep = lax.optimization_barrier((do_u, wo_keep))
+        dq_u, dkv = flash_bwd(tab, q_u, do_u, attn_u, kv_all, lse, start_r, q_index_r, koff, cos_ut, sin_ut)
+        wo_sum = wo_keep + wo_come
 
         x_flat = hidden.reshape(n_rows, d_model)
         wo_own, dkv_own, wq_own, block_out, d_part, h_u = reduce_pairs(
@@ -1065,19 +1132,18 @@
             Products,
             (attn_u, dq_u, x_flat, normed.reshape((TWO,) * 3 + (CHUNK, d_model)), w_o, w_q),
         )
-        cos_uf, sin_uf = jnp.concatenate([cos_u, cos_u], axis=-1), jnp.concatenate([sin_u, -sin_u], axis=-1)
         grad_wo, grad_wq, grad_wk, grad_wv, grad_x, d_gain = gather_all(
             wo_own,
             wq_own,
             dkv_own,
-            cos_uf.reshape(-1, HEAD_DIM),
-            sin_uf.reshape(-1, HEAD_DIM),
+            cos_ut,
+            sin_ut,
             h_u,
             d_part,
             w_k,
             w_v,
             x_flat,
-            grad_out.reshape(n_rows, d_model),
+            dy_flat,
             gain[NEW],
             [w_o.shape, w_q.shape, w_k.shape, w_v.shape],
         )

time: 606 us -> 579 us (0.955)
  waiting for transfers between devices: 18.3 us -> 43.6 us
  Pallas kernels: 494 us -> 474 us
  matrix products: 15 us -> 0 us
  other arithmetic: 12.3 us -> 5.98 us
    ppermute x6 -> x7, waiting for transfers between devices: 18.3 us -> 43.6 us  [perm(): return lax.ppermute(x, 'cp', pairs)]
    pallas_call x1, Pallas kernels: 207 us -> 187 us  [reduce_pairs(): pl.pallas_call(functools.partial(reduce_kernel, cuts, kinds, work), name=...]
    dot_general x3 -> x0, matrix products: 15 us -> none  [dot(): lax.dot_general(a, b, ((ca, cb), ((), ())), preferred_element_type=F32)]
    pallas_call x1, Pallas kernels: 176 us -> 168 us  [gather_all(): pl.pallas_call(gather_kernel, name='gather_all', out_shape=[jax.ShapeDtyp...]
    pallas_call x1, Pallas kernels: 6.8 us -> 13.7 us  [wo_terms(): pl.pallas_call(wo_kernel, name='wo_terms', out_shape=[jax.ShapeDtypeStruc...]
    unnamed x60 -> x59, local copies, waits for them, and re-layouts: 42 us -> 41.2 us
  transfers between devices with their start and end apart: 6 -> 7, of which waited for: 1 -> 3; matrix products, arithmetic and copies ran while one was open for 4% -> 1% of each run, Pallas kernels for 19% -> 18%
where the time goes in v6:
time: 579 us; the launch traced here: 575 us
  Pallas kernels  474 us (82%)
  local copies, waits for them, and re-layouts  45.7 us (8%)
  waiting for transfers between devices  43.6 us (8%)
  other arithmetic  5.98 us (1%)
    pallas_call x1, Pallas kernels, reduce_pairs(): pl.pallas_call(functools.partial(reduce_kernel, cuts, kinds, work), name=...  187 us
    pallas_call x1, Pallas kernels, gather_all(): pl.pallas_call(gather_kernel, name='gather_all', out_shape=[jax.ShapeDtyp...  168 us
    pallas_call x1, Pallas kernels, exchange(): pl.pallas_call(exchange_kernel, name='exchange', out_shape=(jax.ShapeDtyp...  60.9 us
    ppermute x7, waiting for transfers between devices, perm(): return lax.ppermute(x, 'cp', pairs)  43.6 us
    unnamed x59, local copies, waits for them, and re-layouts  41.2 us
    pallas_call x1, Pallas kernels, flash_bwd(): pl.pallas_call(bwd_kernel, name='attn_bwd', out_shape=(jax.ShapeDtypeStru...  27.1 us
    pallas_call x1, Pallas kernels, flash_fwd(): pl.pallas_call(fwd_kernel, name='attn_fwd', out_shape=(jax.ShapeDtypeStru...  15.1 us
    pallas_call x1, Pallas kernels, wo_terms(): pl.pallas_call(wo_kernel, name='wo_terms', out_shape=[jax.ShapeDtypeStruc...  13.7 us
  transfers between devices with their start and end apart: 7, of which 3 were waited for; matrix products, arithmetic and copies ran while one was open for 1% of the time, Pallas kernels for 18%

profile of v6, /device:TPU:0, one launch (start us, length us, event | category | flops | bytes accessed | tf_op | source)
XLA Modules:
  0.0 575.3 jit_solution(3317292384353752750)
XLA Ops:
  0.6 0.8 reshape.270
  1.4 2.4 collective-permute-start.2
  5.9 3.3 dynamic-slice_bitcast_fusion
  9.2 1.0 fusion
  10.8 1.9 norm_kv.1
  12.7 60.9 %exchange.1 = (bf16[8,2,2,2,256,128]{5,4,3,2,1,0:T(8,128)(2,1)S(1)}, bf16[2,2,256,1024]{3,2,1,0:T(8,128)(2,1)S(1)}, bf16[2,2,256,1024]{3,2,1,0:T(8,128)(2,1)S(1)}) custom-call(bf16[2,2,2,2,2,64,128]{6,5,4,3,2,1,0:T(8,128)(2,1)S(1)} %bitcast.35, bf16[512,2048]{1,0:T(8,128)(2,1)S(1)} %get-tuple-element.37.refs_1_, bf16[512,2048]{1,0:T(8,128)(2,1)S(1)} %bitcast.29, ...), custom_call_target="tpu_custom_call" | custom-call | flops 1000000000 | bytes 20971520 | tf_op jit(solution)/shard_map/exchange/pallas_call | solution.py:437
  73.6 2.0 copy-done.11
  75.6 1.3 copy-done.13
  76.9 1.3 copy-done.16
  79.7 1.1 collective-permute-start.5
  81.4 2.2 copy-done.12
  83.6 1.6 copy-done.14
  85.2 15.1 %attn_fwd.1 = (bf16[2,2,256,1024]{3,2,1,0:T(8,128)(2,1)S(1)}, f32[2,2,8,1,256]{4,3,2,1,0:T(1,128)S(1)}) custom-call(s32[10]{0:T(128)S(1)} %pad_add_fusion.2.tab, bf16[2,2,256,1024]{3,2,1,0:T(8,128)(2,1)S(1)} %copy-done.14, bf16[8,2,2,2,256,128]{5,4,3,2,1,0:T(8,128)(2,1)S(1)} %copy-done.12, s32[2,2,1,256]{3,2,1,0:T(1,128)S(1)} %broadcast_subtract_fusion.st_ref, ...), custom_call_target="tpu_custom_call" | custom-call | flops 20000000000 | bytes 16777216 | tf_op jit(solution)/shard_map/attn_fwd/pallas_call | solution.py:206
  100.3 1.3 copy-done.3
  101.7 1.0 multiply_sine_fusion
  102.8 1.9 collective-permute-done.4.refs_3_
  104.7 21.3 %collective-permute-done.5.refs_4_ = bf16[2,2,64,2048]{3,2,1,0:T(8,128)(2,1)} collective-permute-done((bf16[2,2,64,2048]{3,2,1,0:T(8,128)(2,1)}, bf16[2,2,64,2048]{3,2,1,0:T(8,128)(2,1)}, u32[]{:S(2)}, u32[]{:S(2)}) %collective-permute-start.5) | collective-permute-done | bytes 1048608 | tf_op jit(solution)/shard_map/ppermute | solution.py:1063
  126.0 1.6 copy-done.4
  127.6 13.7 %wo_terms.1 = (f32[4,64,2048]{2,1,0:T(8,128)S(1)}, f32[4,64,2048]{2,1,0:T(8,128)S(1)}) custom-call(bf16[2,2,256,1024]{3,2,1,0:T(8,128)(2,1)S(1)} %copy-done.4, bf16[2,2,2,64,2048]{4,3,2,1,0:T(8,128)(2,1)S(1)} %bitcast.30, bf16[2,2,64,2048]{3,2,1,0:T(8,128)(2,1)} %collective-permute-done.3.refs_2_, bf16[2,2,64,2048]{3,2,1,0:T(8,128)(2,1)} %collective-permute-done.4.refs_3_, ...), custom_call_target="tpu_custom_call" | custom-call | flops 4000000000 | bytes 20971520 | tf_op jit(solution)/shard_map/wo_terms/pallas_call | solution.py:497
  141.9 27.1 %attn_bwd.1 = (bf16[2,2,256,1024]{3,2,1,0:T(8,128)(2,1)S(1)}, f32[8,2,2,2,256,128]{5,4,3,2,1,0:T(8,128)}) custom-call(s32[10]{0:T(128)S(1)} %pad_add_fusion.2.tab, bf16[2,2,256,1024]{3,2,1,0:T(8,128)(2,1)S(1)} %copy-done.15, bf16[2,2,256,1024]{3,2,1,0:T(8,128)(2,1)} %copy-done.16, bf16[2,2,256,1024]{3,2,1,0:T(8,128)(2,1)} %copy-done.3, ...), custom_call_target="tpu_custom_call" | custom-call | flops 49999998976 | bytes 33554432 | tf_op jit(solution)/shard_map/attn_bwd/pallas_call | solution.py:225
  169.0 20.3 %collective-permute-done.6 = f32[4,64,2048]{2,1,0:T(8,128)S(1)} collective-permute-done((f32[4,64,2048]{2,1,0:T(8,128)S(1)}, f32[4,64,2048]{2,1,0:T(8,128)S(1)}, u32[]{:S(2)}, u32[]{:S(2)}) %collective-permute-start.6) | collective-permute-done | bytes 2097184 | tf_op jit(solution)/shard_map/ppermute | solution.py:1063
  189.3 1.6 add.138.refs_0_
  190.9 187.4 %reduce_pairs.1 = (f32[64,2048]{1,0:T(8,128)}, f32[2048,128]{1,0:T(8,128)}, f32[128,1024]{1,0:T(8,128)}, bf16[512,2048]{1,0:T(8,128)(2,1)}, f32[512,2048]{1,0:T(8,128)}, /*index=5*/bf16[2,2,256,2048]{3,2,1,0:T(8,128)(2,1)}) custom-call(f32[4,64,2048]{2,1,0:T(8,128)} %add.138.refs_0_, f32[4,2,2048,128]{3,2,1,0:T(8,128)} %bitcast.40, ...), custom_call_target="tpu_custom_call" | custom-call | flops 1000000000 | bytes 20971520 | tf_op jit(solution)/shard_map/reduce_pairs/pallas_call | solution.py:836
  378.2 167.5 %gather_all.1 = (f32[2048,2048]{1,0:T(8,128)}, f32[2048,2048]{1,0:T(8,128)}, f32[2048,256]{1,0:T(8,128)}, f32[2048,256]{1,0:T(8,128)}, bf16[512,2048]{1,0:T(8,128)(2,1)}, /*index=5*/f32[1,2048]{1,0:T(1,128)}) custom-call(f32[64,2048]{1,0:T(8,128)} %get-tuple-element.54.refs_0_, f32[128,1024]{1,0:T(8,128)} %get-tuple-element.55.refs_1_, ...), custom_call_target="tpu_custom_call" | custom-call | flops 1000000000 | bytes 79691776 | tf_op jit(solution)/shard_map/gather_all/pallas_call | solution.py:1049
  545.8 1.3 copy.23
  547.1 1.0 copy-done.20
  548.1 1.3 copy.24
  549.5 14.6 %copy.25 = f32[2048,2048]{1,0:T(8,128)} copy(f32[2048,2048]{1,0:T(8,128)} %get-tuple-element.93) | data formatting | bytes 33554432
  564.1 1.3 copy.26
  565.4 1.8 copy-done.18
  567.2 1.3 copy.27
  568.5 6.2 %copy.28 = f32[2048,2048]{1,0:T(8,128)} copy(f32[2048,2048]{1,0:T(8,128)S(1)} %bitcast.39) | data formatting | bytes 33554432
  (80 shorter events, 6.1 us)
Async XLA Ops:
  1.4 79.4 %collective-permute-start.2 = (s32[2,2,64]{2,1,0:T(2,128)S(1)}, s32[2,2,64]{2,1,0:T(2,128)S(1)}, u32[]{:S(2)}, u32[]{:S(2)}) collective-permute-start(s32[2,2,64]{2,1,0:T(2,128)S(1)} %get-tuple-element.74), channel_id=1, source_target_pairs={{0,3},{1,2},{2,1},{3,0},{4,7},{5,6},{6,5},{7,4},{8,11},{9,10},{10,... | collective-permute-start | bytes 3080 | tf_op jit(solution)/shard_map/ppermute | solution.py:1063
  3.8 77.0 %collective-permute-start = (s32[2,2,64]{2,1,0:T(2,128)S(1)}, s32[2,2,64]{2,1,0:T(2,128)S(1)}, u32[]{:S(2)}, u32[]{:S(2)}) collective-permute-start(s32[2,2,64]{2,1,0:T(2,128)S(1)} %get-tuple-element.74), channel_id=1, source_target_pairs={{0,1},{1,0},{2,3},{3,2},{4,5},{5,4},{6,7},{7,6},{8,9},{9,8},{10,11... | collective-permute-start | bytes 3080 | tf_op jit(solution)/shard_map/ppermute | solution.py:1063
  4.5 75.2 %collective-permute-start.1 = (s32[2,2,64]{2,1,0:T(2,128)S(1)}, s32[2,2,64]{2,1,0:T(2,128)S(1)}, u32[]{:S(2)}, u32[]{:S(2)}) collective-permute-start(s32[2,2,64]{2,1,0:T(2,128)S(1)} %bitcast.44), channel_id=1, source_target_pairs={{0,2},{1,3},{2,0},{3,1},{4,6},{5,7},{6,4},{7,5},{8,10},{9,11},{10,... | collective-permute-start | bytes 3080 | tf_op jit(solution)/shard_map/ppermute | solution.py:1063
  5.9 4.5 copy-start.10
  5.9 4.5 copy-start.8
  5.9 4.5 copy-start.9
  9.2 1.6 copy-start.1
  10.8 1.9 copy-start
  12.6 60.9 %copy-start.2 = (bf16[512,2048]{1,0:T(8,128)(2,1)}, bf16[512,2048]{1,0:T(8,128)(2,1)S(1)}, u32[]{:S(2)}) copy-start(bf16[512,2048]{1,0:T(8,128)(2,1)S(1)} %get-tuple-element.37.refs_1_) | copy-start | bytes 6291460
  73.6 2.0 copy-start.11
  75.6 1.3 copy-start.13
  78.2 24.5 %collective-permute-start.3 = (bf16[2,2,64,2048]{3,2,1,0:T(8,128)(2,1)}, bf16[2,2,64,2048]{3,2,1,0:T(8,128)(2,1)}, u32[]{:S(2)}, u32[]{:S(2)}) collective-permute-start(bf16[2,2,64,2048]{3,2,1,0:T(8,128)(2,1)} %get-tuple-element.45), channel_id=1, source_target_pairs={{0,1},{1,0},{2,3},{3,2},{4,5},{5,4},{6,7},{7,6},{8,9},{9,8},{10,11... | collective-permute-start | bytes 3145736 | tf_op jit(solution)/shard_map/ppermute | solution.py:1063
  78.3 26.3 %collective-permute-start.4 = (bf16[2,2,64,2048]{3,2,1,0:T(8,128)(2,1)}, bf16[2,2,64,2048]{3,2,1,0:T(8,128)(2,1)}, u32[]{:S(2)}, u32[]{:S(2)}) collective-permute-start(bf16[2,2,64,2048]{3,2,1,0:T(8,128)(2,1)} %get-tuple-element.44), channel_id=1, source_target_pairs={{0,2},{1,3},{2,0},{3,1},{4,6},{5,7},{6,4},{7,5},{8,10},{9,11},{10,... | collective-permute-start | bytes 3145736 | tf_op jit(solution)/shard_map/ppermute | solution.py:1063
  79.7 46.3 %collective-permute-start.5 = (bf16[2,2,64,2048]{3,2,1,0:T(8,128)(2,1)}, bf16[2,2,64,2048]{3,2,1,0:T(8,128)(2,1)}, u32[]{:S(2)}, u32[]{:S(2)}) collective-permute-start(bf16[2,2,64,2048]{3,2,1,0:T(8,128)(2,1)} %get-tuple-element.45), channel_id=1, source_target_pairs={{0,3},{1,2},{2,1},{3,0},{4,7},{5,6},{6,5},{7,4},{8,11},{9,10},{10,... | collective-permute-start | bytes 3145736 | tf_op jit(solution)/shard_map/ppermute | solution.py:1063
  81.4 2.2 copy-start.12
  83.6 1.6 copy-start.14
  100.3 1.3 copy-start.3
  102.7 39.2 %copy-start.6 = (f32[2,2,64,256]{3,2,1,0:T(8,128)}, f32[2,2,64,256]{3,2,1,0:T(8,128)S(1)}, u32[]{:S(2)}) copy-start(f32[2,2,64,256]{3,2,1,0:T(8,128)S(1)} %get-tuple-element.71.sin_ref.refs_4_) | copy-start | bytes 786436
  102.7 39.2 %copy-start.7 = (f32[2,2,64,256]{3,2,1,0:T(8,128)}, f32[2,2,64,256]{3,2,1,0:T(8,128)S(1)}, u32[]{:S(2)}) copy-start(f32[2,2,64,256]{3,2,1,0:T(8,128)S(1)} %get-tuple-element.72.cos_ref.refs_3_) | copy-start | bytes 786436
  126.0 1.6 copy-start.4
  127.6 14.3 %copy-start.15 = (bf16[2,2,256,1024]{3,2,1,0:T(8,128)(2,1)S(1)}, bf16[2,2,256,1024]{3,2,1,0:T(8,128)(2,1)}, u32[]{:S(2)}) copy-start(bf16[2,2,256,1024]{3,2,1,0:T(8,128)(2,1)} %copy-done.13) | copy-start | bytes 6291460
  141.3 48.0 %collective-permute-start.6 = (f32[4,64,2048]{2,1,0:T(8,128)S(1)}, f32[4,64,2048]{2,1,0:T(8,128)S(1)}, u32[]{:S(2)}, u32[]{:S(2)}) collective-permute-start(f32[4,64,2048]{2,1,0:T(8,128)S(1)} %get-tuple-element.48), channel_id=1, source_target_pairs={{0,4},{1,5},{2,6},{3,7},{4,0},{5,1},{6,2},{7,3},{8,12},{9,13},{10,... | collective-permute-start | bytes 6291464 | tf_op jit(solution)/shard_map/ppermute | solution.py:1063
  169.0 21.9 %copy-start.5 = (bf16[2,2,256,1024]{3,2,1,0:T(8,128)(2,1)}, bf16[2,2,256,1024]{3,2,1,0:T(8,128)(2,1)S(1)}, u32[]{:S(2)}) copy-start(bf16[2,2,256,1024]{3,2,1,0:T(8,128)(2,1)S(1)} %get-tuple-element.52.refs_3_) | copy-start | bytes 6291460
  378.2 167.6 %copy-start.17 = (bf16[512,2048]{1,0:T(8,128)(2,1)S(1)}, bf16[512,2048]{1,0:T(8,128)(2,1)}, u32[]{:S(2)}) copy-start(bf16[512,2048]{1,0:T(8,128)(2,1)} %get-tuple-element.53) | copy-start | bytes 6291460
  545.8 2.3 copy-start.20
  548.1 20.4 %slice-start = ((s8[16777216]{0:T(1024)(128)(4,1)}), s8[4194304]{0:T(1024)(128)(4,1)S(1)}, s32[]{:S(2)}) async-start(s8[16777216]{0:T(1024)(128)(4,1)} %bitcast.38), calls=%async_computation | async-start | bytes 8388608
  549.5 14.6 %copy-start.19 = (f32[2048,256]{1,0:T(8,128)S(1)}, f32[2048,256]{1,0:T(8,128)}, u32[]{:S(2)}) copy-start(f32[2048,256]{1,0:T(8,128)} %get-tuple-element.94) | copy-start | bytes 6291460
  549.5 19.0 %slice-start.1 = ((s8[16777216]{0:T(1024)(128)(4,1)}), s8[4194304]{0:T(1024)(128)(4,1)S(1)}, s32[]{:S(2)}) async-start(s8[16777216]{0:T(1024)(128)(4,1)} %bitcast.38), calls=%async_computation.1 | async-start | bytes 8388608
  549.5 19.0 %slice-start.2 = ((s8[16777216]{0:T(1024)(128)(4,1)}), s8[4194304]{0:T(1024)(128)(4,1)S(1)}, s32[]{:S(2)}) async-start(s8[16777216]{0:T(1024)(128)(4,1)} %bitcast.38), calls=%async_computation.2 | async-start | bytes 8388608
  549.5 19.0 %slice-start.3 = ((s8[16777216]{0:T(1024)(128)(4,1)}), s8[4194304]{0:T(1024)(128)(4,1)S(1)}, s32[]{:S(2)}) async-start(s8[16777216]{0:T(1024)(128)(4,1)} %bitcast.38), calls=%async_computation.3 | async-start | bytes 8388608
  564.1 3.1 copy-start.18
  568.5 6.2 %copy-start.21 = (f32[1,2048]{1,0:T(1,128)S(1)}, f32[1,2048]{1,0:T(1,128)}, u32[]{:S(2)}) copy-start(f32[1,2048]{1,0:T(1,128)} %get-tuple-element.64) | copy-start | bytes 24580
  (1 other events, 1.3 us)

commit v7 on v6

--- a/solution.py
+++ b/solution.py
@@ -26,6 +26,7 @@
 N_SUPER = 2 * N_PAIRS
 MESH = pl.DeviceIdType.MESH
 ONE = pl.Squeezed()
+GROUP = 4
 MADE_AT = 5
 PRODUCTS_AT = 7, 9
 F32 = jnp.float32
@@ -144,11 +145,14 @@
         lse_ref[h] = (m_s[rows] * EXP2_SCALE + jnp.log2(total)).T[:1]
 
 
-def bwd_kernel(tab, q_ref, do_ref, o_ref, kv_ref, lse_ref, st_ref, qi_ref, ko_ref, cos_ref, sin_ref, dq_ref, dkv_ref, dq_acc, delta, off_s):
+def bwd_kernel(tab, q_ref, do_ref, o_ref, kv_ref, lse_ref, st_ref, qi_ref, ko_ref, cos_ref, sin_ref, dq_ref, dkv_ref, *scratch):
+    dq_acc, delta, off_s, q_s, do_s, q_t, do_t, p_s, ds_s = scratch
     dq_acc[...] = jnp.zeros_like(dq_acc)
     for h in range(N_HEADS):
-        terms = do_ref[:, head(h)].astype(F32) * o_ref[:, head(h)].astype(F32)
-        delta[h] = jnp.sum(terms.T, axis=0, keepdims=True)
+        q, do = q_ref[:, head(h)], do_ref[:, head(h)]
+        delta[h] = jnp.sum((do.astype(F32) * o_ref[:, head(h)].astype(F32)).T, axis=0, keepdims=True)
+        q_s[pl.ds(h * BLK, BLK)], do_s[pl.ds(h * BLK, BLK)] = q, do
+        q_t[h], do_t[h] = q.T, do.T
 
     @pl.when(pl.program_id(1) == 0)
     def _():
@@ -162,25 +166,26 @@
         v = kv_ref[pair, 1, hk]
         k_t = k.T
         mask = may_use(s, off_s[hk], st_ref, qi_ref) if masked else None
-        dk = dv = jnp.zeros((BLK, HEAD_DIM), F32)
-        for h in range(N_HEADS):
-            q = q_ref[:, head(h)]
-            do = do_ref[:, head(h)]
-            p = jnp.exp2(dot_t(k, q) * EXP2_SCALE - lse_ref[h])
-            if masked:
-                p = jnp.where(mask, p, 0.0)
-            ds = (p * (dot_t(v, do) - delta[h])).astype(BF16)
-            dv += jnp.dot(p.astype(BF16), do, preferred_element_type=F32)
-            dk += jnp.dot(ds, q, preferred_element_type=F32)
-            dq_acc[h] += jnp.dot(k_t, ds, preferred_element_type=F32)
-        dkv_ref[pair, 0, hk] += dk
-        dkv_ref[pair, 1, hk] += dv
+        for first in range(0, N_HEADS, GROUP):
+            rows = pl.ds(first * BLK, GROUP * BLK)
+            for h in range(first, first + GROUP):
+                cols = pl.ds(h * BLK, BLK)
+                p = jnp.exp2(jnp.dot(k, q_t[h], preferred_element_type=F32) * EXP2_SCALE - lse_ref[h])
+                if masked:
+                    p = jnp.where(mask, p, 0.0)
+                ds = p * (jnp.dot(v, do_t[h], preferred_element_type=F32) - delta[h])
+                p_s[:, cols] = p.astype(BF16)
+                ds_s[:, cols] = ds.astype(BF16)
+            dkv_ref[pair, 0, hk] += jnp.dot(ds_s[:, rows], q_s[rows], preferred_element_type=F32)
+            dkv_ref[pair, 1, hk] += jnp.dot(p_s[:, rows], do_s[rows], preferred_element_type=F32)
+            dq_acc[:, rows] += jnp.dot(k_t, ds_s[:, rows], preferred_element_type=F32)
 
     steps(tab, body)
     cos_t, sin_t = cos_ref[...], sin_ref[...]
     half = HEAD_DIM // TWO
     for h in range(N_HEADS):
-        a, c = dq_acc[h, :half] * ATTN_SCALE, dq_acc[h, half:] * ATTN_SCALE
+        cols = pl.ds(h * BLK, BLK)
+        a, c = dq_acc[:half, cols] * ATTN_SCALE, dq_acc[half:, cols] * ATTN_SCALE
         lin = jnp.concatenate([a * cos_t + c * sin_t, c * cos_t - a * sin_t], axis=0)
         dq_ref[:, head(h)] = lin.T.astype(BF16)
 
@@ -215,7 +220,7 @@
             scratch_shapes=[pltpu.VMEM((N_HEADS * BLK, HEAD_DIM), t) for t in (BF16, F32, F32, F32)]
             + [pltpu.VMEM((N_PAIRS, TWO, HEAD_DIM, BLK), BF16), pltpu.VMEM((TWO, BLK, HEAD_DIM), jnp.int32)],
         ),
-        compiler_params=params(40),
+        compiler_params=params(63),
         cost_estimate=cost(20, 16),
     )(tab, q, kv, start, qidx, koff)
 
@@ -234,10 +239,13 @@
             grid=(TWO, TWO),
             in_specs=[tile, tile, tile, kvs, stat, row, row, ko, rope, rope],
             out_specs=[tile, kvs],
-            scratch_shapes=[pltpu.VMEM((N_HEADS, HEAD_DIM, BLK), F32), pltpu.VMEM((N_HEADS, 1, BLK), F32)]
-            + [pltpu.VMEM((TWO, BLK, BLK), jnp.int32)],
+            scratch_shapes=[pltpu.VMEM((HEAD_DIM, N_HEADS * BLK), F32), pltpu.VMEM((N_HEADS, 1, BLK), F32)]
+            + [pltpu.VMEM((TWO, BLK, BLK), jnp.int32)]
+            + [pltpu.VMEM((N_HEADS * BLK, HEAD_DIM), BF16)] * TWO
+            + [pltpu.VMEM((N_HEADS, HEAD_DIM, BLK), BF16)] * TWO
+            + [pltpu.VMEM((BLK, N_HEADS * BLK), BF16)] * TWO,
         ),
-        compiler_params=params(48),
+        compiler_params=params(63),
         cost_estimate=cost(50, 32),
     )(tab, q, do, o, kv, lse, start, qidx, koff, cos_t, sin_t)
 
@@ -265,7 +273,7 @@
         first_kernel,
         name="norm_kv",
         out_shape=(jax.ShapeDtypeStruct(x.shape, BF16), jax.ShapeDtypeStruct((TWO,) * 3 + (n, HEAD_DIM), BF16)),
-        compiler_params=params(40),
+        compiler_params=params(63),
         cost_estimate=cost(TWO, 7),
     )(x, gain, w_k, w_v, cos_f, sin_f)
 
@@ -333,8 +341,8 @@
 
 def exchange_kernel(*refs):
     take = taker(refs)
-    kv_ref, h_ref, dy_ref, cos_ref, sin_ref, wq_ref, wo_ref, kv_all, q_u, do_u = take(10)
-    own_sem, quad_s, quad_r, z_s, z_r, y_s, y_r, q_home, do_home, wq_buf, wo_buf, w_sem = take(len(refs))
+    kv_ref, h_ref, dy_ref, cos_ref, sin_ref, wq_ref, wo_ref, kv_all, q_u, do_u, *dy_rows = take(12)
+    own_sem, quad_s, quad_r, z_s, z_r, y_s, y_r, q_home, do_home, wq_buf, wo_buf, w_sem, dy_sem = take(len(refs))
     me = lax.axis_index("cp")
     z, y, x, core = place(me)
     quad, line = quad_of(me), Line(me)
@@ -395,6 +403,9 @@
         put(do_home, t, dot_t(dy_ref[...], wo_buf[slot]))
 
     all_moves = list(moves)
+    half = dy_ref.shape[0] // TWO
+    for i, out in enumerate(dy_rows):
+        pltpu.make_async_copy(dy_ref.at[aligned(core if i == 0 else 1 - core, half)], out, dy_sem.at[i]).start()
     for d in (1, TWO, 3):
         quad_copy(0, d).start()
     own_copy(0).start()
@@ -424,6 +435,8 @@
                 quad_copy(a, d).wait_recv()
     own_copy(1).wait()
     own_copy(TWO).wait()
+    for i, out in enumerate(dy_rows):
+        pltpu.make_async_copy(dy_ref.at[aligned(core if i == 0 else 1 - core, half)], out, dy_sem.at[i]).wait()
 
 
 def exchange(kv, h, dy, cos_f, sin_f, w_q, w_o):
@@ -431,17 +444,18 @@
     vmem, hbm = pl.BlockSpec(memory_space=pltpu.VMEM), pl.BlockSpec(memory_space=pl.ANY)
     wide = w_q.shape[1] // TWO
     unit = jax.ShapeDtypeStruct((TWO, TWO, BLK, wide), BF16)
+    dy_half = jax.ShapeDtypeStruct((dy.shape[0] // TWO, dy.shape[1]), BF16)
     home = pltpu.VMEM((TWO,) * FOUR + (CHUNK, wide), BF16)
     sems = [dma((3,))] + [dma((3, FOUR))] * TWO + [dma((TWO, TWO, 7))] + [dma((TWO, 7))] * 3
     bufs = [pltpu.VMEM((TWO,) + b, BF16) for b in ((w_q.shape[0], BLK), (BLK, w_o.shape[1]))]
     return pl.pallas_call(
         exchange_kernel,
         name="exchange",
-        out_shape=(jax.ShapeDtypeStruct((N_PAIRS,) + (TWO,) * 3 + (BLK, HEAD_DIM), BF16), unit, unit),
+        out_shape=(jax.ShapeDtypeStruct((N_PAIRS,) + (TWO,) * 3 + (BLK, HEAD_DIM), BF16), unit, unit, dy_half, dy_half),
         in_specs=[vmem] * 5 + [hbm] * TWO,
-        out_specs=[hbm] * 3,
-        scratch_shapes=sems + [home, home] + bufs + [dma((TWO, TWO))],
-        compiler_params=params(40, collective_id=1),
+        out_specs=[hbm] * 5,
+        scratch_shapes=sems + [home, home] + bufs + [dma((TWO, TWO)), dma((TWO,))],
+        compiler_params=params(63, collective_id=1),
         cost_estimate=cost(1, 20),
     )(kv, h, dy, cos_f, sin_f, w_q, w_o)
 
@@ -453,14 +467,14 @@
 
 def wo_kernel(*refs):
     take = taker(refs)
-    o_ref, dy_ref, pieces = take(1) + take(1) + [take(3)]
+    o_ref, *pieces = take(5)
     keep, away, dy_u, o_t, terms, came, load_sem, core_s, core_r = take(len(refs))
     me = lax.axis_index("cp")
     _, y, _, core = place(me)
     meet(quad_of(me)[1:TWO])
     loads = [
         pltpu.make_async_copy(src, dy_u.at[:, :, pl.ds(d * CHUNK, CHUNK)], load_sem.at[d])
-        for d, src in enumerate([dy_ref.at[core]] + pieces)
+        for d, src in enumerate(pieces)
     ]
     for c in loads:
         c.start()
@@ -468,31 +482,33 @@
         o_t[head(h)] = o_ref[:, :, :, head(h)].reshape(-1, HEAD_DIM).T
     for c in loads:
         c.wait()
-    half = terms.shape[1]
-
-    def half_terms(i, to):
-        @pl.loop(0, terms.shape[TWO] // BLK)
+    half, tiles = terms.shape[1], terms.shape[TWO] // BLK
+
+    def swap(t):
+        return remote(terms.at[0, :, aligned(t)], came.at[:, aligned(t)], core_s.at[t], core_r.at[t], quad_of(me)[1])
+
+    def half_terms(i, to, then):
+        @pl.loop(0, tiles)
         def _(t):
             dy = dy_u[:, :, :, aligned(t)].reshape(-1, BLK)
             terms[to, :, aligned(t)] = jnp.dot(o_t[aligned(i, half)], dy, preferred_element_type=F32)
-
-    half_terms(1 - core, 0)
-    swap = remote(terms.at[0], came, core_s, core_r, quad_of(me)[1])
-    swap.start()
-    half_terms(core, 1)
-    swap.wait_recv()
+            then(t)
+
+    half_terms(1 - core, 0, lambda t: swap(t).start())
+    half_terms(core, 1, lambda t: swap(t).wait_recv())
     rows = keep.shape[1]
     for zz in range(FOUR):
         for out, yy in ((keep, y), (away, 1 - y)):
             at = aligned(TWO * zz + yy, rows)
             out[zz] = terms[1, at] + came[at]
-    swap.wait_send()
-
-
-def wo_terms(o, dy, pieces):
+    for t in range(tiles):
+        swap(t).wait_send()
+
+
+def wo_terms(o, pieces):
     dma = pltpu.SemaphoreType.DMA
     vmem, hbm = pl.BlockSpec(memory_space=pltpu.VMEM), pl.BlockSpec(memory_space=pl.ANY)
-    n, d, wide = o.shape[0] * o.shape[1] * o.shape[TWO], dy.shape[-1], o.shape[-1]
+    n, d, wide = o.shape[0] * o.shape[1] * o.shape[TWO], pieces[0].shape[-1], o.shape[-1]
     half = wide // TWO
     return pl.pallas_call(
         wo_kernel,
@@ -501,10 +517,10 @@
         in_specs=[vmem] + [hbm] * FOUR,
         out_specs=[vmem] * TWO,
         scratch_shapes=[pltpu.VMEM((TWO, TWO, BLK, d), BF16), pltpu.VMEM((wide, n), BF16)]
-        + [pltpu.VMEM((TWO, half, d), F32), pltpu.VMEM((half, d), F32), dma((FOUR,)), dma(()), dma(())],
-        compiler_params=params(40, collective_id=3),
+        + [pltpu.VMEM((TWO, half, d), F32), pltpu.VMEM((half, d), F32), dma((FOUR,)), dma((d // BLK,)), dma((d // BLK,))],
+        compiler_params=params(63, collective_id=3),
         cost_estimate=cost(FOUR, 20),
-    )(o, dy, *pieces)
+    )(o, *pieces)
 
 
 class PairSum:
@@ -847,11 +863,11 @@
 
 HERE = 0, 0, 0
 LINKS = "xyud"
-ORDERS = "zxy", "zyx", "yxz", "zxy"
-WO_CUTS, WQ_CUTS = (0, 3, 7, 8), (0, 3, 6, 8)
-SIZES = 8.4, 9.8, 4.2, 2.8
+ORDERS = "zxy", "zyx", "yxz", "zyx"
+WO_CUTS, WQ_CUTS = (0, 2, 6, 8), (0, 3, 6, 8)
+SIZES = 7.0, 9.8, 5.6, 2.8
 LATENCY, TILES_FROM, TILE_EVERY = 3.0, 14.0, 8.0
-SUM_AT = 30.0, 41.0, 52.0, 63.0
+SUM_AT = 25.0, 31.0, 37.0, 43.0
 
 
 def onward(order, key):
@@ -1094,10 +1110,9 @@
         normed, kv_home = project(hidden.reshape(n_rows, d_model), gain[NEW], w_k, w_v, cos_f, sin_f)
         pos_u = unite(positions)
         kv_home = kv_home.reshape((TWO,) * 5 + (CHUNK, HEAD_DIM))
-        kv_all, q_u, do_u = exchange(kv_home, normed, dy_flat, cos_f, sin_f, w_q, w_o)
-        dy_quad = grad_out.reshape((TWO,) * 3 + (CHUNK, d_model))
-        dy_pieces, q_u = lax.optimization_barrier(([rows_of(grad_out, d) for d in relations], q_u))
-        dy_pieces = swap(dy_pieces)[1:]
+        kv_all, q_u, do_u, *dy_rows = exchange(kv_home, normed, dy_flat, cos_f, sin_f, w_q, w_o)
+        dy_rows = [a.reshape(TWO, TWO, CHUNK, d_model) for a in dy_rows]
+        dy_pieces = swap([dy_rows[d % TWO] for d in relations])
 
         member = quad ^ jnp.arange(FOUR)
         front, back = ((m[:, NEW] * CHUNK + jnp.arange(CHUNK)[NEW]).reshape(BLK) for m in (member, 3 - member))
@@ -1116,7 +1131,7 @@
         koff = offsets[:, NEW]
         attn_u, lse = flash_fwd(tab, q_u, kv_all, start_r, q_index_r, koff)
 
-        wo_keep, wo_away = wo_terms(attn_u, dy_quad, dy_pieces)
+        wo_keep, wo_away = wo_terms(attn_u, dy_pieces)
         wo_come = perm(wo_away, flip_pairs(FOUR))
         do_u, wo_keep = lax.optimization_barrier((do_u, wo_keep))
         dq_u, dkv = flash_bwd(tab, q_u, do_u, attn_u, kv_all, lse, start_r, q_index_r, koff, cos_ut, sin_ut)
@@ -1126,7 +1141,7 @@
         wo_own, dkv_own, wq_own, block_out, d_part, h_u = reduce_pairs(
             [wo_sum, dkv.reshape(FOUR, TWO, -1, HEAD_DIM)],
             [wo_sum.shape[1:], (dkv.size // N_PAIRS // HEAD_DIM, HEAD_DIM), (d_model // TWO // N_PAIRS, wide)],
-            (TWO, 8, FOUR),
+            (TWO, 8, 8),
             ("z", "", "core"),
             TWO,
             Products,

time: 579 us -> 578 us (level)
  local copies, waits for them, and re-layouts: 45.7 us -> 31.9 us
    unnamed x59 -> x25, local copies, waits for them, and re-layouts: 41.2 us -> 29.5 us
  transfers between devices with their start and end apart: 7 -> 7, of which waited for: 3 -> 3; matrix products, arithmetic and copies ran while one was open for 1% -> 2% of each run, Pallas kernels for 18% -> 19%
where the time goes in v7:
time: 578 us; the launch traced here: 576 us
  Pallas kernels  476 us (82%)
  waiting for transfers between devices  48 us (8%)
  local copies, waits for them, and re-layouts  31.9 us (6%)
  other arithmetic  11.7 us (2%)
  starting transfers between devices  7.78 us (1%)
    pallas_call x1, Pallas kernels, reduce_pairs(): pl.pallas_call(functools.partial(reduce_kernel, cuts, kinds, work), name=...  182 us
    pallas_call x1, Pallas kernels, gather_all(): pl.pallas_call(gather_kernel, name='gather_all', out_shape=[jax.ShapeDtyp...  171 us
    pallas_call x1, Pallas kernels, exchange(): pl.pallas_call(exchange_kernel, name='exchange', out_shape=(jax.ShapeDtyp...  62.7 us
    ppermute x7, waiting for transfers between devices, perm(): return lax.ppermute(x, 'cp', pairs)  48 us
    unnamed x25, local copies, waits for them, and re-layouts  29.5 us
    pallas_call x1, Pallas kernels, flash_bwd(): pl.pallas_call(bwd_kernel, name='attn_bwd', out_shape=(jax.ShapeDtypeStru...  23.4 us
    pallas_call x1, Pallas kernels, flash_fwd(): pl.pallas_call(fwd_kernel, name='attn_fwd', out_shape=(jax.ShapeDtypeStru...  18 us
    pallas_call x1, Pallas kernels, wo_terms(): pl.pallas_call(wo_kernel, name='wo_terms', out_shape=[jax.ShapeDtypeStruc...  14 us
  transfers between devices with their start and end apart: 7, of which 3 were waited for; matrix products, arithmetic and copies ran while one was open for 2% of the time, Pallas kernels for 19%

profile of v7, /device:TPU:0, one launch (start us, length us, event | category | flops | bytes accessed | tf_op | source)
XLA Modules:
  0.0 576.4 jit_solution(1088095260619535372)
XLA Ops:
  0.6 0.8 reshape.269
  1.4 2.4 collective-permute-start.2
  3.8 0.7 collective-permute-start
  4.5 0.7 convert_bitcast_fusion
  5.2 1.3 broadcast_in_dim.9
  6.5 1.0 fusion
  7.5 1.0 pad_maximum_fusion
  8.5 4.9 norm_kv.1
  13.4 62.7 %exchange.1 = (bf16[8,2,2,2,256,128]{5,4,3,2,1,0:T(8,128)(2,1)}, bf16[2,2,256,1024]{3,2,1,0:T(8,128)(2,1)}, bf16[2,2,256,1024]{3,2,1,0:T(8,128)(2,1)}, bf16[256,2048]{1,0:T(8,128)(2,1)}, bf16[256,2048]{1,0:T(8,128)(2,1)}) custom-call(bf16[2,2,2,2,2,64,128]{6,5,4,3,2,1,0:T(8,128)(2,1)} %bitcast.35, bf16[512,2048]{1,0:T(8,128)(2,1)} %get-tuple-element.35.refs_1_, ...), custom_call_target="tpu_custom_call" | custom-call | flops 1000000000 | bytes 20971520 | tf_op jit(solution)/shard_map/exchange/pallas_call | solution.py:451
  76.1 1.4 collective-permute-start.5
  77.5 0.8 collective-permute-start.3
  79.6 22.2 %collective-permute-done.1 = s32[2,2,64]{2,1,0:T(2,128)S(1)} collective-permute-done((s32[2,2,64]{2,1,0:T(2,128)S(1)}, s32[2,2,64]{2,1,0:T(2,128)S(1)}, u32[]{:S(2)}, u32[]{:S(2)}) %collective-permute-start.1) | collective-permute-done | bytes 1056 | tf_op jit(solution)/shard_map/ppermute | solution.py:1079
  101.9 1.9 collective-permute-start.4
  104.2 0.7 pad_add_fusion.2.tab
  106.1 18.0 %attn_fwd.1 = (bf16[2,2,256,1024]{3,2,1,0:T(8,128)(2,1)}, f32[2,2,8,1,256]{4,3,2,1,0:T(1,128)}) custom-call(s32[10]{0:T(128)} %pad_add_fusion.2.tab, bf16[2,2,256,1024]{3,2,1,0:T(8,128)(2,1)} %get-tuple-element.37.q_ref, bf16[8,2,2,2,256,128]{5,4,3,2,1,0:T(8,128)(2,1)} %get-tuple-element.38.kv_ref, s32[2,2,1,256]{3,2,1,0:T(1,128)} %broadcast_subtract_fusion.st_ref, ...), custom_call_target="tpu_custom_call" | custom-call | flops 20000000000 | bytes 16777216 | tf_op jit(solution)/shard_map/attn_fwd/pallas_call | solution.py:211
  124.2 1.8 multiply_sine_fusion
  125.9 1.7 collective-permute-done.4.refs_3_
  127.7 14.0 %wo_terms.1 = (f32[4,64,2048]{2,1,0:T(8,128)}, f32[4,64,2048]{2,1,0:T(8,128)}) custom-call(bf16[2,2,256,1024]{3,2,1,0:T(8,128)(2,1)} %get-tuple-element.39.refs_0_.o_ref.refs_2_, bf16[2,2,64,2048]{3,2,1,0:T(8,128)(2,1)} %bitcast.45, bf16[2,2,64,2048]{3,2,1,0:T(8,128)(2,1)} %collective-permute-done.3.refs_2_, ...), custom_call_target="tpu_custom_call" | custom-call | flops 4000000000 | bytes 20971520 | tf_op jit(solution)/shard_map/wo_terms/pallas_call | solution.py:513
  142.2 23.4 %attn_bwd.1 = (bf16[2,2,256,1024]{3,2,1,0:T(8,128)(2,1)}, f32[8,2,2,2,256,128]{5,4,3,2,1,0:T(8,128)}) custom-call(s32[10]{0:T(128)} %pad_add_fusion.2.tab, bf16[2,2,256,1024]{3,2,1,0:T(8,128)(2,1)} %get-tuple-element.37.q_ref, bf16[2,2,256,1024]{3,2,1,0:T(8,128)(2,1)} %get-tuple-element.45.do_ref, ...), custom_call_target="tpu_custom_call" | custom-call | flops 49999998976 | bytes 33554432 | tf_op jit(solution)/shard_map/attn_bwd/pallas_call | solution.py:230
  165.6 24.0 %collective-permute-done.6 = f32[4,64,2048]{2,1,0:T(8,128)} collective-permute-done((f32[4,64,2048]{2,1,0:T(8,128)}, f32[4,64,2048]{2,1,0:T(8,128)}, u32[]{:S(2)}, u32[]{:S(2)}) %collective-permute-start.6) | collective-permute-done | bytes 2097184 | tf_op jit(solution)/shard_map/ppermute | solution.py:1079
  189.7 3.9 add.133.refs_0_
  193.6 182.2 %reduce_pairs.1 = (f32[64,2048]{1,0:T(8,128)}, f32[2048,128]{1,0:T(8,128)}, f32[128,1024]{1,0:T(8,128)}, bf16[512,2048]{1,0:T(8,128)(2,1)}, f32[512,2048]{1,0:T(8,128)}, /*index=5*/bf16[2,2,256,2048]{3,2,1,0:T(8,128)(2,1)}) custom-call(f32[4,64,2048]{2,1,0:T(8,128)} %add.133.refs_0_, f32[4,2,2048,128]{3,2,1,0:T(8,128)} %bitcast.26, ...), custom_call_target="tpu_custom_call" | custom-call | flops 1000000000 | bytes 20971520 | tf_op jit(solution)/shard_map/reduce_pairs/pallas_call | solution.py:852
  375.8 171.1 %gather_all.1 = (f32[2048,2048]{1,0:T(8,128)}, f32[2048,2048]{1,0:T(8,128)}, f32[2048,256]{1,0:T(8,128)}, f32[2048,256]{1,0:T(8,128)}, bf16[512,2048]{1,0:T(8,128)(2,1)}, /*index=5*/f32[1,2048]{1,0:T(1,128)}) custom-call(f32[64,2048]{1,0:T(8,128)} %get-tuple-element.50.refs_0_, f32[128,1024]{1,0:T(8,128)} %get-tuple-element.51.refs_1_, ...), custom_call_target="tpu_custom_call" | custom-call | flops 1000000000 | bytes 79691776 | tf_op jit(solution)/shard_map/gather_all/pallas_call | solution.py:1065
  546.9 1.3 copy.23
  548.2 1.0 copy-done.3
  549.3 1.3 copy.24
  550.6 14.6 %copy.25 = f32[2048,2048]{1,0:T(8,128)} copy(f32[2048,2048]{1,0:T(8,128)} %get-tuple-element.87) | data formatting | bytes 33554432
  565.2 1.3 copy.26
  566.5 1.8 copy-done.1
  568.3 1.3 copy.27
  569.6 6.2 %copy.28 = f32[2048,2048]{1,0:T(8,128)} copy(f32[2048,2048]{1,0:T(8,128)S(1)} %bitcast.25) | data formatting | bytes 33554432
  575.8 0.6 copy.29
  (45 shorter events, 3.7 us)
Async XLA Ops:
  1.4 102.3 %collective-permute-start.2 = (s32[2,2,64]{2,1,0:T(2,128)S(1)}, s32[2,2,64]{2,1,0:T(2,128)S(1)}, u32[]{:S(2)}, u32[]{:S(2)}) collective-permute-start(s32[2,2,64]{2,1,0:T(2,128)S(1)} %get-tuple-element.68), channel_id=1, source_target_pairs={{0,3},{1,2},{2,1},{3,0},{4,7},{5,6},{6,5},{7,4},{8,11},{9,10},{10,... | collective-permute-start | bytes 3080 | tf_op jit(solution)/shard_map/ppermute | solution.py:1079
  3.8 99.9 %collective-permute-start = (s32[2,2,64]{2,1,0:T(2,128)S(1)}, s32[2,2,64]{2,1,0:T(2,128)S(1)}, u32[]{:S(2)}, u32[]{:S(2)}) collective-permute-start(s32[2,2,64]{2,1,0:T(2,128)S(1)} %get-tuple-element.68), channel_id=1, source_target_pairs={{0,1},{1,0},{2,3},{3,2},{4,5},{5,4},{6,7},{7,6},{8,9},{9,8},{10,11... | collective-permute-start | bytes 3080 | tf_op jit(solution)/shard_map/ppermute | solution.py:1079
  76.1 51.6 %collective-permute-start.5 = (bf16[2,2,64,2048]{3,2,1,0:T(8,128)(2,1)}, bf16[2,2,64,2048]{3,2,1,0:T(8,128)(2,1)}, u32[]{:S(2)}, u32[]{:S(2)}) collective-permute-start(bf16[2,2,64,2048]{3,2,1,0:T(8,128)(2,1)} %bitcast.46), channel_id=1, source_target_pairs={{0,3},{1,2},{2,1},{3,0},{4,7},{5,6},{6,5},{7,4},{8,11},{9,10},{10,... | collective-permute-start | bytes 3145736 | tf_op jit(solution)/shard_map/ppermute | solution.py:1079
  77.5 50.1 %collective-permute-start.3 = (bf16[2,2,64,2048]{3,2,1,0:T(8,128)(2,1)}, bf16[2,2,64,2048]{3,2,1,0:T(8,128)(2,1)}, u32[]{:S(2)}, u32[]{:S(2)}) collective-permute-start(bf16[2,2,64,2048]{3,2,1,0:T(8,128)(2,1)} %bitcast.47), channel_id=1, source_target_pairs={{0,1},{1,0},{2,3},{3,2},{4,5},{5,4},{6,7},{7,6},{8,9},{9,8},{10,11... | collective-permute-start | bytes 3145736 | tf_op jit(solution)/shard_map/ppermute | solution.py:1079
  78.3 23.6 %collective-permute-start.1 = (s32[2,2,64]{2,1,0:T(2,128)S(1)}, s32[2,2,64]{2,1,0:T(2,128)S(1)}, u32[]{:S(2)}, u32[]{:S(2)}) collective-permute-start(s32[2,2,64]{2,1,0:T(2,128)S(1)} %bitcast.39), channel_id=1, source_target_pairs={{0,2},{1,3},{2,0},{3,1},{4,6},{5,7},{6,4},{7,5},{8,10},{9,11},{10,... | collective-permute-start | bytes 3080 | tf_op jit(solution)/shard_map/ppermute | solution.py:1079
  101.9 25.8 %collective-permute-start.4 = (bf16[2,2,64,2048]{3,2,1,0:T(8,128)(2,1)}, bf16[2,2,64,2048]{3,2,1,0:T(8,128)(2,1)}, u32[]{:S(2)}, u32[]{:S(2)}) collective-permute-start(bf16[2,2,64,2048]{3,2,1,0:T(8,128)(2,1)} %bitcast.44), channel_id=1, source_target_pairs={{0,2},{1,3},{2,0},{3,1},{4,6},{5,7},{6,4},{7,5},{8,10},{9,11},{10,... | collective-permute-start | bytes 3145736 | tf_op jit(solution)/shard_map/ppermute | solution.py:1079
  141.6 48.0 %collective-permute-start.6 = (f32[4,64,2048]{2,1,0:T(8,128)}, f32[4,64,2048]{2,1,0:T(8,128)}, u32[]{:S(2)}, u32[]{:S(2)}) collective-permute-start(f32[4,64,2048]{2,1,0:T(8,128)} %get-tuple-element.44), channel_id=1, source_target_pairs={{0,4},{1,5},{2,6},{3,7},{4,0},{5,1},{6,2},{7,3},{8,12},{9,13},{10,... | collective-permute-start | bytes 6291464 | tf_op jit(solution)/shard_map/ppermute | solution.py:1079
  375.7 171.2 %copy-start = (bf16[512,2048]{1,0:T(8,128)(2,1)S(1)}, bf16[512,2048]{1,0:T(8,128)(2,1)}, u32[]{:S(2)}) copy-start(bf16[512,2048]{1,0:T(8,128)(2,1)} %get-tuple-element.49) | copy-start | bytes 6291460
  546.9 2.3 copy-start.3
  549.3 20.4 %slice-start = ((s8[16777216]{0:T(1024)(128)(4,1)}), s8[4194304]{0:T(1024)(128)(4,1)S(1)}, s32[]{:S(2)}) async-start(s8[16777216]{0:T(1024)(128)(4,1)} %bitcast.24), calls=%async_computation | async-start | bytes 8388608
  550.6 14.6 %copy-start.2 = (f32[2048,256]{1,0:T(8,128)S(1)}, f32[2048,256]{1,0:T(8,128)}, u32[]{:S(2)}) copy-start(f32[2048,256]{1,0:T(8,128)} %get-tuple-element.88) | copy-start | bytes 6291460
  550.6 19.0 %slice-start.1 = ((s8[16777216]{0:T(1024)(128)(4,1)}), s8[4194304]{0:T(1024)(128)(4,1)S(1)}, s32[]{:S(2)}) async-start(s8[16777216]{0:T(1024)(128)(4,1)} %bitcast.24), calls=%async_computation.1 | async-start | bytes 8388608
  550.6 19.0 %slice-start.2 = ((s8[16777216]{0:T(1024)(128)(4,1)}), s8[4194304]{0:T(1024)(128)(4,1)S(1)}, s32[]{:S(2)}) async-start(s8[16777216]{0:T(1024)(128)(4,1)} %bitcast.24), calls=%async_computation.2 | async-start | bytes 8388608
  550.6 19.0 %slice-start.3 = ((s8[16777216]{0:T(1024)(128)(4,1)}), s8[4194304]{0:T(1024)(128)(4,1)S(1)}, s32[]{:S(2)}) async-start(s8[16777216]{0:T(1024)(128)(4,1)} %bitcast.24), calls=%async_computation.3 | async-start | bytes 8388608
  565.2 3.1 copy-start.1
  569.6 6.2 %copy-start.4 = (f32[1,2048]{1,0:T(1,128)S(1)}, f32[1,2048]{1,0:T(1,128)}, u32[]{:S(2)}) copy-start(f32[1,2048]{1,0:T(1,128)} %get-tuple-element.60) | copy-start | bytes 24580

commit v8 on v7

--- a/solution.py
+++ b/solution.py
@@ -67,10 +67,6 @@
 
 def dot_t(a, b):
     return dot(a, b, (1,), (1,))
-
-
-def pick(x, index, axis):
-    return lax.dynamic_index_in_dim(x, index, axis, keepdims=False)
 
 
 def steps(tab, body):
@@ -341,7 +337,7 @@
 
 def exchange_kernel(*refs):
     take = taker(refs)
-    kv_ref, h_ref, dy_ref, cos_ref, sin_ref, wq_ref, wo_ref, kv_all, q_u, do_u, *dy_rows = take(12)
+    kv_ref, h_ref, dy_ref, pos_ref, cos_ref, sin_ref, wq_ref, wo_ref, kv_all, q_u, do_u, pos_u, *dy_rows = take(14)
     own_sem, quad_s, quad_r, z_s, z_r, y_s, y_r, q_home, do_home, wq_buf, wo_buf, w_sem, dy_sem = take(len(refs))
     me = lax.axis_index("cp")
     z, y, x, core = place(me)
@@ -351,9 +347,11 @@
 
     def source(a, d):
         xx, cc = 1 - x if d // TWO else x, 1 - core if d % TWO else core
-        return (kv_ref, q_home, do_home)[a].at[xx, cc]
+        return pos_ref.at[cc] if a == 3 else (kv_ref, q_home, do_home)[a].at[xx, cc]
 
     def target(a, d):
+        if a == 3:
+            return pos_u.at[d]
         tok = pl.ds(d * CHUNK, CHUNK)
         return kv_all.at[me // FOUR, :, :, :, tok] if a == 0 else (q_u, do_u)[a - 1].at[:, :, tok]
 
@@ -406,9 +404,10 @@
     half = dy_ref.shape[0] // TWO
     for i, out in enumerate(dy_rows):
         pltpu.make_async_copy(dy_ref.at[aligned(core if i == 0 else 1 - core, half)], out, dy_sem.at[i]).start()
-    for d in (1, TWO, 3):
-        quad_copy(0, d).start()
-    own_copy(0).start()
+    for a in (0, 3):
+        for d in (1, TWO, 3):
+            quad_copy(a, d).start()
+        own_copy(a).start()
     for a, (fetch, use) in enumerate(((fetch_q, query), (fetch_o, pull)), 1):
         for near in range(TWO):
             tiled(n, fetch, use, n * (x if near else 1 - x))
@@ -428,36 +427,37 @@
             pl.when(on)(z_copy(part, dz, d).wait_send)
         pl.when(line.held(dz))(y_copy(part, dz, 1 - y).wait_recv)
         pl.when(line.held(dz))(y_copy(part, dz).wait_send)
-    for a in range(3):
+    for a in range(FOUR):
         for d in (1, TWO, 3):
             quad_copy(a, d).wait_send()
             if a > 0:
                 quad_copy(a, d).wait_recv()
-    own_copy(1).wait()
-    own_copy(TWO).wait()
+    for a in (1, TWO, 3):
+        own_copy(a).wait()
     for i, out in enumerate(dy_rows):
         pltpu.make_async_copy(dy_ref.at[aligned(core if i == 0 else 1 - core, half)], out, dy_sem.at[i]).wait()
 
 
-def exchange(kv, h, dy, cos_f, sin_f, w_q, w_o):
+def exchange(kv, h, dy, pos, cos_f, sin_f, w_q, w_o):
     dma = pltpu.SemaphoreType.DMA
     vmem, hbm = pl.BlockSpec(memory_space=pltpu.VMEM), pl.BlockSpec(memory_space=pl.ANY)
     wide = w_q.shape[1] // TWO
     unit = jax.ShapeDtypeStruct((TWO, TWO, BLK, wide), BF16)
+    pos_quad = jax.ShapeDtypeStruct((FOUR,) + pos.shape[1:], pos.dtype)
     dy_half = jax.ShapeDtypeStruct((dy.shape[0] // TWO, dy.shape[1]), BF16)
     home = pltpu.VMEM((TWO,) * FOUR + (CHUNK, wide), BF16)
-    sems = [dma((3,))] + [dma((3, FOUR))] * TWO + [dma((TWO, TWO, 7))] + [dma((TWO, 7))] * 3
+    sems = [dma((FOUR,))] + [dma((FOUR, FOUR))] * TWO + [dma((TWO, TWO, 7))] + [dma((TWO, 7))] * 3
     bufs = [pltpu.VMEM((TWO,) + b, BF16) for b in ((w_q.shape[0], BLK), (BLK, w_o.shape[1]))]
     return pl.pallas_call(
         exchange_kernel,
         name="exchange",
-        out_shape=(jax.ShapeDtypeStruct((N_PAIRS,) + (TWO,) * 3 + (BLK, HEAD_DIM), BF16), unit, unit, dy_half, dy_half),
-        in_specs=[vmem] * 5 + [hbm] * TWO,
-        out_specs=[hbm] * 5,
+        out_shape=(jax.ShapeDtypeStruct((N_PAIRS,) + (TWO,) * 3 + (BLK, HEAD_DIM), BF16), unit, unit, pos_quad, dy_half, dy_half),
+        in_specs=[vmem] * 6 + [hbm] * TWO,
+        out_specs=[hbm] * 6,
         scratch_shapes=sems + [home, home] + bufs + [dma((TWO, TWO)), dma((TWO,))],
         compiler_params=params(63, collective_id=1),
         cost_estimate=cost(1, 20),
-    )(kv, h, dy, cos_f, sin_f, w_q, w_o)
+    )(kv, h, dy, pos, cos_f, sin_f, w_q, w_o)
 
 
 def taker(refs):
@@ -924,8 +924,8 @@
     take = taker(refs)
     wo_ref, wq_ref, dkv_ref, cos_ref, sin_ref, h_ref = take(6)
     grad_ins, outs, (dx_ref, dgain_ref) = take(6), take(FOUR), take(TWO)
-    own_sem, send_sem, come_sem, core_sem, all_terms, g_s, g_r = take(7)
-    terms, wkv_own, wkv_ref, h_own, dk_u, dv_u = take(6)
+    own_sem, send_sem, come_sem, core_sem, put_sem, all_terms, g_s, g_r = take(8)
+    terms, wkv_own, wkv_ref, h_own, dk_u, dv_u, *stores = take(10)
     buffers, sems, refs = take(FOUR), take(7), take(len(refs))
     me = lax.axis_index("cp")
     z, y, x, core = place(me)
@@ -939,13 +939,14 @@
     wkv = PairSum(me, "core", 1, wkv_ref, wkv_own, buffers, [r.at[0] for r in sems])
 
     def windows(part, zz, yy, xx, cc):
-        pair = TWO * zz + yy
+        chip = (TWO * zz + yy) * TWO + xx
         wide, narrow = wq_ref.shape[1], wkv_own.shape[1] // TWO
-        wo_at, wq_at = ((xx * TWO + cc) * N_PAIRS + pair) * wo_ref.shape[0], (cc * N_PAIRS + pair) * wq_ref.shape[0]
+        wo_at = ((xx * TWO + cc) * N_PAIRS + chip // TWO) * wo_ref.shape[0]
+        wq_at = (cc * N_PAIRS + chip // TWO) * wq_ref.shape[0]
         if part == 3:
-            for i, out in enumerate(outs[TWO:]):
-                cols = pl.ds(xx * narrow, narrow)
-                yield wkv_own.at[:, head_slice(i)], out.at[pl.ds(wq_at, wkv_own.shape[0]), cols]
+            for i, (store, out) in enumerate(zip(stores[TWO:], outs[TWO:])):
+                window = out.at[pl.ds(wq_at, wkv_own.shape[0]), pl.ds(xx * narrow, narrow)]
+                yield wkv_own.at[:, head_slice(i)], store.at[chip], window
             return
 
         def cut(ref, cuts):
@@ -953,25 +954,31 @@
             return first, last - first
 
         at, rows = cut(wo_ref, WO_CUTS)
-        yield wo_ref.at[pl.ds(at, rows)], outs[0].at[pl.ds(wo_at + at, rows)]
+        here = pl.ds(at, rows)
+        yield wo_ref.at[here], stores[0].at[chip, here], outs[0].at[pl.ds(wo_at + at, rows)]
         at, rows = cut(wq_ref, WQ_CUTS)
-        yield wq_ref.at[pl.ds(at, rows)], outs[1].at[pl.ds(wq_at + at, rows), pl.ds(xx * wide, wide)]
-
-    def block(part, key, cc=core):
+        here = pl.ds(at, rows)
+        yield wq_ref.at[here], stores[1].at[chip, here], outs[1].at[pl.ds(wq_at + at, rows), pl.ds(xx * wide, wide)]
+
+    def block(part, key):
         dz, ry, rx = key
-        return windows(part, z + dz, 1 - y if ry else y, 1 - x if rx else x, cc)
+        return windows(part, z + dz, 1 - y if ry else y, 1 - x if rx else x, core)
 
     def index(part, key):
         return (part, key[0] + 3) + key[1:]
 
     def send(part, key, link, there):
-        arrive = (core_sem if link is None else come_sem).at[index(part, there)]
-        for shard, window in block(part, key):
-            src = window if any(key) else shard
-            remote(src, window, send_sem.at[index(part, key) + (LINKS.find(link or "-") + 1,)], arrive, to.get(link, partner)).start()
+        sent = send_sem.at[index(part, key) + (LINKS.find(link or "-") + 1,)]
+        for shard, store, window in block(part, key):
+            src = store if any(key) else shard
+            if link:
+                remote(src, store, sent, come_sem.at[index(part, there)], to[link]).start()
+            else:
+                remote(src, window, sent, core_sem.at[index(part, key)], partner).start()
+                pltpu.make_async_copy(src, window, put_sem.at[index(part, key)]).start()
 
     def whole(part, send, arrive):
-        size = sum(shard.size for shard, _ in block(part, HERE)) // outs[0].shape[1]
+        size = sum(shard.size for shard, _, _ in block(part, HERE)) // outs[0].shape[1]
         dst = outs[0].at[pl.ds(0, size)]
         return remote(dst, dst, send, arrive, me)
 
@@ -992,13 +999,6 @@
     def term_copy(i, d):
         return remote(terms, all_terms.at[i], g_s.at[i], g_r.at[i], d)
 
-    owns = []
-
-    def put_own(part):
-        for shard, window in block(part, HERE):
-            owns.append(pltpu.make_async_copy(shard, window, own_sem.at[len(owns)]))
-            owns[-1].start()
-
     def tile(t):
         job.tile(t)
         if t == job.tiles - 1:
@@ -1007,8 +1007,6 @@
 
     def sum_step(h):
         wkv.step(0, h)
-        if h == 3:
-            put_own(3)
 
     steps = [(TILES_FROM + t * TILE_EVERY, functools.partial(tile, t)) for t in range(HiddenGradient.tiles)]
     steps += [(at, functools.partial(sum_step, h)) for h, at in enumerate(SUM_AT)]
@@ -1021,8 +1019,6 @@
     load_h.wait()
     wkv_terms(h_own, dk_u, dv_u, ((wkv_ref, 1 - core), (buffers[0], core)))
     wkv.begin(0)
-    for part in range(3):
-        put_own(part)
     wkv.loaded(0)
     for now, part, key in events:
         while steps and steps[0][0] <= now:
@@ -1033,8 +1029,6 @@
             pass_on(part, key)
         elif part == 3:
             pass_on(part, key)
-    for o in owns:
-        o.wait()
     total_gain = terms[...]
     for i, d in others:
         term_copy(i, d).wait_recv()
@@ -1043,7 +1037,8 @@
     for i, d in others:
         term_copy(i, d).wait_send()
     for _, part, key in events:
-        when(line.held(key[0]), whole(part, own_sem.at[0], core_sem.at[index(part, key)]).wait_recv)
+        for sem in (core_sem, put_sem):
+            when(line.held(key[0]), whole(part, own_sem.at[0], sem.at[index(part, key)]).wait_recv)
         for link, there, on in each_way(part, key):
             sent = send_sem.at[index(part, key) + (LINKS.find(link or "-") + 1,)]
             when(on, whole(part, sent, own_sem.at[0]).wait_send)
@@ -1058,10 +1053,12 @@
     parts = len(ORDERS)
     keys = (parts, 7, TWO, TWO)
     terms = 1, x.shape[1]
-    scratch = [dma((TWO * parts,)), dma(keys + (len(LINKS) + 1,)), dma(keys), dma(keys)]
+    scratch = [dma((1,)), dma(keys + (len(LINKS) + 1,)), dma(keys), dma(keys), dma(keys)]
     scratch += [pltpu.VMEM((32,) + terms, F32), dma((32,)), dma((32,)), pltpu.VMEM(terms, F32), pltpu.VMEM(block, F32)]
     scratch += [pltpu.VMEM((FOUR, TWO) + block, F32), pltpu.VMEM(h_u.shape, BF16)]
     scratch += [pltpu.VMEM((TWO, TWO, BLK, HEAD_DIM), BF16)] * TWO
+    chips = (TWO * N_PAIRS,)
+    scratch += [pltpu.VMEM(chips + b, F32) for b in (wo.shape, wq.shape) + ((block[0], HEAD_DIM),) * TWO]
     return pl.pallas_call(
         gather_kernel,
         name="gather_all",
@@ -1070,7 +1067,7 @@
         in_specs=[vmem] * 5 + [hbm] + [vmem] * 6,
         out_specs=[hbm] * len(shapes) + [vmem] * TWO,
         scratch_shapes=scratch + PairSum.scratch("core", block) + PairSum.sems(1, 1) + HiddenGradient.scratch(x),
-        compiler_params=params(56, collective_id=0),
+        compiler_params=params(63, collective_id=0),
         cost_estimate=cost(1, 76),
     )(wo, wq, dkv, cos_f, sin_f, h_u, part, w_k, w_v, x, dy, gain)
 
@@ -1089,28 +1086,22 @@
         n_rows = n_batch * n_tok
         wide = N_HEADS * HEAD_DIM
         me = lax.axis_index("cp")
-        _, _, _, core = place(me)
+        z, y, x, core = place(me)
         quad, pair = me % FOUR, me // FOUR
         relations = range(FOUR)
 
-        def rows_of(arr, d):
-            return pick(arr.reshape((TWO, TWO, TWO, CHUNK) + arr.shape[TWO:]), core ^ (d % TWO), 0)
-
         def swap(pieces):
             return [perm(p, flip_pairs(d)) if d else p for d, p in enumerate(pieces)]
-
-        def unite(arr):
-            joined = jnp.stack(swap([rows_of(arr, d) for d in relations]), axis=TWO)
-            return joined.reshape((TWO, TWO, BLK) + joined.shape[FOUR:])
 
         gain = norm_gain.astype(F32)
         cos_t, sin_t = rope_tables(positions.reshape(n_rows))
         cos_f, sin_f = jnp.hstack([cos_t, cos_t]), jnp.hstack([-sin_t, sin_t])
         dy_flat = grad_out.reshape(n_rows, d_model)
         normed, kv_home = project(hidden.reshape(n_rows, d_model), gain[NEW], w_k, w_v, cos_f, sin_f)
-        pos_u = unite(positions)
+        pos = jnp.pad(positions.reshape(TWO, TWO, n_tok), ((0, 0), (0, 6), (0, 0)))
         kv_home = kv_home.reshape((TWO,) * 5 + (CHUNK, HEAD_DIM))
-        kv_all, q_u, do_u, *dy_rows = exchange(kv_home, normed, dy_flat, cos_f, sin_f, w_q, w_o)
+        kv_all, q_u, do_u, pos_u, *dy_rows = exchange(kv_home, normed, dy_flat, pos, cos_f, sin_f, w_q, w_o)
+        pos_u = pos_u[:, :TWO].reshape((FOUR, TWO, TWO, CHUNK)).transpose(1, TWO, 0, 3).reshape(TWO, TWO, BLK)
         dy_rows = [a.reshape(TWO, TWO, CHUNK, d_model) for a in dy_rows]
         dy_pieces = swap([dy_rows[d % TWO] for d in relations])
 

time: 578 us -> 558 us (0.965)
  Pallas kernels: 476 us -> 461 us
    pallas_call x1, Pallas kernels: 182 us -> 164 us  [reduce_pairs(): pl.pallas_call(functools.partial(reduce_kernel, cuts, kinds, work), name=...]
    ppermute x7 -> x4, waiting for transfers between devices: 48 us -> 45.9 us  [perm(): return lax.ppermute(x, 'cp', pairs)]
    unnamed x25 -> x23, local copies, waits for them, and re-layouts: 29.5 us -> 30.4 us
  transfers between devices with their start and end apart: 7 -> 4, of which waited for: 3 -> 2; matrix products, arithmetic and copies ran while one was open for 2% -> 1% of each run, Pallas kernels for 19% -> 7%
where the time goes in v8:
time: 558 us; the launch traced here: 557 us
  Pallas kernels  461 us (83%)
  waiting for transfers between devices  45.9 us (8%)
  local copies, waits for them, and re-layouts  34.2 us (6%)
  other arithmetic  11.7 us (2%)
    pallas_call x1, Pallas kernels, gather_all(): pl.pallas_call(gather_kernel, name='gather_all', out_shape=[jax.ShapeDtyp...  172 us
    pallas_call x1, Pallas kernels, reduce_pairs(): pl.pallas_call(functools.partial(reduce_kernel, cuts, kinds, work), name=...  164 us
    pallas_call x1, Pallas kernels, exchange(): pl.pallas_call(exchange_kernel, name='exchange', out_shape=(jax.ShapeDtyp...  65.6 us
    ppermute x4, waiting for transfers between devices, perm(): return lax.ppermute(x, 'cp', pairs)  45.9 us
    unnamed x23, local copies, waits for them, and re-layouts  30.4 us
    pallas_call x1, Pallas kernels, flash_bwd(): pl.pallas_call(bwd_kernel, name='attn_bwd', out_shape=(jax.ShapeDtypeStru...  23.4 us
    pallas_call x1, Pallas kernels, flash_fwd(): pl.pallas_call(fwd_kernel, name='attn_fwd', out_shape=(jax.ShapeDtypeStru...  18 us
    pallas_call x1, Pallas kernels, wo_terms(): pl.pallas_call(wo_kernel, name='wo_terms', out_shape=[jax.ShapeDtypeStruc...  14 us
  transfers between devices with their start and end apart: 4, of which 2 were waited for; matrix products, arithmetic and copies ran while one was open for 1% of the time, Pallas kernels for 7%

profile of v8, /device:TPU:0, one launch (start us, length us, event | category | flops | bytes accessed | tf_op | source)
XLA Modules:
  0.0 556.8 jit_solution(5211384457832638808)
XLA Ops:
  0.6 0.7 convert_bitcast_fusion
  1.3 1.3 broadcast_in_dim.9
  2.6 1.3 pad.4.refs_3_
  3.9 1.0 fusion
  4.9 1.0 pad_maximum_fusion
  5.9 4.9 norm_kv.1
  10.8 65.6 %exchange.1 = (bf16[8,2,2,2,256,128]{5,4,3,2,1,0:T(8,128)(2,1)}, bf16[2,2,256,1024]{3,2,1,0:T(8,128)(2,1)}, bf16[2,2,256,1024]{3,2,1,0:T(8,128)(2,1)}, s32[4,8,1...) custom-call(bf16[2,2,2,2,2,64,128]{6,5,4,3,2,1,0:T(8,128)(2,1)} %bitcast.35, ...), custom_call_target="tpu_custom_call" | custom-call | flops 1000000000 | bytes 20971520 | tf_op jit(solution)/shard_map/exchange/pallas_call | solution.py:451
  76.6 1.9 collective-permute-start.1
  79.2 0.6 broadcast_in_dim.8.ko_ref
  79.8 0.7 slice.3
  80.7 0.2 subtract_reduce_fusion.1
  81.2 0.7 pad_add_fusion.1.tab
  81.8 0.6 broadcast_subtract_fusion.st_ref
  82.4 0.6 sub.45.qi_ref
  83.0 18.0 %attn_fwd.1 = (bf16[2,2,256,1024]{3,2,1,0:T(8,128)(2,1)}, f32[2,2,8,1,256]{4,3,2,1,0:T(1,128)}) custom-call(s32[10]{0:T(128)} %pad_add_fusion.1.tab, bf16[2,2,256,1024]{3,2,1,0:T(8,128)(2,1)} %get-tuple-element.39.q_ref, bf16[8,2,2,2,256,128]{5,4,3,2,1,0:T(8,128)(2,1)} %get-tuple-element.40.kv_ref, s32[2,2,1,256]{3,2,1,0:T(1,128)} %broadcast_subtract_fusion.st_ref, ...), custom_call_target="tpu_custom_call" | custom-call | flops 20000000000 | bytes 16777216 | tf_op jit(solution)/shard_map/attn_fwd/pallas_call | solution.py:207
  101.1 1.8 multiply_sine_fusion
  102.9 21.8 %collective-permute-done.1.refs_3_ = bf16[2,2,64,2048]{3,2,1,0:T(8,128)(2,1)} collective-permute-done((bf16[2,2,64,2048]{3,2,1,0:T(8,128)(2,1)}, bf16[2,2,64,2048]{3,2,1,0:T(8,128)(2,1)}, u32[]{:S(2)}, u32[]{:S(2)}) %collective-permute-start.1) | collective-permute-done | bytes 1048608 | tf_op jit(solution)/shard_map/ppermute | solution.py:1076
  124.7 14.0 %wo_terms.1 = (f32[4,64,2048]{2,1,0:T(8,128)}, f32[4,64,2048]{2,1,0:T(8,128)}) custom-call(bf16[2,2,256,1024]{3,2,1,0:T(8,128)(2,1)} %get-tuple-element.41.refs_0_.o_ref.refs_2_, bf16[2,2,64,2048]{3,2,1,0:T(8,128)(2,1)} %bitcast.41, bf16[2,2,64,2048]{3,2,1,0:T(8,128)(2,1)} %collective-permute-done.refs_2_, ...), custom_call_target="tpu_custom_call" | custom-call | flops 4000000000 | bytes 20971520 | tf_op jit(solution)/shard_map/wo_terms/pallas_call | solution.py:513
  138.7 0.6 collective-permute-start.3
  139.3 23.4 %attn_bwd.1 = (bf16[2,2,256,1024]{3,2,1,0:T(8,128)(2,1)}, f32[8,2,2,2,256,128]{5,4,3,2,1,0:T(8,128)}) custom-call(s32[10]{0:T(128)} %pad_add_fusion.1.tab, bf16[2,2,256,1024]{3,2,1,0:T(8,128)(2,1)} %get-tuple-element.39.q_ref, bf16[2,2,256,1024]{3,2,1,0:T(8,128)(2,1)} %get-tuple-element.47.do_ref, ...), custom_call_target="tpu_custom_call" | custom-call | flops 49999998976 | bytes 33554432 | tf_op jit(solution)/shard_map/attn_bwd/pallas_call | solution.py:226
  162.7 24.0 %collective-permute-done.3 = f32[4,64,2048]{2,1,0:T(8,128)} collective-permute-done((f32[4,64,2048]{2,1,0:T(8,128)}, f32[4,64,2048]{2,1,0:T(8,128)}, u32[]{:S(2)}, u32[]{:S(2)}) %collective-permute-start.3) | collective-permute-done | bytes 2097184 | tf_op jit(solution)/shard_map/ppermute | solution.py:1076
  186.7 3.9 add.124.refs_0_
  190.6 164.1 %reduce_pairs.1 = (f32[64,2048]{1,0:T(8,128)}, f32[2048,128]{1,0:T(8,128)}, f32[128,1024]{1,0:T(8,128)}, bf16[512,2048]{1,0:T(8,128)(2,1)}, f32[512,2048]{1,0:T(8,128)}, /*index=5*/bf16[2,2,256,2048]{3,2,1,0:T(8,128)(2,1)}) custom-call(f32[4,64,2048]{2,1,0:T(8,128)} %add.124.refs_0_, f32[4,2,2048,128]{3,2,1,0:T(8,128)} %bitcast.26, ...), custom_call_target="tpu_custom_call" | custom-call | flops 1000000000 | bytes 20971520 | tf_op jit(solution)/shard_map/reduce_pairs/pallas_call | solution.py:852
  354.7 171.6 %gather_all.1 = (f32[2048,2048]{1,0:T(8,128)}, f32[2048,2048]{1,0:T(8,128)}, f32[2048,256]{1,0:T(8,128)}, f32[2048,256]{1,0:T(8,128)}, bf16[512,2048]{1,0:T(8,128)(2,1)}, /*index=5*/f32[1,2048]{1,0:T(1,128)}) custom-call(f32[64,2048]{1,0:T(8,128)} %get-tuple-element.52.refs_0_, f32[128,1024]{1,0:T(8,128)} %get-tuple-element.53.refs_1_, ...), custom_call_target="tpu_custom_call" | custom-call | flops 1000000000 | bytes 79691776 | tf_op jit(solution)/shard_map/gather_all/pallas_call | solution.py:1062
  526.3 3.3 copy.30
  529.6 1.3 copy.31
  530.9 14.6 %copy.32 = f32[2048,2048]{1,0:T(8,128)} copy(f32[2048,2048]{1,0:T(8,128)} %get-tuple-element.87) | data formatting | bytes 33554432
  545.5 1.3 copy.33
  546.9 1.8 copy-done
  548.6 1.3 copy.34
  550.0 6.2 %copy.35 = f32[2048,2048]{1,0:T(8,128)} copy(f32[2048,2048]{1,0:T(8,128)S(1)} %bitcast.25) | data formatting | bytes 33554432
  556.2 0.6 copy.36
  (38 shorter events, 1.4 us)
Async XLA Ops:
  76.4 48.3 %collective-permute-start.2 = (bf16[2,2,64,2048]{3,2,1,0:T(8,128)(2,1)}, bf16[2,2,64,2048]{3,2,1,0:T(8,128)(2,1)}, u32[]{:S(2)}, u32[]{:S(2)}) collective-permute-start(bf16[2,2,64,2048]{3,2,1,0:T(8,128)(2,1)} %bitcast.42), channel_id=1, source_target_pairs={{0,3},{1,2},{2,1},{3,0},{4,7},{5,6},{6,5},{7,4},{8,11},{9,10},{10,... | collective-permute-start | bytes 3145736 | tf_op jit(solution)/shard_map/ppermute | solution.py:1076
  76.5 48.2 %collective-permute-start = (bf16[2,2,64,2048]{3,2,1,0:T(8,128)(2,1)}, bf16[2,2,64,2048]{3,2,1,0:T(8,128)(2,1)}, u32[]{:S(2)}, u32[]{:S(2)}) collective-permute-start(bf16[2,2,64,2048]{3,2,1,0:T(8,128)(2,1)} %bitcast.43), channel_id=1, source_target_pairs={{0,1},{1,0},{2,3},{3,2},{4,5},{5,4},{6,7},{7,6},{8,9},{9,8},{10,11... | collective-permute-start | bytes 3145736 | tf_op jit(solution)/shard_map/ppermute | solution.py:1076
  76.6 48.0 %collective-permute-start.1 = (bf16[2,2,64,2048]{3,2,1,0:T(8,128)(2,1)}, bf16[2,2,64,2048]{3,2,1,0:T(8,128)(2,1)}, u32[]{:S(2)}, u32[]{:S(2)}) collective-permute-start(bf16[2,2,64,2048]{3,2,1,0:T(8,128)(2,1)} %bitcast.40), channel_id=1, source_target_pairs={{0,2},{1,3},{2,0},{3,1},{4,6},{5,7},{6,4},{7,5},{8,10},{9,11},{10,... | collective-permute-start | bytes 3145736 | tf_op jit(solution)/shard_map/ppermute | solution.py:1076
  138.7 48.0 %collective-permute-start.3 = (f32[4,64,2048]{2,1,0:T(8,128)}, f32[4,64,2048]{2,1,0:T(8,128)}, u32[]{:S(2)}, u32[]{:S(2)}) collective-permute-start(f32[4,64,2048]{2,1,0:T(8,128)} %get-tuple-element.46), channel_id=1, source_target_pairs={{0,4},{1,5},{2,6},{3,7},{4,0},{5,1},{6,2},{7,3},{8,12},{9,13},{10,... | collective-permute-start | bytes 6291464 | tf_op jit(solution)/shard_map/ppermute | solution.py:1076
  526.3 3.3 copy-start.2
  529.6 20.4 %slice-start = ((s8[16777216]{0:T(1024)(128)(4,1)}), s8[4194304]{0:T(1024)(128)(4,1)S(1)}, s32[]{:S(2)}) async-start(s8[16777216]{0:T(1024)(128)(4,1)} %bitcast.24), calls=%async_computation | async-start | bytes 8388608
  530.9 14.6 %copy-start.1 = (f32[2048,256]{1,0:T(8,128)S(1)}, f32[2048,256]{1,0:T(8,128)}, u32[]{:S(2)}) copy-start(f32[2048,256]{1,0:T(8,128)} %get-tuple-element.88) | copy-start | bytes 6291460
  530.9 19.0 %slice-start.1 = ((s8[16777216]{0:T(1024)(128)(4,1)}), s8[4194304]{0:T(1024)(128)(4,1)S(1)}, s32[]{:S(2)}) async-start(s8[16777216]{0:T(1024)(128)(4,1)} %bitcast.24), calls=%async_computation.1 | async-start | bytes 8388608
  530.9 19.0 %slice-start.2 = ((s8[16777216]{0:T(1024)(128)(4,1)}), s8[4194304]{0:T(1024)(128)(4,1)S(1)}, s32[]{:S(2)}) async-start(s8[16777216]{0:T(1024)(128)(4,1)} %bitcast.24), calls=%async_computation.2 | async-start | bytes 8388608
  530.9 19.0 %slice-start.3 = ((s8[16777216]{0:T(1024)(128)(4,1)}), s8[4194304]{0:T(1024)(128)(4,1)S(1)}, s32[]{:S(2)}) async-start(s8[16777216]{0:T(1024)(128)(4,1)} %bitcast.24), calls=%async_computation.3 | async-start | bytes 8388608
  545.5 3.1 copy-start
  550.0 6.2 %copy-start.3 = (f32[1,2048]{1,0:T(1,128)S(1)}, f32[1,2048]{1,0:T(1,128)}, u32[]{:S(2)}) copy-start(f32[1,2048]{1,0:T(1,128)} %get-tuple-element.62) | copy-start | bytes 24580

commit v9 on v8

--- a/solution.py
+++ b/solution.py
@@ -269,7 +269,7 @@
         first_kernel,
         name="norm_kv",
         out_shape=(jax.ShapeDtypeStruct(x.shape, BF16), jax.ShapeDtypeStruct((TWO,) * 3 + (n, HEAD_DIM), BF16)),
-        compiler_params=params(63),
+        compiler_params=params(20),
         cost_estimate=cost(TWO, 7),
     )(x, gain, w_k, w_v, cos_f, sin_f)
 
@@ -541,10 +541,12 @@
         at = self.rows(j)
         return self.own.at[zz, self.y, at] if self.kind == "core" else self.own.at[zz, at]
 
-    def load(self, j):
+    def loads(self, j):
         at = self.rows(j)
-        src = self.src.at[:, at] if self.kind else self.src.at[:, self.y, at]
-        return pltpu.make_async_copy(src, self.own.at[:, at], self.load_sem.at[j])
+        if self.kind == "z":
+            pairs = zip(self.src, (self.own, self.from_y))
+            return [pltpu.make_async_copy(a.at[:, at], b.at[:, at], s.at[j]) for (a, b), s in zip(pairs, (self.load_sem, self.y_r))]
+        return [pltpu.make_async_copy(self.src.at[:, self.y, at], self.own.at[:, at], self.load_sem.at[j])]
 
     def core_copy(self, j):
         src, dst = (r.at[:, :, self.rows(j)] for r in (self.src, self.from_core))
@@ -563,13 +565,15 @@
         if self.kind == "core":
             self.core_copy(j).start()
             return
-        self.load(j).start()
+        for c in self.loads(j):
+            c.start()
         if not self.kind:
             self.y_copy(j).start()
 
     def loaded(self, j):
         if self.kind != "core":
-            self.load(j).wait()
+            for c in self.loads(j):
+                c.wait()
         else:
             self.core_copy(j).wait_recv()
             at = self.rows(j)
@@ -577,7 +581,12 @@
                 self.own[zz, :, at] += self.from_core[zz, :, at]
             self.y_copy(j).start()
         if self.kind == "z":
+            self.add_y(j)
             self.hop(j, 0)
+
+    def add_y(self, j):
+        for zz in range(FOUR):
+            self.mine(j, zz)[...] += self.from_y[zz, self.rows(j)]
 
     def relay(self, j, way, zz, add):
         if add:
@@ -599,8 +608,7 @@
     def step(self, j, h):
         if h == 0 and self.kind != "z":
             self.y_copy(j).wait_recv()
-            for zz in range(FOUR):
-                self.mine(j, zz)[...] += self.from_y[zz, self.rows(j)]
+            self.add_y(j)
             self.hop(j, 0)
         elif 0 < h < 3:
             self.hop(j, h)
@@ -629,7 +637,7 @@
     def scratch(kind, block):
         unused = pltpu.VMEM((8, HEAD_DIM), F32)
         own = pltpu.VMEM(((FOUR, TWO) if kind == "core" else (FOUR,)) + block, F32)
-        from_y = unused if kind == "z" else pltpu.VMEM((FOUR,) + block, F32)
+        from_y = pltpu.VMEM((FOUR,) + block, F32)
         return [own, own if kind == "core" else unused, from_y, pltpu.VMEM((TWO, 3) + block, F32)]
 
     @staticmethod
@@ -642,7 +650,8 @@
     n = len(cuts)
 
     take = taker(refs)
-    ins, more_in, outs, more_out, made = take(n - 1), take(work.ins), take(n), take(work.outs), take(1)
+    ins = [take(TWO) if k == "z" else take(1)[0] for k in kinds[:-1]]
+    more_in, outs, more_out, made = take(work.ins), take(n), take(work.outs), take(1)
     buffers, sems = [take(FOUR) for _ in kinds], take(7)
     me = lax.axis_index("cp")
     z, y, x, core = place(me)
@@ -711,7 +720,7 @@
     def __init__(self, me, ins, outs, scratch):
         attn, self.dq, hidden, normed, self.w_o, self.w_q = ins
         self.block_out, self.d_part, self.h_u = outs
-        self.attn_home, self.dq_home, self.buf_o, self.buf_q, self.h_own, *sems = scratch
+        self.attn_home, self.dq_home, self.buf_o, self.buf_q, stage, self.h_buf, *sems = scratch
         self.w_sem, self.load_sem, own_sem, quad_s, quad_r = sems
         _, _, _, core = place(me)
 
@@ -722,11 +731,8 @@
             return self.h_u.at[:, :, pl.ds(d * CHUNK, CHUNK)]
 
         self.h_copies = [remote(piece(d), tokens(d), quad_s.at[TWO, d], quad_r.at[TWO, d], quad_of(me)[d]) for d in (1, TWO, 3)]
-        self.h_mine = pltpu.make_async_copy(piece(0), self.h_own.at[:, :, pl.ds(0, CHUNK)], own_sem.at[TWO])
-        self.h_rest = pltpu.make_async_copy(
-            self.h_u.at[:, :, pl.ds(CHUNK, BLK - CHUNK)], self.h_own.at[:, :, pl.ds(CHUNK, BLK - CHUNK)], self.load_sem
-        )
-        self.h_back = pltpu.make_async_copy(self.h_own.at[:, :, pl.ds(0, CHUNK)], tokens(0), self.load_sem)
+        self.h_mine = pltpu.make_async_copy(piece(0), stage, own_sem.at[TWO])
+        self.h_back = pltpu.make_async_copy(stage, tokens(0), self.load_sem.at[0])
         self.residual = pltpu.make_async_copy(hidden, self.block_out, own_sem.at[3])
         self.residual.start()
         for c in self.h_copies:
@@ -744,8 +750,9 @@
         dma, d = pltpu.SemaphoreType.DMA, arrays[-1].shape[0]
         home = pltpu.VMEM((TWO,) * 3 + (CHUNK, d), BF16)
         buf = [pltpu.VMEM((TWO,) + b, BF16) for b in ((d, BLK), (BLK, d))]
-        unit = pltpu.VMEM((TWO, TWO, BLK, d), BF16)
-        return [home] * TWO + buf + [unit, dma((TWO, TWO)), dma(()), dma((FOUR,)), dma((3, FOUR)), dma((3, FOUR))]
+        tiles = [pltpu.VMEM((TWO, TWO) + b, BF16) for b in ((CHUNK, d), (TWO, BLK, BLK))]
+        sems = [dma((TWO, TWO)), dma((TWO,)), dma((FOUR,)), dma((3, FOUR)), dma((3, FOUR))]
+        return [home] * TWO + buf + tiles + sems
 
     @staticmethod
     def results(arrays):
@@ -784,16 +791,19 @@
         for c in self.h_copies:
             c.wait_recv()
         self.h_back.wait()
-        self.h_rest.start()
-        self.h_rest.wait()
         core = lax.rem(lax.axis_index("cp"), TWO)
         d_out = self.dq[...].reshape(-1, self.dq.shape[-1])
+
+        def fetch(t, slot):
+            return pltpu.make_async_copy(self.h_u.at[:, :, :, aligned(t)], self.h_buf.at[slot], self.load_sem.at[slot])
+
         for out, half in ((other, 1 - core), (own, core)):
 
-            @pl.loop(0, FOUR)
-            def _(zz, out=out, half=half):
-                h = self.h_own[:, :, :, aligned(half * FOUR + zz)].reshape(-1, BLK)
-                out[zz] = dot(h, d_out, (0,), (0,)).reshape(out.shape[1:])
+            def use(t, slot, out=out, half=half):
+                h = self.h_buf[slot].reshape(-1, BLK)
+                out[t - half * FOUR] = dot(h, d_out, (0,), (0,)).reshape(out.shape[1:])
+
+            tiled(FOUR, fetch, use, half * FOUR)
 
     def finish(self):
         for c in self.h_copies + self.homes:
@@ -866,6 +876,7 @@
 ORDERS = "zxy", "zyx", "yxz", "zyx"
 WO_CUTS, WQ_CUTS = (0, 2, 6, 8), (0, 3, 6, 8)
 SIZES = 7.0, 9.8, 5.6, 2.8
+GAIN_AT = 60.0, 72.0, 84.0, 96.0, 108.0
 LATENCY, TILES_FROM, TILE_EVERY = 3.0, 14.0, 8.0
 SUM_AT = 25.0, 31.0, 37.0, 43.0
 
@@ -924,7 +935,7 @@
     take = taker(refs)
     wo_ref, wq_ref, dkv_ref, cos_ref, sin_ref, h_ref = take(6)
     grad_ins, outs, (dx_ref, dgain_ref) = take(6), take(FOUR), take(TWO)
-    own_sem, send_sem, come_sem, core_sem, put_sem, all_terms, g_s, g_r = take(8)
+    own_sem, send_sem, come_sem, core_sem, put_sem, all_terms, totals, g_s, g_r = take(9)
     terms, wkv_own, wkv_ref, h_own, dk_u, dv_u, *stores = take(10)
     buffers, sems, refs = take(FOUR), take(7), take(len(refs))
     me = lax.axis_index("cp")
@@ -932,8 +943,7 @@
     line = Line(me)
     to = {"x": dev(z, y, 1 - x, core), "y": dev(z, 1 - y, x, core), "u": line.next[1], "d": line.next[-1]}
     partner = dev(z, y, x, 1 - core)
-    others = [(i, me ^ i) for i in range(1, all_terms.shape[0])]
-    meet([d for _, d in others])
+    meet(quad_of(me)[1:] + [to["y"]] + [dev(zz, y, x, core) for _, zz in z_peers(z)])
     load_h = pltpu.make_async_copy(h_ref, h_own, own_sem.at[0])
     load_h.start()
     wkv = PairSum(me, "core", 1, wkv_ref, wkv_own, buffers, [r.at[0] for r in sems])
@@ -996,20 +1006,27 @@
         for link, there, on in each_way(part, key):
             when(on, functools.partial(send, part, key, link, there))
 
-    def term_copy(i, d):
-        return remote(terms, all_terms.at[i], g_s.at[i], g_r.at[i], d)
+    def term_copy(i):
+        src = terms if i == 0 else totals.at[i - 1]
+        return remote(src, all_terms.at[i], g_s.at[i], g_r.at[i], me ^ (1 << i))
+
+    def add_terms(i):
+        term_copy(i).wait_recv()
+        totals[i] = (terms[...] if i == 0 else totals[i - 1]) + all_terms[i]
+        if i + 1 < len(GAIN_AT):
+            term_copy(i + 1).start()
 
     def tile(t):
         job.tile(t)
         if t == job.tiles - 1:
-            for i, d in others:
-                term_copy(i, d).start()
+            term_copy(0).start()
 
     def sum_step(h):
         wkv.step(0, h)
 
     steps = [(TILES_FROM + t * TILE_EVERY, functools.partial(tile, t)) for t in range(HiddenGradient.tiles)]
     steps += [(at, functools.partial(sum_step, h)) for h, at in enumerate(SUM_AT)]
+    steps += [(at, functools.partial(add_terms, i)) for i, at in enumerate(GAIN_AT)]
     steps.sort(key=lambda s: s[0])
     events = arrivals()
     for part in range(3):
@@ -1029,13 +1046,9 @@
             pass_on(part, key)
         elif part == 3:
             pass_on(part, key)
-    total_gain = terms[...]
-    for i, d in others:
-        term_copy(i, d).wait_recv()
-        total_gain += all_terms[i]
-    dgain_ref[...] = total_gain
-    for i, d in others:
-        term_copy(i, d).wait_send()
+    dgain_ref[...] = totals[len(GAIN_AT) - 1]
+    for i in range(len(GAIN_AT)):
+        term_copy(i).wait_send()
     for _, part, key in events:
         for sem in (core_sem, put_sem):
             when(line.held(key[0]), whole(part, own_sem.at[0], sem.at[index(part, key)]).wait_recv)
@@ -1054,7 +1067,8 @@
     keys = (parts, 7, TWO, TWO)
     terms = 1, x.shape[1]
     scratch = [dma((1,)), dma(keys + (len(LINKS) + 1,)), dma(keys), dma(keys), dma(keys)]
-    scratch += [pltpu.VMEM((32,) + terms, F32), dma((32,)), dma((32,)), pltpu.VMEM(terms, F32), pltpu.VMEM(block, F32)]
+    n = len(GAIN_AT)
+    scratch += [pltpu.VMEM((n,) + terms, F32)] * TWO + [dma((n,)), dma((n,)), pltpu.VMEM(terms, F32), pltpu.VMEM(block, F32)]
     scratch += [pltpu.VMEM((FOUR, TWO) + block, F32), pltpu.VMEM(h_u.shape, BF16)]
     scratch += [pltpu.VMEM((TWO, TWO, BLK, HEAD_DIM), BF16)] * TWO
     chips = (TWO * N_PAIRS,)
@@ -1126,12 +1140,11 @@
         wo_come = perm(wo_away, flip_pairs(FOUR))
         do_u, wo_keep = lax.optimization_barrier((do_u, wo_keep))
         dq_u, dkv = flash_bwd(tab, q_u, do_u, attn_u, kv_all, lse, start_r, q_index_r, koff, cos_ut, sin_ut)
-        wo_sum = wo_keep + wo_come
 
         x_flat = hidden.reshape(n_rows, d_model)
         wo_own, dkv_own, wq_own, block_out, d_part, h_u = reduce_pairs(
-            [wo_sum, dkv.reshape(FOUR, TWO, -1, HEAD_DIM)],
-            [wo_sum.shape[1:], (dkv.size // N_PAIRS // HEAD_DIM, HEAD_DIM), (d_model // TWO // N_PAIRS, wide)],
+            [wo_keep, wo_come, dkv.reshape(FOUR, TWO, -1, HEAD_DIM)],
+            [wo_keep.shape[1:], (dkv.size // N_PAIRS // HEAD_DIM, HEAD_DIM), (d_model // TWO // N_PAIRS, wide)],
             (TWO, 8, 8),
             ("z", "", "core"),
             TWO,

time: 558 us -> 554 us (level)
    unnamed x23 -> x39, local copies, waits for them, and re-layouts: 30.4 us -> 35.2 us
where the time goes in v9:
time: 554 us; the launch traced here: 552 us
  Pallas kernels  457 us (82%)
  waiting for transfers between devices  46 us (8%)
  local copies, waits for them, and re-layouts  38.9 us (7%)
  other arithmetic  6.43 us (1%)
    pallas_call x1, Pallas kernels, gather_all(): pl.pallas_call(gather_kernel, name='gather_all', out_shape=[jax.ShapeDtyp...  171 us
    pallas_call x1, Pallas kernels, reduce_pairs(): pl.pallas_call(functools.partial(reduce_kernel, cuts, kinds, work), name=...  164 us
    pallas_call x1, Pallas kernels, exchange(): pl.pallas_call(exchange_kernel, name='exchange', out_shape=(jax.ShapeDtyp...  65.6 us
    ppermute x4, waiting for transfers between devices, perm(): return lax.ppermute(x, 'cp', pairs)  46 us
    unnamed x39, local copies, waits for them, and re-layouts  35.2 us
    pallas_call x1, Pallas kernels, flash_bwd(): pl.pallas_call(bwd_kernel, name='attn_bwd', out_shape=(jax.ShapeDtypeStru...  23.4 us
    pallas_call x1, Pallas kernels, flash_fwd(): pl.pallas_call(fwd_kernel, name='attn_fwd', out_shape=(jax.ShapeDtypeStru...  18 us
    pallas_call x1, Pallas kernels, wo_terms(): pl.pallas_call(wo_kernel, name='wo_terms', out_shape=[jax.ShapeDtypeStruc...  14 us
  transfers between devices with their start and end apart: 4, of which 2 were waited for; matrix products, arithmetic and copies ran while one was open for 1% of the time, Pallas kernels for 7%

profile of v9, /device:TPU:0, one launch (start us, length us, event | category | flops | bytes accessed | tf_op | source)
XLA Modules:
  0.0 552.4 jit_solution(15086506640193894281)
XLA Ops:
  0.7 0.8 convert_bitcast_fusion
  1.5 0.7 broadcast_in_dim.9
  2.2 1.3 pad.4.refs_3_
  3.5 1.0 fusion
  4.7 1.4 copy-done.4
  6.1 1.2 copy-done.5
  7.3 1.8 norm_kv.1
  9.2 1.3 copy-done
  10.5 0.8 copy-done.6
  11.3 65.6 %exchange.1 = (bf16[8,2,2,2,256,128]{5,4,3,2,1,0:T(8,128)(2,1)}, bf16[2,2,256,1024]{3,2,1,0:T(8,128)(2,1)}, bf16[2,2,256,1024]{3,2,1,0:T(8,128)(2,1)}, s32[4,8,1...) custom-call(bf16[2,2,2,2,2,64,128]{6,5,4,3,2,1,0:T(8,128)(2,1)} %bitcast.28, ...), custom_call_target="tpu_custom_call" | custom-call | flops 1000000000 | bytes 20971520 | tf_op jit(solution)/shard_map/exchange/pallas_call | solution.py:451
  77.2 1.9 collective-permute-start.1
  79.7 0.6 broadcast_in_dim.8.ko_ref
  80.3 0.7 slice.3
  82.3 0.6 broadcast_subtract_fusion.st_ref
  82.9 0.6 sub.45.qi_ref
  83.5 18.0 %attn_fwd.1 = (bf16[2,2,256,1024]{3,2,1,0:T(8,128)(2,1)}, f32[2,2,8,1,256]{4,3,2,1,0:T(1,128)}) custom-call(s32[10]{0:T(128)} %pad_add_fusion.1.tab, bf16[2,2,256,1024]{3,2,1,0:T(8,128)(2,1)} %get-tuple-element.39.q_ref, bf16[8,2,2,2,256,128]{5,4,3,2,1,0:T(8,128)(2,1)} %get-tuple-element.40.kv_ref, s32[2,2,1,256]{3,2,1,0:T(1,128)} %broadcast_subtract_fusion.st_ref, ...), custom_call_target="tpu_custom_call" | custom-call | flops 20000000000 | bytes 16777216 | tf_op jit(solution)/shard_map/attn_fwd/pallas_call | solution.py:207
  101.5 1.8 multiply_sine_fusion
  103.3 21.9 %collective-permute-done.1.refs_3_ = bf16[2,2,64,2048]{3,2,1,0:T(8,128)(2,1)} collective-permute-done((bf16[2,2,64,2048]{3,2,1,0:T(8,128)(2,1)}, bf16[2,2,64,2048]{3,2,1,0:T(8,128)(2,1)}, u32[]{:S(2)}, u32[]{:S(2)}) %collective-permute-start.1) | collective-permute-done | bytes 1048608 | tf_op jit(solution)/shard_map/ppermute | solution.py:1090
  125.2 14.0 %wo_terms.1 = (f32[4,64,2048]{2,1,0:T(8,128)}, f32[4,64,2048]{2,1,0:T(8,128)}) custom-call(bf16[2,2,256,1024]{3,2,1,0:T(8,128)(2,1)} %get-tuple-element.41.refs_0_.o_ref.refs_3_, bf16[2,2,64,2048]{3,2,1,0:T(8,128)(2,1)} %bitcast.41, bf16[2,2,64,2048]{3,2,1,0:T(8,128)(2,1)} %collective-permute-done.refs_2_, ...), custom_call_target="tpu_custom_call" | custom-call | flops 4000000000 | bytes 20971520 | tf_op jit(solution)/shard_map/wo_terms/pallas_call | solution.py:513
  139.2 0.6 collective-permute-start.3
  139.8 23.4 %attn_bwd.1 = (bf16[2,2,256,1024]{3,2,1,0:T(8,128)(2,1)}, f32[8,2,2,2,256,128]{5,4,3,2,1,0:T(8,128)}) custom-call(s32[10]{0:T(128)} %pad_add_fusion.1.tab, bf16[2,2,256,1024]{3,2,1,0:T(8,128)(2,1)} %get-tuple-element.39.q_ref, bf16[2,2,256,1024]{3,2,1,0:T(8,128)(2,1)} %get-tuple-element.47.do_ref, ...), custom_call_target="tpu_custom_call" | custom-call | flops 49999998976 | bytes 33554432 | tf_op jit(solution)/shard_map/attn_bwd/pallas_call | solution.py:226
  163.2 24.0 %collective-permute-done.3.refs_1_ = f32[4,64,2048]{2,1,0:T(8,128)} collective-permute-done((f32[4,64,2048]{2,1,0:T(8,128)}, f32[4,64,2048]{2,1,0:T(8,128)}, u32[]{:S(2)}, u32[]{:S(2)}) %collective-permute-start.3) | collective-permute-done | bytes 2097184 | tf_op jit(solution)/shard_map/ppermute | solution.py:1090
  187.2 164.1 %reduce_pairs.1 = (f32[64,2048]{1,0:T(8,128)}, f32[2048,128]{1,0:T(8,128)}, f32[128,1024]{1,0:T(8,128)}, bf16[512,2048]{1,0:T(8,128)(2,1)}, f32[512,2048]{1,0:T(8,128)}, /*index=5*/bf16[2,2,256,2048]{3,2,1,0:T(8,128)(2,1)}) custom-call(f32[4,64,2048]{2,1,0:T(8,128)} %get-tuple-element.45.refs_0_, f32[4,64,2048]{2,1,0:T(8,128)} %collective-permute-done.3.refs_1_, ...), custom_call_target="tpu_custom_call" | custom-call | flops 1000000000 | bytes 20971520 | tf_op jit(solution)/shard_map/reduce_pairs/pallas_call | solution.py:862
  351.4 170.5 %gather_all.1 = (f32[2048,2048]{1,0:T(8,128)}, f32[2048,2048]{1,0:T(8,128)}, f32[2048,256]{1,0:T(8,128)}, f32[2048,256]{1,0:T(8,128)}, bf16[512,2048]{1,0:T(8,128)(2,1)}, /*index=5*/f32[1,2048]{1,0:T(1,128)}) custom-call(f32[64,2048]{1,0:T(8,128)} %get-tuple-element.52.refs_0_, f32[128,1024]{1,0:T(8,128)} %get-tuple-element.53.refs_1_, ...), custom_call_target="tpu_custom_call" | custom-call | flops 1000000000 | bytes 79691776 | tf_op jit(solution)/shard_map/gather_all/pallas_call | solution.py:1076
  521.9 3.3 copy.30
  525.2 1.3 copy.31
  526.6 14.6 %copy.32 = f32[2048,2048]{1,0:T(8,128)} copy(f32[2048,2048]{1,0:T(8,128)} %get-tuple-element.87) | data formatting | bytes 33554432
  541.2 1.3 copy.33
  542.5 1.8 copy-done.8
  544.3 1.3 copy.34
  545.6 6.2 %copy.35 = f32[2048,2048]{1,0:T(8,128)} copy(f32[2048,2048]{1,0:T(8,128)S(1)} %bitcast.32) | data formatting | bytes 33554432
  551.8 0.6 copy.36
  (53 shorter events, 2.4 us)
Async XLA Ops:
  0.6 4.1 copy-start.1
  2.2 7.0 %copy-start.7 = (f32[2048]{0:T(1024)}, f32[2048]{0:T(1024)S(1)}, u32[]{:S(2)}) copy-start(f32[2048]{0:T(1024)S(1)} %broadcast_in_dim.9) | copy-start | bytes 24580
  4.7 4.5 copy-start.2
  4.7 4.5 copy-start.3
  4.7 1.4 copy-start.4
  6.1 1.2 copy-start.5
  9.2 1.3 copy-start
  10.5 0.8 copy-start.6
  76.9 48.3 %collective-permute-start.2 = (bf16[2,2,64,2048]{3,2,1,0:T(8,128)(2,1)}, bf16[2,2,64,2048]{3,2,1,0:T(8,128)(2,1)}, u32[]{:S(2)}, u32[]{:S(2)}) collective-permute-start(bf16[2,2,64,2048]{3,2,1,0:T(8,128)(2,1)} %bitcast.42), channel_id=1, source_target_pairs={{0,3},{1,2},{2,1},{3,0},{4,7},{5,6},{6,5},{7,4},{8,11},{9,10},{10,... | collective-permute-start | bytes 3145736 | tf_op jit(solution)/shard_map/ppermute | solution.py:1090
  77.0 48.2 %collective-permute-start = (bf16[2,2,64,2048]{3,2,1,0:T(8,128)(2,1)}, bf16[2,2,64,2048]{3,2,1,0:T(8,128)(2,1)}, u32[]{:S(2)}, u32[]{:S(2)}) collective-permute-start(bf16[2,2,64,2048]{3,2,1,0:T(8,128)(2,1)} %bitcast.43), channel_id=1, source_target_pairs={{0,1},{1,0},{2,3},{3,2},{4,5},{5,4},{6,7},{7,6},{8,9},{9,8},{10,11... | collective-permute-start | bytes 3145736 | tf_op jit(solution)/shard_map/ppermute | solution.py:1090
  77.2 48.0 %collective-permute-start.1 = (bf16[2,2,64,2048]{3,2,1,0:T(8,128)(2,1)}, bf16[2,2,64,2048]{3,2,1,0:T(8,128)(2,1)}, u32[]{:S(2)}, u32[]{:S(2)}) collective-permute-start(bf16[2,2,64,2048]{3,2,1,0:T(8,128)(2,1)} %bitcast.40), channel_id=1, source_target_pairs={{0,2},{1,3},{2,0},{3,1},{4,6},{5,7},{6,4},{7,5},{8,10},{9,11},{10,... | collective-permute-start | bytes 3145736 | tf_op jit(solution)/shard_map/ppermute | solution.py:1090
  139.2 48.0 %collective-permute-start.3 = (f32[4,64,2048]{2,1,0:T(8,128)}, f32[4,64,2048]{2,1,0:T(8,128)}, u32[]{:S(2)}, u32[]{:S(2)}) collective-permute-start(f32[4,64,2048]{2,1,0:T(8,128)} %get-tuple-element.46), channel_id=1, source_target_pairs={{0,4},{1,5},{2,6},{3,7},{4,0},{5,1},{6,2},{7,3},{8,12},{9,13},{10,... | collective-permute-start | bytes 6291464 | tf_op jit(solution)/shard_map/ppermute | solution.py:1090
  521.9 3.3 copy-start.10
  525.2 20.4 %slice-start = ((s8[16777216]{0:T(1024)(128)(4,1)}), s8[4194304]{0:T(1024)(128)(4,1)S(1)}, s32[]{:S(2)}) async-start(s8[16777216]{0:T(1024)(128)(4,1)} %bitcast.31), calls=%async_computation | async-start | bytes 8388608
  526.5 14.6 %copy-start.9 = (f32[2048,256]{1,0:T(8,128)S(1)}, f32[2048,256]{1,0:T(8,128)}, u32[]{:S(2)}) copy-start(f32[2048,256]{1,0:T(8,128)} %get-tuple-element.88) | copy-start | bytes 6291460
  526.6 19.0 %slice-start.1 = ((s8[16777216]{0:T(1024)(128)(4,1)}), s8[4194304]{0:T(1024)(128)(4,1)S(1)}, s32[]{:S(2)}) async-start(s8[16777216]{0:T(1024)(128)(4,1)} %bitcast.31), calls=%async_computation.1 | async-start | bytes 8388608
  526.6 19.0 %slice-start.2 = ((s8[16777216]{0:T(1024)(128)(4,1)}), s8[4194304]{0:T(1024)(128)(4,1)S(1)}, s32[]{:S(2)}) async-start(s8[16777216]{0:T(1024)(128)(4,1)} %bitcast.31), calls=%async_computation.2 | async-start | bytes 8388608
  526.6 19.0 %slice-start.3 = ((s8[16777216]{0:T(1024)(128)(4,1)}), s8[4194304]{0:T(1024)(128)(4,1)S(1)}, s32[]{:S(2)}) async-start(s8[16777216]{0:T(1024)(128)(4,1)} %bitcast.31), calls=%async_computation.3 | async-start | bytes 8388608
  541.2 3.1 copy-start.8
  545.6 6.2 %copy-start.11 = (f32[1,2048]{1,0:T(1,128)S(1)}, f32[1,2048]{1,0:T(1,128)}, u32[]{:S(2)}) copy-start(f32[1,2048]{1,0:T(1,128)} %get-tuple-element.62) | copy-start | bytes 24580

commit v10 on v9

--- a/solution.py
+++ b/solution.py
@@ -874,11 +874,11 @@
 HERE = 0, 0, 0
 LINKS = "xyud"
 ORDERS = "zxy", "zyx", "yxz", "zyx"
-WO_CUTS, WQ_CUTS = (0, 2, 6, 8), (0, 3, 6, 8)
+CUTS = 0, 40, 96, 128
 SIZES = 7.0, 9.8, 5.6, 2.8
-GAIN_AT = 60.0, 72.0, 84.0, 96.0, 108.0
+GAIN_AT = [60.0 + 12.0 * i for i in range(5)]
 LATENCY, TILES_FROM, TILE_EVERY = 3.0, 14.0, 8.0
-SUM_AT = 25.0, 31.0, 37.0, 43.0
+SUM_AT = [25.0 + 6.0 * i for i in range(4)]
 
 
 def onward(order, key):
@@ -936,59 +936,65 @@
     wo_ref, wq_ref, dkv_ref, cos_ref, sin_ref, h_ref = take(6)
     grad_ins, outs, (dx_ref, dgain_ref) = take(6), take(FOUR), take(TWO)
     own_sem, send_sem, come_sem, core_sem, put_sem, all_terms, totals, g_s, g_r = take(9)
-    terms, wkv_own, wkv_ref, h_own, dk_u, dv_u, *stores = take(10)
+    terms, wkv_ref, h_own, dk_u, dv_u, store, wkv_store = take(7)
     buffers, sems, refs = take(FOUR), take(7), take(len(refs))
     me = lax.axis_index("cp")
     z, y, x, core = place(me)
     line = Line(me)
     to = {"x": dev(z, y, 1 - x, core), "y": dev(z, 1 - y, x, core), "u": line.next[1], "d": line.next[-1]}
     partner = dev(z, y, x, 1 - core)
+    chip_here = me // TWO
+    n_wo, wide = wo_ref.shape[0], wq_ref.shape[1]
+    store[chip_here, pl.ds(0, n_wo)] = wo_ref[...]
+    for i in range(TWO):
+        store[chip_here, pl.ds(n_wo, n_wo), pl.ds(i * wide, wide)] = wq_ref[pl.ds(i * n_wo, n_wo)]
     meet(quad_of(me)[1:] + [to["y"]] + [dev(zz, y, x, core) for _, zz in z_peers(z)])
     load_h = pltpu.make_async_copy(h_ref, h_own, own_sem.at[0])
     load_h.start()
-    wkv = PairSum(me, "core", 1, wkv_ref, wkv_own, buffers, [r.at[0] for r in sems])
-
-    def windows(part, zz, yy, xx, cc):
+    wkv = PairSum(me, "core", 1, wkv_ref, wkv_store.at[chip_here], buffers, [r.at[0] for r in sems])
+
+    def place_of(key):
+        dz, ry, rx = key
+        return z + dz, 1 - y if ry else y, 1 - x if rx else x
+
+    def block(part, key):
+        zz, yy, xx = place_of(key)
         chip = (TWO * zz + yy) * TWO + xx
-        wide, narrow = wq_ref.shape[1], wkv_own.shape[1] // TWO
-        wo_at = ((xx * TWO + cc) * N_PAIRS + chip // TWO) * wo_ref.shape[0]
-        wq_at = (cc * N_PAIRS + chip // TWO) * wq_ref.shape[0]
+        return wkv_store.at[chip] if part == 3 else store.at[chip, pl.ds(CUTS[part], CUTS[part + 1] - CUTS[part])]
+
+    def windows(part, key):
+        zz, yy, xx = place_of(key)
+        pair, src = TWO * zz + yy, block(part, key)
+        wo_at, wq_at = ((xx * TWO + core) * N_PAIRS + pair) * n_wo, (core * N_PAIRS + pair) * wq_ref.shape[0]
         if part == 3:
-            for i, (store, out) in enumerate(zip(stores[TWO:], outs[TWO:])):
-                window = out.at[pl.ds(wq_at, wkv_own.shape[0]), pl.ds(xx * narrow, narrow)]
-                yield wkv_own.at[:, head_slice(i)], store.at[chip], window
+            for i, out in enumerate(outs[TWO:]):
+                yield src.at[:, head(i)], out.at[pl.ds(wq_at, wq_ref.shape[0]), pl.ds(xx * HEAD_DIM, HEAD_DIM)]
             return
-
-        def cut(ref, cuts):
-            first, last = (c * ref.shape[0] // 8 for c in cuts[part : part + TWO])
-            return first, last - first
-
-        at, rows = cut(wo_ref, WO_CUTS)
-        here = pl.ds(at, rows)
-        yield wo_ref.at[here], stores[0].at[chip, here], outs[0].at[pl.ds(wo_at + at, rows)]
-        at, rows = cut(wq_ref, WQ_CUTS)
-        here = pl.ds(at, rows)
-        yield wq_ref.at[here], stores[1].at[chip, here], outs[1].at[pl.ds(wq_at + at, rows), pl.ds(xx * wide, wide)]
-
-    def block(part, key):
-        dz, ry, rx = key
-        return windows(part, z + dz, 1 - y if ry else y, 1 - x if rx else x, core)
+        first, last = CUTS[part : part + TWO]
+        if first < n_wo:
+            rows = min(last, n_wo) - first
+            yield src.at[pl.ds(0, rows)], outs[0].at[pl.ds(wo_at + first, rows)]
+        if last > n_wo:
+            skip = max(n_wo - first, 0)
+            rows, at = last - first - skip, first + skip - n_wo
+            for i in range(TWO):
+                window = outs[1].at[pl.ds(wq_at + i * n_wo + at, rows), pl.ds(xx * wide, wide)]
+                yield src.at[pl.ds(skip, rows), pl.ds(i * wide, wide)], window
 
     def index(part, key):
         return (part, key[0] + 3) + key[1:]
 
     def send(part, key, link, there):
         sent = send_sem.at[index(part, key) + (LINKS.find(link or "-") + 1,)]
-        for shard, store, window in block(part, key):
-            src = store if any(key) else shard
-            if link:
-                remote(src, store, sent, come_sem.at[index(part, there)], to[link]).start()
-            else:
-                remote(src, window, sent, core_sem.at[index(part, key)], partner).start()
-                pltpu.make_async_copy(src, window, put_sem.at[index(part, key)]).start()
+        if link:
+            remote(block(part, key), block(part, key), sent, come_sem.at[index(part, there)], to[link]).start()
+            return
+        for src, window in windows(part, key):
+            remote(src, window, sent, core_sem.at[index(part, key)], partner).start()
+            pltpu.make_async_copy(src, window, put_sem.at[index(part, key)]).start()
 
     def whole(part, send, arrive):
-        size = sum(shard.size for shard, _, _ in block(part, HERE)) // outs[0].shape[1]
+        size = CUTS[part + 1] - CUTS[part] if part < 3 else wkv_store.size // store.shape[0] // outs[0].shape[1]
         dst = outs[0].at[pl.ds(0, size)]
         return remote(dst, dst, send, arrive, me)
 
@@ -1068,11 +1074,10 @@
     terms = 1, x.shape[1]
     scratch = [dma((1,)), dma(keys + (len(LINKS) + 1,)), dma(keys), dma(keys), dma(keys)]
     n = len(GAIN_AT)
-    scratch += [pltpu.VMEM((n,) + terms, F32)] * TWO + [dma((n,)), dma((n,)), pltpu.VMEM(terms, F32), pltpu.VMEM(block, F32)]
+    scratch += [pltpu.VMEM((n,) + terms, F32)] * TWO + [dma((n,)), dma((n,)), pltpu.VMEM(terms, F32)]
     scratch += [pltpu.VMEM((FOUR, TWO) + block, F32), pltpu.VMEM(h_u.shape, BF16)]
     scratch += [pltpu.VMEM((TWO, TWO, BLK, HEAD_DIM), BF16)] * TWO
-    chips = (TWO * N_PAIRS,)
-    scratch += [pltpu.VMEM(chips + b, F32) for b in (wo.shape, wq.shape) + ((block[0], HEAD_DIM),) * TWO]
+    scratch += [pltpu.VMEM((TWO * N_PAIRS,) + b, F32) for b in ((TWO * wo.shape[0], wo.shape[1]), block)]
     return pl.pallas_call(
         gather_kernel,
         name="gather_all",

time: 554 us -> 555 us (level)
  no operation moved by 1% of the time
where the time goes in v10:
time: 555 us; the launch traced here: 552 us
  Pallas kernels  457 us (82%)
  waiting for transfers between devices  46 us (8%)
  local copies, waits for them, and re-layouts  38.9 us (7%)
  other arithmetic  6.43 us (1%)
    pallas_call x1, Pallas kernels, gather_all(): pl.pallas_call(gather_kernel, name='gather_all', out_shape=[jax.ShapeDtyp...  171 us
    pallas_call x1, Pallas kernels, reduce_pairs(): pl.pallas_call(functools.partial(reduce_kernel, cuts, kinds, work), name=...  164 us
    pallas_call x1, Pallas kernels, exchange(): pl.pallas_call(exchange_kernel, name='exchange', out_shape=(jax.ShapeDtyp...  65.6 us
    ppermute x4, waiting for transfers between devices, perm(): return lax.ppermute(x, 'cp', pairs)  46 us
    unnamed x39, local copies, waits for them, and re-layouts  35.2 us
    pallas_call x1, Pallas kernels, flash_bwd(): pl.pallas_call(bwd_kernel, name='attn_bwd', out_shape=(jax.ShapeDtypeStru...  23.4 us
    pallas_call x1, Pallas kernels, flash_fwd(): pl.pallas_call(fwd_kernel, name='attn_fwd', out_shape=(jax.ShapeDtypeStru...  18 us
    pallas_call x1, Pallas kernels, wo_terms(): pl.pallas_call(wo_kernel, name='wo_terms', out_shape=[jax.ShapeDtypeStruc...  14 us
  transfers between devices with their start and end apart: 4, of which 2 were waited for; matrix products, arithmetic and copies ran while one was open for 1% of the time, Pallas kernels for 7%

profile of v10, /device:TPU:0, one launch (start us, length us, event | category | flops | bytes accessed | tf_op | source)
XLA Modules:
  0.0 552.4 jit_solution(17450545064756833052)
XLA Ops:
  0.7 0.8 convert_bitcast_fusion
  1.5 0.7 broadcast_in_dim.9
  2.2 1.3 pad.4.refs_3_
  3.5 1.0 fusion
  4.7 1.4 copy-done.4
  6.1 1.2 copy-done.5
  7.3 1.8 norm_kv.1
  9.2 1.3 copy-done
  10.5 0.8 copy-done.6
  11.3 65.6 %exchange.1 = (bf16[8,2,2,2,256,128]{5,4,3,2,1,0:T(8,128)(2,1)}, bf16[2,2,256,1024]{3,2,1,0:T(8,128)(2,1)}, bf16[2,2,256,1024]{3,2,1,0:T(8,128)(2,1)}, s32[4,8,1...) custom-call(bf16[2,2,2,2,2,64,128]{6,5,4,3,2,1,0:T(8,128)(2,1)} %bitcast.28, ...), custom_call_target="tpu_custom_call" | custom-call | flops 1000000000 | bytes 20971520 | tf_op jit(solution)/shard_map/exchange/pallas_call | solution.py:451
  77.2 1.9 collective-permute-start.1
  79.7 0.6 broadcast_in_dim.8.ko_ref
  80.3 0.7 slice.3
  82.3 0.6 broadcast_subtract_fusion.st_ref
  82.9 0.6 sub.45.qi_ref
  83.5 18.0 %attn_fwd.1 = (bf16[2,2,256,1024]{3,2,1,0:T(8,128)(2,1)}, f32[2,2,8,1,256]{4,3,2,1,0:T(1,128)}) custom-call(s32[10]{0:T(128)} %pad_add_fusion.1.tab, bf16[2,2,256,1024]{3,2,1,0:T(8,128)(2,1)} %get-tuple-element.39.q_ref, bf16[8,2,2,2,256,128]{5,4,3,2,1,0:T(8,128)(2,1)} %get-tuple-element.40.kv_ref, s32[2,2,1,256]{3,2,1,0:T(1,128)} %broadcast_subtract_fusion.st_ref, ...), custom_call_target="tpu_custom_call" | custom-call | flops 20000000000 | bytes 16777216 | tf_op jit(solution)/shard_map/attn_fwd/pallas_call | solution.py:207
  101.5 1.8 multiply_sine_fusion
  103.3 21.9 %collective-permute-done.1.refs_3_ = bf16[2,2,64,2048]{3,2,1,0:T(8,128)(2,1)} collective-permute-done((bf16[2,2,64,2048]{3,2,1,0:T(8,128)(2,1)}, bf16[2,2,64,2048]{3,2,1,0:T(8,128)(2,1)}, u32[]{:S(2)}, u32[]{:S(2)}) %collective-permute-start.1) | collective-permute-done | bytes 1048608 | tf_op jit(solution)/shard_map/ppermute | solution.py:1095
  125.2 14.0 %wo_terms.1 = (f32[4,64,2048]{2,1,0:T(8,128)}, f32[4,64,2048]{2,1,0:T(8,128)}) custom-call(bf16[2,2,256,1024]{3,2,1,0:T(8,128)(2,1)} %get-tuple-element.41.refs_0_.o_ref.refs_3_, bf16[2,2,64,2048]{3,2,1,0:T(8,128)(2,1)} %bitcast.41, bf16[2,2,64,2048]{3,2,1,0:T(8,128)(2,1)} %collective-permute-done.refs_2_, ...), custom_call_target="tpu_custom_call" | custom-call | flops 4000000000 | bytes 20971520 | tf_op jit(solution)/shard_map/wo_terms/pallas_call | solution.py:513
  139.2 0.6 collective-permute-start.3
  139.8 23.4 %attn_bwd.1 = (bf16[2,2,256,1024]{3,2,1,0:T(8,128)(2,1)}, f32[8,2,2,2,256,128]{5,4,3,2,1,0:T(8,128)}) custom-call(s32[10]{0:T(128)} %pad_add_fusion.1.tab, bf16[2,2,256,1024]{3,2,1,0:T(8,128)(2,1)} %get-tuple-element.39.q_ref, bf16[2,2,256,1024]{3,2,1,0:T(8,128)(2,1)} %get-tuple-element.47.do_ref, ...), custom_call_target="tpu_custom_call" | custom-call | flops 49999998976 | bytes 33554432 | tf_op jit(solution)/shard_map/attn_bwd/pallas_call | solution.py:226
  163.2 24.0 %collective-permute-done.3.refs_1_ = f32[4,64,2048]{2,1,0:T(8,128)} collective-permute-done((f32[4,64,2048]{2,1,0:T(8,128)}, f32[4,64,2048]{2,1,0:T(8,128)}, u32[]{:S(2)}, u32[]{:S(2)}) %collective-permute-start.3) | collective-permute-done | bytes 2097184 | tf_op jit(solution)/shard_map/ppermute | solution.py:1095
  187.2 164.1 %reduce_pairs.1 = (f32[64,2048]{1,0:T(8,128)}, f32[2048,128]{1,0:T(8,128)}, f32[128,1024]{1,0:T(8,128)}, bf16[512,2048]{1,0:T(8,128)(2,1)}, f32[512,2048]{1,0:T(8,128)}, /*index=5*/bf16[2,2,256,2048]{3,2,1,0:T(8,128)(2,1)}) custom-call(f32[4,64,2048]{2,1,0:T(8,128)} %get-tuple-element.45.refs_0_, f32[4,64,2048]{2,1,0:T(8,128)} %collective-permute-done.3.refs_1_, ...), custom_call_target="tpu_custom_call" | custom-call | flops 1000000000 | bytes 20971520 | tf_op jit(solution)/shard_map/reduce_pairs/pallas_call | solution.py:862
  351.4 170.5 %gather_all.1 = (f32[2048,2048]{1,0:T(8,128)}, f32[2048,2048]{1,0:T(8,128)}, f32[2048,256]{1,0:T(8,128)}, f32[2048,256]{1,0:T(8,128)}, bf16[512,2048]{1,0:T(8,128)(2,1)}, /*index=5*/f32[1,2048]{1,0:T(1,128)}) custom-call(f32[64,2048]{1,0:T(8,128)} %get-tuple-element.52.refs_0_, f32[128,1024]{1,0:T(8,128)} %get-tuple-element.53.refs_1_, ...), custom_call_target="tpu_custom_call" | custom-call | flops 1000000000 | bytes 79691776 | tf_op jit(solution)/shard_map/gather_all/pallas_call | solution.py:1081
  522.0 3.3 copy.30
  525.3 1.3 copy.31
  526.6 14.6 %copy.32 = f32[2048,2048]{1,0:T(8,128)} copy(f32[2048,2048]{1,0:T(8,128)} %get-tuple-element.87) | data formatting | bytes 33554432
  541.2 1.3 copy.33
  542.5 1.8 copy-done.8
  544.3 1.3 copy.34
  545.7 6.2 %copy.35 = f32[2048,2048]{1,0:T(8,128)} copy(f32[2048,2048]{1,0:T(8,128)S(1)} %bitcast.32) | data formatting | bytes 33554432
  551.8 0.6 copy.36
  (53 shorter events, 2.4 us)
Async XLA Ops:
  0.6 4.1 copy-start.1
  2.2 7.0 %copy-start.7 = (f32[2048]{0:T(1024)}, f32[2048]{0:T(1024)S(1)}, u32[]{:S(2)}) copy-start(f32[2048]{0:T(1024)S(1)} %broadcast_in_dim.9) | copy-start | bytes 24580
  4.7 4.5 copy-start.2
  4.7 4.5 copy-start.3
  4.7 1.4 copy-start.4
  6.1 1.2 copy-start.5
  9.2 1.3 copy-start
  10.5 0.8 copy-start.6
  76.9 48.3 %collective-permute-start.2 = (bf16[2,2,64,2048]{3,2,1,0:T(8,128)(2,1)}, bf16[2,2,64,2048]{3,2,1,0:T(8,128)(2,1)}, u32[]{:S(2)}, u32[]{:S(2)}) collective-permute-start(bf16[2,2,64,2048]{3,2,1,0:T(8,128)(2,1)} %bitcast.42), channel_id=1, source_target_pairs={{0,3},{1,2},{2,1},{3,0},{4,7},{5,6},{6,5},{7,4},{8,11},{9,10},{10,... | collective-permute-start | bytes 3145736 | tf_op jit(solution)/shard_map/ppermute | solution.py:1095
  77.0 48.2 %collective-permute-start = (bf16[2,2,64,2048]{3,2,1,0:T(8,128)(2,1)}, bf16[2,2,64,2048]{3,2,1,0:T(8,128)(2,1)}, u32[]{:S(2)}, u32[]{:S(2)}) collective-permute-start(bf16[2,2,64,2048]{3,2,1,0:T(8,128)(2,1)} %bitcast.43), channel_id=1, source_target_pairs={{0,1},{1,0},{2,3},{3,2},{4,5},{5,4},{6,7},{7,6},{8,9},{9,8},{10,11... | collective-permute-start | bytes 3145736 | tf_op jit(solution)/shard_map/ppermute | solution.py:1095
  77.2 48.0 %collective-permute-start.1 = (bf16[2,2,64,2048]{3,2,1,0:T(8,128)(2,1)}, bf16[2,2,64,2048]{3,2,1,0:T(8,128)(2,1)}, u32[]{:S(2)}, u32[]{:S(2)}) collective-permute-start(bf16[2,2,64,2048]{3,2,1,0:T(8,128)(2,1)} %bitcast.40), channel_id=1, source_target_pairs={{0,2},{1,3},{2,0},{3,1},{4,6},{5,7},{6,4},{7,5},{8,10},{9,11},{10,... | collective-permute-start | bytes 3145736 | tf_op jit(solution)/shard_map/ppermute | solution.py:1095
  139.2 48.0 %collective-permute-start.3 = (f32[4,64,2048]{2,1,0:T(8,128)}, f32[4,64,2048]{2,1,0:T(8,128)}, u32[]{:S(2)}, u32[]{:S(2)}) collective-permute-start(f32[4,64,2048]{2,1,0:T(8,128)} %get-tuple-element.46), channel_id=1, source_target_pairs={{0,4},{1,5},{2,6},{3,7},{4,0},{5,1},{6,2},{7,3},{8,12},{9,13},{10,... | collective-permute-start | bytes 6291464 | tf_op jit(solution)/shard_map/ppermute | solution.py:1095
  521.9 3.3 copy-start.10
  525.3 20.4 %slice-start = ((s8[16777216]{0:T(1024)(128)(4,1)}), s8[4194304]{0:T(1024)(128)(4,1)S(1)}, s32[]{:S(2)}) async-start(s8[16777216]{0:T(1024)(128)(4,1)} %bitcast.31), calls=%async_computation | async-start | bytes 8388608
  526.6 14.6 %copy-start.9 = (f32[2048,256]{1,0:T(8,128)S(1)}, f32[2048,256]{1,0:T(8,128)}, u32[]{:S(2)}) copy-start(f32[2048,256]{1,0:T(8,128)} %get-tuple-element.88) | copy-start | bytes 6291460
  526.6 19.0 %slice-start.1 = ((s8[16777216]{0:T(1024)(128)(4,1)}), s8[4194304]{0:T(1024)(128)(4,1)S(1)}, s32[]{:S(2)}) async-start(s8[16777216]{0:T(1024)(128)(4,1)} %bitcast.31), calls=%async_computation.1 | async-start | bytes 8388608
  526.6 19.0 %slice-start.2 = ((s8[16777216]{0:T(1024)(128)(4,1)}), s8[4194304]{0:T(1024)(128)(4,1)S(1)}, s32[]{:S(2)}) async-start(s8[16777216]{0:T(1024)(128)(4,1)} %bitcast.31), calls=%async_computation.2 | async-start | bytes 8388608
  526.6 19.0 %slice-start.3 = ((s8[16777216]{0:T(1024)(128)(4,1)}), s8[4194304]{0:T(1024)(128)(4,1)S(1)}, s32[]{:S(2)}) async-start(s8[16777216]{0:T(1024)(128)(4,1)} %bitcast.31), calls=%async_computation.3 | async-start | bytes 8388608
  541.2 3.1 copy-start.8
  545.6 6.2 %copy-start.11 = (f32[1,2048]{1,0:T(1,128)S(1)}, f32[1,2048]{1,0:T(1,128)}, u32[]{:S(2)}) copy-start(f32[1,2048]{1,0:T(1,128)} %get-tuple-element.62) | copy-start | bytes 24580

commit v11 on v10

--- a/solution.py
+++ b/solution.py
@@ -18,6 +18,7 @@
 EXP2_SCALE = ATTN_SCALE * LOG2E
 CHUNK = 64
 TWO = 2
+THREE = 3
 FOUR = 4
 NEW = jnp.newaxis
 BLK = 4 * CHUNK
@@ -191,14 +192,14 @@
         return (b, h) + (0,) * TWO
 
     def at_row(b, h, t):
-        return (0, 0, b) + (0,) * 3
+        return (0, 0, b) + (0,) * THREE
 
     tile = pl.BlockSpec((ONE, ONE, BLK, N_HEADS * HEAD_DIM), at_tile)
     row = pl.BlockSpec((ONE, ONE, 1, BLK), at_tile)
-    stat = pl.BlockSpec((ONE, ONE, N_HEADS, 1, BLK), lambda b, h, t: (b, h) + (0,) * 3)
+    stat = pl.BlockSpec((ONE, ONE, N_HEADS, 1, BLK), lambda b, h, t: (b, h) + (0,) * THREE)
     rope = pl.BlockSpec((ONE, ONE, HEAD_DIM // TWO, BLK), at_tile)
     kv = pl.BlockSpec((N_PAIRS, TWO, ONE, TWO, BLK, HEAD_DIM), at_row)
-    ko = pl.BlockSpec((TWO, 1, BLK), lambda b, h, t: (0,) * 3)
+    ko = pl.BlockSpec((TWO, 1, BLK), lambda b, h, t: (0,) * THREE)
     return tile, row, stat, kv, ko, rope
 
 
@@ -256,7 +257,7 @@
     h_ref[...] = h
     k = jnp.dot(h, wk_ref[...], preferred_element_type=F32)
     v = jnp.dot(h, wv_ref[...], preferred_element_type=F32)
-    n = kv_ref.shape[3]
+    n = kv_ref.shape[THREE]
     for i in range(TWO):
         for j, val in enumerate((turn(k[:, head_slice(i)], cos_ref, sin_ref), v[:, head_slice(i)])):
             for c in range(TWO):
@@ -268,7 +269,7 @@
     return pl.pallas_call(
         first_kernel,
         name="norm_kv",
-        out_shape=(jax.ShapeDtypeStruct(x.shape, BF16), jax.ShapeDtypeStruct((TWO,) * 3 + (n, HEAD_DIM), BF16)),
+        out_shape=(jax.ShapeDtypeStruct(x.shape, BF16), jax.ShapeDtypeStruct((TWO,) * THREE + (n, HEAD_DIM), BF16)),
         compiler_params=params(20),
         cost_estimate=cost(TWO, 7),
     )(x, gain, w_k, w_v, cos_f, sin_f)
@@ -283,7 +284,7 @@
 
 
 def z_peers(z):
-    return [(k, lax.rem(z + k, FOUR)) for k in (1, TWO, 3)]
+    return [(k, lax.rem(z + k, FOUR)) for k in (1, TWO, THREE)]
 
 
 def meet(peers):
@@ -300,15 +301,15 @@
 
 
 class Line:
-    order = (0, 1, -1, TWO, -TWO, 3, -3)
+    order = (0, 1, -1, TWO, -TWO, THREE, -THREE)
 
     def __init__(self, me):
         self.z, y, x, core = place(me)
         self.next = {1: dev(self.z + 1, y, x, core), -1: dev(self.z - 1, y, x, core)}
-        self.inside = {1: self.z < 3, -1: self.z > 0}
+        self.inside = {1: self.z < THREE, -1: self.z > 0}
 
     def held(self, dz):
-        return jnp.logical_and(self.z + dz >= 0, self.z + dz <= 3)
+        return jnp.logical_and(self.z + dz >= 0, self.z + dz <= THREE)
 
     def ways(self, dz):
         for d in self.next:
@@ -347,10 +348,10 @@
 
     def source(a, d):
         xx, cc = 1 - x if d // TWO else x, 1 - core if d % TWO else core
-        return pos_ref.at[cc] if a == 3 else (kv_ref, q_home, do_home)[a].at[xx, cc]
+        return pos_ref.at[cc] if a == THREE else (kv_ref, q_home, do_home)[a].at[xx, cc]
 
     def target(a, d):
-        if a == 3:
+        if a == THREE:
             return pos_u.at[d]
         tok = pl.ds(d * CHUNK, CHUNK)
         return kv_all.at[me // FOUR, :, :, :, tok] if a == 0 else (q_u, do_u)[a - 1].at[:, :, tok]
@@ -363,11 +364,11 @@
 
     def z_copy(part, dz, d):
         block = kv_all.at[TWO * (z + dz) + y, part]
-        return remote(block, block, z_s.at[part, (d + 1) // TWO, dz + 3], z_r.at[part, dz - d + 3], line.next[d])
+        return remote(block, block, z_s.at[part, (d + 1) // TWO, dz + THREE], z_r.at[part, dz - d + THREE], line.next[d])
 
     def y_copy(part, dz, yy=y):
         block = kv_all.at[TWO * (z + dz) + yy, part]
-        return remote(block, block, y_s.at[part, dz + 3], y_r.at[part, dz + 3], across)
+        return remote(block, block, y_s.at[part, dz + THREE], y_r.at[part, dz + THREE], across)
 
     parts = range(TWO)
     moves = [(part, dz) for dz in line.order for part in parts]
@@ -376,7 +377,7 @@
         for part, dz in [moves.pop(0) for _ in range(count)]:
             if dz:
                 block = kv_all.at[TWO * (z + dz) + y, part]
-                arrival = remote(block, block, own_sem.at[0], z_r.at[part, dz + 3], me)
+                arrival = remote(block, block, own_sem.at[0], z_r.at[part, dz + THREE], me)
                 pl.when(line.held(dz))(arrival.wait_recv)
             for d, on in line.ways(dz):
                 pl.when(on)(z_copy(part, dz, d).start)
@@ -404,8 +405,8 @@
     half = dy_ref.shape[0] // TWO
     for i, out in enumerate(dy_rows):
         pltpu.make_async_copy(dy_ref.at[aligned(core if i == 0 else 1 - core, half)], out, dy_sem.at[i]).start()
-    for a in (0, 3):
-        for d in (1, TWO, 3):
+    for a in (0, THREE):
+        for d in (1, TWO, THREE):
             quad_copy(a, d).start()
         own_copy(a).start()
     for a, (fetch, use) in enumerate(((fetch_q, query), (fetch_o, pull)), 1):
@@ -418,7 +419,7 @@
                 own_copy(a).start()
             if len(moves) == len(all_moves):
                 own_copy(0).wait()
-                for d in (1, TWO, 3):
+                for d in (1, TWO, THREE):
                     quad_copy(0, d).wait_recv()
             pass_on(TWO)
     pass_on(len(moves))
@@ -428,11 +429,11 @@
         pl.when(line.held(dz))(y_copy(part, dz, 1 - y).wait_recv)
         pl.when(line.held(dz))(y_copy(part, dz).wait_send)
     for a in range(FOUR):
-        for d in (1, TWO, 3):
+        for d in (1, TWO, THREE):
             quad_copy(a, d).wait_send()
             if a > 0:
                 quad_copy(a, d).wait_recv()
-    for a in (1, TWO, 3):
+    for a in (1, TWO, THREE):
         own_copy(a).wait()
     for i, out in enumerate(dy_rows):
         pltpu.make_async_copy(dy_ref.at[aligned(core if i == 0 else 1 - core, half)], out, dy_sem.at[i]).wait()
@@ -446,12 +447,12 @@
     pos_quad = jax.ShapeDtypeStruct((FOUR,) + pos.shape[1:], pos.dtype)
     dy_half = jax.ShapeDtypeStruct((dy.shape[0] // TWO, dy.shape[1]), BF16)
     home = pltpu.VMEM((TWO,) * FOUR + (CHUNK, wide), BF16)
-    sems = [dma((FOUR,))] + [dma((FOUR, FOUR))] * TWO + [dma((TWO, TWO, 7))] + [dma((TWO, 7))] * 3
+    sems = [dma((FOUR,))] + [dma((FOUR, FOUR))] * TWO + [dma((TWO, TWO, 7))] + [dma((TWO, 7))] * THREE
     bufs = [pltpu.VMEM((TWO,) + b, BF16) for b in ((w_q.shape[0], BLK), (BLK, w_o.shape[1]))]
     return pl.pallas_call(
         exchange_kernel,
         name="exchange",
-        out_shape=(jax.ShapeDtypeStruct((N_PAIRS,) + (TWO,) * 3 + (BLK, HEAD_DIM), BF16), unit, unit, pos_quad, dy_half, dy_half),
+        out_shape=(jax.ShapeDtypeStruct((N_PAIRS,) + (TWO,) * THREE + (BLK, HEAD_DIM), BF16), unit, unit, pos_quad, dy_half, dy_half),
         in_specs=[vmem] * 6 + [hbm] * TWO,
         out_specs=[hbm] * 6,
         scratch_shapes=sems + [home, home] + bufs + [dma((TWO, TWO)), dma((TWO,))],
@@ -518,7 +519,7 @@
         out_specs=[vmem] * TWO,
         scratch_shapes=[pltpu.VMEM((TWO, TWO, BLK, d), BF16), pltpu.VMEM((wide, n), BF16)]
         + [pltpu.VMEM((TWO, half, d), F32), pltpu.VMEM((half, d), F32), dma((FOUR,)), dma((d // BLK,)), dma((d // BLK,))],
-        compiler_params=params(63, collective_id=3),
+        compiler_params=params(63, collective_id=THREE),
         cost_estimate=cost(FOUR, 20),
     )(o, *pieces)
 
@@ -597,12 +598,12 @@
     def hop(self, j, h):
         @pl.when(self.z == h)
         def _():
-            for zz in range(3, h, -1):
+            for zz in range(THREE, h, -1):
                 self.relay(j, 0, zz, h > 0)
 
-        @pl.when(self.z == 3 - h)
+        @pl.when(self.z == THREE - h)
         def _():
-            for zz in range(3 - h):
+            for zz in range(THREE - h):
                 self.relay(j, 1, zz, h > 0)
 
     def step(self, j, h):
@@ -610,12 +611,12 @@
             self.y_copy(j).wait_recv()
             self.add_y(j)
             self.hop(j, 0)
-        elif 0 < h < 3:
+        elif 0 < h < THREE:
             self.hop(j, h)
-        elif h == 3:
+        elif h == THREE:
             at = self.rows(j)
             self.out[at] = self.mine(j, self.z)[...]
-            for way, on in enumerate((self.z > 0, self.z < 3)):
+            for way, on in enumerate((self.z > 0, self.z < THREE)):
 
                 @pl.when(on)
                 def _(way=way):
@@ -630,7 +631,7 @@
         for zz in range(FOUR):
             if zz > 0:
                 pl.when(self.z < zz)(self.z_copy(j, 0, zz, self.next_z[0]).wait_send)
-            if zz < 3:
+            if zz < THREE:
                 pl.when(self.z > zz)(self.z_copy(j, 1, zz, self.next_z[1]).wait_send)
 
     @staticmethod
@@ -638,12 +639,12 @@
         unused = pltpu.VMEM((8, HEAD_DIM), F32)
         own = pltpu.VMEM(((FOUR, TWO) if kind == "core" else (FOUR,)) + block, F32)
         from_y = pltpu.VMEM((FOUR,) + block, F32)
-        return [own, own if kind == "core" else unused, from_y, pltpu.VMEM((TWO, 3) + block, F32)]
+        return [own, own if kind == "core" else unused, from_y, pltpu.VMEM((TWO, THREE) + block, F32)]
 
     @staticmethod
     def sems(*dims):
         dma = pltpu.SemaphoreType.DMA
-        return [dma(dims)] * 5 + [dma(dims + (TWO, 3))] * TWO
+        return [dma(dims)] * 5 + [dma(dims + (TWO, THREE))] * TWO
 
 
 def reduce_kernel(cuts, kinds, work, *refs):
@@ -664,7 +665,7 @@
         s.begin(j)
     for s, j in early:
         s.loaded(j)
-    for t in range(len(pieces) + 3):
+    for t in range(len(pieces) + THREE):
         if t == MADE_AT:
             job.wq_terms(sums[-1].own, made[0])
             for s, j in late:
@@ -697,7 +698,7 @@
             return src.at[:, :, pl.ds(d * CHUNK, CHUNK)]
 
         self.own = pltpu.make_async_copy(piece(0), to, own_sem)
-        self.copies = [remote(piece(d), to, send.at[d], arrive.at[d], quad_of(me)[d]) for d in (1, TWO, 3)]
+        self.copies = [remote(piece(d), to, send.at[d], arrive.at[d], quad_of(me)[d]) for d in (1, TWO, THREE)]
 
     def start(self):
         self.own.start()
@@ -715,7 +716,7 @@
 
 
 class Products:
-    ins, outs = 6, 3
+    ins, outs = 6, THREE
 
     def __init__(self, me, ins, outs, scratch):
         attn, self.dq, hidden, normed, self.w_o, self.w_q = ins
@@ -730,10 +731,10 @@
         def tokens(d):
             return self.h_u.at[:, :, pl.ds(d * CHUNK, CHUNK)]
 
-        self.h_copies = [remote(piece(d), tokens(d), quad_s.at[TWO, d], quad_r.at[TWO, d], quad_of(me)[d]) for d in (1, TWO, 3)]
+        self.h_copies = [remote(piece(d), tokens(d), quad_s.at[TWO, d], quad_r.at[TWO, d], quad_of(me)[d]) for d in (1, TWO, THREE)]
         self.h_mine = pltpu.make_async_copy(piece(0), stage, own_sem.at[TWO])
         self.h_back = pltpu.make_async_copy(stage, tokens(0), self.load_sem.at[0])
-        self.residual = pltpu.make_async_copy(hidden, self.block_out, own_sem.at[3])
+        self.residual = pltpu.make_async_copy(hidden, self.block_out, own_sem.at[THREE])
         self.residual.start()
         for c in self.h_copies:
             c.start()
@@ -748,10 +749,10 @@
     @staticmethod
     def scratch(arrays):
         dma, d = pltpu.SemaphoreType.DMA, arrays[-1].shape[0]
-        home = pltpu.VMEM((TWO,) * 3 + (CHUNK, d), BF16)
+        home = pltpu.VMEM((TWO,) * THREE + (CHUNK, d), BF16)
         buf = [pltpu.VMEM((TWO,) + b, BF16) for b in ((d, BLK), (BLK, d))]
         tiles = [pltpu.VMEM((TWO, TWO) + b, BF16) for b in ((CHUNK, d), (TWO, BLK, BLK))]
-        sems = [dma((TWO, TWO)), dma((TWO,)), dma((FOUR,)), dma((3, FOUR)), dma((3, FOUR))]
+        sems = [dma((TWO, TWO)), dma((TWO,)), dma((FOUR,)), dma((THREE, FOUR)), dma((THREE, FOUR))]
         return [home] * TWO + buf + tiles + sems
 
     @staticmethod
@@ -816,7 +817,7 @@
     def __init__(self, me, dk, dv, ins, outs, scratch):
         self.part, self.w_k, self.w_v, self.x, self.dy, self.gain = ins
         self.dx, self.terms = outs
-        self.dk_home, self.dv_home, self.rows, *sems = scratch
+        self.dk_home, self.dv_home, self.rows, self.part_tile, self.part_sem, *sems = scratch
         pairs = (dk, self.dk_home), (dv, self.dv_home)
         self.homes = [Home(me, src, out, *[r.at[i] for r in sems]) for i, (src, out) in enumerate(pairs)]
         for h in self.homes:
@@ -825,8 +826,8 @@
     @staticmethod
     def scratch(x):
         dma = pltpu.SemaphoreType.DMA
-        home = pltpu.VMEM((TWO,) * 3 + (CHUNK, TWO * HEAD_DIM), BF16)
-        return [home, home, pltpu.VMEM((8, x.shape[1]), F32), dma((TWO,)), dma((TWO, FOUR)), dma((TWO, FOUR))]
+        home = pltpu.VMEM((TWO,) * THREE + (CHUNK, TWO * HEAD_DIM), BF16)
+        return [home, home, pltpu.VMEM((8, x.shape[1]), F32), pltpu.VMEM((TWO * CHUNK, x.shape[1]), F32), dma(()), dma((TWO,)), dma((TWO, FOUR)), dma((TWO, FOUR))]
 
     def tile(self, t):
         if t == 0:
@@ -835,7 +836,10 @@
             self.rows[...] = jnp.zeros_like(self.rows)
         size = TWO * CHUNK
         at = pl.ds(t * size, size)
-        d = self.part[at]
+        load = pltpu.make_async_copy(self.part.at[at], self.part_tile, self.part_sem)
+        load.start()
+        load.wait()
+        d = self.part_tile[...]
         for home, w in ((self.dk_home, self.w_k), (self.dv_home, self.w_v)):
             d += dot_t(home[t // TWO, t % TWO].reshape(size, -1), w[...])
         d = d.astype(BF16).astype(F32)
@@ -877,6 +881,7 @@
 CUTS = 0, 40, 96, 128
 SIZES = 7.0, 9.8, 5.6, 2.8
 GAIN_AT = [60.0 + 12.0 * i for i in range(5)]
+BEHIND = 4
 LATENCY, TILES_FROM, TILE_EVERY = 3.0, 14.0, 8.0
 SUM_AT = [25.0 + 6.0 * i for i in range(4)]
 
@@ -892,20 +897,20 @@
         else:
             yield "u", (-1, ry, rx)
             yield "d", (1, ry, rx)
-    if stage >= 0 and order[stage] == "z" and abs(dz) < 3:
+    if stage >= 0 and order[stage] == "z" and abs(dz) < THREE:
         yield ("u", (dz - 1, ry, rx)) if dz < 0 else ("d", (dz + 1, ry, rx))
 
 
 def arrivals():
     busy, times = {}, {}
-    starts = [0.0] * 3 + [SUM_AT[-1] + LATENCY]
+    starts = [0.0] * THREE + [SUM_AT[-1] + LATENCY]
     here = [(t, z, part, HERE) for part, t in enumerate(starts) for z in range(FOUR)]
     while here:
         now, z, part, key = heapq.heappop(here)
         times.setdefault((part, key), []).append(now)
         for link, there in onward(ORDERS[part], key):
             to = z + {"u": 1, "d": -1}.get(link, 0)
-            if 0 <= to <= 3:
+            if 0 <= to <= THREE:
                 busy[z, link] = max(busy.get((z, link), 0), now) + SIZES[part]
                 heapq.heappush(here, (busy[z, link] + LATENCY, to, part, there))
     return sorted((sum(t) / len(t), *at) for at, t in times.items())
@@ -945,28 +950,28 @@
     partner = dev(z, y, x, 1 - core)
     chip_here = me // TWO
     n_wo, wide = wo_ref.shape[0], wq_ref.shape[1]
-    store[chip_here, pl.ds(0, n_wo)] = wo_ref[...]
+    store[core, chip_here, pl.ds(0, n_wo)] = wo_ref[...]
     for i in range(TWO):
-        store[chip_here, pl.ds(n_wo, n_wo), pl.ds(i * wide, wide)] = wq_ref[pl.ds(i * n_wo, n_wo)]
+        store[core, chip_here, pl.ds(n_wo, n_wo), pl.ds(i * wide, wide)] = wq_ref[pl.ds(i * n_wo, n_wo)]
     meet(quad_of(me)[1:] + [to["y"]] + [dev(zz, y, x, core) for _, zz in z_peers(z)])
     load_h = pltpu.make_async_copy(h_ref, h_own, own_sem.at[0])
     load_h.start()
-    wkv = PairSum(me, "core", 1, wkv_ref, wkv_store.at[chip_here], buffers, [r.at[0] for r in sems])
+    wkv = PairSum(me, "core", 1, wkv_ref, wkv_store.at[core, chip_here], buffers, [r.at[0] for r in sems])
 
     def place_of(key):
         dz, ry, rx = key
         return z + dz, 1 - y if ry else y, 1 - x if rx else x
 
-    def block(part, key):
+    def block(part, key, cc=core):
         zz, yy, xx = place_of(key)
         chip = (TWO * zz + yy) * TWO + xx
-        return wkv_store.at[chip] if part == 3 else store.at[chip, pl.ds(CUTS[part], CUTS[part + 1] - CUTS[part])]
-
-    def windows(part, key):
+        return wkv_store.at[cc, chip] if part == THREE else store.at[cc, chip, pl.ds(CUTS[part], CUTS[part + 1] - CUTS[part])]
+
+    def windows(part, key, cc):
         zz, yy, xx = place_of(key)
-        pair, src = TWO * zz + yy, block(part, key)
-        wo_at, wq_at = ((xx * TWO + core) * N_PAIRS + pair) * n_wo, (core * N_PAIRS + pair) * wq_ref.shape[0]
-        if part == 3:
+        pair, src = TWO * zz + yy, block(part, key, cc)
+        wo_at, wq_at = ((xx * TWO + cc) * N_PAIRS + pair) * n_wo, (cc * N_PAIRS + pair) * wq_ref.shape[0]
+        if part == THREE:
             for i, out in enumerate(outs[TWO:]):
                 yield src.at[:, head(i)], out.at[pl.ds(wq_at, wq_ref.shape[0]), pl.ds(xx * HEAD_DIM, HEAD_DIM)]
             return
@@ -982,19 +987,25 @@
                 yield src.at[pl.ds(skip, rows), pl.ds(i * wide, wide)], window
 
     def index(part, key):
-        return (part, key[0] + 3) + key[1:]
+        return (part, key[0] + THREE) + key[1:]
 
     def send(part, key, link, there):
         sent = send_sem.at[index(part, key) + (LINKS.find(link or "-") + 1,)]
-        if link:
-            remote(block(part, key), block(part, key), sent, come_sem.at[index(part, there)], to[link]).start()
-            return
-        for src, window in windows(part, key):
-            remote(src, window, sent, core_sem.at[index(part, key)], partner).start()
-            pltpu.make_async_copy(src, window, put_sem.at[index(part, key)]).start()
+        arrive, device = (come_sem.at[index(part, there)], to[link]) if link else (core_sem.at[index(part, key)], partner)
+        remote(block(part, key), block(part, key), sent, arrive, device).start()
+        if not link:
+            put(part, key, core)
+
+    def put(part, key, cc):
+        for src, window in windows(part, key, cc):
+            pltpu.make_async_copy(src, window, put_sem.at[(cc,) + index(part, key)]).start()
+
+    def put_other(part, key):
+        whole(part, own_sem.at[0], core_sem.at[index(part, key)]).wait_recv()
+        put(part, key, 1 - core)
 
     def whole(part, send, arrive):
-        size = CUTS[part + 1] - CUTS[part] if part < 3 else wkv_store.size // store.shape[0] // outs[0].shape[1]
+        size = CUTS[part + 1] - CUTS[part] if part < THREE else wq_ref.shape[0] * TWO * HEAD_DIM // outs[0].shape[1]
         dst = outs[0].at[pl.ds(0, size)]
         return remote(dst, dst, send, arrive, me)
 
@@ -1035,7 +1046,7 @@
     steps += [(at, functools.partial(add_terms, i)) for i, at in enumerate(GAIN_AT)]
     steps.sort(key=lambda s: s[0])
     events = arrivals()
-    for part in range(3):
+    for part in range(THREE):
         pass_on(part, HERE)
     turn_back(dkv_ref, cos_ref, sin_ref, dk_u, dv_u)
     job = HiddenGradient(me, dk_u, dv_u, grad_ins, (dx_ref, terms), refs)
@@ -1043,21 +1054,27 @@
     wkv_terms(h_own, dk_u, dv_u, ((wkv_ref, 1 - core), (buffers[0], core)))
     wkv.begin(0)
     wkv.loaded(0)
+    waiting = [(part, HERE) for part in range(THREE)]
     for now, part, key in events:
         while steps and steps[0][0] <= now:
             steps.pop(0)[1]()
         if any(key):
             arrive = come_sem.at[index(part, key)]
             when(line.held(key[0]), whole(part, own_sem.at[0], arrive).wait_recv)
+        if any(key) or part == THREE:
             pass_on(part, key)
-        elif part == 3:
-            pass_on(part, key)
+            waiting.append((part, key))
+        if len(waiting) > BEHIND:
+            at = waiting.pop(0)
+            when(line.held(at[1][0]), functools.partial(put_other, *at))
+    for at in waiting:
+        when(line.held(at[1][0]), functools.partial(put_other, *at))
     dgain_ref[...] = totals[len(GAIN_AT) - 1]
     for i in range(len(GAIN_AT)):
         term_copy(i).wait_send()
     for _, part, key in events:
-        for sem in (core_sem, put_sem):
-            when(line.held(key[0]), whole(part, own_sem.at[0], sem.at[index(part, key)]).wait_recv)
+        for cc in range(TWO):
+            when(line.held(key[0]), whole(part, own_sem.at[0], put_sem.at[(cc,) + index(part, key)]).wait_recv)
         for link, there, on in each_way(part, key):
             sent = send_sem.at[index(part, key) + (LINKS.find(link or "-") + 1,)]
             when(on, whole(part, sent, own_sem.at[0]).wait_send)
@@ -1072,18 +1089,18 @@
     parts = len(ORDERS)
     keys = (parts, 7, TWO, TWO)
     terms = 1, x.shape[1]
-    scratch = [dma((1,)), dma(keys + (len(LINKS) + 1,)), dma(keys), dma(keys), dma(keys)]
+    scratch = [dma((1,)), dma(keys + (len(LINKS) + 1,)), dma(keys), dma(keys), dma((TWO,) + keys)]
     n = len(GAIN_AT)
     scratch += [pltpu.VMEM((n,) + terms, F32)] * TWO + [dma((n,)), dma((n,)), pltpu.VMEM(terms, F32)]
     scratch += [pltpu.VMEM((FOUR, TWO) + block, F32), pltpu.VMEM(h_u.shape, BF16)]
     scratch += [pltpu.VMEM((TWO, TWO, BLK, HEAD_DIM), BF16)] * TWO
-    scratch += [pltpu.VMEM((TWO * N_PAIRS,) + b, F32) for b in ((TWO * wo.shape[0], wo.shape[1]), block)]
+    scratch += [pltpu.VMEM((TWO, TWO * N_PAIRS) + b, F32) for b in ((TWO * wo.shape[0], wo.shape[1]), block)]
     return pl.pallas_call(
         gather_kernel,
         name="gather_all",
         out_shape=[jax.ShapeDtypeStruct(s, F32) for s in shapes]
         + [jax.ShapeDtypeStruct(x.shape, BF16), jax.ShapeDtypeStruct(terms, F32)],
-        in_specs=[vmem] * 5 + [hbm] + [vmem] * 6,
+        in_specs=[vmem] * 5 + [hbm] * TWO + [vmem] * 5,
         out_specs=[hbm] * len(shapes) + [vmem] * TWO,
         scratch_shapes=scratch + PairSum.scratch("core", block) + PairSum.sems(1, 1) + HiddenGradient.scratch(x),
         compiler_params=params(63, collective_id=0),
@@ -1120,12 +1137,12 @@
         pos = jnp.pad(positions.reshape(TWO, TWO, n_tok), ((0, 0), (0, 6), (0, 0)))
         kv_home = kv_home.reshape((TWO,) * 5 + (CHUNK, HEAD_DIM))
         kv_all, q_u, do_u, pos_u, *dy_rows = exchange(kv_home, normed, dy_flat, pos, cos_f, sin_f, w_q, w_o)
-        pos_u = pos_u[:, :TWO].reshape((FOUR, TWO, TWO, CHUNK)).transpose(1, TWO, 0, 3).reshape(TWO, TWO, BLK)
+        pos_u = pos_u[:, :TWO].reshape((FOUR, TWO, TWO, CHUNK)).transpose(1, TWO, 0, THREE).reshape(TWO, TWO, BLK)
         dy_rows = [a.reshape(TWO, TWO, CHUNK, d_model) for a in dy_rows]
         dy_pieces = swap([dy_rows[d % TWO] for d in relations])
 
         member = quad ^ jnp.arange(FOUR)
-        front, back = ((m[:, NEW] * CHUNK + jnp.arange(CHUNK)[NEW]).reshape(BLK) for m in (member, 3 - member))
+        front, back = ((m[:, NEW] * CHUNK + jnp.arange(CHUNK)[NEW]).reshape(BLK) for m in (member, THREE - member))
         offsets = jnp.stack([front, back]).astype(jnp.int32)
         own_super = jnp.stack([pair, N_SUPER - 1 - pair]).astype(jnp.int32)
         q_index = own_super[:, NEW] * BLK + offsets
@@ -1136,7 +1153,7 @@
         start_r = start[:, :, NEW, :]
         q_index_r = jnp.broadcast_to(q_index[NEW, :, NEW, :], start_r.shape)
         cos_u, sin_u = rope_tables(pos_u)
-        cos_ut, sin_ut = jnp.swapaxes(cos_u, TWO, 3), jnp.swapaxes(sin_u, TWO, 3)
+        cos_ut, sin_ut = jnp.swapaxes(cos_u, TWO, THREE), jnp.swapaxes(sin_u, TWO, THREE)
 
         koff = offsets[:, NEW]
         attn_u, lse = flash_fwd(tab, q_u, kv_all, start_r, q_index_r, koff)
@@ -1154,7 +1171,7 @@
             ("z", "", "core"),
             TWO,
             Products,
-            (attn_u, dq_u, x_flat, normed.reshape((TWO,) * 3 + (CHUNK, d_model)), w_o, w_q),
+            (attn_u, dq_u, x_flat, normed.reshape((TWO,) * THREE + (CHUNK, d_model)), w_o, w_q),
         )
         grad_wo, grad_wq, grad_wk, grad_wv, grad_x, d_gain = gather_all(
             wo_own,

time: 555 us -> 563 us (1.014)
  Pallas kernels: 457 us -> 466 us
    pallas_call x1, Pallas kernels: 171 us -> 179 us  [gather_all(): pl.pallas_call(gather_kernel, name='gather_all', out_shape=[jax.ShapeDtyp...]
where the time goes in v11:
time: 563 us; the launch traced here: 561 us
  Pallas kernels  466 us (83%)
  waiting for transfers between devices  46 us (8%)
  local copies, waits for them, and re-layouts  38.9 us (7%)
  other arithmetic  6.43 us (1%)
    pallas_call x1, Pallas kernels, gather_all(): pl.pallas_call(gather_kernel, name='gather_all', out_shape=[jax.ShapeDtyp...  179 us
    pallas_call x1, Pallas kernels, reduce_pairs(): pl.pallas_call(functools.partial(reduce_kernel, cuts, kinds, work), name=...  164 us
    pallas_call x1, Pallas kernels, exchange(): pl.pallas_call(exchange_kernel, name='exchange', out_shape=(jax.ShapeDtyp...  65.6 us
    ppermute x4, waiting for transfers between devices, perm(): return lax.ppermute(x, 'cp', pairs)  46 us
    unnamed x39, local copies, waits for them, and re-layouts  35.2 us
    pallas_call x1, Pallas kernels, flash_bwd(): pl.pallas_call(bwd_kernel, name='attn_bwd', out_shape=(jax.ShapeDtypeStru...  23.4 us
    pallas_call x1, Pallas kernels, flash_fwd(): pl.pallas_call(fwd_kernel, name='attn_fwd', out_shape=(jax.ShapeDtypeStru...  18 us
    pallas_call x1, Pallas kernels, wo_terms(): pl.pallas_call(wo_kernel, name='wo_terms', out_shape=[jax.ShapeDtypeStruc...  14 us
  transfers between devices with their start and end apart: 4, of which 2 were waited for; matrix products, arithmetic and copies ran while one was open for 1% of the time, Pallas kernels for 7%

profile of v11, /device:TPU:0, one launch (start us, length us, event | category | flops | bytes accessed | tf_op | source)
XLA Modules:
  0.0 560.6 jit_solution(14112875672903793792)
XLA Ops:
  0.7 0.8 convert_bitcast_fusion
  1.5 0.7 broadcast_in_dim.9
  2.2 1.3 pad.4.refs_3_
  3.5 1.0 fusion
  4.7 1.4 copy-done.4
  6.1 1.2 copy-done.5
  7.3 1.8 norm_kv.1
  9.2 1.3 copy-done
  10.5 0.8 copy-done.6
  11.3 65.6 %exchange.1 = (bf16[8,2,2,2,256,128]{5,4,3,2,1,0:T(8,128)(2,1)}, bf16[2,2,256,1024]{3,2,1,0:T(8,128)(2,1)}, bf16[2,2,256,1024]{3,2,1,0:T(8,128)(2,1)}, s32[4,8,1...) custom-call(bf16[2,2,2,2,2,64,128]{6,5,4,3,2,1,0:T(8,128)(2,1)} %bitcast.28, ...), custom_call_target="tpu_custom_call" | custom-call | flops 1000000000 | bytes 20971520 | tf_op jit(solution)/shard_map/exchange/pallas_call | solution.py:452
  77.2 1.9 collective-permute-start.1
  79.7 0.6 broadcast_in_dim.8.ko_ref
  80.3 0.7 slice.3
  82.3 0.6 broadcast_subtract_fusion.st_ref
  82.9 0.6 sub.45.qi_ref
  83.5 18.0 %attn_fwd.1 = (bf16[2,2,256,1024]{3,2,1,0:T(8,128)(2,1)}, f32[2,2,8,1,256]{4,3,2,1,0:T(1,128)}) custom-call(s32[10]{0:T(128)} %pad_add_fusion.1.tab, bf16[2,2,256,1024]{3,2,1,0:T(8,128)(2,1)} %get-tuple-element.39.q_ref, bf16[8,2,2,2,256,128]{5,4,3,2,1,0:T(8,128)(2,1)} %get-tuple-element.40.kv_ref, s32[2,2,1,256]{3,2,1,0:T(1,128)} %broadcast_subtract_fusion.st_ref, ...), custom_call_target="tpu_custom_call" | custom-call | flops 20000000000 | bytes 16777216 | tf_op jit(solution)/shard_map/attn_fwd/pallas_call | solution.py:208
  101.5 1.8 multiply_sine_fusion
  103.3 21.9 %collective-permute-done.1.refs_3_ = bf16[2,2,64,2048]{3,2,1,0:T(8,128)(2,1)} collective-permute-done((bf16[2,2,64,2048]{3,2,1,0:T(8,128)(2,1)}, bf16[2,2,64,2048]{3,2,1,0:T(8,128)(2,1)}, u32[]{:S(2)}, u32[]{:S(2)}) %collective-permute-start.1) | collective-permute-done | bytes 1048608 | tf_op jit(solution)/shard_map/ppermute | solution.py:1112
  125.2 14.0 %wo_terms.1 = (f32[4,64,2048]{2,1,0:T(8,128)}, f32[4,64,2048]{2,1,0:T(8,128)}) custom-call(bf16[2,2,256,1024]{3,2,1,0:T(8,128)(2,1)} %get-tuple-element.41.refs_0_.o_ref.refs_3_, bf16[2,2,64,2048]{3,2,1,0:T(8,128)(2,1)} %bitcast.41, bf16[2,2,64,2048]{3,2,1,0:T(8,128)(2,1)} %collective-permute-done.refs_2_, ...), custom_call_target="tpu_custom_call" | custom-call | flops 4000000000 | bytes 20971520 | tf_op jit(solution)/shard_map/wo_terms/pallas_call | solution.py:514
  139.2 0.6 collective-permute-start.3
  139.8 23.4 %attn_bwd.1 = (bf16[2,2,256,1024]{3,2,1,0:T(8,128)(2,1)}, f32[8,2,2,2,256,128]{5,4,3,2,1,0:T(8,128)}) custom-call(s32[10]{0:T(128)} %pad_add_fusion.1.tab, bf16[2,2,256,1024]{3,2,1,0:T(8,128)(2,1)} %get-tuple-element.39.q_ref, bf16[2,2,256,1024]{3,2,1,0:T(8,128)(2,1)} %get-tuple-element.47.do_ref, ...), custom_call_target="tpu_custom_call" | custom-call | flops 49999998976 | bytes 33554432 | tf_op jit(solution)/shard_map/attn_bwd/pallas_call | solution.py:227
  163.2 24.0 %collective-permute-done.3.refs_1_ = f32[4,64,2048]{2,1,0:T(8,128)} collective-permute-done((f32[4,64,2048]{2,1,0:T(8,128)}, f32[4,64,2048]{2,1,0:T(8,128)}, u32[]{:S(2)}, u32[]{:S(2)}) %collective-permute-start.3) | collective-permute-done | bytes 2097184 | tf_op jit(solution)/shard_map/ppermute | solution.py:1112
  187.2 164.1 %reduce_pairs.1 = (f32[64,2048]{1,0:T(8,128)}, f32[2048,128]{1,0:T(8,128)}, f32[128,1024]{1,0:T(8,128)}, bf16[512,2048]{1,0:T(8,128)(2,1)}, f32[512,2048]{1,0:T(8,128)}, /*index=5*/bf16[2,2,256,2048]{3,2,1,0:T(8,128)(2,1)}) custom-call(f32[4,64,2048]{2,1,0:T(8,128)} %get-tuple-element.45.refs_0_, f32[4,64,2048]{2,1,0:T(8,128)} %collective-permute-done.3.refs_1_, ...), custom_call_target="tpu_custom_call" | custom-call | flops 1000000000 | bytes 20971520 | tf_op jit(solution)/shard_map/reduce_pairs/pallas_call | solution.py:866
  351.4 178.8 %gather_all.1 = (f32[2048,2048]{1,0:T(8,128)}, f32[2048,2048]{1,0:T(8,128)}, f32[2048,256]{1,0:T(8,128)}, f32[2048,256]{1,0:T(8,128)}, bf16[512,2048]{1,0:T(8,128)(2,1)}, /*index=5*/f32[1,2048]{1,0:T(1,128)}) custom-call(f32[64,2048]{1,0:T(8,128)} %get-tuple-element.52.refs_0_, f32[128,1024]{1,0:T(8,128)} %get-tuple-element.53.refs_1_, ...), custom_call_target="tpu_custom_call" | custom-call | flops 1000000000 | bytes 79691776 | tf_op jit(solution)/shard_map/gather_all/pallas_call | solution.py:1098
  530.2 3.3 copy.30
  533.5 1.3 copy.31
  534.8 14.6 %copy.32 = f32[2048,2048]{1,0:T(8,128)} copy(f32[2048,2048]{1,0:T(8,128)} %get-tuple-element.87) | data formatting | bytes 33554432
  549.4 1.3 copy.33
  550.8 1.8 copy-done.8
  552.5 1.3 copy.34
  553.9 6.2 %copy.35 = f32[2048,2048]{1,0:T(8,128)} copy(f32[2048,2048]{1,0:T(8,128)S(1)} %bitcast.32) | data formatting | bytes 33554432
  560.0 0.6 copy.36
  (53 shorter events, 2.4 us)
Async XLA Ops:
  0.6 4.1 copy-start.1
  2.2 7.0 %copy-start.7 = (f32[2048]{0:T(1024)}, f32[2048]{0:T(1024)S(1)}, u32[]{:S(2)}) copy-start(f32[2048]{0:T(1024)S(1)} %broadcast_in_dim.9) | copy-start | bytes 24580
  4.7 4.5 copy-start.2
  4.7 4.5 copy-start.3
  4.7 1.4 copy-start.4
  6.1 1.2 copy-start.5
  9.2 1.3 copy-start
  10.5 0.8 copy-start.6
  76.9 48.3 %collective-permute-start.2 = (bf16[2,2,64,2048]{3,2,1,0:T(8,128)(2,1)}, bf16[2,2,64,2048]{3,2,1,0:T(8,128)(2,1)}, u32[]{:S(2)}, u32[]{:S(2)}) collective-permute-start(bf16[2,2,64,2048]{3,2,1,0:T(8,128)(2,1)} %bitcast.42), channel_id=1, source_target_pairs={{0,3},{1,2},{2,1},{3,0},{4,7},{5,6},{6,5},{7,4},{8,11},{9,10},{10,... | collective-permute-start | bytes 3145736 | tf_op jit(solution)/shard_map/ppermute | solution.py:1112
  77.0 48.2 %collective-permute-start = (bf16[2,2,64,2048]{3,2,1,0:T(8,128)(2,1)}, bf16[2,2,64,2048]{3,2,1,0:T(8,128)(2,1)}, u32[]{:S(2)}, u32[]{:S(2)}) collective-permute-start(bf16[2,2,64,2048]{3,2,1,0:T(8,128)(2,1)} %bitcast.43), channel_id=1, source_target_pairs={{0,1},{1,0},{2,3},{3,2},{4,5},{5,4},{6,7},{7,6},{8,9},{9,8},{10,11... | collective-permute-start | bytes 3145736 | tf_op jit(solution)/shard_map/ppermute | solution.py:1112
  77.2 48.0 %collective-permute-start.1 = (bf16[2,2,64,2048]{3,2,1,0:T(8,128)(2,1)}, bf16[2,2,64,2048]{3,2,1,0:T(8,128)(2,1)}, u32[]{:S(2)}, u32[]{:S(2)}) collective-permute-start(bf16[2,2,64,2048]{3,2,1,0:T(8,128)(2,1)} %bitcast.40), channel_id=1, source_target_pairs={{0,2},{1,3},{2,0},{3,1},{4,6},{5,7},{6,4},{7,5},{8,10},{9,11},{10,... | collective-permute-start | bytes 3145736 | tf_op jit(solution)/shard_map/ppermute | solution.py:1112
  139.2 48.0 %collective-permute-start.3 = (f32[4,64,2048]{2,1,0:T(8,128)}, f32[4,64,2048]{2,1,0:T(8,128)}, u32[]{:S(2)}, u32[]{:S(2)}) collective-permute-start(f32[4,64,2048]{2,1,0:T(8,128)} %get-tuple-element.46), channel_id=1, source_target_pairs={{0,4},{1,5},{2,6},{3,7},{4,0},{5,1},{6,2},{7,3},{8,12},{9,13},{10,... | collective-permute-start | bytes 6291464 | tf_op jit(solution)/shard_map/ppermute | solution.py:1112
  530.2 3.3 copy-start.10
  533.5 20.4 %slice-start = ((s8[16777216]{0:T(1024)(128)(4,1)}), s8[4194304]{0:T(1024)(128)(4,1)S(1)}, s32[]{:S(2)}) async-start(s8[16777216]{0:T(1024)(128)(4,1)} %bitcast.31), calls=%async_computation | async-start | bytes 8388608
  534.8 14.6 %copy-start.9 = (f32[2048,256]{1,0:T(8,128)S(1)}, f32[2048,256]{1,0:T(8,128)}, u32[]{:S(2)}) copy-start(f32[2048,256]{1,0:T(8,128)} %get-tuple-element.88) | copy-start | bytes 6291460
  534.8 19.0 %slice-start.1 = ((s8[16777216]{0:T(1024)(128)(4,1)}), s8[4194304]{0:T(1024)(128)(4,1)S(1)}, s32[]{:S(2)}) async-start(s8[16777216]{0:T(1024)(128)(4,1)} %bitcast.31), calls=%async_computation.1 | async-start | bytes 8388608
  534.8 19.0 %slice-start.2 = ((s8[16777216]{0:T(1024)(128)(4,1)}), s8[4194304]{0:T(1024)(128)(4,1)S(1)}, s32[]{:S(2)}) async-start(s8[16777216]{0:T(1024)(128)(4,1)} %bitcast.31), calls=%async_computation.2 | async-start | bytes 8388608
  534.8 19.0 %slice-start.3 = ((s8[16777216]{0:T(1024)(128)(4,1)}), s8[4194304]{0:T(1024)(128)(4,1)S(1)}, s32[]{:S(2)}) async-start(s8[16777216]{0:T(1024)(128)(4,1)} %bitcast.31), calls=%async_computation.3 | async-start | bytes 8388608
  549.4 3.1 copy-start.8
  553.9 6.2 %copy-start.11 = (f32[1,2048]{1,0:T(1,128)S(1)}, f32[1,2048]{1,0:T(1,128)}, u32[]{:S(2)}) copy-start(f32[1,2048]{1,0:T(1,128)} %get-tuple-element.62) | copy-start | bytes 24580

commit v12 on v11

--- a/solution.py
+++ b/solution.py
@@ -28,6 +28,7 @@
 MESH = pl.DeviceIdType.MESH
 ONE = pl.Squeezed()
 GROUP = 4
+DIRECT = 2
 MADE_AT = 5
 PRODUCTS_AT = 7, 9
 F32 = jnp.float32
@@ -525,13 +526,15 @@
 
 
 class PairSum:
-    def __init__(self, me, kind, cut, src, out, buffers, sems):
+    def __init__(self, me, kind, cut, src, out, buffers, sems, direct=0):
         self.me, self.kind, self.src, self.out = me, kind, src, out
+        self.direct_from = cut - direct
         self.size = out.shape[0] // cut
         self.own, self.from_core, self.from_y, self.from_z = buffers
         self.load_sem, self.core_s, self.core_r, self.y_s, self.y_r, self.z_s, self.z_r = sems
         self.z, self.y, x, core = place(me)
         self.partner = dev(self.z, self.y, x, 1 - core)
+        self.line = [(k, zz, dev(zz, self.y, x, core)) for k, zz in z_peers(self.z)]
         self.across = dev(self.z, 1 - self.y, x, core)
         self.next_z = dev(self.z + 1, self.y, x, core), dev(self.z - 1, self.y, x, core)
 
@@ -606,11 +609,28 @@
             for zz in range(THREE - h):
                 self.relay(j, 1, zz, h > 0)
 
+    def z_direct(self, j):
+        for k, zz, to in self.line:
+            at, there = (j, 0, k - 1), self.from_z.at[0, k - 1, self.rows(j)]
+            yield remote(self.mine(j, zz), there, self.z_s.at[at], self.z_r.at[at], to), there
+
     def step(self, j, h):
+        if j >= self.direct_from and h > 0:
+            if h == 1:
+                at = self.rows(j)
+                self.out[at] = self.mine(j, self.z)[...]
+                for c, arrived in self.z_direct(j):
+                    c.wait_recv()
+                    self.out[at] += arrived[...]
+            return
         if h == 0 and self.kind != "z":
             self.y_copy(j).wait_recv()
             self.add_y(j)
-            self.hop(j, 0)
+            if j < self.direct_from:
+                self.hop(j, 0)
+            else:
+                for c, _ in self.z_direct(j):
+                    c.start()
         elif 0 < h < THREE:
             self.hop(j, h)
         elif h == THREE:
@@ -628,6 +648,10 @@
             self.core_copy(j).wait_send()
         if self.kind != "z":
             self.y_copy(j).wait_send()
+        if j >= self.direct_from:
+            for c, _ in self.z_direct(j):
+                c.wait_send()
+            return
         for zz in range(FOUR):
             if zz > 0:
                 pl.when(self.z < zz)(self.z_copy(j, 0, zz, self.next_z[0]).wait_send)
@@ -658,7 +682,8 @@
     z, y, x, core = place(me)
     meet(quad_of(me)[1:] + [dev(z, 1 - y, x, core)] + [dev(zz, y, x, core) for _, zz in z_peers(z)])
     job = work(me, more_in, more_out, take(len(refs)))
-    sums = [PairSum(me, *a, [r.at[i] for r in sems]) for i, a in enumerate(zip(kinds, cuts, ins + made, outs, buffers))]
+    inputs = enumerate(zip(kinds, cuts, ins + made, outs, buffers))
+    sums = [PairSum(me, *a, [r.at[i] for r in sems], DIRECT if i == n - 1 else 0) for i, a in inputs]
     pieces = [(s, j) for s, cut in zip(sums, cuts) for j in range(cut)]
     early, late = pieces[: -cuts[-1]], pieces[-cuts[-1] :]
     for s, j in early:
@@ -817,7 +842,7 @@
     def __init__(self, me, dk, dv, ins, outs, scratch):
         self.part, self.w_k, self.w_v, self.x, self.dy, self.gain = ins
         self.dx, self.terms = outs
-        self.dk_home, self.dv_home, self.rows, self.part_tile, self.part_sem, *sems = scratch
+        self.dk_home, self.dv_home, self.rows, *sems = scratch
         pairs = (dk, self.dk_home), (dv, self.dv_home)
         self.homes = [Home(me, src, out, *[r.at[i] for r in sems]) for i, (src, out) in enumerate(pairs)]
         for h in self.homes:
@@ -827,7 +852,7 @@
     def scratch(x):
         dma = pltpu.SemaphoreType.DMA
         home = pltpu.VMEM((TWO,) * THREE + (CHUNK, TWO * HEAD_DIM), BF16)
-        return [home, home, pltpu.VMEM((8, x.shape[1]), F32), pltpu.VMEM((TWO * CHUNK, x.shape[1]), F32), dma(()), dma((TWO,)), dma((TWO, FOUR)), dma((TWO, FOUR))]
+        return [home, home, pltpu.VMEM((8, x.shape[1]), F32), dma((TWO,)), dma((TWO, FOUR)), dma((TWO, FOUR))]
 
     def tile(self, t):
         if t == 0:
@@ -836,10 +861,7 @@
             self.rows[...] = jnp.zeros_like(self.rows)
         size = TWO * CHUNK
         at = pl.ds(t * size, size)
-        load = pltpu.make_async_copy(self.part.at[at], self.part_tile, self.part_sem)
-        load.start()
-        load.wait()
-        d = self.part_tile[...]
+        d = self.part[at]
         for home, w in ((self.dk_home, self.w_k), (self.dv_home, self.w_v)):
             d += dot_t(home[t // TWO, t % TWO].reshape(size, -1), w[...])
         d = d.astype(BF16).astype(F32)
@@ -878,10 +900,9 @@
 HERE = 0, 0, 0
 LINKS = "xyud"
 ORDERS = "zxy", "zyx", "yxz", "zyx"
-CUTS = 0, 40, 96, 128
-SIZES = 7.0, 9.8, 5.6, 2.8
+CUTS = 0, 48, 96, 128
+SIZES = 8.4, 8.4, 5.6, 2.8
 GAIN_AT = [60.0 + 12.0 * i for i in range(5)]
-BEHIND = 4
 LATENCY, TILES_FROM, TILE_EVERY = 3.0, 14.0, 8.0
 SUM_AT = [25.0 + 6.0 * i for i in range(4)]
 
@@ -950,27 +971,27 @@
     partner = dev(z, y, x, 1 - core)
     chip_here = me // TWO
     n_wo, wide = wo_ref.shape[0], wq_ref.shape[1]
-    store[core, chip_here, pl.ds(0, n_wo)] = wo_ref[...]
+    store[chip_here, pl.ds(0, n_wo)] = wo_ref[...]
     for i in range(TWO):
-        store[core, chip_here, pl.ds(n_wo, n_wo), pl.ds(i * wide, wide)] = wq_ref[pl.ds(i * n_wo, n_wo)]
+        store[chip_here, pl.ds(n_wo, n_wo), pl.ds(i * wide, wide)] = wq_ref[pl.ds(i * n_wo, n_wo)]
     meet(quad_of(me)[1:] + [to["y"]] + [dev(zz, y, x, core) for _, zz in z_peers(z)])
     load_h = pltpu.make_async_copy(h_ref, h_own, own_sem.at[0])
     load_h.start()
-    wkv = PairSum(me, "core", 1, wkv_ref, wkv_store.at[core, chip_here], buffers, [r.at[0] for r in sems])
+    wkv = PairSum(me, "core", 1, wkv_ref, wkv_store.at[chip_here], buffers, [r.at[0] for r in sems])
 
     def place_of(key):
         dz, ry, rx = key
         return z + dz, 1 - y if ry else y, 1 - x if rx else x
 
-    def block(part, key, cc=core):
+    def block(part, key):
         zz, yy, xx = place_of(key)
         chip = (TWO * zz + yy) * TWO + xx
-        return wkv_store.at[cc, chip] if part == THREE else store.at[cc, chip, pl.ds(CUTS[part], CUTS[part + 1] - CUTS[part])]
-
-    def windows(part, key, cc):
+        return wkv_store.at[chip] if part == THREE else store.at[chip, pl.ds(CUTS[part], CUTS[part + 1] - CUTS[part])]
+
+    def windows(part, key):
         zz, yy, xx = place_of(key)
-        pair, src = TWO * zz + yy, block(part, key, cc)
-        wo_at, wq_at = ((xx * TWO + cc) * N_PAIRS + pair) * n_wo, (cc * N_PAIRS + pair) * wq_ref.shape[0]
+        pair, src = TWO * zz + yy, block(part, key)
+        wo_at, wq_at = ((xx * TWO + core) * N_PAIRS + pair) * n_wo, (core * N_PAIRS + pair) * wq_ref.shape[0]
         if part == THREE:
             for i, out in enumerate(outs[TWO:]):
                 yield src.at[:, head(i)], out.at[pl.ds(wq_at, wq_ref.shape[0]), pl.ds(xx * HEAD_DIM, HEAD_DIM)]
@@ -991,21 +1012,15 @@
 
     def send(part, key, link, there):
         sent = send_sem.at[index(part, key) + (LINKS.find(link or "-") + 1,)]
-        arrive, device = (come_sem.at[index(part, there)], to[link]) if link else (core_sem.at[index(part, key)], partner)
-        remote(block(part, key), block(part, key), sent, arrive, device).start()
-        if not link:
-            put(part, key, core)
-
-    def put(part, key, cc):
-        for src, window in windows(part, key, cc):
-            pltpu.make_async_copy(src, window, put_sem.at[(cc,) + index(part, key)]).start()
-
-    def put_other(part, key):
-        whole(part, own_sem.at[0], core_sem.at[index(part, key)]).wait_recv()
-        put(part, key, 1 - core)
+        if link:
+            remote(block(part, key), block(part, key), sent, come_sem.at[index(part, there)], to[link]).start()
+            return
+        for src, window in windows(part, key):
+            remote(src, window, sent, core_sem.at[index(part, key)], partner).start()
+            pltpu.make_async_copy(src, window, put_sem.at[index(part, key)]).start()
 
     def whole(part, send, arrive):
-        size = CUTS[part + 1] - CUTS[part] if part < THREE else wq_ref.shape[0] * TWO * HEAD_DIM // outs[0].shape[1]
+        size = CUTS[part + 1] - CUTS[part] if part < THREE else wkv_store.size // store.shape[0] // outs[0].shape[1]
         dst = outs[0].at[pl.ds(0, size)]
         return remote(dst, dst, send, arrive, me)
 
@@ -1054,27 +1069,21 @@
     wkv_terms(h_own, dk_u, dv_u, ((wkv_ref, 1 - core), (buffers[0], core)))
     wkv.begin(0)
     wkv.loaded(0)
-    waiting = [(part, HERE) for part in range(THREE)]
     for now, part, key in events:
         while steps and steps[0][0] <= now:
             steps.pop(0)[1]()
         if any(key):
             arrive = come_sem.at[index(part, key)]
             when(line.held(key[0]), whole(part, own_sem.at[0], arrive).wait_recv)
-        if any(key) or part == THREE:
             pass_on(part, key)
-            waiting.append((part, key))
-        if len(waiting) > BEHIND:
-            at = waiting.pop(0)
-            when(line.held(at[1][0]), functools.partial(put_other, *at))
-    for at in waiting:
-        when(line.held(at[1][0]), functools.partial(put_other, *at))
+        elif part == THREE:
+            pass_on(part, key)
     dgain_ref[...] = totals[len(GAIN_AT) - 1]
     for i in range(len(GAIN_AT)):
         term_copy(i).wait_send()
     for _, part, key in events:
-        for cc in range(TWO):
-            when(line.held(key[0]), whole(part, own_sem.at[0], put_sem.at[(cc,) + index(part, key)]).wait_recv)
+        for sem in (core_sem, put_sem):
+            when(line.held(key[0]), whole(part, own_sem.at[0], sem.at[index(part, key)]).wait_recv)
         for link, there, on in each_way(part, key):
             sent = send_sem.at[index(part, key) + (LINKS.find(link or "-") + 1,)]
             when(on, whole(part, sent, own_sem.at[0]).wait_send)
@@ -1089,18 +1098,18 @@
     parts = len(ORDERS)
     keys = (parts, 7, TWO, TWO)
     terms = 1, x.shape[1]
-    scratch = [dma((1,)), dma(keys + (len(LINKS) + 1,)), dma(keys), dma(keys), dma((TWO,) + keys)]
+    scratch = [dma((1,)), dma(keys + (len(LINKS) + 1,)), dma(keys), dma(keys), dma(keys)]
     n = len(GAIN_AT)
     scratch += [pltpu.VMEM((n,) + terms, F32)] * TWO + [dma((n,)), dma((n,)), pltpu.VMEM(terms, F32)]
     scratch += [pltpu.VMEM((FOUR, TWO) + block, F32), pltpu.VMEM(h_u.shape, BF16)]
     scratch += [pltpu.VMEM((TWO, TWO, BLK, HEAD_DIM), BF16)] * TWO
-    scratch += [pltpu.VMEM((TWO, TWO * N_PAIRS) + b, F32) for b in ((TWO * wo.shape[0], wo.shape[1]), block)]
+    scratch += [pltpu.VMEM((TWO * N_PAIRS,) + b, F32) for b in ((TWO * wo.shape[0], wo.shape[1]), block)]
     return pl.pallas_call(
         gather_kernel,
         name="gather_all",
         out_shape=[jax.ShapeDtypeStruct(s, F32) for s in shapes]
         + [jax.ShapeDtypeStruct(x.shape, BF16), jax.ShapeDtypeStruct(terms, F32)],
-        in_specs=[vmem] * 5 + [hbm] * TWO + [vmem] * 5,
+        in_specs=[vmem] * 5 + [hbm] + [vmem] * 6,
         out_specs=[hbm] * len(shapes) + [vmem] * TWO,
         scratch_shapes=scratch + PairSum.scratch("core", block) + PairSum.sems(1, 1) + HiddenGradient.scratch(x),
         compiler_params=params(63, collective_id=0),

time: 563 us -> 551 us (0.979)
  Pallas kernels: 466 us -> 454 us
    pallas_call x1, Pallas kernels: 179 us -> 172 us  [gather_all(): pl.pallas_call(gather_kernel, name='gather_all', out_shape=[jax.ShapeDtyp...]
  transfers between devices with their start and end apart: 4 -> 4, of which waited for: 2 -> 2; matrix products, arithmetic and copies ran while one was open for 1% -> 1% of each run, Pallas kernels for 7% -> 8%
where the time goes in v12:
time: 551 us; the launch traced here: 549 us
  Pallas kernels  454 us (82%)
  waiting for transfers between devices  46 us (8%)
  local copies, waits for them, and re-layouts  38.9 us (7%)
  other arithmetic  6.43 us (1%)
    pallas_call x1, Pallas kernels, gather_all(): pl.pallas_call(gather_kernel, name='gather_all', out_shape=[jax.ShapeDtyp...  172 us
    pallas_call x1, Pallas kernels, reduce_pairs(): pl.pallas_call(functools.partial(reduce_kernel, cuts, kinds, work), name=...  159 us
    pallas_call x1, Pallas kernels, exchange(): pl.pallas_call(exchange_kernel, name='exchange', out_shape=(jax.ShapeDtyp...  65.6 us
    ppermute x4, waiting for transfers between devices, perm(): return lax.ppermute(x, 'cp', pairs)  46 us
    unnamed x39, local copies, waits for them, and re-layouts  35.2 us
    pallas_call x1, Pallas kernels, flash_bwd(): pl.pallas_call(bwd_kernel, name='attn_bwd', out_shape=(jax.ShapeDtypeStru...  23.4 us
    pallas_call x1, Pallas kernels, flash_fwd(): pl.pallas_call(fwd_kernel, name='attn_fwd', out_shape=(jax.ShapeDtypeStru...  18 us
    pallas_call x1, Pallas kernels, wo_terms(): pl.pallas_call(wo_kernel, name='wo_terms', out_shape=[jax.ShapeDtypeStruc...  14 us
  transfers between devices with their start and end apart: 4, of which 2 were waited for; matrix products, arithmetic and copies ran while one was open for 1% of the time, Pallas kernels for 8%

profile of v12, /device:TPU:0, one launch (start us, length us, event | category | flops | bytes accessed | tf_op | source)
XLA Modules:
  0.0 548.7 jit_solution(3992330880108553611)
XLA Ops:
  0.7 0.8 convert_bitcast_fusion
  1.5 0.7 broadcast_in_dim.9
  2.2 1.3 pad.4.refs_3_
  3.5 1.0 fusion
  4.7 1.4 copy-done.4
  6.1 1.2 copy-done.5
  7.3 1.8 norm_kv.1
  9.2 1.3 copy-done
  10.5 0.8 copy-done.6
  11.3 65.6 %exchange.1 = (bf16[8,2,2,2,256,128]{5,4,3,2,1,0:T(8,128)(2,1)}, bf16[2,2,256,1024]{3,2,1,0:T(8,128)(2,1)}, bf16[2,2,256,1024]{3,2,1,0:T(8,128)(2,1)}, s32[4,8,1...) custom-call(bf16[2,2,2,2,2,64,128]{6,5,4,3,2,1,0:T(8,128)(2,1)} %bitcast.28, ...), custom_call_target="tpu_custom_call" | custom-call | flops 1000000000 | bytes 20971520 | tf_op jit(solution)/shard_map/exchange/pallas_call | solution.py:453
  77.2 1.9 collective-permute-start.1
  79.7 0.6 broadcast_in_dim.8.ko_ref
  80.3 0.7 slice.3
  82.3 0.6 broadcast_subtract_fusion.st_ref
  82.9 0.6 sub.45.qi_ref
  83.5 18.0 %attn_fwd.1 = (bf16[2,2,256,1024]{3,2,1,0:T(8,128)(2,1)}, f32[2,2,8,1,256]{4,3,2,1,0:T(1,128)}) custom-call(s32[10]{0:T(128)} %pad_add_fusion.1.tab, bf16[2,2,256,1024]{3,2,1,0:T(8,128)(2,1)} %get-tuple-element.39.q_ref, bf16[8,2,2,2,256,128]{5,4,3,2,1,0:T(8,128)(2,1)} %get-tuple-element.40.kv_ref, s32[2,2,1,256]{3,2,1,0:T(1,128)} %broadcast_subtract_fusion.st_ref, ...), custom_call_target="tpu_custom_call" | custom-call | flops 20000000000 | bytes 16777216 | tf_op jit(solution)/shard_map/attn_fwd/pallas_call | solution.py:209
  101.5 1.8 multiply_sine_fusion
  103.3 21.9 %collective-permute-done.1.refs_3_ = bf16[2,2,64,2048]{3,2,1,0:T(8,128)(2,1)} collective-permute-done((bf16[2,2,64,2048]{3,2,1,0:T(8,128)(2,1)}, bf16[2,2,64,2048]{3,2,1,0:T(8,128)(2,1)}, u32[]{:S(2)}, u32[]{:S(2)}) %collective-permute-start.1) | collective-permute-done | bytes 1048608 | tf_op jit(solution)/shard_map/ppermute | solution.py:1121
  125.2 14.0 %wo_terms.1 = (f32[4,64,2048]{2,1,0:T(8,128)}, f32[4,64,2048]{2,1,0:T(8,128)}) custom-call(bf16[2,2,256,1024]{3,2,1,0:T(8,128)(2,1)} %get-tuple-element.41.refs_0_.o_ref.refs_3_, bf16[2,2,64,2048]{3,2,1,0:T(8,128)(2,1)} %bitcast.41, bf16[2,2,64,2048]{3,2,1,0:T(8,128)(2,1)} %collective-permute-done.refs_2_, ...), custom_call_target="tpu_custom_call" | custom-call | flops 4000000000 | bytes 20971520 | tf_op jit(solution)/shard_map/wo_terms/pallas_call | solution.py:515
  139.2 0.6 collective-permute-start.3
  139.8 23.4 %attn_bwd.1 = (bf16[2,2,256,1024]{3,2,1,0:T(8,128)(2,1)}, f32[8,2,2,2,256,128]{5,4,3,2,1,0:T(8,128)}) custom-call(s32[10]{0:T(128)} %pad_add_fusion.1.tab, bf16[2,2,256,1024]{3,2,1,0:T(8,128)(2,1)} %get-tuple-element.39.q_ref, bf16[2,2,256,1024]{3,2,1,0:T(8,128)(2,1)} %get-tuple-element.47.do_ref, ...), custom_call_target="tpu_custom_call" | custom-call | flops 49999998976 | bytes 33554432 | tf_op jit(solution)/shard_map/attn_bwd/pallas_call | solution.py:228
  163.2 24.0 %collective-permute-done.3.refs_1_ = f32[4,64,2048]{2,1,0:T(8,128)} collective-permute-done((f32[4,64,2048]{2,1,0:T(8,128)}, f32[4,64,2048]{2,1,0:T(8,128)}, u32[]{:S(2)}, u32[]{:S(2)}) %collective-permute-start.3) | collective-permute-done | bytes 2097184 | tf_op jit(solution)/shard_map/ppermute | solution.py:1121
  187.2 159.2 %reduce_pairs.1 = (f32[64,2048]{1,0:T(8,128)}, f32[2048,128]{1,0:T(8,128)}, f32[128,1024]{1,0:T(8,128)}, bf16[512,2048]{1,0:T(8,128)(2,1)}, f32[512,2048]{1,0:T(8,128)}, /*index=5*/bf16[2,2,256,2048]{3,2,1,0:T(8,128)(2,1)}) custom-call(f32[4,64,2048]{2,1,0:T(8,128)} %get-tuple-element.45.refs_0_, f32[4,64,2048]{2,1,0:T(8,128)} %collective-permute-done.3.refs_1_, ...), custom_call_target="tpu_custom_call" | custom-call | flops 1000000000 | bytes 20971520 | tf_op jit(solution)/shard_map/reduce_pairs/pallas_call | solution.py:888
  346.5 171.7 %gather_all.1 = (f32[2048,2048]{1,0:T(8,128)}, f32[2048,2048]{1,0:T(8,128)}, f32[2048,256]{1,0:T(8,128)}, f32[2048,256]{1,0:T(8,128)}, bf16[512,2048]{1,0:T(8,128)(2,1)}, /*index=5*/f32[1,2048]{1,0:T(1,128)}) custom-call(f32[64,2048]{1,0:T(8,128)} %get-tuple-element.52.refs_0_, f32[128,1024]{1,0:T(8,128)} %get-tuple-element.53.refs_1_, ...), custom_call_target="tpu_custom_call" | custom-call | flops 1000000000 | bytes 79691776 | tf_op jit(solution)/shard_map/gather_all/pallas_call | solution.py:1107
  518.2 3.3 copy.30
  521.5 1.3 copy.31
  522.9 14.6 %copy.32 = f32[2048,2048]{1,0:T(8,128)} copy(f32[2048,2048]{1,0:T(8,128)} %get-tuple-element.87) | data formatting | bytes 33554432
  537.5 1.3 copy.33
  538.8 1.8 copy-done.8
  540.6 1.3 copy.34
  541.9 6.2 %copy.35 = f32[2048,2048]{1,0:T(8,128)} copy(f32[2048,2048]{1,0:T(8,128)S(1)} %bitcast.32) | data formatting | bytes 33554432
  548.1 0.6 copy.36
  (53 shorter events, 2.4 us)
Async XLA Ops:
  0.6 4.1 copy-start.1
  2.2 7.0 %copy-start.7 = (f32[2048]{0:T(1024)}, f32[2048]{0:T(1024)S(1)}, u32[]{:S(2)}) copy-start(f32[2048]{0:T(1024)S(1)} %broadcast_in_dim.9) | copy-start | bytes 24580
  4.7 4.5 copy-start.2
  4.7 4.5 copy-start.3
  4.7 1.4 copy-start.4
  6.1 1.2 copy-start.5
  9.2 1.3 copy-start
  10.5 0.8 copy-start.6
  76.9 48.3 %collective-permute-start.2 = (bf16[2,2,64,2048]{3,2,1,0:T(8,128)(2,1)}, bf16[2,2,64,2048]{3,2,1,0:T(8,128)(2,1)}, u32[]{:S(2)}, u32[]{:S(2)}) collective-permute-start(bf16[2,2,64,2048]{3,2,1,0:T(8,128)(2,1)} %bitcast.42), channel_id=1, source_target_pairs={{0,3},{1,2},{2,1},{3,0},{4,7},{5,6},{6,5},{7,4},{8,11},{9,10},{10,... | collective-permute-start | bytes 3145736 | tf_op jit(solution)/shard_map/ppermute | solution.py:1121
  77.0 48.2 %collective-permute-start = (bf16[2,2,64,2048]{3,2,1,0:T(8,128)(2,1)}, bf16[2,2,64,2048]{3,2,1,0:T(8,128)(2,1)}, u32[]{:S(2)}, u32[]{:S(2)}) collective-permute-start(bf16[2,2,64,2048]{3,2,1,0:T(8,128)(2,1)} %bitcast.43), channel_id=1, source_target_pairs={{0,1},{1,0},{2,3},{3,2},{4,5},{5,4},{6,7},{7,6},{8,9},{9,8},{10,11... | collective-permute-start | bytes 3145736 | tf_op jit(solution)/shard_map/ppermute | solution.py:1121
  77.2 48.0 %collective-permute-start.1 = (bf16[2,2,64,2048]{3,2,1,0:T(8,128)(2,1)}, bf16[2,2,64,2048]{3,2,1,0:T(8,128)(2,1)}, u32[]{:S(2)}, u32[]{:S(2)}) collective-permute-start(bf16[2,2,64,2048]{3,2,1,0:T(8,128)(2,1)} %bitcast.40), channel_id=1, source_target_pairs={{0,2},{1,3},{2,0},{3,1},{4,6},{5,7},{6,4},{7,5},{8,10},{9,11},{10,... | collective-permute-start | bytes 3145736 | tf_op jit(solution)/shard_map/ppermute | solution.py:1121
  139.2 48.0 %collective-permute-start.3 = (f32[4,64,2048]{2,1,0:T(8,128)}, f32[4,64,2048]{2,1,0:T(8,128)}, u32[]{:S(2)}, u32[]{:S(2)}) collective-permute-start(f32[4,64,2048]{2,1,0:T(8,128)} %get-tuple-element.46), channel_id=1, source_target_pairs={{0,4},{1,5},{2,6},{3,7},{4,0},{5,1},{6,2},{7,3},{8,12},{9,13},{10,... | collective-permute-start | bytes 6291464 | tf_op jit(solution)/shard_map/ppermute | solution.py:1121
  518.2 3.3 copy-start.10
  521.5 20.4 %slice-start = ((s8[16777216]{0:T(1024)(128)(4,1)}), s8[4194304]{0:T(1024)(128)(4,1)S(1)}, s32[]{:S(2)}) async-start(s8[16777216]{0:T(1024)(128)(4,1)} %bitcast.31), calls=%async_computation | async-start | bytes 8388608
  522.9 14.6 %copy-start.9 = (f32[2048,256]{1,0:T(8,128)S(1)}, f32[2048,256]{1,0:T(8,128)}, u32[]{:S(2)}) copy-start(f32[2048,256]{1,0:T(8,128)} %get-tuple-element.88) | copy-start | bytes 6291460
  522.9 19.0 %slice-start.1 = ((s8[16777216]{0:T(1024)(128)(4,1)}), s8[4194304]{0:T(1024)(128)(4,1)S(1)}, s32[]{:S(2)}) async-start(s8[16777216]{0:T(1024)(128)(4,1)} %bitcast.31), calls=%async_computation.1 | async-start | bytes 8388608
  522.9 19.0 %slice-start.2 = ((s8[16777216]{0:T(1024)(128)(4,1)}), s8[4194304]{0:T(1024)(128)(4,1)S(1)}, s32[]{:S(2)}) async-start(s8[16777216]{0:T(1024)(128)(4,1)} %bitcast.31), calls=%async_computation.2 | async-start | bytes 8388608
  522.9 19.0 %slice-start.3 = ((s8[16777216]{0:T(1024)(128)(4,1)}), s8[4194304]{0:T(1024)(128)(4,1)S(1)}, s32[]{:S(2)}) async-start(s8[16777216]{0:T(1024)(128)(4,1)} %bitcast.31), calls=%async_computation.3 | async-start | bytes 8388608
  537.5 3.1 copy-start.8
  541.9 6.2 %copy-start.11 = (f32[1,2048]{1,0:T(1,128)S(1)}, f32[1,2048]{1,0:T(1,128)}, u32[]{:S(2)}) copy-start(f32[1,2048]{1,0:T(1,128)} %get-tuple-element.62) | copy-start | bytes 24580

commit v13 on v12

--- a/solution.py
+++ b/solution.py
@@ -75,15 +75,24 @@
     b, hf = pl.program_id(0), pl.program_id(1)
     own, first, last_start = tab[T_SQ + hf], tab[T_LO + TWO * b + hf], tab[T_MX + TWO * b + hf]
 
-    def step(s, carry):
+    def place_of(s):
         late = s >= N_PAIRS
-        at = jnp.where(late, N_SUPER - 1 - s, s), late.astype(jnp.int32)
-        full = jnp.logical_and(s < own, s * BLK >= last_start)
-        pl.when(full)(lambda: body(s, at, False))
-        pl.when(jnp.logical_not(full))(lambda: body(s, at, True))
-        return carry
-
-    lax.fori_loop(first, own + 1, step, 0)
+        return jnp.where(late, N_SUPER - 1 - s, s), late.astype(jnp.int32)
+
+    full_from = jnp.minimum((last_start + BLK - 1) // BLK, own)
+    full_from += lax.rem(own - full_from, TWO)
+    count = full_from - first
+
+    @pl.loop(0, count + 1)
+    def _(t):
+        s = jnp.where(t < count, first + t, own)
+        body(s, place_of(s), True)
+
+    @pl.loop(0, (own - full_from) // TWO)
+    def _(t):
+        for i in range(TWO):
+            s = full_from + TWO * t + i
+            body(s, place_of(s), False)
 
 
 def down(row, n):

time: 551 us -> 551 us (level)
  no operation moved by 1% of the time
where the time goes in v13:
time: 551 us; the launch traced here: 549 us
  Pallas kernels  454 us (82%)
  waiting for transfers between devices  45.9 us (8%)
  local copies, waits for them, and re-layouts  38.9 us (7%)
  other arithmetic  6.43 us (1%)
    pallas_call x1, Pallas kernels, gather_all(): pl.pallas_call(gather_kernel, name='gather_all', out_shape=[jax.ShapeDtyp...  174 us
    pallas_call x1, Pallas kernels, reduce_pairs(): pl.pallas_call(functools.partial(reduce_kernel, cuts, kinds, work), name=...  157 us
    pallas_call x1, Pallas kernels, exchange(): pl.pallas_call(exchange_kernel, name='exchange', out_shape=(jax.ShapeDtyp...  65.6 us
    ppermute x4, waiting for transfers between devices, perm(): return lax.ppermute(x, 'cp', pairs)  45.9 us
    unnamed x39, local copies, waits for them, and re-layouts  35.2 us
    pallas_call x1, Pallas kernels, flash_bwd(): pl.pallas_call(bwd_kernel, name='attn_bwd', out_shape=(jax.ShapeDtypeStru...  23.5 us
    pallas_call x1, Pallas kernels, flash_fwd(): pl.pallas_call(fwd_kernel, name='attn_fwd', out_shape=(jax.ShapeDtypeStru...  18 us
    pallas_call x1, Pallas kernels, wo_terms(): pl.pallas_call(wo_kernel, name='wo_terms', out_shape=[jax.ShapeDtypeStruc...  14 us
  transfers between devices with their start and end apart: 4, of which 2 were waited for; matrix products, arithmetic and copies ran while one was open for 1% of the time, Pallas kernels for 8%

profile of v13, /device:TPU:0, one launch (start us, length us, event | category | flops | bytes accessed | tf_op | source)
XLA Modules:
  0.0 548.6 jit_solution(2709933664738227189)
XLA Ops:
  0.7 0.8 convert_bitcast_fusion
  1.5 0.7 broadcast_in_dim.9
  2.2 1.3 pad.4.refs_3_
  3.5 1.0 fusion
  4.7 1.4 copy-done.4
  6.1 1.2 copy-done.5
  7.3 1.8 norm_kv.1
  9.2 1.3 copy-done
  10.5 0.8 copy-done.6
  11.3 65.6 %exchange.1 = (bf16[8,2,2,2,256,128]{5,4,3,2,1,0:T(8,128)(2,1)}, bf16[2,2,256,1024]{3,2,1,0:T(8,128)(2,1)}, bf16[2,2,256,1024]{3,2,1,0:T(8,128)(2,1)}, s32[4,8,1...) custom-call(bf16[2,2,2,2,2,64,128]{6,5,4,3,2,1,0:T(8,128)(2,1)} %bitcast.28, ...), custom_call_target="tpu_custom_call" | custom-call | flops 1000000000 | bytes 20971520 | tf_op jit(solution)/shard_map/exchange/pallas_call | solution.py:462
  77.2 1.9 collective-permute-start.1
  79.7 0.6 broadcast_in_dim.8.ko_ref
  80.3 0.7 slice.3
  82.3 0.6 broadcast_subtract_fusion.st_ref
  82.9 0.6 sub.45.qi_ref
  83.5 18.0 %attn_fwd.1 = (bf16[2,2,256,1024]{3,2,1,0:T(8,128)(2,1)}, f32[2,2,8,1,256]{4,3,2,1,0:T(1,128)}) custom-call(s32[10]{0:T(128)} %pad_add_fusion.1.tab, bf16[2,2,256,1024]{3,2,1,0:T(8,128)(2,1)} %get-tuple-element.39.q_ref, bf16[8,2,2,2,256,128]{5,4,3,2,1,0:T(8,128)(2,1)} %get-tuple-element.40.kv_ref, s32[2,2,1,256]{3,2,1,0:T(1,128)} %broadcast_subtract_fusion.st_ref, ...), custom_call_target="tpu_custom_call" | custom-call | flops 20000000000 | bytes 16777216 | tf_op jit(solution)/shard_map/attn_fwd/pallas_call | solution.py:218
  101.5 1.8 multiply_sine_fusion
  103.3 21.9 %collective-permute-done.1.refs_3_ = bf16[2,2,64,2048]{3,2,1,0:T(8,128)(2,1)} collective-permute-done((bf16[2,2,64,2048]{3,2,1,0:T(8,128)(2,1)}, bf16[2,2,64,2048]{3,2,1,0:T(8,128)(2,1)}, u32[]{:S(2)}, u32[]{:S(2)}) %collective-permute-start.1) | collective-permute-done | bytes 1048608 | tf_op jit(solution)/shard_map/ppermute | solution.py:1130
  125.2 14.0 %wo_terms.1 = (f32[4,64,2048]{2,1,0:T(8,128)}, f32[4,64,2048]{2,1,0:T(8,128)}) custom-call(bf16[2,2,256,1024]{3,2,1,0:T(8,128)(2,1)} %get-tuple-element.41.refs_0_.o_ref.refs_3_, bf16[2,2,64,2048]{3,2,1,0:T(8,128)(2,1)} %bitcast.41, bf16[2,2,64,2048]{3,2,1,0:T(8,128)(2,1)} %collective-permute-done.refs_2_, ...), custom_call_target="tpu_custom_call" | custom-call | flops 4000000000 | bytes 20971520 | tf_op jit(solution)/shard_map/wo_terms/pallas_call | solution.py:524
  139.2 0.6 collective-permute-start.3
  139.8 23.5 %attn_bwd.1 = (bf16[2,2,256,1024]{3,2,1,0:T(8,128)(2,1)}, f32[8,2,2,2,256,128]{5,4,3,2,1,0:T(8,128)}) custom-call(s32[10]{0:T(128)} %pad_add_fusion.1.tab, bf16[2,2,256,1024]{3,2,1,0:T(8,128)(2,1)} %get-tuple-element.39.q_ref, bf16[2,2,256,1024]{3,2,1,0:T(8,128)(2,1)} %get-tuple-element.47.do_ref, ...), custom_call_target="tpu_custom_call" | custom-call | flops 49999998976 | bytes 33554432 | tf_op jit(solution)/shard_map/attn_bwd/pallas_call | solution.py:237
  163.2 24.0 %collective-permute-done.3.refs_1_ = f32[4,64,2048]{2,1,0:T(8,128)} collective-permute-done((f32[4,64,2048]{2,1,0:T(8,128)}, f32[4,64,2048]{2,1,0:T(8,128)}, u32[]{:S(2)}, u32[]{:S(2)}) %collective-permute-start.3) | collective-permute-done | bytes 2097184 | tf_op jit(solution)/shard_map/ppermute | solution.py:1130
  187.2 157.0 %reduce_pairs.1 = (f32[64,2048]{1,0:T(8,128)}, f32[2048,128]{1,0:T(8,128)}, f32[128,1024]{1,0:T(8,128)}, bf16[512,2048]{1,0:T(8,128)(2,1)}, f32[512,2048]{1,0:T(8,128)}, /*index=5*/bf16[2,2,256,2048]{3,2,1,0:T(8,128)(2,1)}) custom-call(f32[4,64,2048]{2,1,0:T(8,128)} %get-tuple-element.45.refs_0_, f32[4,64,2048]{2,1,0:T(8,128)} %collective-permute-done.3.refs_1_, ...), custom_call_target="tpu_custom_call" | custom-call | flops 1000000000 | bytes 20971520 | tf_op jit(solution)/shard_map/reduce_pairs/pallas_call | solution.py:897
  344.2 173.9 %gather_all.1 = (f32[2048,2048]{1,0:T(8,128)}, f32[2048,2048]{1,0:T(8,128)}, f32[2048,256]{1,0:T(8,128)}, f32[2048,256]{1,0:T(8,128)}, bf16[512,2048]{1,0:T(8,128)(2,1)}, /*index=5*/f32[1,2048]{1,0:T(1,128)}) custom-call(f32[64,2048]{1,0:T(8,128)} %get-tuple-element.52.refs_0_, f32[128,1024]{1,0:T(8,128)} %get-tuple-element.53.refs_1_, ...), custom_call_target="tpu_custom_call" | custom-call | flops 1000000000 | bytes 79691776 | tf_op jit(solution)/shard_map/gather_all/pallas_call | solution.py:1116
  518.1 3.3 copy.30
  521.4 1.3 copy.31
  522.8 14.6 %copy.32 = f32[2048,2048]{1,0:T(8,128)} copy(f32[2048,2048]{1,0:T(8,128)} %get-tuple-element.87) | data formatting | bytes 33554432
  537.4 1.3 copy.33
  538.7 1.8 copy-done.8
  540.5 1.3 copy.34
  541.8 6.2 %copy.35 = f32[2048,2048]{1,0:T(8,128)} copy(f32[2048,2048]{1,0:T(8,128)S(1)} %bitcast.32) | data formatting | bytes 33554432
  548.0 0.6 copy.36
  (53 shorter events, 2.4 us)
Async XLA Ops:
  0.6 4.1 copy-start.1
  2.2 7.0 %copy-start.7 = (f32[2048]{0:T(1024)}, f32[2048]{0:T(1024)S(1)}, u32[]{:S(2)}) copy-start(f32[2048]{0:T(1024)S(1)} %broadcast_in_dim.9) | copy-start | bytes 24580
  4.7 4.5 copy-start.2
  4.7 4.5 copy-start.3
  4.7 1.4 copy-start.4
  6.1 1.2 copy-start.5
  9.2 1.3 copy-start
  10.5 0.8 copy-start.6
  76.9 48.3 %collective-permute-start.2 = (bf16[2,2,64,2048]{3,2,1,0:T(8,128)(2,1)}, bf16[2,2,64,2048]{3,2,1,0:T(8,128)(2,1)}, u32[]{:S(2)}, u32[]{:S(2)}) collective-permute-start(bf16[2,2,64,2048]{3,2,1,0:T(8,128)(2,1)} %bitcast.42), channel_id=1, source_target_pairs={{0,3},{1,2},{2,1},{3,0},{4,7},{5,6},{6,5},{7,4},{8,11},{9,10},{10,... | collective-permute-start | bytes 3145736 | tf_op jit(solution)/shard_map/ppermute | solution.py:1130
  77.0 48.2 %collective-permute-start = (bf16[2,2,64,2048]{3,2,1,0:T(8,128)(2,1)}, bf16[2,2,64,2048]{3,2,1,0:T(8,128)(2,1)}, u32[]{:S(2)}, u32[]{:S(2)}) collective-permute-start(bf16[2,2,64,2048]{3,2,1,0:T(8,128)(2,1)} %bitcast.43), channel_id=1, source_target_pairs={{0,1},{1,0},{2,3},{3,2},{4,5},{5,4},{6,7},{7,6},{8,9},{9,8},{10,11... | collective-permute-start | bytes 3145736 | tf_op jit(solution)/shard_map/ppermute | solution.py:1130
  77.2 48.0 %collective-permute-start.1 = (bf16[2,2,64,2048]{3,2,1,0:T(8,128)(2,1)}, bf16[2,2,64,2048]{3,2,1,0:T(8,128)(2,1)}, u32[]{:S(2)}, u32[]{:S(2)}) collective-permute-start(bf16[2,2,64,2048]{3,2,1,0:T(8,128)(2,1)} %bitcast.40), channel_id=1, source_target_pairs={{0,2},{1,3},{2,0},{3,1},{4,6},{5,7},{6,4},{7,5},{8,10},{9,11},{10,... | collective-permute-start | bytes 3145736 | tf_op jit(solution)/shard_map/ppermute | solution.py:1130
  139.2 48.0 %collective-permute-start.3 = (f32[4,64,2048]{2,1,0:T(8,128)}, f32[4,64,2048]{2,1,0:T(8,128)}, u32[]{:S(2)}, u32[]{:S(2)}) collective-permute-start(f32[4,64,2048]{2,1,0:T(8,128)} %get-tuple-element.46), channel_id=1, source_target_pairs={{0,4},{1,5},{2,6},{3,7},{4,0},{5,1},{6,2},{7,3},{8,12},{9,13},{10,... | collective-permute-start | bytes 6291464 | tf_op jit(solution)/shard_map/ppermute | solution.py:1130
  518.1 3.3 copy-start.10
  521.4 20.4 %slice-start = ((s8[16777216]{0:T(1024)(128)(4,1)}), s8[4194304]{0:T(1024)(128)(4,1)S(1)}, s32[]{:S(2)}) async-start(s8[16777216]{0:T(1024)(128)(4,1)} %bitcast.31), calls=%async_computation | async-start | bytes 8388608
  522.8 14.6 %copy-start.9 = (f32[2048,256]{1,0:T(8,128)S(1)}, f32[2048,256]{1,0:T(8,128)}, u32[]{:S(2)}) copy-start(f32[2048,256]{1,0:T(8,128)} %get-tuple-element.88) | copy-start | bytes 6291460
  522.8 19.0 %slice-start.1 = ((s8[16777216]{0:T(1024)(128)(4,1)}), s8[4194304]{0:T(1024)(128)(4,1)S(1)}, s32[]{:S(2)}) async-start(s8[16777216]{0:T(1024)(128)(4,1)} %bitcast.31), calls=%async_computation.1 | async-start | bytes 8388608
  522.8 19.0 %slice-start.2 = ((s8[16777216]{0:T(1024)(128)(4,1)}), s8[4194304]{0:T(1024)(128)(4,1)S(1)}, s32[]{:S(2)}) async-start(s8[16777216]{0:T(1024)(128)(4,1)} %bitcast.31), calls=%async_computation.2 | async-start | bytes 8388608
  522.8 19.0 %slice-start.3 = ((s8[16777216]{0:T(1024)(128)(4,1)}), s8[4194304]{0:T(1024)(128)(4,1)S(1)}, s32[]{:S(2)}) async-start(s8[16777216]{0:T(1024)(128)(4,1)} %bitcast.31), calls=%async_computation.3 | async-start | bytes 8388608
  537.4 3.1 copy-start.8
  541.8 6.2 %copy-start.11 = (f32[1,2048]{1,0:T(1,128)S(1)}, f32[1,2048]{1,0:T(1,128)}, u32[]{:S(2)}) copy-start(f32[1,2048]{1,0:T(1,128)} %get-tuple-element.62) | copy-start | bytes 24580

commit v14 on v13

--- a/solution.py
+++ b/solution.py
@@ -297,11 +297,15 @@
     return [(k, lax.rem(z + k, FOUR)) for k in (1, TWO, THREE)]
 
 
-def meet(peers):
+def announce(peers):
     barrier = pltpu.get_barrier_semaphore()
     for d in peers:
         pl.semaphore_signal(barrier, device_id=(d,), device_id_type=MESH)
-    pl.semaphore_wait(barrier, len(peers))
+    return lambda: pl.semaphore_wait(barrier, len(peers))
+
+
+def meet(peers):
+    announce(peers)()
 
 
 def remote(src, dst, send, arrive, to):
@@ -482,7 +486,7 @@
     keep, away, dy_u, o_t, terms, came, load_sem, core_s, core_r = take(len(refs))
     me = lax.axis_index("cp")
     _, y, _, core = place(me)
-    meet(quad_of(me)[1:TWO])
+    all_here = announce(quad_of(me)[1:TWO])
     loads = [
         pltpu.make_async_copy(src, dy_u.at[:, :, pl.ds(d * CHUNK, CHUNK)], load_sem.at[d])
         for d, src in enumerate(pieces)
@@ -493,6 +497,7 @@
         o_t[head(h)] = o_ref[:, :, :, head(h)].reshape(-1, HEAD_DIM).T
     for c in loads:
         c.wait()
+    all_here()
     half, tiles = terms.shape[1], terms.shape[TWO] // BLK
 
     def swap(t):
@@ -978,12 +983,14 @@
     line = Line(me)
     to = {"x": dev(z, y, 1 - x, core), "y": dev(z, 1 - y, x, core), "u": line.next[1], "d": line.next[-1]}
     partner = dev(z, y, x, 1 - core)
+    all_here = announce(quad_of(me)[1:] + [to["y"]] + [dev(zz, y, x, core) for _, zz in z_peers(z)])
     chip_here = me // TWO
     n_wo, wide = wo_ref.shape[0], wq_ref.shape[1]
     store[chip_here, pl.ds(0, n_wo)] = wo_ref[...]
     for i in range(TWO):
         store[chip_here, pl.ds(n_wo, n_wo), pl.ds(i * wide, wide)] = wq_ref[pl.ds(i * n_wo, n_wo)]
-    meet(quad_of(me)[1:] + [to["y"]] + [dev(zz, y, x, core) for _, zz in z_peers(z)])
+    turn_back(dkv_ref, cos_ref, sin_ref, dk_u, dv_u)
+    all_here()
     load_h = pltpu.make_async_copy(h_ref, h_own, own_sem.at[0])
     load_h.start()
     wkv = PairSum(me, "core", 1, wkv_ref, wkv_store.at[chip_here], buffers, [r.at[0] for r in sems])
@@ -1072,7 +1079,6 @@
     events = arrivals()
     for part in range(THREE):
         pass_on(part, HERE)
-    turn_back(dkv_ref, cos_ref, sin_ref, dk_u, dv_u)
     job = HiddenGradient(me, dk_u, dv_u, grad_ins, (dx_ref, terms), refs)
     load_h.wait()
     wkv_terms(h_own, dk_u, dv_u, ((wkv_ref, 1 - core), (buffers[0], core)))

time: 551 us -> 551 us (level)
  no operation moved by 1% of the time
where the time goes in v14:
time: 551 us; the launch traced here: 549 us
  Pallas kernels  454 us (82%)
  waiting for transfers between devices  46.1 us (8%)
  local copies, waits for them, and re-layouts  38.9 us (7%)
  other arithmetic  6.43 us (1%)
    pallas_call x1, Pallas kernels, gather_all(): pl.pallas_call(gather_kernel, name='gather_all', out_shape=[jax.ShapeDtyp...  174 us
    pallas_call x1, Pallas kernels, reduce_pairs(): pl.pallas_call(functools.partial(reduce_kernel, cuts, kinds, work), name=...  157 us
    pallas_call x1, Pallas kernels, exchange(): pl.pallas_call(exchange_kernel, name='exchange', out_shape=(jax.ShapeDtyp...  65.6 us
    ppermute x4, waiting for transfers between devices, perm(): return lax.ppermute(x, 'cp', pairs)  46.1 us
    unnamed x39, local copies, waits for them, and re-layouts  35.2 us
    pallas_call x1, Pallas kernels, flash_bwd(): pl.pallas_call(bwd_kernel, name='attn_bwd', out_shape=(jax.ShapeDtypeStru...  23.5 us
    pallas_call x1, Pallas kernels, flash_fwd(): pl.pallas_call(fwd_kernel, name='attn_fwd', out_shape=(jax.ShapeDtypeStru...  18 us
    pallas_call x1, Pallas kernels, wo_terms(): pl.pallas_call(wo_kernel, name='wo_terms', out_shape=[jax.ShapeDtypeStruc...  13.6 us
  transfers between devices with their start and end apart: 4, of which 2 were waited for; matrix products, arithmetic and copies ran while one was open for 1% of the time, Pallas kernels for 8%

profile of v14, /device:TPU:0, one launch (start us, length us, event | category | flops | bytes accessed | tf_op | source)
XLA Modules:
  0.0 548.8 jit_solution(125498649125403921)
XLA Ops:
  0.7 0.8 convert_bitcast_fusion
  1.5 0.7 broadcast_in_dim.9
  2.2 1.3 pad.4.refs_3_
  3.5 1.0 fusion
  4.7 1.4 copy-done.4
  6.1 1.2 copy-done.5
  7.3 1.8 norm_kv.1
  9.2 1.3 copy-done
  10.5 0.8 copy-done.6
  11.3 65.6 %exchange.1 = (bf16[8,2,2,2,256,128]{5,4,3,2,1,0:T(8,128)(2,1)}, bf16[2,2,256,1024]{3,2,1,0:T(8,128)(2,1)}, bf16[2,2,256,1024]{3,2,1,0:T(8,128)(2,1)}, s32[4,8,1...) custom-call(bf16[2,2,2,2,2,64,128]{6,5,4,3,2,1,0:T(8,128)(2,1)} %bitcast.28, ...), custom_call_target="tpu_custom_call" | custom-call | flops 1000000000 | bytes 20971520 | tf_op jit(solution)/shard_map/exchange/pallas_call | solution.py:466
  77.2 1.9 collective-permute-start.1
  79.7 0.6 broadcast_in_dim.8.ko_ref
  80.3 0.7 slice.3
  82.3 0.6 broadcast_subtract_fusion.st_ref
  82.9 0.6 sub.45.qi_ref
  83.5 18.0 %attn_fwd.1 = (bf16[2,2,256,1024]{3,2,1,0:T(8,128)(2,1)}, f32[2,2,8,1,256]{4,3,2,1,0:T(1,128)}) custom-call(s32[10]{0:T(128)} %pad_add_fusion.1.tab, bf16[2,2,256,1024]{3,2,1,0:T(8,128)(2,1)} %get-tuple-element.39.q_ref, bf16[8,2,2,2,256,128]{5,4,3,2,1,0:T(8,128)(2,1)} %get-tuple-element.40.kv_ref, s32[2,2,1,256]{3,2,1,0:T(1,128)} %broadcast_subtract_fusion.st_ref, ...), custom_call_target="tpu_custom_call" | custom-call | flops 20000000000 | bytes 16777216 | tf_op jit(solution)/shard_map/attn_fwd/pallas_call | solution.py:218
  101.5 1.8 multiply_sine_fusion
  103.3 21.9 %collective-permute-done.1.refs_3_ = bf16[2,2,64,2048]{3,2,1,0:T(8,128)(2,1)} collective-permute-done((bf16[2,2,64,2048]{3,2,1,0:T(8,128)(2,1)}, bf16[2,2,64,2048]{3,2,1,0:T(8,128)(2,1)}, u32[]{:S(2)}, u32[]{:S(2)}) %collective-permute-start.1) | collective-permute-done | bytes 1048608 | tf_op jit(solution)/shard_map/ppermute | solution.py:1136
  125.2 13.6 %wo_terms.1 = (f32[4,64,2048]{2,1,0:T(8,128)}, f32[4,64,2048]{2,1,0:T(8,128)}) custom-call(bf16[2,2,256,1024]{3,2,1,0:T(8,128)(2,1)} %get-tuple-element.41.refs_0_.o_ref.refs_3_, bf16[2,2,64,2048]{3,2,1,0:T(8,128)(2,1)} %bitcast.41, bf16[2,2,64,2048]{3,2,1,0:T(8,128)(2,1)} %collective-permute-done.refs_2_, ...), custom_call_target="tpu_custom_call" | custom-call | flops 4000000000 | bytes 20971520 | tf_op jit(solution)/shard_map/wo_terms/pallas_call | solution.py:529
  138.8 0.6 collective-permute-start.3
  139.4 23.5 %attn_bwd.1 = (bf16[2,2,256,1024]{3,2,1,0:T(8,128)(2,1)}, f32[8,2,2,2,256,128]{5,4,3,2,1,0:T(8,128)}) custom-call(s32[10]{0:T(128)} %pad_add_fusion.1.tab, bf16[2,2,256,1024]{3,2,1,0:T(8,128)(2,1)} %get-tuple-element.39.q_ref, bf16[2,2,256,1024]{3,2,1,0:T(8,128)(2,1)} %get-tuple-element.47.do_ref, ...), custom_call_target="tpu_custom_call" | custom-call | flops 49999998976 | bytes 33554432 | tf_op jit(solution)/shard_map/attn_bwd/pallas_call | solution.py:237
  162.9 24.2 %collective-permute-done.3.refs_1_ = f32[4,64,2048]{2,1,0:T(8,128)} collective-permute-done((f32[4,64,2048]{2,1,0:T(8,128)}, f32[4,64,2048]{2,1,0:T(8,128)}, u32[]{:S(2)}, u32[]{:S(2)}) %collective-permute-start.3) | collective-permute-done | bytes 2097184 | tf_op jit(solution)/shard_map/ppermute | solution.py:1136
  187.1 157.3 %reduce_pairs.1 = (f32[64,2048]{1,0:T(8,128)}, f32[2048,128]{1,0:T(8,128)}, f32[128,1024]{1,0:T(8,128)}, bf16[512,2048]{1,0:T(8,128)(2,1)}, f32[512,2048]{1,0:T(8,128)}, /*index=5*/bf16[2,2,256,2048]{3,2,1,0:T(8,128)(2,1)}) custom-call(f32[4,64,2048]{2,1,0:T(8,128)} %get-tuple-element.45.refs_0_, f32[4,64,2048]{2,1,0:T(8,128)} %collective-permute-done.3.refs_1_, ...), custom_call_target="tpu_custom_call" | custom-call | flops 1000000000 | bytes 20971520 | tf_op jit(solution)/shard_map/reduce_pairs/pallas_call | solution.py:902
  344.4 174.0 %gather_all.1 = (f32[2048,2048]{1,0:T(8,128)}, f32[2048,2048]{1,0:T(8,128)}, f32[2048,256]{1,0:T(8,128)}, f32[2048,256]{1,0:T(8,128)}, bf16[512,2048]{1,0:T(8,128)(2,1)}, /*index=5*/f32[1,2048]{1,0:T(1,128)}) custom-call(f32[64,2048]{1,0:T(8,128)} %get-tuple-element.52.refs_0_, f32[128,1024]{1,0:T(8,128)} %get-tuple-element.53.refs_1_, ...), custom_call_target="tpu_custom_call" | custom-call | flops 1000000000 | bytes 79691776 | tf_op jit(solution)/shard_map/gather_all/pallas_call | solution.py:1122
  518.4 3.3 copy.30
  521.7 1.3 copy.31
  523.0 14.6 %copy.32 = f32[2048,2048]{1,0:T(8,128)} copy(f32[2048,2048]{1,0:T(8,128)} %get-tuple-element.87) | data formatting | bytes 33554432
  537.6 1.3 copy.33
  539.0 1.8 copy-done.8
  540.7 1.3 copy.34
  542.1 6.2 %copy.35 = f32[2048,2048]{1,0:T(8,128)} copy(f32[2048,2048]{1,0:T(8,128)S(1)} %bitcast.32) | data formatting | bytes 33554432
  548.2 0.6 copy.36
  (53 shorter events, 2.4 us)
Async XLA Ops:
  0.6 4.1 copy-start.1
  2.2 7.0 %copy-start.7 = (f32[2048]{0:T(1024)}, f32[2048]{0:T(1024)S(1)}, u32[]{:S(2)}) copy-start(f32[2048]{0:T(1024)S(1)} %broadcast_in_dim.9) | copy-start | bytes 24580
  4.7 4.5 copy-start.2
  4.7 4.5 copy-start.3
  4.7 1.4 copy-start.4
  6.1 1.2 copy-start.5
  9.2 1.3 copy-start
  10.5 0.8 copy-start.6
  76.9 48.3 %collective-permute-start.2 = (bf16[2,2,64,2048]{3,2,1,0:T(8,128)(2,1)}, bf16[2,2,64,2048]{3,2,1,0:T(8,128)(2,1)}, u32[]{:S(2)}, u32[]{:S(2)}) collective-permute-start(bf16[2,2,64,2048]{3,2,1,0:T(8,128)(2,1)} %bitcast.42), channel_id=1, source_target_pairs={{0,3},{1,2},{2,1},{3,0},{4,7},{5,6},{6,5},{7,4},{8,11},{9,10},{10,... | collective-permute-start | bytes 3145736 | tf_op jit(solution)/shard_map/ppermute | solution.py:1136
  77.0 48.2 %collective-permute-start = (bf16[2,2,64,2048]{3,2,1,0:T(8,128)(2,1)}, bf16[2,2,64,2048]{3,2,1,0:T(8,128)(2,1)}, u32[]{:S(2)}, u32[]{:S(2)}) collective-permute-start(bf16[2,2,64,2048]{3,2,1,0:T(8,128)(2,1)} %bitcast.43), channel_id=1, source_target_pairs={{0,1},{1,0},{2,3},{3,2},{4,5},{5,4},{6,7},{7,6},{8,9},{9,8},{10,11... | collective-permute-start | bytes 3145736 | tf_op jit(solution)/shard_map/ppermute | solution.py:1136
  77.2 48.0 %collective-permute-start.1 = (bf16[2,2,64,2048]{3,2,1,0:T(8,128)(2,1)}, bf16[2,2,64,2048]{3,2,1,0:T(8,128)(2,1)}, u32[]{:S(2)}, u32[]{:S(2)}) collective-permute-start(bf16[2,2,64,2048]{3,2,1,0:T(8,128)(2,1)} %bitcast.40), channel_id=1, source_target_pairs={{0,2},{1,3},{2,0},{3,1},{4,6},{5,7},{6,4},{7,5},{8,10},{9,11},{10,... | collective-permute-start | bytes 3145736 | tf_op jit(solution)/shard_map/ppermute | solution.py:1136
  138.8 48.3 %collective-permute-start.3 = (f32[4,64,2048]{2,1,0:T(8,128)}, f32[4,64,2048]{2,1,0:T(8,128)}, u32[]{:S(2)}, u32[]{:S(2)}) collective-permute-start(f32[4,64,2048]{2,1,0:T(8,128)} %get-tuple-element.46), channel_id=1, source_target_pairs={{0,4},{1,5},{2,6},{3,7},{4,0},{5,1},{6,2},{7,3},{8,12},{9,13},{10,... | collective-permute-start | bytes 6291464 | tf_op jit(solution)/shard_map/ppermute | solution.py:1136
  518.4 3.3 copy-start.10
  521.7 20.4 %slice-start = ((s8[16777216]{0:T(1024)(128)(4,1)}), s8[4194304]{0:T(1024)(128)(4,1)S(1)}, s32[]{:S(2)}) async-start(s8[16777216]{0:T(1024)(128)(4,1)} %bitcast.31), calls=%async_computation | async-start | bytes 8388608
  523.0 14.6 %copy-start.9 = (f32[2048,256]{1,0:T(8,128)S(1)}, f32[2048,256]{1,0:T(8,128)}, u32[]{:S(2)}) copy-start(f32[2048,256]{1,0:T(8,128)} %get-tuple-element.88) | copy-start | bytes 6291460
  523.0 19.0 %slice-start.1 = ((s8[16777216]{0:T(1024)(128)(4,1)}), s8[4194304]{0:T(1024)(128)(4,1)S(1)}, s32[]{:S(2)}) async-start(s8[16777216]{0:T(1024)(128)(4,1)} %bitcast.31), calls=%async_computation.1 | async-start | bytes 8388608
  523.0 19.0 %slice-start.2 = ((s8[16777216]{0:T(1024)(128)(4,1)}), s8[4194304]{0:T(1024)(128)(4,1)S(1)}, s32[]{:S(2)}) async-start(s8[16777216]{0:T(1024)(128)(4,1)} %bitcast.31), calls=%async_computation.2 | async-start | bytes 8388608
  523.0 19.0 %slice-start.3 = ((s8[16777216]{0:T(1024)(128)(4,1)}), s8[4194304]{0:T(1024)(128)(4,1)S(1)}, s32[]{:S(2)}) async-start(s8[16777216]{0:T(1024)(128)(4,1)} %bitcast.31), calls=%async_computation.3 | async-start | bytes 8388608
  537.6 3.1 copy-start.8
  542.1 6.2 %copy-start.11 = (f32[1,2048]{1,0:T(1,128)S(1)}, f32[1,2048]{1,0:T(1,128)}, u32[]{:S(2)}) copy-start(f32[1,2048]{1,0:T(1,128)} %get-tuple-element.62) | copy-start | bytes 24580

commit v15 on v14

--- a/solution.py
+++ b/solution.py
@@ -267,20 +267,24 @@
     h_ref[...] = h
     k = jnp.dot(h, wk_ref[...], preferred_element_type=F32)
     v = jnp.dot(h, wv_ref[...], preferred_element_type=F32)
-    n = kv_ref.shape[THREE]
     for i in range(TWO):
-        for j, val in enumerate((turn(k[:, head_slice(i)], cos_ref, sin_ref), v[:, head_slice(i)])):
-            for c in range(TWO):
-                kv_ref[i, c, j] = val[c * n : (c + 1) * n].astype(BF16)
+        kv_ref[i, 0] = turn(k[:, head_slice(i)], cos_ref, sin_ref).astype(BF16)
+        kv_ref[i, 1] = v[:, head_slice(i)].astype(BF16)
 
 
 def project(x, gain, w_k, w_v, cos_f, sin_f):
-    n = x.shape[0] // TWO
+    n = TWO * CHUNK
+    tile = pl.BlockSpec((n, x.shape[1]), lambda i: (i, 0))
+    rope = pl.BlockSpec((n, HEAD_DIM), lambda i: (i, 0))
+    whole = [pl.BlockSpec(a.shape, lambda i: (0, 0)) for a in (gain, w_k, w_v)]
     return pl.pallas_call(
         first_kernel,
         name="norm_kv",
-        out_shape=(jax.ShapeDtypeStruct(x.shape, BF16), jax.ShapeDtypeStruct((TWO,) * THREE + (n, HEAD_DIM), BF16)),
-        compiler_params=params(20),
+        grid=(x.shape[0] // n,),
+        out_shape=(jax.ShapeDtypeStruct(x.shape, BF16), jax.ShapeDtypeStruct((TWO,) * THREE + (TWO * n, HEAD_DIM), BF16)),
+        in_specs=[tile] + whole + [rope, rope],
+        out_specs=[tile, pl.BlockSpec((TWO, ONE, TWO, n, HEAD_DIM), lambda i: (0, i // TWO, 0, i % TWO, 0))],
+        compiler_params=params(63),
         cost_estimate=cost(TWO, 7),
     )(x, gain, w_k, w_v, cos_f, sin_f)
 
@@ -353,7 +357,7 @@
 def exchange_kernel(*refs):
     take = taker(refs)
     kv_ref, h_ref, dy_ref, pos_ref, cos_ref, sin_ref, wq_ref, wo_ref, kv_all, q_u, do_u, pos_u, *dy_rows = take(14)
-    own_sem, quad_s, quad_r, z_s, z_r, y_s, y_r, q_home, do_home, wq_buf, wo_buf, w_sem, dy_sem = take(len(refs))
+    own_sem, quad_s, quad_r, z_s, z_r, y_s, y_r, q_home, do_home, wq_buf, wo_buf, w_sem, dy_sem, h_own, dy_own = take(len(refs))
     me = lax.axis_index("cp")
     z, y, x, core = place(me)
     quad, line = quad_of(me), Line(me)
@@ -409,20 +413,29 @@
         home[t // n, :, :, :, :, aligned(lax.rem(t, n))] = val.astype(BF16).reshape(home.shape[1:-1] + (BLK,))
 
     def query(t, slot):
-        q = jnp.dot(h_ref[...], wq_buf[slot], preferred_element_type=F32)
+        q = jnp.dot(h_own[...], wq_buf[slot], preferred_element_type=F32)
         put(q_home, t, jnp.hstack([turn(q[:, head_slice(j)], cos_ref, sin_ref) for j in range(BLK // HEAD_DIM)]))
 
     def pull(t, slot):
-        put(do_home, t, dot_t(dy_ref[...], wo_buf[slot]))
+        put(do_home, t, dot_t(dy_own[...], wo_buf[slot]))
 
     all_moves = list(moves)
-    half = dy_ref.shape[0] // TWO
-    for i, out in enumerate(dy_rows):
-        pltpu.make_async_copy(dy_ref.at[aligned(core if i == 0 else 1 - core, half)], out, dy_sem.at[i]).start()
+    loads = [pltpu.make_async_copy(a, b, dy_sem.at[i]) for i, (a, b) in enumerate(((h_ref, h_own), (dy_ref, dy_own)))]
+    half = dy_own.shape[0] // TWO
+
+    def dy_copy(i):
+        return pltpu.make_async_copy(dy_own.at[aligned(1 - core if i else core, half)], dy_rows[i], dy_sem.at[i])
+
     for a in (0, THREE):
         for d in (1, TWO, THREE):
             quad_copy(a, d).start()
         own_copy(a).start()
+    for c in loads:
+        c.start()
+    for c in loads:
+        c.wait()
+    for i in range(TWO):
+        dy_copy(i).start()
     for a, (fetch, use) in enumerate(((fetch_q, query), (fetch_o, pull)), 1):
         for near in range(TWO):
             tiled(n, fetch, use, n * (x if near else 1 - x))
@@ -449,8 +462,8 @@
                 quad_copy(a, d).wait_recv()
     for a in (1, TWO, THREE):
         own_copy(a).wait()
-    for i, out in enumerate(dy_rows):
-        pltpu.make_async_copy(dy_ref.at[aligned(core if i == 0 else 1 - core, half)], out, dy_sem.at[i]).wait()
+    for i in range(TWO):
+        dy_copy(i).wait()
 
 
 def exchange(kv, h, dy, pos, cos_f, sin_f, w_q, w_o):
@@ -467,9 +480,9 @@
         exchange_kernel,
         name="exchange",
         out_shape=(jax.ShapeDtypeStruct((N_PAIRS,) + (TWO,) * THREE + (BLK, HEAD_DIM), BF16), unit, unit, pos_quad, dy_half, dy_half),
-        in_specs=[vmem] * 6 + [hbm] * TWO,
+        in_specs=[vmem] + [hbm] * TWO + [vmem] * THREE + [hbm] * TWO,
         out_specs=[hbm] * 6,
-        scratch_shapes=sems + [home, home] + bufs + [dma((TWO, TWO)), dma((TWO,))],
+        scratch_shapes=sems + [home, home] + bufs + [dma((TWO, TWO)), dma((TWO,))] + [pltpu.VMEM(h.shape, BF16)] * TWO,
         compiler_params=params(63, collective_id=1),
         cost_estimate=cost(1, 20),
     )(kv, h, dy, pos, cos_f, sin_f, w_q, w_o)
@@ -483,7 +496,7 @@
 def wo_kernel(*refs):
     take = taker(refs)
     o_ref, *pieces = take(5)
-    keep, away, dy_u, o_t, terms, came, load_sem, core_s, core_r = take(len(refs))
+    keep_ref, away_ref, dy_u, o_t, terms, came, load_sem, core_s, core_r, keep, away, out_sem = take(len(refs))
     me = lax.axis_index("cp")
     _, y, _, core = place(me)
     all_here = announce(quad_of(me)[1:TWO])
@@ -513,10 +526,20 @@
     half_terms(1 - core, 0, lambda t: swap(t).start())
     half_terms(core, 1, lambda t: swap(t).wait_recv())
     rows = keep.shape[1]
+
+    def results(zz):
+        pairs = (keep, keep_ref), (away, away_ref)
+        return [pltpu.make_async_copy(a.at[zz], b.at[zz], out_sem.at[i, zz]) for i, (a, b) in enumerate(pairs)]
+
     for zz in range(FOUR):
         for out, yy in ((keep, y), (away, 1 - y)):
             at = aligned(TWO * zz + yy, rows)
             out[zz] = terms[1, at] + came[at]
+        for c in results(zz):
+            c.start()
+    for zz in range(FOUR):
+        for c in results(zz):
+            c.wait()
     for t in range(tiles):
         swap(t).wait_send()
 
@@ -531,9 +554,11 @@
         name="wo_terms",
         out_shape=[jax.ShapeDtypeStruct((FOUR, half // N_PAIRS, d), F32)] * TWO,
         in_specs=[vmem] + [hbm] * FOUR,
-        out_specs=[vmem] * TWO,
+        out_specs=[hbm] * TWO,
         scratch_shapes=[pltpu.VMEM((TWO, TWO, BLK, d), BF16), pltpu.VMEM((wide, n), BF16)]
-        + [pltpu.VMEM((TWO, half, d), F32), pltpu.VMEM((half, d), F32), dma((FOUR,)), dma((d // BLK,)), dma((d // BLK,))],
+        + [pltpu.VMEM((TWO, half, d), F32), pltpu.VMEM((half, d), F32), dma((FOUR,)), dma((d // BLK,)), dma((d // BLK,))]
+        + [pltpu.VMEM((FOUR, half // N_PAIRS, d), F32)] * TWO
+        + [dma((TWO, FOUR))],
         compiler_params=params(63, collective_id=THREE),
         cost_estimate=cost(FOUR, 20),
     )(o, *pieces)
@@ -759,8 +784,8 @@
 
     def __init__(self, me, ins, outs, scratch):
         attn, self.dq, hidden, normed, self.w_o, self.w_q = ins
-        self.block_out, self.d_part, self.h_u = outs
-        self.attn_home, self.dq_home, self.buf_o, self.buf_q, stage, self.h_buf, *sems = scratch
+        self.out_refs, self.h_u = outs[:TWO], outs[TWO]
+        self.block_out, self.d_part, self.attn_home, self.dq_home, self.buf_o, self.buf_q, stage, self.h_buf, *sems = scratch
         self.w_sem, self.load_sem, own_sem, quad_s, quad_r = sems
         _, _, _, core = place(me)
 
@@ -792,14 +817,15 @@
         buf = [pltpu.VMEM((TWO,) + b, BF16) for b in ((d, BLK), (BLK, d))]
         tiles = [pltpu.VMEM((TWO, TWO) + b, BF16) for b in ((CHUNK, d), (TWO, BLK, BLK))]
         sems = [dma((TWO, TWO)), dma((TWO,)), dma((FOUR,)), dma((THREE, FOUR)), dma((THREE, FOUR))]
-        return [home] * TWO + buf + tiles + sems
+        products = [pltpu.VMEM(arrays[TWO].shape, t) for t in (BF16, F32)]
+        return products + [home] * TWO + buf + tiles + sems
 
     @staticmethod
     def results(arrays):
         unit = TWO, TWO, BLK, arrays[-1].shape[0]
         return [jax.ShapeDtypeStruct(arrays[TWO].shape, t) for t in (BF16, F32)] + [jax.ShapeDtypeStruct(unit, BF16)]
 
-    spaces, out_spaces = [pl.ANY, pltpu.VMEM] + [pl.ANY] * FOUR, [pltpu.VMEM] * TWO + [pl.ANY]
+    spaces, out_spaces = [pl.ANY, pltpu.VMEM] + [pl.ANY] * FOUR, [pl.ANY] * THREE
 
     def step(self, t):
         def fetch_o(t, slot):
@@ -824,6 +850,11 @@
             if i == 0:
                 self.residual.wait()
             tiled(self.w_o.shape[0] // BLK, *((fetch_o, project), (fetch_q, pull))[i])
+            self.write(i).start()
+
+    def write(self, i):
+        src = (self.block_out, self.d_part)[i]
+        return pltpu.make_async_copy(src, self.out_refs[i], self.w_sem.at[i, 0])
 
     def wq_terms(self, own, other):
         self.h_mine.wait()
@@ -848,15 +879,22 @@
     def finish(self):
         for c in self.h_copies + self.homes:
             c.wait_send()
+        for i in range(TWO):
+            self.write(i).wait()
 
 
 class HiddenGradient:
     tiles = FOUR
 
     def __init__(self, me, dk, dv, ins, outs, scratch):
-        self.part, self.w_k, self.w_v, self.x, self.dy, self.gain = ins
+        self.part, w_k, w_v, self.x, self.dy, self.gain = ins
         self.dx, self.terms = outs
-        self.dk_home, self.dv_home, self.rows, *sems = scratch
+        self.dk_home, self.dv_home, self.rows, self.w_k, self.w_v, *rest = scratch
+        self.part_tile, self.x_tile, self.dy_tile, self.dx_tile, self.tile_sem, *sems = rest
+        pairs = (w_k, self.w_k), (w_v, self.w_v)
+        self.weights = [pltpu.make_async_copy(src, dst, self.tile_sem.at[i]) for i, (src, dst) in enumerate(pairs)]
+        for c in self.weights:
+            c.start()
         pairs = (dk, self.dk_home), (dv, self.dv_home)
         self.homes = [Home(me, src, out, *[r.at[i] for r in sems]) for i, (src, out) in enumerate(pairs)]
         for h in self.homes:
@@ -866,25 +904,40 @@
     def scratch(x):
         dma = pltpu.SemaphoreType.DMA
         home = pltpu.VMEM((TWO,) * THREE + (CHUNK, TWO * HEAD_DIM), BF16)
-        return [home, home, pltpu.VMEM((8, x.shape[1]), F32), dma((TWO,)), dma((TWO, FOUR)), dma((TWO, FOUR))]
+        tile = TWO * CHUNK, x.shape[1]
+        weight = pltpu.VMEM((x.shape[1], TWO * HEAD_DIM), BF16)
+        tiles = [pltpu.VMEM(tile, F32)] + [pltpu.VMEM(tile, BF16)] * THREE
+        sems = [dma((FOUR,)), dma((TWO,)), dma((TWO, FOUR)), dma((TWO, FOUR))]
+        return [home, home, pltpu.VMEM((8, x.shape[1]), F32), weight, weight] + tiles + sems
 
     def tile(self, t):
         if t == 0:
+            for c in self.weights:
+                c.wait()
             for h in self.homes:
                 h.wait_recv()
             self.rows[...] = jnp.zeros_like(self.rows)
         size = TWO * CHUNK
         at = pl.ds(t * size, size)
-        d = self.part[at]
+        pairs = (self.part, self.part_tile), (self.x, self.x_tile), (self.dy, self.dy_tile)
+        loads = [pltpu.make_async_copy(src.at[at], dst, self.tile_sem.at[i]) for i, (src, dst) in enumerate(pairs)]
+        for c in loads:
+            c.start()
+        for c in loads:
+            c.wait()
+        d = self.part_tile[...]
         for home, w in ((self.dk_home, self.w_k), (self.dv_home, self.w_v)):
             d += dot_t(home[t // TWO, t % TWO].reshape(size, -1), w[...])
         d = d.astype(BF16).astype(F32)
-        x = self.x[at].astype(F32)
+        x = self.x_tile[...].astype(F32)
         inv_rms = lax.rsqrt(row_mean(x * x) + NORM_EPS)
         unit, scaled = x * inv_rms, d * self.gain[...]
         dx = inv_rms * (scaled - unit * row_mean(scaled * unit))
-        self.dx[at] = (self.dy[at].astype(F32) + dx).astype(BF16)
+        self.dx_tile[...] = (self.dy_tile[...].astype(F32) + dx).astype(BF16)
+        store = pltpu.make_async_copy(self.dx_tile, self.dx.at[at], self.tile_sem.at[THREE])
+        store.start()
         self.rows[...] += jnp.sum((d * unit).reshape((-1,) + self.rows.shape), axis=0)
+        store.wait()
         if t == self.tiles - 1:
             self.terms[...] = jnp.sum(self.rows[...], axis=0, keepdims=True)
 
@@ -961,14 +1014,19 @@
     dv_u[...] = dkv_ref[pl.ds(n, n)].astype(BF16).reshape(dv_u.shape)
 
 
-def wkv_terms(h_own, dk_u, dv_u, outs):
+def wkv_terms(h_ref, h_buf, sem, dk_u, dv_u, outs):
     d_out = jnp.hstack([r[...].reshape(-1, HEAD_DIM) for r in (dk_u, dv_u)])
+
+    def fetch(t, slot):
+        return pltpu.make_async_copy(h_ref.at[:, :, :, aligned(t)], h_buf.at[slot], sem.at[slot])
+
     for out, half in outs:
 
-        @pl.loop(0, FOUR)
-        def _(zz, out=out, half=half):
-            h = h_own[:, :, :, aligned(half * FOUR + zz)].reshape(-1, BLK)
-            out[zz] = dot(h, d_out, (0,), (0,)).reshape(out.shape[1:])
+        def use(t, slot, out=out, half=half):
+            h = h_buf[slot].reshape(-1, BLK)
+            out[t - half * FOUR] = dot(h, d_out, (0,), (0,)).reshape(out.shape[1:])
+
+        tiled(FOUR, fetch, use, half * FOUR)
 
 
 def gather_kernel(*refs):
@@ -976,7 +1034,7 @@
     wo_ref, wq_ref, dkv_ref, cos_ref, sin_ref, h_ref = take(6)
     grad_ins, outs, (dx_ref, dgain_ref) = take(6), take(FOUR), take(TWO)
     own_sem, send_sem, come_sem, core_sem, put_sem, all_terms, totals, g_s, g_r = take(9)
-    terms, wkv_ref, h_own, dk_u, dv_u, store, wkv_store = take(7)
+    terms, wkv_ref, h_buf, h_sem, dk_u, dv_u, store, wkv_store = take(8)
     buffers, sems, refs = take(FOUR), take(7), take(len(refs))
     me = lax.axis_index("cp")
     z, y, x, core = place(me)
@@ -991,8 +1049,6 @@
         store[chip_here, pl.ds(n_wo, n_wo), pl.ds(i * wide, wide)] = wq_ref[pl.ds(i * n_wo, n_wo)]
     turn_back(dkv_ref, cos_ref, sin_ref, dk_u, dv_u)
     all_here()
-    load_h = pltpu.make_async_copy(h_ref, h_own, own_sem.at[0])
-    load_h.start()
     wkv = PairSum(me, "core", 1, wkv_ref, wkv_store.at[chip_here], buffers, [r.at[0] for r in sems])
 
     def place_of(key):
@@ -1080,8 +1136,7 @@
     for part in range(THREE):
         pass_on(part, HERE)
     job = HiddenGradient(me, dk_u, dv_u, grad_ins, (dx_ref, terms), refs)
-    load_h.wait()
-    wkv_terms(h_own, dk_u, dv_u, ((wkv_ref, 1 - core), (buffers[0], core)))
+    wkv_terms(h_ref, h_buf, h_sem, dk_u, dv_u, ((wkv_ref, 1 - core), (buffers[0], core)))
     wkv.begin(0)
     wkv.loaded(0)
     for now, part, key in events:
@@ -1116,7 +1171,7 @@
     scratch = [dma((1,)), dma(keys + (len(LINKS) + 1,)), dma(keys), dma(keys), dma(keys)]
     n = len(GAIN_AT)
     scratch += [pltpu.VMEM((n,) + terms, F32)] * TWO + [dma((n,)), dma((n,)), pltpu.VMEM(terms, F32)]
-    scratch += [pltpu.VMEM((FOUR, TWO) + block, F32), pltpu.VMEM(h_u.shape, BF16)]
+    scratch += [pltpu.VMEM((FOUR, TWO) + block, F32), pltpu.VMEM((TWO, TWO, TWO, BLK, BLK), BF16), dma((TWO,))]
     scratch += [pltpu.VMEM((TWO, TWO, BLK, HEAD_DIM), BF16)] * TWO
     scratch += [pltpu.VMEM((TWO * N_PAIRS,) + b, F32) for b in ((TWO * wo.shape[0], wo.shape[1]), block)]
     return pl.pallas_call(
@@ -1124,8 +1179,8 @@
         name="gather_all",
         out_shape=[jax.ShapeDtypeStruct(s, F32) for s in shapes]
         + [jax.ShapeDtypeStruct(x.shape, BF16), jax.ShapeDtypeStruct(terms, F32)],
-        in_specs=[vmem] * 5 + [hbm] + [vmem] * 6,
-        out_specs=[hbm] * len(shapes) + [vmem] * TWO,
+        in_specs=[vmem] * 5 + [hbm] * 6 + [vmem],
+        out_specs=[hbm] * (len(shapes) + 1) + [vmem],
         scratch_shapes=scratch + PairSum.scratch("core", block) + PairSum.sems(1, 1) + HiddenGradient.scratch(x),
         compiler_params=params(63, collective_id=0),
         cost_estimate=cost(1, 76),

time: 551 us -> 544 us (0.987)
    pallas_call x1, Pallas kernels: 174 us -> 168 us  [gather_all(): pl.pallas_call(gather_kernel, name='gather_all', out_shape=[jax.ShapeDtyp...]
    unnamed x39 -> x23, local copies, waits for them, and re-layouts: 35.2 us -> 30.4 us
where the time goes in v15:
time: 544 us; the launch traced here: 540 us
  Pallas kernels  449 us (83%)
  waiting for transfers between devices  46.1 us (8%)
  local copies, waits for them, and re-layouts  34.2 us (6%)
  other arithmetic  7.73 us (1%)
    pallas_call x1, Pallas kernels, gather_all(): pl.pallas_call(gather_kernel, name='gather_all', out_shape=[jax.ShapeDtyp...  168 us
    pallas_call x1, Pallas kernels, reduce_pairs(): pl.pallas_call(functools.partial(reduce_kernel, cuts, kinds, work), name=...  156 us
    pallas_call x1, Pallas kernels, exchange(): pl.pallas_call(exchange_kernel, name='exchange', out_shape=(jax.ShapeDtyp...  64.1 us
    ppermute x4, waiting for transfers between devices, perm(): return lax.ppermute(x, 'cp', pairs)  46.1 us
    unnamed x23, local copies, waits for them, and re-layouts  30.4 us
    pallas_call x1, Pallas kernels, flash_bwd(): pl.pallas_call(bwd_kernel, name='attn_bwd', out_shape=(jax.ShapeDtypeStru...  23.4 us
    pallas_call x1, Pallas kernels, flash_fwd(): pl.pallas_call(fwd_kernel, name='attn_fwd', out_shape=(jax.ShapeDtypeStru...  18 us
    pallas_call x1, Pallas kernels, wo_terms(): pl.pallas_call(wo_kernel, name='wo_terms', out_shape=[jax.ShapeDtypeStruc...  13.3 us
  transfers between devices with their start and end apart: 4, of which 2 were waited for; matrix products, arithmetic and copies ran while one was open for 1% of the time, Pallas kernels for 8%

profile of v15, /device:TPU:0, one launch (start us, length us, event | category | flops | bytes accessed | tf_op | source)
XLA Modules:
  0.0 540.4 jit_solution(11175176085208532859)
XLA Ops:
  0.6 0.7 convert_bitcast_fusion
  1.3 1.3 broadcast_in_dim.9
  2.6 1.3 pad.4.refs_3_
  3.9 1.0 fusion
  4.9 1.0 pad_maximum_fusion
  5.9 5.7 %norm_kv.1 = (bf16[512,2048]{1,0:T(8,128)(2,1)}, bf16[2,2,2,256,128]{4,3,2,1,0:T(8,128)(2,1)}) custom-call(bf16[512,2048]{1,0:T(8,128)(2,1)} %bitcast.28, f32[1,2048]{1,0:T(1,128)} %bitcast.36, bf16[2048,256]{1,0:T(8,128)(2,1)} %refs_7_.5, bf16[2048,256]{1,0:T(8,128)(2,1)} %refs_8_.3, f32[512,128]{1,0:T(8,128)} %get-tuple-element.74.cos_ref.refs_4_, ...), custom_call_target="tpu_custom_call" | custom-call | flops 2000000000 | bytes 7340032 | tf_op jit(solution)/shard_map/norm_kv/pallas_call | solution.py:280
  11.6 64.1 %exchange.1 = (bf16[8,2,2,2,256,128]{5,4,3,2,1,0:T(8,128)(2,1)}, bf16[2,2,256,1024]{3,2,1,0:T(8,128)(2,1)}, bf16[2,2,256,1024]{3,2,1,0:T(8,128)(2,1)}, s32[4,8,1...) custom-call(bf16[2,2,2,2,2,64,128]{6,5,4,3,2,1,0:T(8,128)(2,1)} %bitcast.35, ...), custom_call_target="tpu_custom_call" | custom-call | flops 1000000000 | bytes 20971520 | tf_op jit(solution)/shard_map/exchange/pallas_call | solution.py:479
  75.7 1.6 collective-permute-start
  77.3 0.5 collective-permute-start.1
  78.5 0.6 broadcast_in_dim.8.ko_ref
  79.1 0.7 slice.3
  80.0 0.2 subtract_reduce_fusion.1
  80.4 0.6 pad_add_fusion.1.tab
  81.1 0.6 broadcast_subtract_fusion.st_ref
  81.7 0.6 sub.45.qi_ref
  82.3 18.0 %attn_fwd.1 = (bf16[2,2,256,1024]{3,2,1,0:T(8,128)(2,1)}, f32[2,2,8,1,256]{4,3,2,1,0:T(1,128)}) custom-call(s32[10]{0:T(128)} %pad_add_fusion.1.tab, bf16[2,2,256,1024]{3,2,1,0:T(8,128)(2,1)} %get-tuple-element.39.q_ref, bf16[8,2,2,2,256,128]{5,4,3,2,1,0:T(8,128)(2,1)} %get-tuple-element.40.kv_ref, s32[2,2,1,256]{3,2,1,0:T(1,128)} %broadcast_subtract_fusion.st_ref, ...), custom_call_target="tpu_custom_call" | custom-call | flops 20000000000 | bytes 16777216 | tf_op jit(solution)/shard_map/attn_fwd/pallas_call | solution.py:218
  100.3 1.8 multiply_sine_fusion
  102.1 21.8 %collective-permute-done.1.refs_3_ = bf16[2,2,64,2048]{3,2,1,0:T(8,128)(2,1)} collective-permute-done((bf16[2,2,64,2048]{3,2,1,0:T(8,128)(2,1)}, bf16[2,2,64,2048]{3,2,1,0:T(8,128)(2,1)}, u32[]{:S(2)}, u32[]{:S(2)}) %collective-permute-start.1) | collective-permute-done | bytes 1048608 | tf_op jit(solution)/shard_map/ppermute | solution.py:1191
  124.0 13.3 %wo_terms.1 = (f32[4,64,2048]{2,1,0:T(8,128)}, f32[4,64,2048]{2,1,0:T(8,128)}) custom-call(bf16[2,2,256,1024]{3,2,1,0:T(8,128)(2,1)} %get-tuple-element.41.refs_0_.o_ref.refs_3_, bf16[2,2,64,2048]{3,2,1,0:T(8,128)(2,1)} %bitcast.41, bf16[2,2,64,2048]{3,2,1,0:T(8,128)(2,1)} %collective-permute-done.refs_2_, ...), custom_call_target="tpu_custom_call" | custom-call | flops 4000000000 | bytes 20971520 | tf_op jit(solution)/shard_map/wo_terms/pallas_call | solution.py:552
  137.2 0.6 collective-permute-start.3
  137.8 23.4 %attn_bwd.1 = (bf16[2,2,256,1024]{3,2,1,0:T(8,128)(2,1)}, f32[8,2,2,2,256,128]{5,4,3,2,1,0:T(8,128)}) custom-call(s32[10]{0:T(128)} %pad_add_fusion.1.tab, bf16[2,2,256,1024]{3,2,1,0:T(8,128)(2,1)} %get-tuple-element.39.q_ref, bf16[2,2,256,1024]{3,2,1,0:T(8,128)(2,1)} %get-tuple-element.47.do_ref, ...), custom_call_target="tpu_custom_call" | custom-call | flops 49999998976 | bytes 33554432 | tf_op jit(solution)/shard_map/attn_bwd/pallas_call | solution.py:237
  161.2 24.3 %collective-permute-done.3.refs_1_ = f32[4,64,2048]{2,1,0:T(8,128)} collective-permute-done((f32[4,64,2048]{2,1,0:T(8,128)}, f32[4,64,2048]{2,1,0:T(8,128)}, u32[]{:S(2)}, u32[]{:S(2)}) %collective-permute-start.3) | collective-permute-done | bytes 2097184 | tf_op jit(solution)/shard_map/ppermute | solution.py:1191
  185.5 156.4 %reduce_pairs.1 = (f32[64,2048]{1,0:T(8,128)}, f32[2048,128]{1,0:T(8,128)}, f32[128,1024]{1,0:T(8,128)}, bf16[512,2048]{1,0:T(8,128)(2,1)}, f32[512,2048]{1,0:T(8,128)}, /*index=5*/bf16[2,2,256,2048]{3,2,1,0:T(8,128)(2,1)}) custom-call(f32[4,64,2048]{2,1,0:T(8,128)} %get-tuple-element.45.refs_0_, f32[4,64,2048]{2,1,0:T(8,128)} %collective-permute-done.3.refs_1_, ...), custom_call_target="tpu_custom_call" | custom-call | flops 1000000000 | bytes 20971520 | tf_op jit(solution)/shard_map/reduce_pairs/pallas_call | solution.py:955
  342.0 167.9 %gather_all.1 = (f32[2048,2048]{1,0:T(8,128)}, f32[2048,2048]{1,0:T(8,128)}, f32[2048,256]{1,0:T(8,128)}, f32[2048,256]{1,0:T(8,128)}, bf16[512,2048]{1,0:T(8,128)(2,1)}, /*index=5*/f32[1,2048]{1,0:T(1,128)}) custom-call(f32[64,2048]{1,0:T(8,128)} %get-tuple-element.52.refs_0_, f32[128,1024]{1,0:T(8,128)} %get-tuple-element.53.refs_1_, ...), custom_call_target="tpu_custom_call" | custom-call | flops 1000000000 | bytes 79691776 | tf_op jit(solution)/shard_map/gather_all/pallas_call | solution.py:1177
  509.9 3.3 copy.30
  513.2 1.3 copy.31
  514.5 14.6 %copy.32 = f32[2048,2048]{1,0:T(8,128)} copy(f32[2048,2048]{1,0:T(8,128)} %get-tuple-element.87) | data formatting | bytes 33554432
  529.2 1.3 copy.33
  530.5 1.8 copy-done
  532.3 1.3 copy.34
  533.6 6.2 %copy.35 = f32[2048,2048]{1,0:T(8,128)} copy(f32[2048,2048]{1,0:T(8,128)S(1)} %bitcast.25) | data formatting | bytes 33554432
  539.8 0.6 copy.36
  (37 shorter events, 1.2 us)
Async XLA Ops:
  75.7 48.3 %collective-permute-start.2 = (bf16[2,2,64,2048]{3,2,1,0:T(8,128)(2,1)}, bf16[2,2,64,2048]{3,2,1,0:T(8,128)(2,1)}, u32[]{:S(2)}, u32[]{:S(2)}) collective-permute-start(bf16[2,2,64,2048]{3,2,1,0:T(8,128)(2,1)} %bitcast.42), channel_id=1, source_target_pairs={{0,3},{1,2},{2,1},{3,0},{4,7},{5,6},{6,5},{7,4},{8,11},{9,10},{10,... | collective-permute-start | bytes 3145736 | tf_op jit(solution)/shard_map/ppermute | solution.py:1191
  75.7 48.2 %collective-permute-start = (bf16[2,2,64,2048]{3,2,1,0:T(8,128)(2,1)}, bf16[2,2,64,2048]{3,2,1,0:T(8,128)(2,1)}, u32[]{:S(2)}, u32[]{:S(2)}) collective-permute-start(bf16[2,2,64,2048]{3,2,1,0:T(8,128)(2,1)} %bitcast.43), channel_id=1, source_target_pairs={{0,1},{1,0},{2,3},{3,2},{4,5},{5,4},{6,7},{7,6},{8,9},{9,8},{10,11... | collective-permute-start | bytes 3145736 | tf_op jit(solution)/shard_map/ppermute | solution.py:1191
  77.3 46.6 %collective-permute-start.1 = (bf16[2,2,64,2048]{3,2,1,0:T(8,128)(2,1)}, bf16[2,2,64,2048]{3,2,1,0:T(8,128)(2,1)}, u32[]{:S(2)}, u32[]{:S(2)}) collective-permute-start(bf16[2,2,64,2048]{3,2,1,0:T(8,128)(2,1)} %bitcast.40), channel_id=1, source_target_pairs={{0,2},{1,3},{2,0},{3,1},{4,6},{5,7},{6,4},{7,5},{8,10},{9,11},{10,... | collective-permute-start | bytes 3145736 | tf_op jit(solution)/shard_map/ppermute | solution.py:1191
  137.2 48.3 %collective-permute-start.3 = (f32[4,64,2048]{2,1,0:T(8,128)}, f32[4,64,2048]{2,1,0:T(8,128)}, u32[]{:S(2)}, u32[]{:S(2)}) collective-permute-start(f32[4,64,2048]{2,1,0:T(8,128)} %get-tuple-element.46), channel_id=1, source_target_pairs={{0,4},{1,5},{2,6},{3,7},{4,0},{5,1},{6,2},{7,3},{8,12},{9,13},{10,... | collective-permute-start | bytes 6291464 | tf_op jit(solution)/shard_map/ppermute | solution.py:1191
  509.9 3.3 copy-start.2
  513.2 20.4 %slice-start = ((s8[16777216]{0:T(1024)(128)(4,1)}), s8[4194304]{0:T(1024)(128)(4,1)S(1)}, s32[]{:S(2)}) async-start(s8[16777216]{0:T(1024)(128)(4,1)} %bitcast.24), calls=%async_computation | async-start | bytes 8388608
  514.5 14.6 %copy-start.1 = (f32[2048,256]{1,0:T(8,128)S(1)}, f32[2048,256]{1,0:T(8,128)}, u32[]{:S(2)}) copy-start(f32[2048,256]{1,0:T(8,128)} %get-tuple-element.88) | copy-start | bytes 6291460
  514.5 19.0 %slice-start.1 = ((s8[16777216]{0:T(1024)(128)(4,1)}), s8[4194304]{0:T(1024)(128)(4,1)S(1)}, s32[]{:S(2)}) async-start(s8[16777216]{0:T(1024)(128)(4,1)} %bitcast.24), calls=%async_computation.1 | async-start | bytes 8388608
  514.5 19.0 %slice-start.2 = ((s8[16777216]{0:T(1024)(128)(4,1)}), s8[4194304]{0:T(1024)(128)(4,1)S(1)}, s32[]{:S(2)}) async-start(s8[16777216]{0:T(1024)(128)(4,1)} %bitcast.24), calls=%async_computation.2 | async-start | bytes 8388608
  514.5 19.0 %slice-start.3 = ((s8[16777216]{0:T(1024)(128)(4,1)}), s8[4194304]{0:T(1024)(128)(4,1)S(1)}, s32[]{:S(2)}) async-start(s8[16777216]{0:T(1024)(128)(4,1)} %bitcast.24), calls=%async_computation.3 | async-start | bytes 8388608
  529.1 3.1 copy-start
  533.6 6.2 %copy-start.3 = (f32[1,2048]{1,0:T(1,128)S(1)}, f32[1,2048]{1,0:T(1,128)}, u32[]{:S(2)}) copy-start(f32[1,2048]{1,0:T(1,128)} %get-tuple-element.62) | copy-start | bytes 24580
